TPU v7x, 8 devices: a whole 2x2x1 slice. The times are simulated.
8 devices in a mesh: dp: 1 (over z), cp: 8 (over y, x, core).
Axes of the slice: x: 2, y: 2, z: 1, core: 2. Of those that a mesh axis runs over, the one named last changes fastest.
Arguments:
- query: bfloat16 [32, 1024, 8, 256], P('dp', 'cp')
- keys: bfloat16 [32, 1024, 1, 256], P('dp', 'cp')
- values: bfloat16 [32, 1024, 1, 256], P('dp', 'cp')
- grad_out: bfloat16 [32, 1024, 8, 256], P('dp', 'cp')
- doc_id: int32 [32, 1024], P('dp', 'cp')
Outputs:
- output 1: bfloat16 [32, 1024, 8, 256], P('dp', 'cp')
- output 2: bfloat16 [32, 1024, 8, 256], P('dp', 'cp')
- output 3: bfloat16 [32, 1024, 1, 256], P('dp', 'cp')
- output 4: bfloat16 [32, 1024, 1, 256], P('dp', 'cp')
All inputs are finite; a program needn't handle non-finite values.
Results may differ from a plain program's by a relative error of at most 0.0107405.
Values are sent between devices in bfloat16 or wider.
A program may use at most 1 GiB of HBM per device.

v0:
```python
import jax
import jax.numpy as jnp
from jax import lax
from jax.sharding import PartitionSpec as P, NamedSharding

NEG_BIG = -1e30


def solution(mesh):
    n_grp = mesh.shape['cp']
    to_next = [(src_dev, (src_dev + 1) % n_grp) for src_dev in range(n_grp)]
    seq_spec = P('dp', 'cp', None, None)
    id_spec = P('dp', 'cp')

    def per_device(query, keys, values, grad_out, doc_id):
        n_batch, piece_len, n_heads, head_dim = query.shape
        score_scale = head_dim ** -0.5
        dev_rank = lax.axis_index('cp')
        offsets = jnp.arange(piece_len)
        q_pos = dev_rank * piece_len + offsets
        key_loc = keys[:, :, 0, :]
        val_loc = values[:, :, 0, :]

        def masked_scores(step, key_cur, doc_cur):
            src_rank = (dev_rank - step) % n_grp
            k_pos = src_rank * piece_len + offsets
            causal = k_pos[None, :] <= q_pos[:, None]
            same_doc = doc_id[:, :, None] == doc_cur[:, None, :]
            visible = (causal[None] & same_doc)[:, :, None, :]
            raw_scores = jnp.einsum('crie,cle->cril', query, key_cur, preferred_element_type=jnp.float32)
            return jnp.where(visible, raw_scores * score_scale, NEG_BIG), visible

        def stats_update(step, key_cur, doc_cur, row_max, row_sum):
            scores, visible = masked_scores(step, key_cur, doc_cur)
            new_max = jnp.maximum(row_max, jnp.max(scores, axis=-1))
            exp_scores = jnp.where(visible, jnp.exp(scores - new_max[..., None]), 0.0)
            new_sum = row_sum * jnp.exp(row_max - new_max) + jnp.sum(exp_scores, axis=-1)
            return new_max, new_sum

        def stats_body(step, carry):
            key_cur, doc_cur, row_max, row_sum = carry
            key_cur = lax.ppermute(key_cur, 'cp', to_next)
            doc_cur = lax.ppermute(doc_cur, 'cp', to_next)
            row_max, row_sum = stats_update(step, key_cur, doc_cur, row_max, row_sum)
            return key_cur, doc_cur, row_max, row_sum

        stat_shape = (n_batch, piece_len, n_heads)
        row_max, row_sum = stats_update(0, key_loc, doc_id, jnp.full(stat_shape, NEG_BIG, jnp.float32), jnp.zeros(stat_shape, jnp.float32))
        stats_out = lax.fori_loop(1, n_grp, stats_body, (key_loc, doc_id, row_max, row_sum))
        log_norm = stats_out[2] + jnp.log(stats_out[3])

        def prob_at(step, key_cur, doc_cur):
            scores = masked_scores(step, key_cur, doc_cur)[0]
            return jnp.exp(scores - log_norm[..., None])

        def out_update(step, key_cur, val_cur, doc_cur, out_acc):
            prob_bf16 = prob_at(step, key_cur, doc_cur).astype(jnp.bfloat16)
            return out_acc + jnp.einsum('cril,cle->crie', prob_bf16, val_cur, preferred_element_type=jnp.float32)

        def out_body(step, carry):
            key_cur, val_cur, doc_cur, out_acc = carry
            key_cur = lax.ppermute(key_cur, 'cp', to_next)
            val_cur = lax.ppermute(val_cur, 'cp', to_next)
            doc_cur = lax.ppermute(doc_cur, 'cp', to_next)
            return key_cur, val_cur, doc_cur, out_update(step, key_cur, val_cur, doc_cur, out_acc)

        out_acc = out_update(0, key_loc, val_loc, doc_id, jnp.zeros(query.shape, jnp.float32))
        out_acc = lax.fori_loop(1, n_grp, out_body, (key_loc, val_loc, doc_id, out_acc))[3]
        attn_out = out_acc.astype(jnp.bfloat16)
        row_delta = jnp.einsum('bqhd,bqhd->bqh', grad_out, attn_out, preferred_element_type=jnp.float32)

        def grad_update(step, key_cur, val_cur, doc_cur, dq_acc, dk_acc, dv_acc):
            prob_f32 = prob_at(step, key_cur, doc_cur)
            prob_bf16 = prob_f32.astype(jnp.bfloat16)
            grad_prob = jnp.einsum('crie,cle->cril', grad_out, val_cur, preferred_element_type=jnp.float32)
            grad_score = (prob_f32 * (grad_prob - row_delta[..., None])).astype(jnp.bfloat16)
            dq_acc = dq_acc + jnp.einsum('cril,cle->crie', grad_score, key_cur, preferred_element_type=jnp.float32)
            dk_acc = dk_acc + jnp.einsum('cril,crie->cle', grad_score, query, preferred_element_type=jnp.float32)
            dv_acc = dv_acc + jnp.einsum('cril,crie->cle', prob_bf16, grad_out, preferred_element_type=jnp.float32)
            return dq_acc, dk_acc, dv_acc

        def grad_body(step, carry):
            key_cur, val_cur, doc_cur, dq_acc, dk_acc, dv_acc = carry
            key_cur = lax.ppermute(key_cur, 'cp', to_next)
            val_cur = lax.ppermute(val_cur, 'cp', to_next)
            doc_cur = lax.ppermute(doc_cur, 'cp', to_next)
            dk_acc = lax.ppermute(dk_acc, 'cp', to_next)
            dv_acc = lax.ppermute(dv_acc, 'cp', to_next)
            dq_acc, dk_acc, dv_acc = grad_update(step, key_cur, val_cur, doc_cur, dq_acc, dk_acc, dv_acc)
            return key_cur, val_cur, doc_cur, dq_acc, dk_acc, dv_acc

        kv_zero = jnp.zeros(key_loc.shape, jnp.float32)
        grads = grad_update(0, key_loc, val_loc, doc_id, jnp.zeros(query.shape, jnp.float32), kv_zero, kv_zero)
        grads = lax.fori_loop(1, n_grp, grad_body, (key_loc, val_loc, doc_id) + grads)
        dk_home = lax.ppermute(grads[4], 'cp', to_next)
        dv_home = lax.ppermute(grads[5], 'cp', to_next)
        grad_query = (grads[3] * score_scale).astype(jnp.bfloat16)
        grad_keys = (dk_home * score_scale).astype(jnp.bfloat16)[:, :, None, :]
        grad_values = dv_home.astype(jnp.bfloat16)[:, :, None, :]
        return attn_out, grad_query, grad_keys, grad_values

    return jax.shard_map(per_device, mesh=mesh, in_specs=(seq_spec, seq_spec, seq_spec, seq_spec, id_spec), out_specs=(seq_spec, seq_spec, seq_spec, seq_spec), check_vma=False)
```

profile of v0, /device:TPU:0, one launch (start us, length us, event | category | flops | bytes accessed | tf_op | source)
XLA Modules:
  0.0 2302.1 jit_solution(2514620616505606474)
XLA Ops:
  64.8 354.8 %while.70 = (s32[]{:T(128)}, bf16[32,128,256]{2,1,0:T(8,128)(2,1)}, s32[32,128]{1,0:T(8,128)}, f32[32,128,8]{1,2,0:T(8,128)S(1)}, f32[32,128,8]{1,2,0:T(8,128)S(...) while((s32[]{:T(128)}, bf16[32,128,256]{2,1,0:T(8,128)(2,1)}, ...), condition=%wide.region_5.6_spmd.clone, body=%wide.region_2.5_spmd.clone.sunk | while | flops 2182168832 | bytes 68454752 | solution.py:49
  455.0 598.0 %while.71 = (s32[]{:T(128)}, bf16[32,128,256]{2,1,0:T(8,128)(2,1)}, bf16[32,128,256]{2,1,0:T(8,128)(2,1)}, s32[32,128]{1,0:T(8,128)S(1)}, f32[32,128,8,256]{3,1,...) while((s32[]{:T(128)}, bf16[32,128,256]{2,1,0:T(8,128)(2,1)}, ...), condition=%wide.region_7.8_spmd.clone, body=%wide.region_6.7_spmd.clone.sunk | while | flops 4321198592 | bytes 114592144 | solution.py:68
  456.1 48.3 %collective-permute-done.4 = s32[32,128]{1,0:T(8,128)S(1)} collective-permute-done((s32[32,128]{1,0:T(8,128)S(1)}, s32[32,128]{1,0:T(8,128)S(1)}, u32[]{:S(2)}, u32[]{:S(2)}) %collective-permute-start.4) | collective-permute-done | bytes 16416 | tf_op jit(solution)/shard_map/while/body/eval_jaxpr/ppermute | solution.py:64
  509.6 31.2 %convolution_add_fusion.4 = f32[32,128,8,256]{3,1,2,0:T(8,128)} fusion(f32[32,128,8,256]{3,1,2,0:T(8,128)} %get-tuple-element.1315, bf16[32,128,8,256]{3,2,1,0:T(8,128)(2,1)} %get-tuple-element.1333, f32[32,128,8]{1,2,0:T(8,128)S(1)} %get-tuple-element.1334, pred[32,128,128]{2,1,0:T(8,128)(4,1)S(1)} %compare_and_fusion.8, ...), kind=kOutput, calls=%fused_computation.19.clone.1 | convolution fusion | flops 4320133120 | bytes 88735744 | tf_op jit(solution)/shard_map/while/body/eval_jaxpr/cril,cle->crie/dot_general | solution.py:58
  541.4 48.3 %collective-permute-done.4 = s32[32,128]{1,0:T(8,128)S(1)} collective-permute-done((s32[32,128]{1,0:T(8,128)S(1)}, s32[32,128]{1,0:T(8,128)S(1)}, u32[]{:S(2)}, u32[]{:S(2)}) %collective-permute-start.4) | collective-permute-done | bytes 16416 | tf_op jit(solution)/shard_map/while/body/eval_jaxpr/ppermute | solution.py:64
  595.0 31.2 %convolution_add_fusion.4 = f32[32,128,8,256]{3,1,2,0:T(8,128)} fusion(f32[32,128,8,256]{3,1,2,0:T(8,128)} %get-tuple-element.1315, bf16[32,128,8,256]{3,2,1,0:T(8,128)(2,1)} %get-tuple-element.1333, f32[32,128,8]{1,2,0:T(8,128)S(1)} %get-tuple-element.1334, pred[32,128,128]{2,1,0:T(8,128)(4,1)S(1)} %compare_and_fusion.8, ...), kind=kOutput, calls=%fused_computation.19.clone.1 | convolution fusion | flops 4320133120 | bytes 88735744 | tf_op jit(solution)/shard_map/while/body/eval_jaxpr/cril,cle->crie/dot_general | solution.py:58
  626.8 48.3 %collective-permute-done.4 = s32[32,128]{1,0:T(8,128)S(1)} collective-permute-done((s32[32,128]{1,0:T(8,128)S(1)}, s32[32,128]{1,0:T(8,128)S(1)}, u32[]{:S(2)}, u32[]{:S(2)}) %collective-permute-start.4) | collective-permute-done | bytes 16416 | tf_op jit(solution)/shard_map/while/body/eval_jaxpr/ppermute | solution.py:64
  680.3 31.2 %convolution_add_fusion.4 = f32[32,128,8,256]{3,1,2,0:T(8,128)} fusion(f32[32,128,8,256]{3,1,2,0:T(8,128)} %get-tuple-element.1315, bf16[32,128,8,256]{3,2,1,0:T(8,128)(2,1)} %get-tuple-element.1333, f32[32,128,8]{1,2,0:T(8,128)S(1)} %get-tuple-element.1334, pred[32,128,128]{2,1,0:T(8,128)(4,1)S(1)} %compare_and_fusion.8, ...), kind=kOutput, calls=%fused_computation.19.clone.1 | convolution fusion | flops 4320133120 | bytes 88735744 | tf_op jit(solution)/shard_map/while/body/eval_jaxpr/cril,cle->crie/dot_general | solution.py:58
  712.2 48.3 %collective-permute-done.4 = s32[32,128]{1,0:T(8,128)S(1)} collective-permute-done((s32[32,128]{1,0:T(8,128)S(1)}, s32[32,128]{1,0:T(8,128)S(1)}, u32[]{:S(2)}, u32[]{:S(2)}) %collective-permute-start.4) | collective-permute-done | bytes 16416 | tf_op jit(solution)/shard_map/while/body/eval_jaxpr/ppermute | solution.py:64
  765.7 31.2 %convolution_add_fusion.4 = f32[32,128,8,256]{3,1,2,0:T(8,128)} fusion(f32[32,128,8,256]{3,1,2,0:T(8,128)} %get-tuple-element.1315, bf16[32,128,8,256]{3,2,1,0:T(8,128)(2,1)} %get-tuple-element.1333, f32[32,128,8]{1,2,0:T(8,128)S(1)} %get-tuple-element.1334, pred[32,128,128]{2,1,0:T(8,128)(4,1)S(1)} %compare_and_fusion.8, ...), kind=kOutput, calls=%fused_computation.19.clone.1 | convolution fusion | flops 4320133120 | bytes 88735744 | tf_op jit(solution)/shard_map/while/body/eval_jaxpr/cril,cle->crie/dot_general | solution.py:58
  797.5 48.3 %collective-permute-done.4 = s32[32,128]{1,0:T(8,128)S(1)} collective-permute-done((s32[32,128]{1,0:T(8,128)S(1)}, s32[32,128]{1,0:T(8,128)S(1)}, u32[]{:S(2)}, u32[]{:S(2)}) %collective-permute-start.4) | collective-permute-done | bytes 16416 | tf_op jit(solution)/shard_map/while/body/eval_jaxpr/ppermute | solution.py:64
  851.0 31.2 %convolution_add_fusion.4 = f32[32,128,8,256]{3,1,2,0:T(8,128)} fusion(f32[32,128,8,256]{3,1,2,0:T(8,128)} %get-tuple-element.1315, bf16[32,128,8,256]{3,2,1,0:T(8,128)(2,1)} %get-tuple-element.1333, f32[32,128,8]{1,2,0:T(8,128)S(1)} %get-tuple-element.1334, pred[32,128,128]{2,1,0:T(8,128)(4,1)S(1)} %compare_and_fusion.8, ...), kind=kOutput, calls=%fused_computation.19.clone.1 | convolution fusion | flops 4320133120 | bytes 88735744 | tf_op jit(solution)/shard_map/while/body/eval_jaxpr/cril,cle->crie/dot_general | solution.py:58
  882.9 48.3 %collective-permute-done.4 = s32[32,128]{1,0:T(8,128)S(1)} collective-permute-done((s32[32,128]{1,0:T(8,128)S(1)}, s32[32,128]{1,0:T(8,128)S(1)}, u32[]{:S(2)}, u32[]{:S(2)}) %collective-permute-start.4) | collective-permute-done | bytes 16416 | tf_op jit(solution)/shard_map/while/body/eval_jaxpr/ppermute | solution.py:64
  936.4 31.2 %convolution_add_fusion.4 = f32[32,128,8,256]{3,1,2,0:T(8,128)} fusion(f32[32,128,8,256]{3,1,2,0:T(8,128)} %get-tuple-element.1315, bf16[32,128,8,256]{3,2,1,0:T(8,128)(2,1)} %get-tuple-element.1333, f32[32,128,8]{1,2,0:T(8,128)S(1)} %get-tuple-element.1334, pred[32,128,128]{2,1,0:T(8,128)(4,1)S(1)} %compare_and_fusion.8, ...), kind=kOutput, calls=%fused_computation.19.clone.1 | convolution fusion | flops 4320133120 | bytes 88735744 | tf_op jit(solution)/shard_map/while/body/eval_jaxpr/cril,cle->crie/dot_general | solution.py:58
  968.2 48.3 %collective-permute-done.4 = s32[32,128]{1,0:T(8,128)S(1)} collective-permute-done((s32[32,128]{1,0:T(8,128)S(1)}, s32[32,128]{1,0:T(8,128)S(1)}, u32[]{:S(2)}, u32[]{:S(2)}) %collective-permute-start.4) | collective-permute-done | bytes 16416 | tf_op jit(solution)/shard_map/while/body/eval_jaxpr/ppermute | solution.py:64
  1021.8 31.2 %convolution_add_fusion.4 = f32[32,128,8,256]{3,1,2,0:T(8,128)} fusion(f32[32,128,8,256]{3,1,2,0:T(8,128)} %get-tuple-element.1315, bf16[32,128,8,256]{3,2,1,0:T(8,128)(2,1)} %get-tuple-element.1333, f32[32,128,8]{1,2,0:T(8,128)S(1)} %get-tuple-element.1334, pred[32,128,128]{2,1,0:T(8,128)(4,1)S(1)} %compare_and_fusion.8, ...), kind=kOutput, calls=%fused_computation.19.clone.1 | convolution fusion | flops 4320133120 | bytes 88735744 | tf_op jit(solution)/shard_map/while/body/eval_jaxpr/cril,cle->crie/dot_general | solution.py:58
  1053.0 32.8 %fusion.45 = (f32[32,128,8]{2,1,0:T(8,128)}, bf16[32,128,8,256]{3,2,1,0:T(8,128)(2,1)}) fusion(bf16[32,128,8,256]{3,2,1,0:T(8,128)(2,1)} %param.14, f32[32,128,8,256]{3,1,2,0:T(8,128)} %get-tuple-element.870), kind=kLoop, calls=%fused_computation.54 | loop fusion | flops 33521664 | bytes 67239936
  1087.9 28.1 %multiply_convert_fusion.1 = bf16[32,128,8,128]{1,3,2,0:T(8,128)(2,1)} fusion(f32[32,128,8,128]{1,3,2,0:T(8,128)} %get-tuple-element.1046, f32[32,128,8]{1,2,0:T(8,128)S(1)} %copy.41, f32[32,128,8]{1,2,0:T(8,128)S(1)} %get-tuple-element.1412, pred[32,128,128]{1,2,0:T(8,128)(4,1)S(1)} %copy-done.9, bf16[32,128,1,256]{3,1,2,0:T(8,128)(2,1)S(1)} %copy-done.6, ...), kind=kOutput, calls=%fused_computation.58 | convolution fusion | flops 2172649472 | bytes 44826624 | tf_op jit(solution)/shard_map/crie,cle->cril/dot_general | solution.py:75
  1145.5 1081.7 %while.72 = (s32[]{:T(128)}, bf16[32,128,256]{2,1,0:T(8,128)(2,1)S(1)}, bf16[32,128,256]{2,1,0:T(8,128)(2,1)}, s32[32,128]{1,0:T(8,128)S(1)}, f32[32,128,8,256]{...) while((s32[]{:T(128)}, ...), condition=%wide.region_9.10_spmd.clone, body=%wide.region_8.9_spmd.clone.sunk | while | flops 10790912000 | bytes 343968352 | solution.py:94
  1208.9 27.7 %convolution_add_fusion.5 = f32[32,128,8,256]{3,1,2,0:T(8,128)} fusion(f32[32,128,8,256]{3,1,2,0:T(8,128)} %get-tuple-element.1364, bf16[32,128,8,128]{3,1,2,0:T(8,128)(2,1)S(1)} %multiply_convert_fusion.4, bf16[32,128,256]{2,1,0:T(8,128)(2,1)S(1)} %collective-permute-done.5), kind=kOutput, calls=%fused_computation.35.clone.1 | convolution fusion | flops 2155872256 | bytes 77594624 | tf_op jit(solution)/shard_map/while/body/eval_jaxpr/cril,cle->crie/dot_general | solution.py:77
  1258.8 27.1 %collective-permute-done.8 = f32[32,128,256]{2,1,0:T(8,128)} collective-permute-done((f32[32,128,256]{2,1,0:T(8,128)}, f32[32,128,256]{2,1,0:T(8,128)}, u32[]{:S(2)}, u32[]{:S(2)}) %collective-permute-start.8) | collective-permute-done | bytes 4194336 | tf_op jit(solution)/shard_map/while/body/eval_jaxpr/ppermute | solution.py:87
  1363.3 27.7 %convolution_add_fusion.5 = f32[32,128,8,256]{3,1,2,0:T(8,128)} fusion(f32[32,128,8,256]{3,1,2,0:T(8,128)} %get-tuple-element.1364, bf16[32,128,8,128]{3,1,2,0:T(8,128)(2,1)S(1)} %multiply_convert_fusion.4, bf16[32,128,256]{2,1,0:T(8,128)(2,1)S(1)} %collective-permute-done.5), kind=kOutput, calls=%fused_computation.35.clone.1 | convolution fusion | flops 2155872256 | bytes 77594624 | tf_op jit(solution)/shard_map/while/body/eval_jaxpr/cril,cle->crie/dot_general | solution.py:77
  1517.8 27.7 %convolution_add_fusion.5 = f32[32,128,8,256]{3,1,2,0:T(8,128)} fusion(f32[32,128,8,256]{3,1,2,0:T(8,128)} %get-tuple-element.1364, bf16[32,128,8,128]{3,1,2,0:T(8,128)(2,1)S(1)} %multiply_convert_fusion.4, bf16[32,128,256]{2,1,0:T(8,128)(2,1)S(1)} %collective-permute-done.5), kind=kOutput, calls=%fused_computation.35.clone.1 | convolution fusion | flops 2155872256 | bytes 77594624 | tf_op jit(solution)/shard_map/while/body/eval_jaxpr/cril,cle->crie/dot_general | solution.py:77
  1672.2 27.7 %convolution_add_fusion.5 = f32[32,128,8,256]{3,1,2,0:T(8,128)} fusion(f32[32,128,8,256]{3,1,2,0:T(8,128)} %get-tuple-element.1364, bf16[32,128,8,128]{3,1,2,0:T(8,128)(2,1)S(1)} %multiply_convert_fusion.4, bf16[32,128,256]{2,1,0:T(8,128)(2,1)S(1)} %collective-permute-done.5), kind=kOutput, calls=%fused_computation.35.clone.1 | convolution fusion | flops 2155872256 | bytes 77594624 | tf_op jit(solution)/shard_map/while/body/eval_jaxpr/cril,cle->crie/dot_general | solution.py:77
  1722.2 27.1 %collective-permute-done.8 = f32[32,128,256]{2,1,0:T(8,128)} collective-permute-done((f32[32,128,256]{2,1,0:T(8,128)}, f32[32,128,256]{2,1,0:T(8,128)}, u32[]{:S(2)}, u32[]{:S(2)}) %collective-permute-start.8) | collective-permute-done | bytes 4194336 | tf_op jit(solution)/shard_map/while/body/eval_jaxpr/ppermute | solution.py:87
  1826.7 27.7 %convolution_add_fusion.5 = f32[32,128,8,256]{3,1,2,0:T(8,128)} fusion(f32[32,128,8,256]{3,1,2,0:T(8,128)} %get-tuple-element.1364, bf16[32,128,8,128]{3,1,2,0:T(8,128)(2,1)S(1)} %multiply_convert_fusion.4, bf16[32,128,256]{2,1,0:T(8,128)(2,1)S(1)} %collective-permute-done.5), kind=kOutput, calls=%fused_computation.35.clone.1 | convolution fusion | flops 2155872256 | bytes 77594624 | tf_op jit(solution)/shard_map/while/body/eval_jaxpr/cril,cle->crie/dot_general | solution.py:77
  1981.2 27.7 %convolution_add_fusion.5 = f32[32,128,8,256]{3,1,2,0:T(8,128)} fusion(f32[32,128,8,256]{3,1,2,0:T(8,128)} %get-tuple-element.1364, bf16[32,128,8,128]{3,1,2,0:T(8,128)(2,1)S(1)} %multiply_convert_fusion.4, bf16[32,128,256]{2,1,0:T(8,128)(2,1)S(1)} %collective-permute-done.5), kind=kOutput, calls=%fused_computation.35.clone.1 | convolution fusion | flops 2155872256 | bytes 77594624 | tf_op jit(solution)/shard_map/while/body/eval_jaxpr/cril,cle->crie/dot_general | solution.py:77
  2031.1 27.1 %collective-permute-done.8 = f32[32,128,256]{2,1,0:T(8,128)} collective-permute-done((f32[32,128,256]{2,1,0:T(8,128)}, f32[32,128,256]{2,1,0:T(8,128)}, u32[]{:S(2)}, u32[]{:S(2)}) %collective-permute-start.8) | collective-permute-done | bytes 4194336 | tf_op jit(solution)/shard_map/while/body/eval_jaxpr/ppermute | solution.py:87
  2135.6 27.7 %convolution_add_fusion.5 = f32[32,128,8,256]{3,1,2,0:T(8,128)} fusion(f32[32,128,8,256]{3,1,2,0:T(8,128)} %get-tuple-element.1364, bf16[32,128,8,128]{3,1,2,0:T(8,128)(2,1)S(1)} %multiply_convert_fusion.4, bf16[32,128,256]{2,1,0:T(8,128)(2,1)S(1)} %collective-permute-done.5), kind=kOutput, calls=%fused_computation.35.clone.1 | convolution fusion | flops 2155872256 | bytes 77594624 | tf_op jit(solution)/shard_map/while/body/eval_jaxpr/cril,cle->crie/dot_general | solution.py:77
  2185.6 27.1 %collective-permute-done.8 = f32[32,128,256]{2,1,0:T(8,128)} collective-permute-done((f32[32,128,256]{2,1,0:T(8,128)}, f32[32,128,256]{2,1,0:T(8,128)}, u32[]{:S(2)}, u32[]{:S(2)}) %collective-permute-start.8) | collective-permute-done | bytes 4194336 | tf_op jit(solution)/shard_map/while/body/eval_jaxpr/ppermute | solution.py:87
  2229.7 31.0 %fusion.46 = bf16[32,128,8,256]{3,2,1,0:T(8,128)(2,1)} fusion(f32[32,128,8,256]{3,1,2,0:T(8,128)} %get-tuple-element.871), kind=kLoop, calls=%fused_computation.56 | loop fusion | flops 16777216 | bytes 50331648 | tf_op jit(solution)/shard_map/convert_element_type | solution.py:97
  2260.7 37.8 %collective-permute-done.11 = bf16[32,128,256]{2,1,0:T(8,128)(2,1)S(1)} collective-permute-done((bf16[32,128,256]{2,1,0:T(8,128)(2,1)S(1)}, bf16[32,128,256]{2,1,0:T(8,128)(2,1)S(1)}, u32[]{:S(2)}, u32[]{:S(2)}) %collective-permute-start.11) | collective-permute-done | bytes 2097184 | tf_op jit(solution)/shard_map/ppermute | solution.py:96
  (430 shorter events, 1310.2 us)
Async XLA Ops:
  455.4 49.7 %collective-permute-start.3 = (bf16[32,128,256]{2,1,0:T(8,128)(2,1)}, bf16[32,128,256]{2,1,0:T(8,128)(2,1)S(1)}, u32[]{:S(2)}, u32[]{:S(2)}) collective-permute-start(bf16[32,128,256]{2,1,0:T(8,128)(2,1)} %get-tuple-element.1313), channel_id=1, source_target_pairs={{0,1},{1,2},{2,3},{3,4},{4,5},{5,6},{6,7},{7,0}} | collective-permute-start | bytes 6291464 | tf_op jit(solution)/shard_map/while/body/eval_jaxpr/ppermute | solution.py:63
  455.4 51.0 %collective-permute-start.2 = (bf16[32,128,256]{2,1,0:T(8,128)(2,1)}, bf16[32,128,256]{2,1,0:T(8,128)(2,1)}, u32[]{:S(2)}, u32[]{:S(2)}) collective-permute-start(bf16[32,128,256]{2,1,0:T(8,128)(2,1)} %get-tuple-element.1312), channel_id=1, source_target_pairs={{0,1},{1,2},{2,3},{3,4},{4,5},{5,6},{6,7},{7,0}} | collective-permute-start | bytes 6291464 | tf_op jit(solution)/shard_map/while/body/eval_jaxpr/ppermute | solution.py:62
  540.8 49.7 %collective-permute-start.3 = (bf16[32,128,256]{2,1,0:T(8,128)(2,1)}, bf16[32,128,256]{2,1,0:T(8,128)(2,1)S(1)}, u32[]{:S(2)}, u32[]{:S(2)}) collective-permute-start(bf16[32,128,256]{2,1,0:T(8,128)(2,1)} %get-tuple-element.1313), channel_id=1, source_target_pairs={{0,1},{1,2},{2,3},{3,4},{4,5},{5,6},{6,7},{7,0}} | collective-permute-start | bytes 6291464 | tf_op jit(solution)/shard_map/while/body/eval_jaxpr/ppermute | solution.py:63
  540.8 51.1 %collective-permute-start.2 = (bf16[32,128,256]{2,1,0:T(8,128)(2,1)}, bf16[32,128,256]{2,1,0:T(8,128)(2,1)}, u32[]{:S(2)}, u32[]{:S(2)}) collective-permute-start(bf16[32,128,256]{2,1,0:T(8,128)(2,1)} %get-tuple-element.1312), channel_id=1, source_target_pairs={{0,1},{1,2},{2,3},{3,4},{4,5},{5,6},{6,7},{7,0}} | collective-permute-start | bytes 6291464 | tf_op jit(solution)/shard_map/while/body/eval_jaxpr/ppermute | solution.py:62
  626.1 49.7 %collective-permute-start.3 = (bf16[32,128,256]{2,1,0:T(8,128)(2,1)}, bf16[32,128,256]{2,1,0:T(8,128)(2,1)S(1)}, u32[]{:S(2)}, u32[]{:S(2)}) collective-permute-start(bf16[32,128,256]{2,1,0:T(8,128)(2,1)} %get-tuple-element.1313), channel_id=1, source_target_pairs={{0,1},{1,2},{2,3},{3,4},{4,5},{5,6},{6,7},{7,0}} | collective-permute-start | bytes 6291464 | tf_op jit(solution)/shard_map/while/body/eval_jaxpr/ppermute | solution.py:63
  626.1 51.1 %collective-permute-start.2 = (bf16[32,128,256]{2,1,0:T(8,128)(2,1)}, bf16[32,128,256]{2,1,0:T(8,128)(2,1)}, u32[]{:S(2)}, u32[]{:S(2)}) collective-permute-start(bf16[32,128,256]{2,1,0:T(8,128)(2,1)} %get-tuple-element.1312), channel_id=1, source_target_pairs={{0,1},{1,2},{2,3},{3,4},{4,5},{5,6},{6,7},{7,0}} | collective-permute-start | bytes 6291464 | tf_op jit(solution)/shard_map/while/body/eval_jaxpr/ppermute | solution.py:62
  711.5 49.7 %collective-permute-start.3 = (bf16[32,128,256]{2,1,0:T(8,128)(2,1)}, bf16[32,128,256]{2,1,0:T(8,128)(2,1)S(1)}, u32[]{:S(2)}, u32[]{:S(2)}) collective-permute-start(bf16[32,128,256]{2,1,0:T(8,128)(2,1)} %get-tuple-element.1313), channel_id=1, source_target_pairs={{0,1},{1,2},{2,3},{3,4},{4,5},{5,6},{6,7},{7,0}} | collective-permute-start | bytes 6291464 | tf_op jit(solution)/shard_map/while/body/eval_jaxpr/ppermute | solution.py:63
  711.5 51.1 %collective-permute-start.2 = (bf16[32,128,256]{2,1,0:T(8,128)(2,1)}, bf16[32,128,256]{2,1,0:T(8,128)(2,1)}, u32[]{:S(2)}, u32[]{:S(2)}) collective-permute-start(bf16[32,128,256]{2,1,0:T(8,128)(2,1)} %get-tuple-element.1312), channel_id=1, source_target_pairs={{0,1},{1,2},{2,3},{3,4},{4,5},{5,6},{6,7},{7,0}} | collective-permute-start | bytes 6291464 | tf_op jit(solution)/shard_map/while/body/eval_jaxpr/ppermute | solution.py:62
  796.9 49.7 %collective-permute-start.3 = (bf16[32,128,256]{2,1,0:T(8,128)(2,1)}, bf16[32,128,256]{2,1,0:T(8,128)(2,1)S(1)}, u32[]{:S(2)}, u32[]{:S(2)}) collective-permute-start(bf16[32,128,256]{2,1,0:T(8,128)(2,1)} %get-tuple-element.1313), channel_id=1, source_target_pairs={{0,1},{1,2},{2,3},{3,4},{4,5},{5,6},{6,7},{7,0}} | collective-permute-start | bytes 6291464 | tf_op jit(solution)/shard_map/while/body/eval_jaxpr/ppermute | solution.py:63
  796.9 51.1 %collective-permute-start.2 = (bf16[32,128,256]{2,1,0:T(8,128)(2,1)}, bf16[32,128,256]{2,1,0:T(8,128)(2,1)}, u32[]{:S(2)}, u32[]{:S(2)}) collective-permute-start(bf16[32,128,256]{2,1,0:T(8,128)(2,1)} %get-tuple-element.1312), channel_id=1, source_target_pairs={{0,1},{1,2},{2,3},{3,4},{4,5},{5,6},{6,7},{7,0}} | collective-permute-start | bytes 6291464 | tf_op jit(solution)/shard_map/while/body/eval_jaxpr/ppermute | solution.py:62
  882.2 49.7 %collective-permute-start.3 = (bf16[32,128,256]{2,1,0:T(8,128)(2,1)}, bf16[32,128,256]{2,1,0:T(8,128)(2,1)S(1)}, u32[]{:S(2)}, u32[]{:S(2)}) collective-permute-start(bf16[32,128,256]{2,1,0:T(8,128)(2,1)} %get-tuple-element.1313), channel_id=1, source_target_pairs={{0,1},{1,2},{2,3},{3,4},{4,5},{5,6},{6,7},{7,0}} | collective-permute-start | bytes 6291464 | tf_op jit(solution)/shard_map/while/body/eval_jaxpr/ppermute | solution.py:63
  882.2 51.1 %collective-permute-start.2 = (bf16[32,128,256]{2,1,0:T(8,128)(2,1)}, bf16[32,128,256]{2,1,0:T(8,128)(2,1)}, u32[]{:S(2)}, u32[]{:S(2)}) collective-permute-start(bf16[32,128,256]{2,1,0:T(8,128)(2,1)} %get-tuple-element.1312), channel_id=1, source_target_pairs={{0,1},{1,2},{2,3},{3,4},{4,5},{5,6},{6,7},{7,0}} | collective-permute-start | bytes 6291464 | tf_op jit(solution)/shard_map/while/body/eval_jaxpr/ppermute | solution.py:62
  967.6 49.7 %collective-permute-start.3 = (bf16[32,128,256]{2,1,0:T(8,128)(2,1)}, bf16[32,128,256]{2,1,0:T(8,128)(2,1)S(1)}, u32[]{:S(2)}, u32[]{:S(2)}) collective-permute-start(bf16[32,128,256]{2,1,0:T(8,128)(2,1)} %get-tuple-element.1313), channel_id=1, source_target_pairs={{0,1},{1,2},{2,3},{3,4},{4,5},{5,6},{6,7},{7,0}} | collective-permute-start | bytes 6291464 | tf_op jit(solution)/shard_map/while/body/eval_jaxpr/ppermute | solution.py:63
  967.6 51.1 %collective-permute-start.2 = (bf16[32,128,256]{2,1,0:T(8,128)(2,1)}, bf16[32,128,256]{2,1,0:T(8,128)(2,1)}, u32[]{:S(2)}, u32[]{:S(2)}) collective-permute-start(bf16[32,128,256]{2,1,0:T(8,128)(2,1)} %get-tuple-element.1312), channel_id=1, source_target_pairs={{0,1},{1,2},{2,3},{3,4},{4,5},{5,6},{6,7},{7,0}} | collective-permute-start | bytes 6291464 | tf_op jit(solution)/shard_map/while/body/eval_jaxpr/ppermute | solution.py:62
  1147.0 49.0 %collective-permute-start.6 = (bf16[32,128,256]{2,1,0:T(8,128)(2,1)}, bf16[32,128,256]{2,1,0:T(8,128)(2,1)}, u32[]{:S(2)}, u32[]{:S(2)}) collective-permute-start(bf16[32,128,256]{2,1,0:T(8,128)(2,1)} %get-tuple-element.1362), channel_id=1, source_target_pairs={{0,1},{1,2},{2,3},{3,4},{4,5},{5,6},{6,7},{7,0}} | collective-permute-start | bytes 6291464 | tf_op jit(solution)/shard_map/while/body/eval_jaxpr/ppermute | solution.py:85
  1147.5 93.5 %collective-permute-start.9 = (f32[32,128,256]{2,1,0:T(8,128)}, f32[32,128,256]{2,1,0:T(8,128)}, u32[]{:S(2)}, u32[]{:S(2)}) collective-permute-start(f32[32,128,256]{2,1,0:T(8,128)} %get-tuple-element.1366), channel_id=1, source_target_pairs={{0,1},{1,2},{2,3},{3,4},{4,5},{5,6},{6,7},{7,0}} | collective-permute-start | bytes 12582920 | tf_op jit(solution)/shard_map/while/body/eval_jaxpr/ppermute | solution.py:88
  1151.0 134.9 %collective-permute-start.8 = (f32[32,128,256]{2,1,0:T(8,128)}, f32[32,128,256]{2,1,0:T(8,128)}, u32[]{:S(2)}, u32[]{:S(2)}) collective-permute-start(f32[32,128,256]{2,1,0:T(8,128)} %get-tuple-element.1365), channel_id=1, source_target_pairs={{0,1},{1,2},{2,3},{3,4},{4,5},{5,6},{6,7},{7,0}} | collective-permute-start | bytes 12582920 | tf_op jit(solution)/shard_map/while/body/eval_jaxpr/ppermute | solution.py:87
  1302.0 93.5 %collective-permute-start.9 = (f32[32,128,256]{2,1,0:T(8,128)}, f32[32,128,256]{2,1,0:T(8,128)}, u32[]{:S(2)}, u32[]{:S(2)}) collective-permute-start(f32[32,128,256]{2,1,0:T(8,128)} %get-tuple-element.1366), channel_id=1, source_target_pairs={{0,1},{1,2},{2,3},{3,4},{4,5},{5,6},{6,7},{7,0}} | collective-permute-start | bytes 12582920 | tf_op jit(solution)/shard_map/while/body/eval_jaxpr/ppermute | solution.py:88
  1305.4 134.9 %collective-permute-start.8 = (f32[32,128,256]{2,1,0:T(8,128)}, f32[32,128,256]{2,1,0:T(8,128)}, u32[]{:S(2)}, u32[]{:S(2)}) collective-permute-start(f32[32,128,256]{2,1,0:T(8,128)} %get-tuple-element.1365), channel_id=1, source_target_pairs={{0,1},{1,2},{2,3},{3,4},{4,5},{5,6},{6,7},{7,0}} | collective-permute-start | bytes 12582920 | tf_op jit(solution)/shard_map/while/body/eval_jaxpr/ppermute | solution.py:87
  1455.9 49.0 %collective-permute-start.6 = (bf16[32,128,256]{2,1,0:T(8,128)(2,1)}, bf16[32,128,256]{2,1,0:T(8,128)(2,1)}, u32[]{:S(2)}, u32[]{:S(2)}) collective-permute-start(bf16[32,128,256]{2,1,0:T(8,128)(2,1)} %get-tuple-element.1362), channel_id=1, source_target_pairs={{0,1},{1,2},{2,3},{3,4},{4,5},{5,6},{6,7},{7,0}} | collective-permute-start | bytes 6291464 | tf_op jit(solution)/shard_map/while/body/eval_jaxpr/ppermute | solution.py:85
  1456.5 93.5 %collective-permute-start.9 = (f32[32,128,256]{2,1,0:T(8,128)}, f32[32,128,256]{2,1,0:T(8,128)}, u32[]{:S(2)}, u32[]{:S(2)}) collective-permute-start(f32[32,128,256]{2,1,0:T(8,128)} %get-tuple-element.1366), channel_id=1, source_target_pairs={{0,1},{1,2},{2,3},{3,4},{4,5},{5,6},{6,7},{7,0}} | collective-permute-start | bytes 12582920 | tf_op jit(solution)/shard_map/while/body/eval_jaxpr/ppermute | solution.py:88
  1459.9 134.9 %collective-permute-start.8 = (f32[32,128,256]{2,1,0:T(8,128)}, f32[32,128,256]{2,1,0:T(8,128)}, u32[]{:S(2)}, u32[]{:S(2)}) collective-permute-start(f32[32,128,256]{2,1,0:T(8,128)} %get-tuple-element.1365), channel_id=1, source_target_pairs={{0,1},{1,2},{2,3},{3,4},{4,5},{5,6},{6,7},{7,0}} | collective-permute-start | bytes 12582920 | tf_op jit(solution)/shard_map/while/body/eval_jaxpr/ppermute | solution.py:87
  1610.9 93.5 %collective-permute-start.9 = (f32[32,128,256]{2,1,0:T(8,128)}, f32[32,128,256]{2,1,0:T(8,128)}, u32[]{:S(2)}, u32[]{:S(2)}) collective-permute-start(f32[32,128,256]{2,1,0:T(8,128)} %get-tuple-element.1366), channel_id=1, source_target_pairs={{0,1},{1,2},{2,3},{3,4},{4,5},{5,6},{6,7},{7,0}} | collective-permute-start | bytes 12582920 | tf_op jit(solution)/shard_map/while/body/eval_jaxpr/ppermute | solution.py:88
  1614.3 134.9 %collective-permute-start.8 = (f32[32,128,256]{2,1,0:T(8,128)}, f32[32,128,256]{2,1,0:T(8,128)}, u32[]{:S(2)}, u32[]{:S(2)}) collective-permute-start(f32[32,128,256]{2,1,0:T(8,128)} %get-tuple-element.1365), channel_id=1, source_target_pairs={{0,1},{1,2},{2,3},{3,4},{4,5},{5,6},{6,7},{7,0}} | collective-permute-start | bytes 12582920 | tf_op jit(solution)/shard_map/while/body/eval_jaxpr/ppermute | solution.py:87
  1765.4 93.5 %collective-permute-start.9 = (f32[32,128,256]{2,1,0:T(8,128)}, f32[32,128,256]{2,1,0:T(8,128)}, u32[]{:S(2)}, u32[]{:S(2)}) collective-permute-start(f32[32,128,256]{2,1,0:T(8,128)} %get-tuple-element.1366), channel_id=1, source_target_pairs={{0,1},{1,2},{2,3},{3,4},{4,5},{5,6},{6,7},{7,0}} | collective-permute-start | bytes 12582920 | tf_op jit(solution)/shard_map/while/body/eval_jaxpr/ppermute | solution.py:88
  1768.8 134.9 %collective-permute-start.8 = (f32[32,128,256]{2,1,0:T(8,128)}, f32[32,128,256]{2,1,0:T(8,128)}, u32[]{:S(2)}, u32[]{:S(2)}) collective-permute-start(f32[32,128,256]{2,1,0:T(8,128)} %get-tuple-element.1365), channel_id=1, source_target_pairs={{0,1},{1,2},{2,3},{3,4},{4,5},{5,6},{6,7},{7,0}} | collective-permute-start | bytes 12582920 | tf_op jit(solution)/shard_map/while/body/eval_jaxpr/ppermute | solution.py:87
  1919.9 93.5 %collective-permute-start.9 = (f32[32,128,256]{2,1,0:T(8,128)}, f32[32,128,256]{2,1,0:T(8,128)}, u32[]{:S(2)}, u32[]{:S(2)}) collective-permute-start(f32[32,128,256]{2,1,0:T(8,128)} %get-tuple-element.1366), channel_id=1, source_target_pairs={{0,1},{1,2},{2,3},{3,4},{4,5},{5,6},{6,7},{7,0}} | collective-permute-start | bytes 12582920 | tf_op jit(solution)/shard_map/while/body/eval_jaxpr/ppermute | solution.py:88
  1923.3 134.9 %collective-permute-start.8 = (f32[32,128,256]{2,1,0:T(8,128)}, f32[32,128,256]{2,1,0:T(8,128)}, u32[]{:S(2)}, u32[]{:S(2)}) collective-permute-start(f32[32,128,256]{2,1,0:T(8,128)} %get-tuple-element.1365), channel_id=1, source_target_pairs={{0,1},{1,2},{2,3},{3,4},{4,5},{5,6},{6,7},{7,0}} | collective-permute-start | bytes 12582920 | tf_op jit(solution)/shard_map/while/body/eval_jaxpr/ppermute | solution.py:87
  2074.3 93.5 %collective-permute-start.9 = (f32[32,128,256]{2,1,0:T(8,128)}, f32[32,128,256]{2,1,0:T(8,128)}, u32[]{:S(2)}, u32[]{:S(2)}) collective-permute-start(f32[32,128,256]{2,1,0:T(8,128)} %get-tuple-element.1366), channel_id=1, source_target_pairs={{0,1},{1,2},{2,3},{3,4},{4,5},{5,6},{6,7},{7,0}} | collective-permute-start | bytes 12582920 | tf_op jit(solution)/shard_map/while/body/eval_jaxpr/ppermute | solution.py:88
  2077.7 134.9 %collective-permute-start.8 = (f32[32,128,256]{2,1,0:T(8,128)}, f32[32,128,256]{2,1,0:T(8,128)}, u32[]{:S(2)}, u32[]{:S(2)}) collective-permute-start(f32[32,128,256]{2,1,0:T(8,128)} %get-tuple-element.1365), channel_id=1, source_target_pairs={{0,1},{1,2},{2,3},{3,4},{4,5},{5,6},{6,7},{7,0}} | collective-permute-start | bytes 12582920 | tf_op jit(solution)/shard_map/while/body/eval_jaxpr/ppermute | solution.py:87
  2227.2 71.3 %collective-permute-start.10 = (f32[32,128,256]{2,1,0:T(8,128)}, f32[32,128,256]{2,1,0:T(8,128)S(1)}, u32[]{:S(2)}, u32[]{:S(2)}) collective-permute-start(f32[32,128,256]{2,1,0:T(8,128)} %get-tuple-element.872), channel_id=1, source_target_pairs={{0,1},{1,2},{2,3},{3,4},{4,5},{5,6},{6,7},{7,0}} | collective-permute-start | bytes 12582920 | tf_op jit(solution)/shard_map/ppermute | solution.py:95
  2229.7 68.8 %collective-permute-start.11 = (bf16[32,128,256]{2,1,0:T(8,128)(2,1)S(1)}, bf16[32,128,256]{2,1,0:T(8,128)(2,1)S(1)}, u32[]{:S(2)}, u32[]{:S(2)}) collective-permute-start(bf16[32,128,256]{2,1,0:T(8,128)(2,1)S(1)} %convert.16), channel_id=1, source_target_pairs={{0,1},{1,2},{2,3},{3,4},{4,5},{5,6},{6,7},{7,0}} | collective-permute-start | bytes 6291464 | tf_op jit(solution)/shard_map/ppermute | solution.py:96
  (74 other events, 2535.5 us)
where the time goes:
time: 2310 us; the launch traced here: 2300 us
  matrix products  1040 us (45%)
  waiting for transfers between devices  941 us (41%)
  other arithmetic  155 us (7%)
  local copies, waits for them, and re-layouts  128 us (6%)
  starting transfers between devices  37.4 us (2%)
    ppermute x7, waiting for transfers between devices, out_body(): doc_cur = lax.ppermute(doc_cur, 'cp', to_next)  338 us
    dot_general x8, matrix products, out_update(): jnp.einsum('cril,cle->crie', prob_bf16, val_cur, preferred_element_type=j...  235 us
    dot_general x15, matrix products, masked_scores(): jnp.einsum('crie,cle->cril', query, key_cur, preferred_element_type=jnp.f...  220 us
    dot_general x8, matrix products, grad_update(): jnp.einsum('cril,cle->crie', grad_score, key_cur, preferred_element_type=...  209 us
    ppermute x7, waiting for transfers between devices, grad_body(): dk_acc = lax.ppermute(dk_acc, 'cp', to_next)  189 us
    ppermute x7, waiting for transfers between devices, stats_body(): doc_cur = lax.ppermute(doc_cur, 'cp', to_next)  181 us
    ppermute x7, waiting for transfers between devices, grad_body(): doc_cur = lax.ppermute(doc_cur, 'cp', to_next)  157 us
    dot_general x8, matrix products, grad_update(): jnp.einsum('cril,crie->cle', prob_bf16, grad_out, preferred_element_type=...  142 us
  transfers between devices with their start and end apart: 72, of which 36 were waited for; matrix products, arithmetic and copies ran while one was open for 27% of the time, Pallas kernels for 0%

commit v1 on v0

v1 whole, which is shorter than its diff:
```python
import functools

import jax
import jax.numpy as jnp
from jax import lax
from jax.experimental import pallas as pl
from jax.experimental.pallas import tpu as pltpu
from jax.sharding import PartitionSpec as P


NEG_BIG = -1e30
LOG2E = 1.4426950408889634
G = 32
NS = 16
NCH = 4
T = 4
F_CAP = ((32, 32, 32, 32),) * 3
B_CAP = ((32, 32, 32, 32),) * 3

NR, OR, NSD, OSD, DM, ST, SGO, SGR, CE, NTAB = 0, 48, 96, 144, 192, 224, 232, 256, 280, 288


def bounds(caps):
    out = [0]
    for cap in caps:
        out.append(out[-1] + cap)
    return out


F_LO = [bounds(cap) for cap in F_CAP]


def table_kernel(ks, me, tab):
    c = me[0]
    tab[CE] = c
    tab[CE + 1] = me[1]
    tab[ST] = 0
    for d in range(1, NCH):
        for s in range(NS):
            tab[NR + (d - 1) * NS + s] = 0
            tab[OR + (d - 1) * NS + s] = 0
            tab[NSD + (d - 1) * NS + s] = 0
            tab[OSD + (d - 1) * NS + s] = 0
        for v in range(T + 1):
            tab[SGO + (d - 1) * (T + 1) + v] = 0
            tab[SGR + (d - 1) * (T + 1) + v] = 0

    for s in range(NS):
        for h in range(2):
            need = jnp.maximum(256 * c - ks[s * 8 + 2 * c + h], 0)
            tab[DM + s * 2 + h] = (need + 255) >> 8

    for cc in range(NCH):
        here = cc == c

        def scan(s, carry):
            off, ready, avail = carry
            back = 256 * cc - ks[s * 8 + 2 * cc]
            nxt = []
            for d in range(1, NCH):
                if d <= cc:
                    x = jnp.clip(back - 256 * (d - 1), 0, 256)
                    n = (x + G - 1) // G
                else:
                    n = jnp.int32(0)
                nxt.append(off[d - 1] + n)

                @pl.when(here)
                def _():
                    tab[NR + (d - 1) * NS + s] = n
                    tab[OR + (d - 1) * NS + s] = off[d - 1]

                @pl.when(c + d == cc)
                def _():
                    tab[NSD + (d - 1) * NS + s] = n
                    tab[OSD + (d - 1) * NS + s] = off[d - 1]
            ready2, avail2 = [], []
            for t in range(T):
                ok = nxt[0] <= F_LO[0][t + 1]
                for d in range(2, NCH):
                    ok = ok & (nxt[d - 1] <= F_LO[d - 1][t + 1])
                one = jnp.where(ok, 1, 0)
                ready2.append(ready[t] + one)
                avail2.append(tuple(jnp.where(ok, nxt[d - 1], avail[t][d - 1]) for d in range(1, NCH)))
            return tuple(nxt), tuple(ready2), tuple(avail2)

        zero = jnp.int32(0)
        init = ((zero,) * 3, (zero,) * T, ((zero,) * 3,) * T)
        _, ready, avail = lax.fori_loop(0, NS, scan, init)

        @pl.when(here)
        def _():
            for t in range(T):
                tab[ST + t + 1] = ready[t]

        for d in range(1, NCH):
            sent = zero
            for v in range(T):
                sent = jnp.minimum(sent + B_CAP[d - 1][v], avail[v][d - 1])

                @pl.when(here)
                def _():
                    tab[SGO + (d - 1) * (T + 1) + v + 1] = sent

                @pl.when(c + d == cc)
                def _():
                    tab[SGR + (d - 1) * (T + 1) + v + 1] = sent


def pack_kernel(tab, own, mate, kvcol, *rest):
    chunks = [rest[d * T:(d + 1) * T] for d in range(3)]
    stage, sem = rest[3 * T:]
    s = pl.program_id(0)
    slot = lax.rem(s, 2)
    e = tab[CE + 1]

    def wait(ss, sl):
        for d in range(3):
            def one(k, _):
                pltpu.make_async_copy(stage.at[sl, 0], chunks[d][0].at[0], sem.at[sl]).wait()
                return 0

            lax.fori_loop(0, tab[NSD + d * NS + ss], one, 0)

    @pl.when(s >= 2)
    def _():
        wait(s - 2, slot)

    kvcol[0, e] = own[0]
    kvcol[0, 1 - e] = mate[0]
    stage[slot, pl.ds(e * 4, 4)] = own[0].reshape(4, G, 512)
    stage[slot, pl.ds(4 - e * 4, 4)] = mate[0].reshape(4, G, 512)
    for d in range(3):
        n = tab[NSD + d * NS + s]
        off = tab[OSD + d * NS + s]

        def send(k, _):
            j = off + k
            for t in range(T):
                @pl.when((j >= F_LO[d][t]) & (j < F_LO[d][t + 1]))
                def _():
                    pltpu.make_async_copy(stage.at[slot, 8 - n + k], chunks[d][t].at[j - F_LO[d][t]], sem.at[slot]).start()
            return 0

        lax.fori_loop(0, n, send, 0)

    @pl.when(s == NS - 1)
    def _():
        wait(s - 1, 1 - slot)
        wait(s, slot)


def dot_nt(a, b):
    return lax.dot_general(a, b, (((1,), (1,)), ((), ())), preferred_element_type=jnp.float32)


def dot_nn(a, b):
    return lax.dot_general(a, b, (((1,), (0,)), ((), ())), preferred_element_type=jnp.float32)


def dot_tn(a, b):
    return lax.dot_general(a, b, (((0,), (0,)), ((), ())), preferred_element_type=jnp.float32)


def compute_kernel(t, n_alias, scale, tab, docs, q_all, q_mate, g_all, g_mate, kvcol, *rest):
    fbuf = [rest[d * (t + 1):(d + 1) * (t + 1)] for d in range(3)]
    rest = rest[3 * (t + 1) + n_alias:]
    o_all, o_send, dq_all, dq_send, acc = rest[:5]
    rest = rest[5:]
    live = T - t
    bbuf = [rest[d * live:(d + 1) * live] for d in range(3)]
    qg, outb, kvs, dkv, s_scr, p_scr, m_scr, l_scr, docr, o_acc, dq_acc, isem, osem = rest[3 * live:]

    base = tab[ST + t]
    n = tab[ST + t + 1] - base
    c = tab[CE]
    e = tab[CE + 1]

    def inputs(ss, sl):
        own = e * NS + ss
        return [
            pltpu.make_async_copy(src, dst, isem.at[sl])
            for src, dst in (
                (kvcol.at[ss], kvs.at[sl, 0]),
                (q_all.at[own], qg.at[sl, 0]), (q_mate.at[ss], qg.at[sl, 1]),
                (g_all.at[own], qg.at[sl, 2]), (g_mate.at[ss], qg.at[sl, 3]),
            )
        ]

    def outputs(ss, sl):
        own = e * NS + ss
        return [
            pltpu.make_async_copy(src, dst, osem.at[sl])
            for src, dst in (
                (outb.at[sl, 0], o_all.at[own]), (outb.at[sl, 1], o_send.at[ss]),
                (outb.at[sl, 2], dq_all.at[own]), (outb.at[sl, 3], dq_send.at[ss]),
                (dkv.at[sl, 0], acc.at[ss]),
            )
        ]

    def fetch(ss, sl):
        for copy in inputs(ss, sl):
            copy.start()
        for d in range(3):
            cnt = tab[NR + d * NS + ss]
            off = tab[OR + d * NS + ss]

            def one(k, _):
                j = off + k
                for u in range(t + 1):
                    @pl.when((j >= F_LO[d][u]) & (j < F_LO[d][u + 1]))
                    def _():
                        row = pl.multiple_of((8 - cnt + k) * G, G)
                        pltpu.make_async_copy(fbuf[d][u].at[j - F_LO[d][u]], kvs.at[sl, d + 1, pl.ds(row, G)], isem.at[sl]).start()
                return 0

            lax.fori_loop(0, cnt, one, 0)

    def fetch_wait(ss, sl):
        for copy in inputs(ss, sl):
            copy.wait()
        for d in range(3):
            def one(k, _):
                pltpu.make_async_copy(fbuf[d][0].at[0], kvs.at[sl, d + 1, pl.ds(0, G)], isem.at[sl]).wait()
                return 0

            lax.fori_loop(0, tab[NR + d * NS + ss], one, 0)

    def put(ss, sl):
        for copy in outputs(ss, sl):
            copy.start()
        for d in range(3):
            cnt = tab[NR + d * NS + ss]
            off = tab[OR + d * NS + ss]

            def one(k, _):
                j = off + k
                for v in range(t, T):
                    lo = tab[SGO + d * (T + 1) + v]
                    hi = tab[SGO + d * (T + 1) + v + 1]

                    @pl.when((j >= lo) & (j < hi))
                    def _():
                        row = pl.multiple_of((8 - cnt + k) * G, G)
                        pltpu.make_async_copy(dkv.at[sl, d + 1, pl.ds(row, G)], bbuf[d][v - t].at[j - lo], osem.at[sl]).start()
                return 0

            lax.fori_loop(0, cnt, one, 0)

    def put_wait(ss, sl):
        for copy in outputs(ss, sl):
            copy.wait()
        for d in range(3):
            def one(k, _):
                pltpu.make_async_copy(dkv.at[sl, d + 1, pl.ds(0, G)], bbuf[d][0].at[0], osem.at[sl]).wait()
                return 0

            lax.fori_loop(0, tab[NR + d * NS + ss], one, 0)

    row_tok = lax.broadcasted_iota(jnp.int32, (1024, 128), 0) >> 3
    lane = lax.broadcasted_iota(jnp.int32, (1024, 128), 1)

    def attend(role, s, slot):
        q_ref, g_ref = qg.at[slot, role], qg.at[slot, 2 + role]
        h = e if role == 0 else 1 - e
        dm = tab[DM + s * 2 + h]
        dq_row = docs[s, pl.ds(2 * c + h, 1), :]
        d_t = jnp.transpose(jnp.broadcast_to(dq_row, (128, 128)))
        docr[...] = jnp.broadcast_to(d_t[:, None, :], (128, 8, 128)).reshape(1024, 128)

        def scores(d, causal):
            sc = dot_nt(q_ref[...], kvs[slot, d, :, :256]) * (scale * LOG2E)
            halves = []
            for j in range(2):
                dk = docs[s, pl.ds(2 * (c - d) + j, 1), :]
                vis = docr[...] == dk
                if causal:
                    vis = vis & (lane + 128 * j <= row_tok + 128 * h)
                x = jnp.where(vis, sc[:, 128 * j:128 * (j + 1)], NEG_BIG)
                s_scr[d, :, 128 * j:128 * (j + 1)] = x
                halves.append(x)
            return jnp.maximum(halves[0], halves[1])

        m_scr[...] = scores(0, True)

        def more_scores(d, _):
            m_scr[...] = jnp.maximum(m_scr[...], scores(d, False))
            return 0

        lax.fori_loop(1, dm + 1, more_scores, 0)
        m_scr[...] = jnp.broadcast_to(jnp.max(m_scr[...], axis=1, keepdims=True), (1024, 128))

        def exps(d):
            tot = None
            for j in range(2):
                x = jnp.exp2(s_scr[d, :, 128 * j:128 * (j + 1)] - m_scr[...])
                s_scr[d, :, 128 * j:128 * (j + 1)] = x
                tot = x if tot is None else tot + x
            return tot

        l_scr[...] = exps(0)

        def more_exps(d, _):
            l_scr[...] = l_scr[...] + exps(d)
            return 0

        lax.fori_loop(1, dm + 1, more_exps, 0)
        l_scr[...] = jnp.broadcast_to(1.0 / jnp.sum(l_scr[...], axis=1, keepdims=True), (1024, 128))

        def weighted(d):
            for j in range(2):
                p = s_scr[d, :, 128 * j:128 * (j + 1)] * l_scr[...]
                s_scr[d, :, 128 * j:128 * (j + 1)] = p
                p_scr[d, :, 128 * j:128 * (j + 1)] = p.astype(jnp.bfloat16)
            return dot_nn(p_scr[d], kvs[slot, d, :, 256:])

        o_acc[...] = weighted(0)

        def more_weighted(d, _):
            o_acc[...] = o_acc[...] + weighted(d)
            return 0

        lax.fori_loop(1, dm + 1, more_weighted, 0)
        o_low = o_acc[...].astype(jnp.bfloat16)
        outb[slot, role] = o_low
        delta = jnp.sum(g_ref[...].astype(jnp.float32) * o_low.astype(jnp.float32), axis=1, keepdims=True)
        m_scr[...] = jnp.broadcast_to(delta, (1024, 128))

        def grads(d):
            dp = dot_nt(g_ref[...], kvs[slot, d, :, 256:])
            ds = []
            for j in range(2):
                p = s_scr[d, :, 128 * j:128 * (j + 1)]
                ds.append((p * (dp[:, 128 * j:128 * (j + 1)] - m_scr[...])).astype(jnp.bfloat16))
            ds = jnp.concatenate(ds, axis=1)
            return dot_nn(ds, kvs[slot, d, :, :256]), dot_tn(ds, q_ref[...]), dot_tn(p_scr[d], g_ref[...])

        dq0, dk0, dv0 = grads(0)
        dq_acc[...] = dq0
        if role == 0:
            dkv[slot, 0, :, :256] = dk0
            dkv[slot, 0, :, 256:] = dv0
        else:
            dkv[slot, 0, :, :256] = dkv[slot, 0, :, :256] + dk0
            dkv[slot, 0, :, 256:] = dkv[slot, 0, :, 256:] + dv0

        def more_grads(d, _):
            dq1, dk1, dv1 = grads(d)
            dq_acc[...] = dq_acc[...] + dq1
            dkv[slot, d, :, :256] = dkv[slot, d, :, :256] + dk1
            dkv[slot, d, :, 256:] = dkv[slot, d, :, 256:] + dv1
            return 0

        lax.fori_loop(1, dm + 1, more_grads, 0)
        outb[slot, 2 + role] = (dq_acc[...] * scale).astype(jnp.bfloat16)

    @pl.when(n > 0)
    def _():
        kvs[...] = jnp.zeros_like(kvs)
        fetch(base, 0)

    def step(i, _):
        slot = lax.rem(i, 2)
        s = base + i

        @pl.when(i + 1 < n)
        def _():
            fetch(s + 1, 1 - slot)

        @pl.when(i >= 2)
        def _():
            put_wait(s - 2, slot)

        fetch_wait(s, slot)
        any_dm = jnp.maximum(tab[DM + s * 2], tab[DM + s * 2 + 1])

        def clear(d, _):
            dkv[slot, d] = jnp.zeros((256, 512), jnp.float32)
            return 0

        lax.fori_loop(1, any_dm + 1, clear, 0)
        attend(0, s, slot)
        attend(1, s, slot)
        put(s, slot)
        return 0

    lax.fori_loop(0, n, step, 0)

    @pl.when(n >= 2)
    def _():
        put_wait(base + n - 2, lax.rem(n, 2))

    @pl.when(n >= 1)
    def _():
        put_wait(base + n - 1, lax.rem(n + 1, 2))


def final_kernel(scale, tab, acc, *rest):
    bufs = [rest[d * T:(d + 1) * T] for d in range(3)]
    dk_own, dv_own, dkv_send, got, sem = rest[3 * T:]
    s = pl.program_id(0)
    slot = lax.rem(s, 2)
    e = tab[CE + 1]

    def fetch(ss, sl):
        for d in range(3):
            cnt = tab[NSD + d * NS + ss]
            off = tab[OSD + d * NS + ss]

            def one(k, _):
                j = off + k
                for v in range(T):
                    lo = tab[SGR + d * (T + 1) + v]
                    hi = tab[SGR + d * (T + 1) + v + 1]

                    @pl.when((j >= lo) & (j < hi))
                    def _():
                        pltpu.make_async_copy(bufs[d][v].at[j - lo], got.at[sl, d, 8 - cnt + k], sem.at[sl]).start()
                return 0

            lax.fori_loop(0, cnt, one, 0)

    @pl.when(s == 0)
    def _():
        fetch(s, 0)

    @pl.when(s + 1 < NS)
    def _():
        fetch(s + 1, 1 - slot)

    for d in range(3):
        cnt = tab[NSD + d * NS + s]

        def one(k, _):
            pltpu.make_async_copy(bufs[d][0].at[0], got.at[slot, d, 0], sem.at[slot]).wait()
            return 0

        lax.fori_loop(0, cnt, one, 0)
    for d in range(3):
        cnt = tab[NSD + d * NS + s]

        def add(k, _):
            acc[0, k] = acc[0, k] + got[slot, d, k]
            return 0

        lax.fori_loop(8 - cnt, 8, add, 0)
    mine = acc[0, pl.ds(4 * e, 4)].reshape(128, 512)
    other = acc[0, pl.ds(4 - 4 * e, 4)].reshape(128, 512)
    dk_own[0] = (mine[:, :256] * scale).astype(jnp.bfloat16)
    dv_own[0] = mine[:, 256:].astype(jnp.bfloat16)
    dkv_send[0, :, :256] = (other[:, :256] * scale).astype(jnp.bfloat16)
    dkv_send[0, :, 256:] = other[:, 256:].astype(jnp.bfloat16)


ANY = pl.BlockSpec(memory_space=pl.ANY)
SMEM = pl.BlockSpec(memory_space=pltpu.SMEM)


def solution(mesh):
    n_dev = mesh.shape['cp']
    seq_spec = P('dp', 'cp', None, None)
    id_spec = P('dp', 'cp')
    swap = [(k, k ^ 1) for k in range(n_dev)]

    def per_device(query, keys, values, grad_out, doc_id):
        nb, piece, heads, hd = query.shape
        rows = piece * heads
        scale = hd ** -0.5
        rank = lax.axis_index('cp')
        c = rank // 2
        e = rank % 2
        q3 = query.reshape(nb, rows, hd)
        g3 = grad_out.reshape(nb, rows, hd)
        kv = jnp.concatenate([keys[:, :, 0, :], values[:, :, 0, :]], axis=-1)
        other = NS * (1 - e)

        def to_mate(x):
            return lax.ppermute(lax.dynamic_slice_in_dim(x, other, NS, 0), 'cp', swap)

        kv_mate = to_mate(kv)
        docs_all = lax.all_gather(doc_id, 'cp')
        docs = lax.dynamic_slice_in_dim(docs_all, e * NS, NS, 1).transpose(1, 0, 2)
        flat = docs.reshape(NS, n_dev * piece)
        ks = jnp.sum((flat[:, None, :] < docs[:, :, :1]).astype(jnp.int32), axis=-1)
        me = jnp.stack([c, e]).astype(jnp.int32)
        tab = pl.pallas_call(
            table_kernel,
            out_shape=jax.ShapeDtypeStruct((NTAB,), jnp.int32),
            in_specs=[SMEM, SMEM],
            out_specs=SMEM,
            name="tables",
        )(ks.reshape(-1), me)

        bf = jnp.bfloat16
        f32 = jnp.float32
        fshape = [jax.ShapeDtypeStruct((F_CAP[d][t], G, 512), bf) for d in range(3) for t in range(T)]
        packed = pl.pallas_call(
            pack_kernel,
            grid_spec=pltpu.PrefetchScalarGridSpec(
                num_scalar_prefetch=1,
                grid=(NS,),
                in_specs=[
                    pl.BlockSpec((1, piece, 512), lambda s, tab: (tab[CE + 1] * NS + s, 0, 0)),
                    pl.BlockSpec((1, piece, 512), lambda s, tab: (s, 0, 0)),
                ],
                out_specs=[pl.BlockSpec((1, 2, piece, 512), lambda s, tab: (s, 0, 0, 0))] + [ANY] * (3 * T),
                scratch_shapes=[pltpu.VMEM((2, 8, G, 512), bf), pltpu.SemaphoreType.DMA((2,))],
            ),
            out_shape=[jax.ShapeDtypeStruct((NS, 2, piece, 512), bf)] + fshape,
            name="pack",
        )(tab, kv, kv_mate)
        kvcol = packed[0].reshape(NS, 2 * piece, 512)
        fsend = packed[1:]
        frecv = [None] * (3 * T)
        for t in range(T):
            for d in range(3):
                hop = 2 * (d + 1)
                frecv[d * T + t] = lax.ppermute(fsend[d * T + t], 'cp', [(k, k + hop) for k in range(n_dev - hop)])
        q_mate = to_mate(q3)
        g_mate = to_mate(g3)

        state = None
        brecv = [[None] * T for _ in range(3)]
        for t in range(T):
            live = T - t
            n_alias = 0 if state is None else 5 + 3 * live
            out_shape = [
                jax.ShapeDtypeStruct((nb, rows, hd), bf), jax.ShapeDtypeStruct((NS, rows, hd), bf),
                jax.ShapeDtypeStruct((nb, rows, hd), bf), jax.ShapeDtypeStruct((NS, rows, hd), bf),
                jax.ShapeDtypeStruct((NS, 2 * piece, 512), f32),
            ] + [jax.ShapeDtypeStruct((B_CAP[d][v], G, 512), f32) for d in range(3) for v in range(t, T)]
            n_in = 1 + 1 + 4 + 1 + 3 * (t + 1)
            outs = pl.pallas_call(
                functools.partial(compute_kernel, t, n_alias, scale),
                in_specs=[SMEM, pl.BlockSpec(memory_space=pltpu.VMEM)] + [ANY] * (5 + 3 * (t + 1) + n_alias),
                out_specs=[ANY] * (5 + 3 * live),
                scratch_shapes=[
                    pltpu.VMEM((2, 4, rows, hd), bf), pltpu.VMEM((2, 4, rows, hd), bf),
                    pltpu.VMEM((2, 4, 256, 512), bf), pltpu.VMEM((2, 4, 256, 512), f32),
                    pltpu.VMEM((4, rows, 256), f32), pltpu.VMEM((4, rows, 256), bf),
                    pltpu.VMEM((rows, 128), f32), pltpu.VMEM((rows, 128), f32), pltpu.VMEM((rows, 128), jnp.int32),
                    pltpu.VMEM((rows, hd), f32), pltpu.VMEM((rows, hd), f32),
                    pltpu.SemaphoreType.DMA((2,)), pltpu.SemaphoreType.DMA((2,)),
                ],
                out_shape=out_shape,
                input_output_aliases={n_in + k: k for k in range(n_alias)},
                compiler_params=pltpu.CompilerParams(vmem_limit_bytes=56 * 1024 * 1024),
                cost_estimate=pl.CostEstimate(flops=60_000_000_000 // T, bytes_accessed=100_000_000 // T, transcendentals=0),
            )(tab, docs, q3, q_mate, g3, g_mate, kvcol, *[frecv[d * T + u] for d in range(3) for u in range(t + 1)],
              *([] if state is None else state))
            sends = [outs[5 + d * live] for d in range(3)]
            state = list(outs[:5]) + [outs[5 + d * live + k] for d in range(3) for k in range(1, live)]
            for d in range(3):
                hop = 2 * (d + 1)
                brecv[d][t] = lax.ppermute(sends[d], 'cp', [(k + hop, k) for k in range(n_dev - hop)])

        o_own, o_send, dq_own, dq_send, acc = state[:5]
        dk_own, dv_own, dkv_send = pl.pallas_call(
            functools.partial(final_kernel, scale),
            grid_spec=pltpu.PrefetchScalarGridSpec(
                num_scalar_prefetch=1,
                grid=(NS,),
                in_specs=[pl.BlockSpec((1, 8, G, 512), lambda s, tab: (s, 0, 0, 0))] + [ANY] * (3 * T),
                out_specs=[
                    pl.BlockSpec((1, piece, hd), lambda s, tab: (tab[CE + 1] * NS + s, 0, 0)),
                    pl.BlockSpec((1, piece, hd), lambda s, tab: (tab[CE + 1] * NS + s, 0, 0)),
                    pl.BlockSpec((1, piece, 512), lambda s, tab: (s, 0, 0)),
                ],
                scratch_shapes=[pltpu.VMEM((2, 3, 8, G, 512), f32), pltpu.SemaphoreType.DMA((2,))],
            ),
            out_shape=[
                jax.ShapeDtypeStruct((nb, piece, hd), bf), jax.ShapeDtypeStruct((nb, piece, hd), bf),
                jax.ShapeDtypeStruct((NS, piece, 512), bf),
            ],
            name="finish",
        )(tab, acc.reshape(NS, 8, G, 512), *[b for row in brecv for b in row])

        def place(mine, send):
            got = lax.ppermute(send, 'cp', swap)
            return lax.dynamic_update_slice_in_dim(mine, got, other, 0)

        attn_out = place(o_own, o_send).reshape(query.shape)
        grad_query = place(dq_own, dq_send).reshape(query.shape)
        dkv_got = lax.ppermute(dkv_send, 'cp', swap)
        grad_keys = lax.dynamic_update_slice_in_dim(dk_own, dkv_got[:, :, :hd], other, 0)
        grad_values = lax.dynamic_update_slice_in_dim(dv_own, dkv_got[:, :, hd:], other, 0)
        return attn_out, grad_query, grad_keys.reshape(keys.shape), grad_values.reshape(values.shape)

    return jax.shard_map(per_device, mesh=mesh, in_specs=(seq_spec, seq_spec, seq_spec, seq_spec, id_spec),
                         out_specs=(seq_spec, seq_spec, seq_spec, seq_spec), check_vma=False)
```

time: 2310 us -> 752 us (0.33)
  matrix products: 1040 us -> 0 us
  waiting for transfers between devices: 941 us -> 443 us
  other arithmetic: 155 us -> 6.49 us
  Pallas kernels: 0 us -> 117 us
  local copies, waits for them, and re-layouts: 128 us -> 36.6 us
  starting transfers between devices: 37.4 us -> 112 us
  blocking collectives: 0 us -> 26.3 us
    dot_general x55 -> x0, matrix products: 1040 us -> none  [the longest x8 235 us: out_update(): jnp.einsum('cril,cle->crie', prob_bf16, val_cur, preferred_element_type=j...]
    ppermute x72 -> x30, waiting for transfers between devices: 941 us -> 443 us  [the longest x12 358 us: per_device(): lax.ppermute(sends[d], 'cp', [(k + hop, k) for k in range(n_dev - hop)])]
    pallas_call x0 -> x7, Pallas kernels: none -> 117 us  [the longest x4 83.4 us: per_device(): pl.pallas_call(functools.partial(compute_kernel, t, n_alias, scale), in_s...]
    while x105 -> x0, local copies, waits for them, and re-layouts: 85.1 us -> none
    ppermute x72 -> x30, starting transfers between devices: 37.4 us -> 112 us  [the longest x12 65.1 us: per_device(): lax.ppermute(fsend[d * T + t], 'cp', [(k, k + hop) for k in range(n_dev -...]
    reduce_sum x8 -> x1, other arithmetic: 68.5 us -> 0.42 us  [per_device(): ks = jnp.sum((flat[:, None, :] < docs[:, :, :1]).astype(jnp.int32), axis=-1)]
    unnamed x37 -> x56, local copies, waits for them, and re-layouts: 40.4 us -> 3.96 us
    unnamed x3 -> x0, other arithmetic: 35.3 us -> none
  transfers between devices with their start and end apart: 72 -> 30, of which waited for: 36 -> 14; matrix products, arithmetic and copies ran while one was open for 27% -> 3% of each run, Pallas kernels for 0% -> 16%
where the time goes in v1:
time: 752 us; the launch traced here: 742 us
  waiting for transfers between devices  443 us (59%)
  Pallas kernels  117 us (16%)
  starting transfers between devices  112 us (15%)
  local copies, waits for them, and re-layouts  36.6 us (5%)
  blocking collectives  26.3 us (3%)
    ppermute x12, waiting for transfers between devices, per_device(): lax.ppermute(sends[d], 'cp', [(k + hop, k) for k in range(n_dev - hop)])  358 us
    pallas_call x4, Pallas kernels, per_device(): pl.pallas_call(functools.partial(compute_kernel, t, n_alias, scale), in_s...  83.4 us
    ppermute x12, waiting for transfers between devices, per_device(): lax.ppermute(fsend[d * T + t], 'cp', [(k, k + hop) for k in range(n_dev -...  79.8 us
    ppermute x12, starting transfers between devices, per_device(): lax.ppermute(fsend[d * T + t], 'cp', [(k, k + hop) for k in range(n_dev -...  65.1 us
    ppermute x2, starting transfers between devices, place(): got = lax.ppermute(send, 'cp', swap)  29.8 us
    all_gather x1, blocking collectives, per_device(): docs_all = lax.all_gather(doc_id, 'cp')  26.3 us
    pallas_call x1, Pallas kernels, per_device(): pl.pallas_call(functools.partial(final_kernel, scale), grid_spec=pltpu.Pr...  15.9 us
    ppermute x12, starting transfers between devices, per_device(): lax.ppermute(sends[d], 'cp', [(k + hop, k) for k in range(n_dev - hop)])  15.6 us
  transfers between devices with their start and end apart: 30, of which 14 were waited for; matrix products, arithmetic and copies ran while one was open for 3% of the time, Pallas kernels for 16%

profile of v1, /device:TPU:0, one launch (start us, length us, event | category | flops | bytes accessed | tf_op | source)
XLA Modules:
  0.0 742.1 jit_solution(2811909684773404676)
XLA Ops:
  0.6 7.5 %constant_dynamic-slice_fusion = bf16[16,1024,256]{2,1,0:T(8,128)(2,1)} fusion(bf16[32,1024,256]{2,1,0:T(8,128)(2,1)} %bitcast.37, s32[]{:T(128)S(6)} %select_n.26), kind=kLoop, calls=%fused_computation.12 | loop fusion | bytes 16777220 | tf_op jit(solution)/shard_map/dynamic_slice | solution.py:478
  9.0 7.7 %constant_dynamic-slice_fusion.1 = bf16[16,1024,256]{2,1,0:T(8,128)(2,1)} fusion(bf16[32,1024,256]{2,1,0:T(8,128)(2,1)} %bitcast.32, s32[]{:T(128)S(6)} %select_n.26), kind=kLoop, calls=%fused_computation.13 | loop fusion | bytes 16777220 | tf_op jit(solution)/shard_map/dynamic_slice | solution.py:478
  18.7 26.3 %all-gather = s32[256,128]{1,0:T(8,128)S(1)} all-gather(s32[32,128]{1,0:T(8,128)S(1)} %copy-done.26), channel_id=2, replica_groups=mesh['dp'=1,'cp'=8] {'cp'}, dimensions={0}, use_global_device_ids=true | all-gather | bytes 147456 | tf_op jit(solution)/shard_map/all_gather | solution.py:481
  46.9 3.9 tables.1.tab
  50.8 4.0 pad_maximum_fusion.own
  54.8 13.7 %pack.1 = (bf16[16,2,128,512]{3,2,1,0:T(8,128)(2,1)}, bf16[32,32,512]{2,1,0:T(8,128)(2,1)}, bf16[32,32,512]{2,1,0:T(8,128)(2,1)}, bf16[32,32,512]{2,1,0:T(8,128)...) custom-call(s32[288]{0:T(512)} %tables.1.tab, ...), custom_call_target="tpu_custom_call" | custom-call | tf_op jit(solution)/shard_map/pack/pallas_call | solution.py:497
  68.4 2.2 collective-permute-start.3
  73.6 20.9 %collective-permute-done.3.rest_0_ = bf16[32,32,512]{2,1,0:T(8,128)(2,1)S(1)} collective-permute-done((bf16[32,32,512]{2,1,0:T(8,128)(2,1)}, bf16[32,32,512]{2,1,0:T(8,128)(2,1)S(1)}, u32[]{:S(2)}, u32[]{:S(2)}) %collective-permute-start.3) | collective-permute-done | bytes 1048608 | tf_op jit(solution)/shard_map/ppermute | solution.py:518
  94.4 4.3 collective-permute-start.4
  98.8 39.0 %collective-permute-done.7.rest_1_.rest_2_.rest_3_.rest_4_ = bf16[32,32,512]{2,1,0:T(8,128)(2,1)S(1)} collective-permute-done((bf16[32,32,512]{2,1,0:T(8,128)(2,1)}, bf16[32,32,512]{2,1,0:T(8,128)(2,1)S(1)}, u32[]{:S(2)}, u32[]{:S(2)}) %collective-permute-start.7) | collective-permute-done | bytes 1048608 | tf_op jit(solution)/shard_map/ppermute | solution.py:518
  139.2 7.3 collective-permute-start.6
  149.2 70.2 %shard_map.84 = (bf16[32,1024,256]{2,1,0:T(8,128)(2,1)}, bf16[16,1024,256]{2,1,0:T(8,128)(2,1)}, bf16[32,1024,256]{2,1,0:T(8,128)(2,1)}, bf16[16,1024,256]{2,1,0...) custom-call(s32[288]{0:T(512)} %tables.1.tab, ...), custom_call_target="tpu_custom_call" | custom-call | flops 15000000512 | bytes 25000000 | tf_op jit(solution)/shard_map/pallas_call | solution.py:533
  223.6 10.9 %shard_map.85 = (bf16[32,1024,256]{2,1,0:T(8,128)(2,1)}, bf16[16,1024,256]{2,1,0:T(8,128)(2,1)}, bf16[32,1024,256]{2,1,0:T(8,128)(2,1)}, bf16[16,1024,256]{2,1,0...) custom-call(s32[288]{0:T(512)} %tables.1.tab, ...), custom_call_target="tpu_custom_call", output_to_operand_aliasing={{0}: (13, {}), {1}: (14, {}), {2}: (15, {}), {3}: (16, {}),... | custom-call | flops 15000000512 | bytes 25000000 | tf_op jit(solution)/shard_map/pallas_call | solution.py:533
  234.6 40.2 %collective-permute-start.14 = (bf16[32,32,512]{2,1,0:T(8,128)(2,1)}, bf16[32,32,512]{2,1,0:T(8,128)(2,1)S(1)}, u32[]{:S(2)}, u32[]{:S(2)}) collective-permute-start(bf16[32,32,512]{2,1,0:T(8,128)(2,1)} %get-tuple-element.82), channel_id=1, source_target_pairs={{0,6},{1,7}} | collective-permute-start | bytes 3145736 | tf_op jit(solution)/shard_map/ppermute | solution.py:518
  277.3 19.9 %collective-permute-done.14.rest_11_ = bf16[32,32,512]{2,1,0:T(8,128)(2,1)S(1)} collective-permute-done((bf16[32,32,512]{2,1,0:T(8,128)(2,1)}, bf16[32,32,512]{2,1,0:T(8,128)(2,1)S(1)}, u32[]{:S(2)}, u32[]{:S(2)}) %collective-permute-start.14) | collective-permute-done | bytes 1048608 | tf_op jit(solution)/shard_map/ppermute | solution.py:518
  306.1 31.1 %collective-permute-done.20.rest_3_ = f32[32,32,512]{2,1,0:T(8,128)S(1)} collective-permute-done((f32[32,32,512]{2,1,0:T(8,128)}, f32[32,32,512]{2,1,0:T(8,128)S(1)}, u32[]{:S(2)}, u32[]{:S(2)}) %collective-permute-start.20) | collective-permute-done | bytes 2097184 | tf_op jit(solution)/shard_map/ppermute | solution.py:555
  338.5 40.8 %collective-permute-done.24.rest_7_ = f32[32,32,512]{2,1,0:T(8,128)S(1)} collective-permute-done((f32[32,32,512]{2,1,0:T(8,128)}, f32[32,32,512]{2,1,0:T(8,128)S(1)}, u32[]{:S(2)}, u32[]{:S(2)}) %collective-permute-start.24) | collective-permute-done | bytes 2097184 | tf_op jit(solution)/shard_map/ppermute | solution.py:555
  379.3 7.5 %collective-permute-start.15 = (bf16[16,1024,256]{2,1,0:T(8,128)(2,1)}, bf16[16,1024,256]{2,1,0:T(8,128)(2,1)}, u32[]{:S(2)}, u32[]{:S(2)}) collective-permute-start(bf16[16,1024,256]{2,1,0:T(8,128)(2,1)} %get-tuple-element.117), channel_id=1, source_target_pairs={{0,1},{1,0},{2,3},{3,2},{4,5},{5,4},{6,7},{7,6}} | collective-permute-start | bytes 25165832 | tf_op jit(solution)/shard_map/ppermute | solution.py:579
  386.7 31.1 %collective-permute-done.28.rest_11_ = f32[32,32,512]{2,1,0:T(8,128)S(1)} collective-permute-done((f32[32,32,512]{2,1,0:T(8,128)}, f32[32,32,512]{2,1,0:T(8,128)S(1)}, u32[]{:S(2)}, u32[]{:S(2)}) %collective-permute-start.28) | collective-permute-done | bytes 2097184 | tf_op jit(solution)/shard_map/ppermute | solution.py:555
  417.8 22.3 %collective-permute-start.16 = (bf16[16,1024,256]{2,1,0:T(8,128)(2,1)}, bf16[16,1024,256]{2,1,0:T(8,128)(2,1)}, u32[]{:S(2)}, u32[]{:S(2)}) collective-permute-start(bf16[16,1024,256]{2,1,0:T(8,128)(2,1)} %get-tuple-element.119), channel_id=1, source_target_pairs={{0,1},{1,0},{2,3},{3,2},{4,5},{5,4},{6,7},{7,6}} | collective-permute-start | bytes 25165832 | tf_op jit(solution)/shard_map/ppermute | solution.py:579
  441.4 27.7 %collective-permute-done.23.rest_6_ = f32[32,32,512]{2,1,0:T(8,128)S(1)} collective-permute-done((f32[32,32,512]{2,1,0:T(8,128)S(1)}, f32[32,32,512]{2,1,0:T(8,128)S(1)}, u32[]{:S(2)}, u32[]{:S(2)}) %collective-permute-start.23) | collective-permute-done | bytes 2097184 | tf_op jit(solution)/shard_map/ppermute | solution.py:555
  470.4 37.4 %collective-permute-done.27.rest_10_ = f32[32,32,512]{2,1,0:T(8,128)S(1)} collective-permute-done((f32[32,32,512]{2,1,0:T(8,128)S(1)}, f32[32,32,512]{2,1,0:T(8,128)S(1)}, u32[]{:S(2)}, u32[]{:S(2)}) %collective-permute-start.27) | collective-permute-done | bytes 2097184 | tf_op jit(solution)/shard_map/ppermute | solution.py:555
  509.1 7.5 %collective-permute-done.18.rest_1_ = f32[32,32,512]{2,1,0:T(8,128)S(1)} collective-permute-done((f32[32,32,512]{2,1,0:T(8,128)}, f32[32,32,512]{2,1,0:T(8,128)S(1)}, u32[]{:S(2)}, u32[]{:S(2)}) %collective-permute-start.18) | collective-permute-done | bytes 2097184 | tf_op jit(solution)/shard_map/ppermute | solution.py:555
  517.9 35.4 %collective-permute-done.22.rest_5_ = f32[32,32,512]{2,1,0:T(8,128)S(1)} collective-permute-done((f32[32,32,512]{2,1,0:T(8,128)}, f32[32,32,512]{2,1,0:T(8,128)S(1)}, u32[]{:S(2)}, u32[]{:S(2)}) %collective-permute-start.22) | collective-permute-done | bytes 2097184 | tf_op jit(solution)/shard_map/ppermute | solution.py:555
  555.9 53.3 %collective-permute-done.26.rest_9_ = f32[32,32,512]{2,1,0:T(8,128)S(1)} collective-permute-done((f32[32,32,512]{2,1,0:T(8,128)}, f32[32,32,512]{2,1,0:T(8,128)S(1)}, u32[]{:S(2)}, u32[]{:S(2)}) %collective-permute-start.26) | collective-permute-done | bytes 2097184 | tf_op jit(solution)/shard_map/ppermute | solution.py:555
  610.6 43.3 %collective-permute-done.21.rest_4_ = f32[32,32,512]{2,1,0:T(8,128)} collective-permute-done((f32[32,32,512]{2,1,0:T(8,128)}, f32[32,32,512]{2,1,0:T(8,128)}, u32[]{:S(2)}, u32[]{:S(2)}) %collective-permute-start.21) | collective-permute-done | bytes 2097184 | tf_op jit(solution)/shard_map/ppermute | solution.py:555
  653.8 51.0 %collective-permute-done.25.rest_8_ = f32[32,32,512]{2,1,0:T(8,128)} collective-permute-done((f32[32,32,512]{2,1,0:T(8,128)}, f32[32,32,512]{2,1,0:T(8,128)}, u32[]{:S(2)}, u32[]{:S(2)}) %collective-permute-start.25) | collective-permute-done | bytes 2097184 | tf_op jit(solution)/shard_map/ppermute | solution.py:555
  704.8 15.9 %finish.1 = (bf16[32,128,256]{2,1,0:T(8,128)(2,1)}, bf16[32,128,256]{2,1,0:T(8,128)(2,1)}, bf16[16,128,512]{2,1,0:T(8,128)(2,1)}) custom-call(s32[288]{0:T(512)} %tables.1.tab, f32[16,8,32,512]{3,2,1,0:T(8,128)} %bitcast.44, f32[32,32,512]{2,1,0:T(8,128)} %collective-permute-done.17.rest_0_, f32[32,32,512]{2,1,0:T(8,128)} %copy-done.21, ...), custom_call_target="tpu_custom_call" | custom-call | tf_op jit(solution)/shard_map/finish/pallas_call | solution.py:558
  720.7 4.4 collective-permute-done.29
  725.1 1.6 fusion.1
  726.7 7.5 %constant_dynamic-update-slice_fusion.1 = bf16[32,1024,256]{2,1,0:T(8,128)(2,1)} fusion(bf16[32,1024,256]{2,1,0:T(8,128)(2,1)} %get-tuple-element.116, bf16[16,1024,256]{2,1,0:T(8,128)(2,1)} %collective-permute-done.15, s32[]{:T(128)S(6)} %select_n.26), kind=kLoop, calls=%fused_computation.11 | loop fusion | bytes 16777220 | tf_op jit(solution)/shard_map/dynamic_update_slice | solution.py:580
  734.2 7.5 %constant_dynamic-update-slice_fusion = bf16[32,1024,256]{2,1,0:T(8,128)(2,1)} fusion(bf16[32,1024,256]{2,1,0:T(8,128)(2,1)} %get-tuple-element.118, bf16[16,1024,256]{2,1,0:T(8,128)(2,1)} %collective-permute-done.16, s32[]{:T(128)S(6)} %select_n.26), kind=kLoop, calls=%fused_computation.10 | loop fusion | bytes 16777220 | tf_op jit(solution)/shard_map/dynamic_update_slice | solution.py:580
  (104 shorter events, 37.5 us)
Async XLA Ops:
  8.2 138.3 %collective-permute-start.1 = (bf16[16,1024,256]{2,1,0:T(8,128)(2,1)}, bf16[16,1024,256]{2,1,0:T(8,128)(2,1)}, u32[]{:S(2)}, u32[]{:S(2)}) collective-permute-start(bf16[16,1024,256]{2,1,0:T(8,128)(2,1)} %constant_dynamic-slice_fusion), channel_id=1, source_target_pairs={{0,1},{1,0},{2,3},{3,2},{4,5},{5,4},{6,7},{7,6}} | collective-permute-start | bytes 25165832 | tf_op jit(solution)/shard_map/ppermute | solution.py:478
  16.7 131.1 %collective-permute-start = (bf16[16,1024,256]{2,1,0:T(8,128)(2,1)}, bf16[16,1024,256]{2,1,0:T(8,128)(2,1)}, u32[]{:S(2)}, u32[]{:S(2)}) collective-permute-start(bf16[16,1024,256]{2,1,0:T(8,128)(2,1)} %constant_dynamic-slice_fusion.1), channel_id=1, source_target_pairs={{0,1},{1,0},{2,3},{3,2},{4,5},{5,4},{6,7},{7,6}} | collective-permute-start | bytes 25165832 | tf_op jit(solution)/shard_map/ppermute | solution.py:478
  18.2 36.5 %collective-permute-start.2 = (bf16[16,128,512]{2,1,0:T(8,128)(2,1)}, bf16[16,128,512]{2,1,0:T(8,128)(2,1)}, u32[]{:S(2)}, u32[]{:S(2)}) collective-permute-start(bf16[16,128,512]{2,1,0:T(8,128)(2,1)} %fusion), channel_id=1, source_target_pairs={{0,1},{1,0},{2,3},{3,2},{4,5},{5,4},{6,7},{7,6}} | collective-permute-start | bytes 6291464 | tf_op jit(solution)/shard_map/ppermute | solution.py:478
  68.4 26.0 %collective-permute-start.3 = (bf16[32,32,512]{2,1,0:T(8,128)(2,1)}, bf16[32,32,512]{2,1,0:T(8,128)(2,1)S(1)}, u32[]{:S(2)}, u32[]{:S(2)}) collective-permute-start(bf16[32,32,512]{2,1,0:T(8,128)(2,1)} %get-tuple-element.71), channel_id=1, source_target_pairs={{0,2},{1,3},{2,4},{3,5},{4,6},{5,7}} | collective-permute-start | bytes 3145736 | tf_op jit(solution)/shard_map/ppermute | solution.py:518
  70.7 67.1 %collective-permute-start.7 = (bf16[32,32,512]{2,1,0:T(8,128)(2,1)}, bf16[32,32,512]{2,1,0:T(8,128)(2,1)S(1)}, u32[]{:S(2)}, u32[]{:S(2)}) collective-permute-start(bf16[32,32,512]{2,1,0:T(8,128)(2,1)} %get-tuple-element.75), channel_id=1, source_target_pairs={{0,4},{1,5},{2,6},{3,7}} | collective-permute-start | bytes 3145736 | tf_op jit(solution)/shard_map/ppermute | solution.py:518
  72.2 66.9 %collective-permute-start.11 = (bf16[32,32,512]{2,1,0:T(8,128)(2,1)}, bf16[32,32,512]{2,1,0:T(8,128)(2,1)S(1)}, u32[]{:S(2)}, u32[]{:S(2)}) collective-permute-start(bf16[32,32,512]{2,1,0:T(8,128)(2,1)} %get-tuple-element.79), channel_id=1, source_target_pairs={{0,6},{1,7}} | collective-permute-start | bytes 3145736 | tf_op jit(solution)/shard_map/ppermute | solution.py:518
  94.4 125.0 %collective-permute-start.4 = (bf16[32,32,512]{2,1,0:T(8,128)(2,1)}, bf16[32,32,512]{2,1,0:T(8,128)(2,1)S(1)}, u32[]{:S(2)}, u32[]{:S(2)}) collective-permute-start(bf16[32,32,512]{2,1,0:T(8,128)(2,1)} %get-tuple-element.72), channel_id=1, source_target_pairs={{0,2},{1,3},{2,4},{3,5},{4,6},{5,7}} | collective-permute-start | bytes 3145736 | tf_op jit(solution)/shard_map/ppermute | solution.py:518
  137.8 96.7 %collective-permute-start.5 = (bf16[32,32,512]{2,1,0:T(8,128)(2,1)}, bf16[32,32,512]{2,1,0:T(8,128)(2,1)S(1)}, u32[]{:S(2)}, u32[]{:S(2)}) collective-permute-start(bf16[32,32,512]{2,1,0:T(8,128)(2,1)} %get-tuple-element.73), channel_id=1, source_target_pairs={{0,2},{1,3},{2,4},{3,5},{4,6},{5,7}} | collective-permute-start | bytes 3145736 | tf_op jit(solution)/shard_map/ppermute | solution.py:518
  139.2 138.1 %collective-permute-start.6 = (bf16[32,32,512]{2,1,0:T(8,128)(2,1)}, bf16[32,32,512]{2,1,0:T(8,128)(2,1)}, u32[]{:S(2)}, u32[]{:S(2)}) collective-permute-start(bf16[32,32,512]{2,1,0:T(8,128)(2,1)} %get-tuple-element.74), channel_id=1, source_target_pairs={{0,2},{1,3},{2,4},{3,5},{4,6},{5,7}} | collective-permute-start | bytes 3145736 | tf_op jit(solution)/shard_map/ppermute | solution.py:518
  146.5 74.4 %collective-permute-start.8 = (bf16[32,32,512]{2,1,0:T(8,128)(2,1)}, bf16[32,32,512]{2,1,0:T(8,128)(2,1)S(1)}, u32[]{:S(2)}, u32[]{:S(2)}) collective-permute-start(bf16[32,32,512]{2,1,0:T(8,128)(2,1)} %get-tuple-element.76), channel_id=1, source_target_pairs={{0,4},{1,5},{2,6},{3,7}} | collective-permute-start | bytes 3145736 | tf_op jit(solution)/shard_map/ppermute | solution.py:518
  147.8 74.4 %collective-permute-start.12 = (bf16[32,32,512]{2,1,0:T(8,128)(2,1)}, bf16[32,32,512]{2,1,0:T(8,128)(2,1)S(1)}, u32[]{:S(2)}, u32[]{:S(2)}) collective-permute-start(bf16[32,32,512]{2,1,0:T(8,128)(2,1)} %get-tuple-element.80), channel_id=1, source_target_pairs={{0,6},{1,7}} | collective-permute-start | bytes 3145736 | tf_op jit(solution)/shard_map/ppermute | solution.py:518
  219.5 55.3 %collective-permute-start.9 = (bf16[32,32,512]{2,1,0:T(8,128)(2,1)}, bf16[32,32,512]{2,1,0:T(8,128)(2,1)S(1)}, u32[]{:S(2)}, u32[]{:S(2)}) collective-permute-start(bf16[32,32,512]{2,1,0:T(8,128)(2,1)} %get-tuple-element.77), channel_id=1, source_target_pairs={{0,4},{1,5},{2,6},{3,7}} | collective-permute-start | bytes 3145736 | tf_op jit(solution)/shard_map/ppermute | solution.py:518
  220.9 56.4 %collective-permute-start.10 = (bf16[32,32,512]{2,1,0:T(8,128)(2,1)}, bf16[32,32,512]{2,1,0:T(8,128)(2,1)S(1)}, u32[]{:S(2)}, u32[]{:S(2)}) collective-permute-start(bf16[32,32,512]{2,1,0:T(8,128)(2,1)} %get-tuple-element.78), channel_id=1, source_target_pairs={{0,4},{1,5},{2,6},{3,7}} | collective-permute-start | bytes 3145736 | tf_op jit(solution)/shard_map/ppermute | solution.py:518
  222.3 52.6 %collective-permute-start.13 = (bf16[32,32,512]{2,1,0:T(8,128)(2,1)}, bf16[32,32,512]{2,1,0:T(8,128)(2,1)S(1)}, u32[]{:S(2)}, u32[]{:S(2)}) collective-permute-start(bf16[32,32,512]{2,1,0:T(8,128)(2,1)} %get-tuple-element.81), channel_id=1, source_target_pairs={{0,6},{1,7}} | collective-permute-start | bytes 3145736 | tf_op jit(solution)/shard_map/ppermute | solution.py:518
  234.6 62.6 %collective-permute-start.14 = (bf16[32,32,512]{2,1,0:T(8,128)(2,1)}, bf16[32,32,512]{2,1,0:T(8,128)(2,1)S(1)}, u32[]{:S(2)}, u32[]{:S(2)}) collective-permute-start(bf16[32,32,512]{2,1,0:T(8,128)(2,1)} %get-tuple-element.82), channel_id=1, source_target_pairs={{0,6},{1,7}} | collective-permute-start | bytes 3145736 | tf_op jit(solution)/shard_map/ppermute | solution.py:518
  299.5 37.7 %collective-permute-start.20 = (f32[32,32,512]{2,1,0:T(8,128)}, f32[32,32,512]{2,1,0:T(8,128)S(1)}, u32[]{:S(2)}, u32[]{:S(2)}) collective-permute-start(f32[32,32,512]{2,1,0:T(8,128)} %get-tuple-element.124), channel_id=1, source_target_pairs={{2,0},{3,1},{4,2},{5,3},{6,4},{7,5}} | collective-permute-start | bytes 6291464 | tf_op jit(solution)/shard_map/ppermute | solution.py:555
  300.9 78.4 %collective-permute-start.24 = (f32[32,32,512]{2,1,0:T(8,128)}, f32[32,32,512]{2,1,0:T(8,128)S(1)}, u32[]{:S(2)}, u32[]{:S(2)}) collective-permute-start(f32[32,32,512]{2,1,0:T(8,128)} %get-tuple-element.128), channel_id=1, source_target_pairs={{4,0},{5,1},{6,2},{7,3}} | collective-permute-start | bytes 6291464 | tf_op jit(solution)/shard_map/ppermute | solution.py:555
  302.2 115.6 %collective-permute-start.28 = (f32[32,32,512]{2,1,0:T(8,128)}, f32[32,32,512]{2,1,0:T(8,128)S(1)}, u32[]{:S(2)}, u32[]{:S(2)}) collective-permute-start(f32[32,32,512]{2,1,0:T(8,128)} %get-tuple-element.132), channel_id=1, source_target_pairs={{6,0},{7,1}} | collective-permute-start | bytes 6291464 | tf_op jit(solution)/shard_map/ppermute | solution.py:555
  303.5 136.7 %collective-permute-start.19 = (f32[32,32,512]{2,1,0:T(8,128)S(1)}, f32[32,32,512]{2,1,0:T(8,128)S(1)}, u32[]{:S(2)}, u32[]{:S(2)}) collective-permute-start(f32[32,32,512]{2,1,0:T(8,128)S(1)} %copy-done.6), channel_id=1, source_target_pairs={{2,0},{3,1},{4,2},{5,3},{6,4},{7,5}} | collective-permute-start | bytes 6291464 | tf_op jit(solution)/shard_map/ppermute | solution.py:555
  304.8 164.3 %collective-permute-start.23 = (f32[32,32,512]{2,1,0:T(8,128)S(1)}, f32[32,32,512]{2,1,0:T(8,128)S(1)}, u32[]{:S(2)}, u32[]{:S(2)}) collective-permute-start(f32[32,32,512]{2,1,0:T(8,128)S(1)} %copy-done.7), channel_id=1, source_target_pairs={{4,0},{5,1},{6,2},{7,3}} | collective-permute-start | bytes 6291464 | tf_op jit(solution)/shard_map/ppermute | solution.py:555
  337.2 170.6 %copy-start.15 = (f32[32,32,512]{2,1,0:T(8,128)}, f32[32,32,512]{2,1,0:T(8,128)S(1)}, u32[]{:S(2)}) copy-start(f32[32,32,512]{2,1,0:T(8,128)S(1)} %collective-permute-done.20.rest_3_) | copy-start | bytes 6291460
  337.2 170.6 %collective-permute-start.27 = (f32[32,32,512]{2,1,0:T(8,128)S(1)}, f32[32,32,512]{2,1,0:T(8,128)S(1)}, u32[]{:S(2)}, u32[]{:S(2)}) collective-permute-start(f32[32,32,512]{2,1,0:T(8,128)S(1)} %copy-done.8), channel_id=1, source_target_pairs={{6,0},{7,1}} | collective-permute-start | bytes 6291464 | tf_op jit(solution)/shard_map/ppermute | solution.py:555
  379.3 128.5 %copy-start.16 = (f32[32,32,512]{2,1,0:T(8,128)}, f32[32,32,512]{2,1,0:T(8,128)S(1)}, u32[]{:S(2)}) copy-start(f32[32,32,512]{2,1,0:T(8,128)S(1)} %collective-permute-done.24.rest_7_) | copy-start | bytes 6291460
  379.3 347.4 %collective-permute-start.15 = (bf16[16,1024,256]{2,1,0:T(8,128)(2,1)}, bf16[16,1024,256]{2,1,0:T(8,128)(2,1)}, u32[]{:S(2)}, u32[]{:S(2)}) collective-permute-start(bf16[16,1024,256]{2,1,0:T(8,128)(2,1)} %get-tuple-element.117), channel_id=1, source_target_pairs={{0,1},{1,0},{2,3},{3,2},{4,5},{5,4},{6,7},{7,6}} | collective-permute-start | bytes 25165832 | tf_op jit(solution)/shard_map/ppermute | solution.py:579
  417.8 316.4 %collective-permute-start.16 = (bf16[16,1024,256]{2,1,0:T(8,128)(2,1)}, bf16[16,1024,256]{2,1,0:T(8,128)(2,1)}, u32[]{:S(2)}, u32[]{:S(2)}) collective-permute-start(bf16[16,1024,256]{2,1,0:T(8,128)(2,1)} %get-tuple-element.119), channel_id=1, source_target_pairs={{0,1},{1,0},{2,3},{3,2},{4,5},{5,4},{6,7},{7,6}} | collective-permute-start | bytes 25165832 | tf_op jit(solution)/shard_map/ppermute | solution.py:579
  440.2 76.4 %collective-permute-start.18 = (f32[32,32,512]{2,1,0:T(8,128)}, f32[32,32,512]{2,1,0:T(8,128)S(1)}, u32[]{:S(2)}, u32[]{:S(2)}) collective-permute-start(f32[32,32,512]{2,1,0:T(8,128)} %get-tuple-element.122), channel_id=1, source_target_pairs={{2,0},{3,1},{4,2},{5,3},{6,4},{7,5}} | collective-permute-start | bytes 6291464 | tf_op jit(solution)/shard_map/ppermute | solution.py:555
  469.1 84.2 %collective-permute-start.22 = (f32[32,32,512]{2,1,0:T(8,128)}, f32[32,32,512]{2,1,0:T(8,128)S(1)}, u32[]{:S(2)}, u32[]{:S(2)}) collective-permute-start(f32[32,32,512]{2,1,0:T(8,128)} %get-tuple-element.126), channel_id=1, source_target_pairs={{4,0},{5,1},{6,2},{7,3}} | collective-permute-start | bytes 6291464 | tf_op jit(solution)/shard_map/ppermute | solution.py:555
  507.8 101.5 %collective-permute-start.26 = (f32[32,32,512]{2,1,0:T(8,128)}, f32[32,32,512]{2,1,0:T(8,128)S(1)}, u32[]{:S(2)}, u32[]{:S(2)}) collective-permute-start(f32[32,32,512]{2,1,0:T(8,128)} %get-tuple-element.130), channel_id=1, source_target_pairs={{6,0},{7,1}} | collective-permute-start | bytes 6291464 | tf_op jit(solution)/shard_map/ppermute | solution.py:555
  516.6 94.0 %collective-permute-start.17 = (f32[32,32,512]{2,1,0:T(8,128)}, f32[32,32,512]{2,1,0:T(8,128)}, u32[]{:S(2)}, u32[]{:S(2)}) collective-permute-start(f32[32,32,512]{2,1,0:T(8,128)} %get-tuple-element.121), channel_id=1, source_target_pairs={{2,0},{3,1},{4,2},{5,3},{6,4},{7,5}} | collective-permute-start | bytes 6291464 | tf_op jit(solution)/shard_map/ppermute | solution.py:555
  554.6 99.2 %collective-permute-start.21 = (f32[32,32,512]{2,1,0:T(8,128)}, f32[32,32,512]{2,1,0:T(8,128)}, u32[]{:S(2)}, u32[]{:S(2)}) collective-permute-start(f32[32,32,512]{2,1,0:T(8,128)} %get-tuple-element.125), channel_id=1, source_target_pairs={{4,0},{5,1},{6,2},{7,3}} | collective-permute-start | bytes 6291464 | tf_op jit(solution)/shard_map/ppermute | solution.py:555
  609.3 95.5 %collective-permute-start.25 = (f32[32,32,512]{2,1,0:T(8,128)}, f32[32,32,512]{2,1,0:T(8,128)}, u32[]{:S(2)}, u32[]{:S(2)}) collective-permute-start(f32[32,32,512]{2,1,0:T(8,128)} %get-tuple-element.129), channel_id=1, source_target_pairs={{6,0},{7,1}} | collective-permute-start | bytes 6291464 | tf_op jit(solution)/shard_map/ppermute | solution.py:555
  720.7 4.4 collective-permute-start.29
  (25 other events, 585.1 us)

commit v2 on v0

v2 whole, which is shorter than its diff:
```python
import functools

import jax
import jax.numpy as jnp
from jax import lax
from jax.experimental import pallas as pl
from jax.experimental.pallas import tpu as pltpu
from jax.sharding import PartitionSpec as P


NEG_BIG = -1e30
LOG2E = 1.4426950408889634
G = 32
NS = 16
NCH = 4

FAST = (
    ((24, 34, 34, 32), (20, 24, 22, 20), (12, 14, 12, 12)),
    ((20, 32, 34, 38), (12, 22, 24, 24), (6, 10, 12, 18)),
)
SLOW_SEQS = 4
SLOW = (((8 * SLOW_SEQS,),) * 3,) * 2

CNT, OFF, DM, ST, SG, CE, FIT = 0, 336, 672, 704, 712, 840, 844
NTAB = 848


def at(base, cc, d, s):
    return base + (cc * 3 + d) * NS + s


def sg(cc, d, v):
    return SG + (cc * 3 + d) * 6 + v


def bounds(caps):
    out = [0]
    for cap in caps:
        out.append(out[-1] + cap)
    return out


def gather_kernel(doc, out, ks, send_sem, recv_sem):
    me = lax.axis_index('cp')
    n = out.shape[0]
    out[me] = doc[...]
    copies = []
    for k in range(1, n):
        copy = pltpu.make_async_remote_copy(
            src_ref=doc, dst_ref=out.at[me], send_sem=send_sem.at[k], recv_sem=recv_sem.at[k],
            device_id={'cp': lax.rem(me + k, n)}, device_id_type=pl.DeviceIdType.MESH)
        copy.start()
        copies.append(copy)
    for copy in copies:
        copy.wait()
    lane = lax.broadcasted_iota(jnp.int32, ks.shape, 1)
    total = jnp.zeros(ks.shape, jnp.int32)
    for p in range(n):
        first = out[p][:, :1]
        below = jnp.zeros(ks.shape, jnp.int32)
        for j in range(n):
            below = below + (out[j] < first).astype(jnp.int32)
        total = jnp.where(lane == p, jnp.sum(below, axis=1, keepdims=True), total)
    ks[...] = total


def table_kernel(plan, ks, me, tab):
    f_cap, b_cap = plan
    n_t = len(f_cap[0])
    f_lo = [bounds(cap) for cap in f_cap]
    c, e, lo, hi = me[0], me[1], me[2], me[3]
    zero = jnp.int32(0)
    tab[CE] = c
    tab[CE + 1] = e
    tab[ST] = lo
    for cc in range(7):
        for d in range(3):
            if not 1 <= cc <= 3 or d >= cc:
                for s in range(NS):
                    tab[at(CNT, cc, d, s)] = zero
                    tab[at(OFF, cc, d, s)] = zero
                for v in range(n_t + 1):
                    tab[sg(cc, d, v)] = zero
    for s in range(NS):
        for h in range(2):
            need = jnp.maximum(256 * c - ks[e * NS + s, 2 * c + h], 0)
            tab[DM + s * 2 + h] = (need + 255) >> 8

    fit = jnp.bool_(True)
    for col in range(2):
        row0 = jnp.where(e == 0, col, 1 - col) * NS
        for cc in range(NCH):
            off = [zero] * 3
            ready = [zero] * n_t
            avail = [[zero] * 3 for _ in range(n_t)]
            for s in range(NS):
                back = 256 * cc - ks[row0 + s, 2 * cc]
                live = (lo <= s) & (s < hi)
                for d in range(min(cc, 3)):
                    x = jnp.where(live, jnp.clip(back - 256 * d, 0, 256), 0)
                    n = (x + G - 1) >> 5
                    if col == 0:
                        tab[at(CNT, cc, d, s)] = n
                        tab[at(OFF, cc, d, s)] = off[d]
                    off[d] = off[d] + n
                for t in range(n_t):
                    ok = s < hi
                    for d in range(min(cc, 3)):
                        ok = ok & (off[d] <= f_lo[d][t + 1])
                    ready[t] = ready[t] + jnp.where(ok, 1, 0)
                    for d in range(min(cc, 3)):
                        avail[t][d] = jnp.where(ok, off[d], avail[t][d])
            fit = fit & (ready[n_t - 1] == hi)
            if col == 0:
                for t in range(n_t):
                    @pl.when(cc == c)
                    def _():
                        tab[ST + t + 1] = ready[t]
            for d in range(min(cc, 3)):
                sent = zero
                if col == 0:
                    tab[sg(cc, d, 0)] = sent
                for v in range(n_t):
                    sent = jnp.minimum(sent + b_cap[d][v], avail[v][d])
                    if col == 0:
                        tab[sg(cc, d, v + 1)] = sent
                fit = fit & (sent == off[d])
    tab[FIT] = jnp.where(fit, 1, 0)


def run_copies(lo_of, n_chunks, off, n, issue):
    for v in range(n_chunks):
        lo, hi = lo_of(v), lo_of(v + 1)
        a = jnp.maximum(off, lo)
        cnt = jnp.minimum(off + n, hi) - a

        @pl.when(cnt > 0)
        def _():
            for size in (8, 4, 2, 1):
                @pl.when((cnt & size) != 0)
                def _():
                    skip = cnt & (16 - 2 * size)
                    issue(v, a - lo + skip, a - off + skip, size)


def run_waits(n, wait):
    for size in (8, 4, 2, 1):
        @pl.when((n & size) != 0)
        def _():
            wait(size)


def pack_kernel(n_t, f_lo, tab, k_all, v_all, mate, kvcol, *rest):
    chunks = [rest[d * n_t:(d + 1) * n_t] for d in range(3)]
    inb, stage, isem, sem, csem = rest[3 * n_t:]
    lo = tab[ST]
    n = tab[ST + n_t] if n_t == 1 else NS
    n = n - lo
    c, e = tab[CE], tab[CE + 1]

    def inputs(s, sl):
        return [
            pltpu.make_async_copy(k_all.at[e * NS + s], inb.at[sl, 0], isem.at[sl]),
            pltpu.make_async_copy(v_all.at[e * NS + s], inb.at[sl, 1], isem.at[sl]),
            pltpu.make_async_copy(mate.at[s], stage.at[sl, pl.ds(4 - 4 * e, 4)], isem.at[sl]),
        ]

    def out_copy(s, sl):
        return pltpu.make_async_copy(stage.at[sl], kvcol.at[s], csem.at[sl])

    def drain(s, sl):
        out_copy(s, sl).wait()
        for d in range(3):
            run_waits(tab[at(CNT, c + d + 1, d, s)],
                      lambda size: pltpu.make_async_copy(stage.at[sl, pl.ds(0, size)], kvcol.at[s, pl.ds(0, size)], sem.at[sl]).wait())

    @pl.when(n > 0)
    def _():
        for copy in inputs(lo, 0):
            copy.start()

    def step(i, _):
        s = lo + i
        sl = lax.rem(i, 3)
        nx = lax.rem(i + 1, 3)

        @pl.when(i >= 2)
        def _():
            drain(s - 2, nx)

        @pl.when(i + 1 < n)
        def _():
            for copy in inputs(s + 1, nx):
                copy.start()

        for copy in inputs(s, sl):
            copy.wait()
        stage[sl, pl.ds(4 * e, 4)] = jnp.concatenate([inb[sl, 0], inb[sl, 1]], axis=1).reshape(4, G, 512)
        out_copy(s, sl).start()
        for d in range(3):
            cnt = tab[at(CNT, c + d + 1, d, s)]
            off = tab[at(OFF, c + d + 1, d, s)]
            run_copies(lambda v: f_lo[d][v], n_t, off, cnt,
                       lambda v, slot, k, size: pltpu.make_async_copy(
                           stage.at[sl, pl.ds(8 - cnt + k, size)], chunks[d][v].at[pl.ds(slot, size)], sem.at[sl]).start())
        return 0

    lax.fori_loop(0, n, step, 0)

    @pl.when(n >= 2)
    def _():
        drain(lo + n - 2, lax.rem(n + 1, 3))

    @pl.when(n >= 1)
    def _():
        drain(lo + n - 1, lax.rem(n + 2, 3))


def dot_nt(a, b):
    return lax.dot_general(a, b, (((1,), (1,)), ((), ())), preferred_element_type=jnp.float32)


def dot_nn(a, b):
    return lax.dot_general(a, b, (((1,), (0,)), ((), ())), preferred_element_type=jnp.float32)


def dot_tn(a, b):
    return lax.dot_general(a, b, (((0,), (0,)), ((), ())), preferred_element_type=jnp.float32)


def compute_kernel(t, n_t, f_lo, n_alias, scale, tab, docs, q_all, q_mate, g_all, g_mate, kvcol, *rest):
    fbuf = [rest[d * (t + 1):(d + 1) * (t + 1)] for d in range(3)]
    rest = rest[3 * (t + 1) + n_alias:]
    o_all, o_send, dq_all, dq_send, acc = rest[:5]
    rest = rest[5:]
    live = n_t - t
    bbuf = [rest[d * live:(d + 1) * live] for d in range(3)]
    qg, outb, kvs, dkv, e_scr, p_scr, m_scr, l_scr, f_scr, docr, o_acc, dq_acc, isem, osem = rest[3 * live:]

    base = tab[ST + t]
    n = tab[ST + t + 1] - base
    c = tab[CE]
    e = tab[CE + 1]

    def inputs(ss, sl):
        own = e * NS + ss
        return [
            pltpu.make_async_copy(src, dst, isem.at[sl])
            for src, dst in (
                (kvcol.at[ss], kvs.at[sl, 0]),
                (q_all.at[own], qg.at[sl, 0]), (q_mate.at[ss], qg.at[sl, 1]),
                (g_all.at[own], qg.at[sl, 2]), (g_mate.at[ss], qg.at[sl, 3]),
            )
        ]

    def outputs(ss, sl):
        own = e * NS + ss
        return [
            pltpu.make_async_copy(src, dst, osem.at[sl])
            for src, dst in (
                (outb.at[sl, 0], o_all.at[own]), (outb.at[sl, 1], o_send.at[ss]),
                (outb.at[sl, 2], dq_all.at[own]), (outb.at[sl, 3], dq_send.at[ss]),
                (dkv.at[sl, 0], acc.at[ss]),
            )
        ]

    def fetch(ss, sl):
        for copy in inputs(ss, sl):
            copy.start()
        for d in range(3):
            cnt = tab[at(CNT, c, d, ss)]
            off = tab[at(OFF, c, d, ss)]
            run_copies(lambda v: f_lo[d][v], t + 1, off, cnt,
                       lambda v, slot, k, size: pltpu.make_async_copy(
                           fbuf[d][v].at[pl.ds(slot, size)], kvs.at[sl, d + 1, pl.ds(8 - cnt + k, size)], isem.at[sl]).start())

    def fetch_wait(ss, sl):
        for copy in inputs(ss, sl):
            copy.wait()
        for d in range(3):
            run_waits(tab[at(CNT, c, d, ss)],
                      lambda size: pltpu.make_async_copy(
                          kvcol.at[ss, pl.ds(0, size)], kvs.at[sl, d + 1, pl.ds(0, size)], isem.at[sl]).wait())

    def put(ss, sl):
        for copy in outputs(ss, sl):
            copy.start()
        for d in range(3):
            cnt = tab[at(CNT, c, d, ss)]
            off = tab[at(OFF, c, d, ss)]
            run_copies(lambda v: tab[sg(c, d, t + v)], live, off, cnt,
                       lambda v, slot, k, size: pltpu.make_async_copy(
                           dkv.at[sl, d + 1, pl.ds(8 - cnt + k, size)], bbuf[d][v].at[pl.ds(slot, size)], osem.at[sl]).start())

    def put_wait(ss, sl):
        for copy in outputs(ss, sl):
            copy.wait()
        for d in range(3):
            run_waits(tab[at(CNT, c, d, ss)],
                      lambda size: pltpu.make_async_copy(
                          dkv.at[sl, d + 1, pl.ds(0, size)], acc.at[ss, pl.ds(0, size)], osem.at[sl]).wait())

    row_tok = lax.broadcasted_iota(jnp.int32, (1024, 128), 0) >> 3
    lane = lax.broadcasted_iota(jnp.int32, (1024, 128), 1)
    cs = scale * LOG2E

    def keys_of(slot, d):
        return kvs[slot, d, :, :, :256].reshape(256, 256)

    def values_of(slot, d):
        return kvs[slot, d, :, :, 256:].reshape(256, 256)

    def attend(role, s, slot):
        q_ref, g_ref = qg.at[slot, role], qg.at[slot, 2 + role]
        h = e if role == 0 else 1 - e
        dm = tab[DM + s * 2 + h]
        row = e * NS + s
        dq_row = docs[2 * c + h, pl.ds(row, 1), :]
        d_t = jnp.transpose(jnp.broadcast_to(dq_row, (128, 128)))
        docr[...] = jnp.broadcast_to(d_t[:, None, :], (128, 8, 128)).reshape(1024, 128)

        def scores(d, causal):
            sc = dot_nt(q_ref[...], keys_of(slot, d)) * cs
            xs = []
            for j in range(2):
                dk = docs[2 * (c - d) + j, pl.ds(row, 1), :]
                vis = docr[...] == dk
                if causal:
                    vis = vis & (lane + 128 * j <= row_tok + 128 * h)
                xs.append(jnp.where(vis, sc[:, 128 * j:128 * (j + 1)], NEG_BIG))
            top = jnp.max(jnp.maximum(xs[0], xs[1]), axis=1, keepdims=True)
            es = [jnp.exp2(x - top) for x in xs]
            e_scr[d, :, :128] = es[0]
            e_scr[d, :, 128:] = es[1]
            m_scr[d] = jnp.broadcast_to(top, (1024, 128))
            l_scr[d] = es[0] + es[1]

        scores(0, True)

        def more_scores(d, _):
            scores(d, False)
            return 0

        lax.fori_loop(1, dm + 1, more_scores, 0)

        @pl.when(dm == 0)
        def _():
            f_scr[0] = jnp.broadcast_to(1.0 / jnp.sum(l_scr[0], axis=1, keepdims=True), (1024, 128))

        @pl.when(dm > 0)
        def _():
            def top_of(d, m):
                o_acc[:, :128] = jnp.maximum(o_acc[:, :128], m_scr[d])
                return m

            o_acc[:, :128] = m_scr[0]
            lax.fori_loop(1, dm + 1, top_of, 0)
            o_acc[:, 128:] = jnp.zeros((1024, 128), jnp.float32)

            def sum_of(d, x):
                f = jnp.exp2(m_scr[d] - o_acc[:, :128])
                f_scr[d] = f
                o_acc[:, 128:] = o_acc[:, 128:] + l_scr[d] * f
                return x

            lax.fori_loop(0, dm + 1, sum_of, 0)
            o_acc[:, 128:] = jnp.broadcast_to(1.0 / jnp.sum(o_acc[:, 128:], axis=1, keepdims=True), (1024, 128))

            def scale_of(d, x):
                f_scr[d] = f_scr[d] * o_acc[:, 128:]
                return x

            lax.fori_loop(0, dm + 1, scale_of, 0)

        def weighted(d):
            for j in range(2):
                p = e_scr[d, :, 128 * j:128 * (j + 1)] * f_scr[d]
                p_scr[d, :, 128 * j:128 * (j + 1)] = p.astype(jnp.bfloat16)
            return dot_nn(p_scr[d], values_of(slot, d))

        o_acc[...] = weighted(0)

        def more_weighted(d, _):
            o_acc[...] = o_acc[...] + weighted(d)
            return 0

        lax.fori_loop(1, dm + 1, more_weighted, 0)
        o_low = o_acc[...].astype(jnp.bfloat16)
        outb[slot, role] = o_low
        delta = jnp.sum(g_ref[...].astype(jnp.float32) * o_low.astype(jnp.float32), axis=1, keepdims=True)
        m_scr[0] = jnp.broadcast_to(delta, (1024, 128))

        def grads(d):
            dp = dot_nt(g_ref[...], values_of(slot, d))
            ds = []
            for j in range(2):
                p = e_scr[d, :, 128 * j:128 * (j + 1)] * f_scr[d]
                ds.append((p * (dp[:, 128 * j:128 * (j + 1)] - m_scr[0])).astype(jnp.bfloat16))
            ds = jnp.concatenate(ds, axis=1)
            dk = dot_tn(ds, q_ref[...]).reshape(8, G, 256)
            dv = dot_tn(p_scr[d], g_ref[...]).reshape(8, G, 256)
            return dot_nn(ds, keys_of(slot, d)), dk, dv

        dq0, dk0, dv0 = grads(0)
        dq_acc[...] = dq0
        if role == 0:
            dkv[slot, 0, :, :, :256] = dk0
            dkv[slot, 0, :, :, 256:] = dv0
        else:
            dkv[slot, 0, :, :, :256] = dkv[slot, 0, :, :, :256] + dk0
            dkv[slot, 0, :, :, 256:] = dkv[slot, 0, :, :, 256:] + dv0

        def more_grads(d, _):
            dq1, dk1, dv1 = grads(d)
            dq_acc[...] = dq_acc[...] + dq1
            dkv[slot, d, :, :, :256] = dkv[slot, d, :, :, :256] + dk1
            dkv[slot, d, :, :, 256:] = dkv[slot, d, :, :, 256:] + dv1
            return 0

        lax.fori_loop(1, dm + 1, more_grads, 0)
        outb[slot, 2 + role] = (dq_acc[...] * scale).astype(jnp.bfloat16)

    @pl.when(n > 0)
    def _():
        kvs[...] = jnp.zeros_like(kvs)
        fetch(base, 0)

    def step(i, _):
        slot = lax.rem(i, 2)
        s = base + i

        @pl.when(i + 1 < n)
        def _():
            fetch(s + 1, 1 - slot)

        @pl.when(i >= 2)
        def _():
            put_wait(s - 2, slot)

        fetch_wait(s, slot)
        any_dm = jnp.maximum(tab[DM + s * 2], tab[DM + s * 2 + 1])

        def clear(d, _):
            dkv[slot, d] = jnp.zeros((8, G, 512), jnp.float32)
            return 0

        lax.fori_loop(1, any_dm + 1, clear, 0)
        attend(0, s, slot)
        attend(1, s, slot)
        put(s, slot)
        return 0

    lax.fori_loop(0, n, step, 0)

    @pl.when(n >= 2)
    def _():
        put_wait(base + n - 2, lax.rem(n, 2))

    @pl.when(n >= 1)
    def _():
        put_wait(base + n - 1, lax.rem(n + 1, 2))


def finish_kernel(n_t, n_alias, scale, tab, acc, *rest):
    bufs = [rest[d * n_t:(d + 1) * n_t] for d in range(3)]
    dk_all, dv_all, dkv_send, own, got, kb, vb, sb, sem, osem = rest[3 * n_t + n_alias:]
    lo = tab[ST]
    n = tab[ST + n_t] if n_t == 1 else NS
    n = n - lo
    c, e = tab[CE], tab[CE + 1]

    def fetch(ss, sl):
        pltpu.make_async_copy(acc.at[ss], own.at[sl], sem.at[sl]).start()
        for d in range(3):
            cnt = tab[at(CNT, c + d + 1, d, ss)]
            off = tab[at(OFF, c + d + 1, d, ss)]
            run_copies(lambda v: tab[sg(c + d + 1, d, v)], n_t, off, cnt,
                       lambda v, slot, k, size: pltpu.make_async_copy(
                           bufs[d][v].at[pl.ds(slot, size)], got.at[sl, d, pl.ds(8 - cnt + k, size)], sem.at[sl]).start())

    def fetch_wait(ss, sl):
        pltpu.make_async_copy(acc.at[ss], own.at[sl], sem.at[sl]).wait()
        for d in range(3):
            run_waits(tab[at(CNT, c + d + 1, d, ss)],
                      lambda size: pltpu.make_async_copy(
                          acc.at[ss, pl.ds(0, size)], got.at[sl, d, pl.ds(0, size)], sem.at[sl]).wait())

    def outputs(ss, sl):
        row = e * NS + ss
        return [
            pltpu.make_async_copy(kb.at[sl], dk_all.at[row], osem.at[sl]),
            pltpu.make_async_copy(vb.at[sl], dv_all.at[row], osem.at[sl]),
            pltpu.make_async_copy(sb.at[sl], dkv_send.at[ss], osem.at[sl]),
        ]

    @pl.when(n > 0)
    def _():
        fetch(lo, 0)

    def step(i, _):
        s = lo + i
        sl = lax.rem(i, 2)

        @pl.when(i + 1 < n)
        def _():
            fetch(s + 1, 1 - sl)

        @pl.when(i >= 2)
        def _():
            for copy in outputs(s - 2, sl):
                copy.wait()

        fetch_wait(s, sl)
        for d in range(3):
            cnt = tab[at(CNT, c + d + 1, d, s)]

            def add(k, _):
                own[sl, k] = own[sl, k] + got[sl, d, k]
                return 0

            lax.fori_loop(8 - cnt, 8, add, 0)
        mine = own[sl, pl.ds(4 * e, 4)].reshape(128, 512)
        other = own[sl, pl.ds(4 - 4 * e, 4)].reshape(128, 512)
        kb[sl] = (mine[:, :256] * scale).astype(jnp.bfloat16)
        vb[sl] = mine[:, 256:].astype(jnp.bfloat16)
        sb[sl, :, :256] = (other[:, :256] * scale).astype(jnp.bfloat16)
        sb[sl, :, 256:] = other[:, 256:].astype(jnp.bfloat16)
        for copy in outputs(s, sl):
            copy.start()
        return 0

    lax.fori_loop(0, n, step, 0)

    @pl.when(n >= 2)
    def _():
        for copy in outputs(lo + n - 2, lax.rem(n, 2)):
            copy.wait()

    @pl.when(n >= 1)
    def _():
        for copy in outputs(lo + n - 1, lax.rem(n + 1, 2)):
            copy.wait()


ANY = pl.BlockSpec(memory_space=pl.ANY)
SMEM = pl.BlockSpec(memory_space=pltpu.SMEM)
VMEM = pl.BlockSpec(memory_space=pltpu.VMEM)
BIG = pltpu.CompilerParams(vmem_limit_bytes=58 * 1024 * 1024)


def solution(mesh):
    n_dev = mesh.shape['cp']
    seq_spec = P('dp', 'cp', None, None)
    id_spec = P('dp', 'cp')
    swap = [(k, k ^ 1) for k in range(n_dev)]
    bf, f32 = jnp.bfloat16, jnp.float32
    shape = jax.ShapeDtypeStruct

    def per_device(query, keys, values, grad_out, doc_id):
        nb, piece, heads, hd = query.shape
        rows = piece * heads
        scale = hd ** -0.5
        rank = lax.axis_index('cp')
        c = rank >> 1
        e = rank & 1
        other = NS * (1 - e)
        q3 = query.reshape(nb, rows, hd)
        g3 = grad_out.reshape(nb, rows, hd)
        k3 = keys.reshape(nb, piece, hd)
        v3 = values.reshape(nb, piece, hd)

        def half(x):
            return lax.dynamic_slice_in_dim(x, other, NS, 0)

        kv_mate = lax.ppermute(jnp.concatenate([half(k3), half(v3)], axis=-1), 'cp', swap)
        docs, ks = pl.pallas_call(
            gather_kernel,
            out_shape=[shape((n_dev, nb, piece), jnp.int32), shape((nb, 128), jnp.int32)],
            in_specs=[VMEM],
            out_specs=[VMEM, VMEM],
            scratch_shapes=[pltpu.SemaphoreType.DMA((n_dev,)), pltpu.SemaphoreType.DMA((n_dev,))],
            compiler_params=pltpu.CompilerParams(has_side_effects=True),
            name="docs",
        )(doc_id)

        def tables(plan, lo, hi):
            me = jnp.stack([c, e, lo, hi]).astype(jnp.int32)
            return pl.pallas_call(
                functools.partial(table_kernel, plan),
                out_shape=shape((NTAB,), jnp.int32),
                in_specs=[SMEM, SMEM],
                out_specs=SMEM,
                name="tables",
            )(ks, me)

        def pack(plan, tab):
            f_cap = plan[0]
            n_t = len(f_cap[0])
            return pl.pallas_call(
                functools.partial(pack_kernel, n_t, [bounds(cap) for cap in f_cap]),
                in_specs=[SMEM] + [ANY] * 3,
                out_specs=[ANY] * (1 + 3 * n_t),
                out_shape=[shape((NS, 8, G, 512), bf)] + [shape((f_cap[d][t], G, 512), bf) for d in range(3) for t in range(n_t)],
                scratch_shapes=[
                    pltpu.VMEM((3, 2, piece, hd), bf), pltpu.VMEM((3, 8, G, 512), bf),
                    pltpu.SemaphoreType.DMA((3,)), pltpu.SemaphoreType.DMA((3,)), pltpu.SemaphoreType.DMA((3,)),
                ],
                name="pack",
            )(tab, k3, v3, kv_mate.reshape(NS, 4, G, 512))

        def forward_hop(x, d):
            hop = 2 * (d + 1)
            return lax.ppermute(x, 'cp', [(k, k + hop) for k in range(n_dev - hop)])

        def backward_hop(x, d):
            hop = 2 * (d + 1)
            return lax.ppermute(x, 'cp', [(k + hop, k) for k in range(n_dev - hop)])

        def attend(plan, t, tab, q_mate, g_mate, kvcol, frecv, state):
            f_cap, b_cap = plan
            n_t = len(f_cap[0])
            live = n_t - t
            n_alias = 0 if state is None else len(state)
            n_in = 7 + 3 * (t + 1)
            return pl.pallas_call(
                functools.partial(compute_kernel, t, n_t, [bounds(cap) for cap in f_cap], n_alias, scale),
                in_specs=[SMEM, VMEM] + [ANY] * (5 + 3 * (t + 1) + n_alias),
                out_specs=[ANY] * (5 + 3 * live),
                scratch_shapes=[
                    pltpu.VMEM((2, 4, rows, hd), bf), pltpu.VMEM((2, 4, rows, hd), bf),
                    pltpu.VMEM((2, 4, 8, G, 512), bf), pltpu.VMEM((2, 4, 8, G, 512), f32),
                    pltpu.VMEM((4, rows, 256), f32), pltpu.VMEM((4, rows, 256), bf),
                    pltpu.VMEM((4, rows, 128), f32), pltpu.VMEM((4, rows, 128), f32), pltpu.VMEM((4, rows, 128), f32),
                    pltpu.VMEM((rows, 128), jnp.int32),
                    pltpu.VMEM((rows, hd), f32), pltpu.VMEM((rows, hd), f32),
                    pltpu.SemaphoreType.DMA((2,)), pltpu.SemaphoreType.DMA((2,)),
                ],
                out_shape=[
                    shape((nb, rows, hd), bf), shape((NS, rows, hd), bf),
                    shape((nb, rows, hd), bf), shape((NS, rows, hd), bf),
                    shape((NS, 8, G, 512), f32),
                ] + [shape((b_cap[d][v], G, 512), f32) for d in range(3) for v in range(t, n_t)],
                input_output_aliases={n_in + k: k for k in range(n_alias)},
                compiler_params=BIG,
                cost_estimate=pl.CostEstimate(flops=60_000_000_000 // n_t, bytes_accessed=100_000_000 // n_t, transcendentals=0),
            )(tab, docs, q3, q_mate, g3, g_mate, kvcol, *[frecv[d][u] for d in range(3) for u in range(t + 1)],
              *([] if state is None else state))

        def finish(plan, tab, acc, brecv, state):
            n_t = len(plan[0][0])
            n_alias = 0 if state is None else 3
            return pl.pallas_call(
                functools.partial(finish_kernel, n_t, n_alias, scale),
                in_specs=[SMEM] + [ANY] * (1 + 3 * n_t + n_alias),
                out_specs=[ANY] * 3,
                out_shape=[shape((nb, piece, hd), bf), shape((nb, piece, hd), bf), shape((NS, piece, 512), bf)],
                scratch_shapes=[
                    pltpu.VMEM((2, 8, G, 512), f32), pltpu.VMEM((2, 3, 8, G, 512), f32),
                    pltpu.VMEM((2, piece, hd), bf), pltpu.VMEM((2, piece, hd), bf), pltpu.VMEM((2, piece, 512), bf),
                    pltpu.SemaphoreType.DMA((2,)), pltpu.SemaphoreType.DMA((2,)),
                ],
                input_output_aliases={2 + 3 * n_t + k: k for k in range(n_alias)},
                name="finish",
            )(tab, acc, *[b for row in brecv for b in row], *([] if state is None else state))

        def place(mine, send):
            got = lax.ppermute(send, 'cp', swap)
            return lax.dynamic_update_slice_in_dim(mine, got, other, 0)

        def place_kv(dk_all, dv_all, dkv_send):
            got = lax.ppermute(dkv_send, 'cp', swap)
            return (lax.dynamic_update_slice_in_dim(dk_all, got[:, :, :hd], other, 0),
                    lax.dynamic_update_slice_in_dim(dv_all, got[:, :, hd:], other, 0))

        def mates():
            q_mate = lax.ppermute(half(q3), 'cp', swap)
            g_mate = lax.ppermute(half(g3), 'cp', swap)
            return q_mate, g_mate

        tab = tables(FAST, jnp.int32(0), jnp.int32(NS))

        def fast():
            n_t = len(FAST[0][0])
            packed = pack(FAST, tab)
            kvcol, fsend = packed[0], packed[1:]
            frecv = [[None] * n_t for _ in range(3)]
            for t in range(n_t):
                for d in range(3):
                    frecv[d][t] = forward_hop(fsend[d * n_t + t], d)
            q_mate, g_mate = mates()
            state = None
            brecv = [[None] * n_t for _ in range(3)]
            for t in range(n_t):
                live = n_t - t
                outs = attend(FAST, t, tab, q_mate, g_mate, kvcol, frecv, state)
                state = list(outs[:5]) + [outs[5 + d * live + k] for d in range(3) for k in range(1, live)]
                for d in range(3):
                    brecv[d][t] = backward_hop(outs[5 + d * live], d)
            o_all, o_send, dq_all, dq_send, acc = state
            attn_out = place(o_all, o_send)
            grad_query = place(dq_all, dq_send)
            return (attn_out, grad_query) + place_kv(*finish(FAST, tab, acc, brecv, None))

        def slow():
            q_mate, g_mate = mates()

            def blank():
                outs = [shape((nb, rows, hd), bf), shape((NS, rows, hd), bf), shape((nb, rows, hd), bf), shape((NS, rows, hd), bf),
                        shape((NS, 8, G, 512), f32), shape((nb, piece, hd), bf), shape((nb, piece, hd), bf), shape((NS, piece, 512), bf)]
                return [jnp.zeros(o.shape, o.dtype) for o in outs]

            def one_round(i, carry):
                state, grads = list(carry[:5]), list(carry[5:])
                tab = tables(SLOW, i * SLOW_SEQS, (i + 1) * SLOW_SEQS)
                packed = pack(SLOW, tab)
                frecv = [[forward_hop(packed[1 + d], d)] for d in range(3)]
                blank_b = [jnp.zeros((SLOW[1][0][0], G, 512), f32) for _ in range(3)]
                outs = attend(SLOW, 0, tab, q_mate, g_mate, packed[0], frecv, state + blank_b)
                brecv = [[backward_hop(outs[5 + d], d)] for d in range(3)]
                return tuple(outs[:5]) + tuple(finish(SLOW, tab, outs[4], brecv, grads))

            out = lax.fori_loop(0, NS // SLOW_SEQS, one_round, tuple(blank()))
            return (place(out[0], out[1]), place(out[2], out[3])) + place_kv(*out[5:])

        attn_out, grad_query, grad_keys, grad_values = lax.cond(tab[FIT] > 0, fast, slow)
        return (attn_out.reshape(query.shape), grad_query.reshape(query.shape),
                grad_keys.reshape(keys.shape), grad_values.reshape(values.shape))

    return jax.shard_map(per_device, mesh=mesh, in_specs=(seq_spec, seq_spec, seq_spec, seq_spec, id_spec),
                         out_specs=(seq_spec, seq_spec, seq_spec, seq_spec), check_vma=False)
```

time: 2310 us -> 663 us (0.29)
  matrix products: 1040 us -> 0 us
  waiting for transfers between devices: 941 us -> 396 us
  other arithmetic: 155 us -> 2.11 us
  Pallas kernels: 0 us -> 124 us
  local copies, waits for them, and re-layouts: 128 us -> 45.7 us
  starting transfers between devices: 37.4 us -> 77.3 us
    dot_general x55 -> x0, matrix products: 1040 us -> none  [the longest x8 235 us: out_update(): jnp.einsum('cril,cle->crie', prob_bf16, val_cur, preferred_element_type=j...]
    ppermute x72 -> x30, waiting for transfers between devices: 941 us -> 396 us  [the longest x12 358 us: backward_hop(): return lax.ppermute(x, 'cp', [(k + hop, k) for k in range(n_dev - hop)])]
    pallas_call x0 -> x8, Pallas kernels: none -> 124 us  [the longest x4 82.8 us: attend(): pl.pallas_call(functools.partial(compute_kernel, t, n_t, [bounds(cap) for...]
    while x105 -> x0, local copies, waits for them, and re-layouts: 85.1 us -> none
    reduce_sum x8 -> x0, other arithmetic: 68.5 us -> none  [stats_update(): jnp.sum(exp_scores, axis=-1)]
    unnamed x37 -> x4, local copies, waits for them, and re-layouts: 40.4 us -> 0.01 us
    ppermute x72 -> x30, starting transfers between devices: 37.4 us -> 77.3 us  [the longest x12 60 us: forward_hop(): return lax.ppermute(x, 'cp', [(k, k + hop) for k in range(n_dev - hop)])]
    unnamed x3 -> x0, other arithmetic: 35.3 us -> none
  transfers between devices with their start and end apart: 72 -> 30, of which waited for: 36 -> 11; matrix products, arithmetic and copies ran while one was open for 27% -> 3% of each run, Pallas kernels for 0% -> 19%
where the time goes in v2:
time: 663 us; the launch traced here: 657 us
  waiting for transfers between devices  396 us (60%)
  Pallas kernels  124 us (19%)
  starting transfers between devices  77.3 us (12%)
  local copies, waits for them, and re-layouts  45.7 us (7%)
  loops' own time  9.38 us (1%)
    ppermute x12, waiting for transfers between devices, backward_hop(): return lax.ppermute(x, 'cp', [(k + hop, k) for k in range(n_dev - hop)])  358 us
    pallas_call x4, Pallas kernels, attend(): pl.pallas_call(functools.partial(compute_kernel, t, n_t, [bounds(cap) for...  82.8 us
    ppermute x12, starting transfers between devices, forward_hop(): return lax.ppermute(x, 'cp', [(k, k + hop) for k in range(n_dev - hop)])  60 us
    ppermute x12, waiting for transfers between devices, forward_hop(): return lax.ppermute(x, 'cp', [(k, k + hop) for k in range(n_dev - hop)])  33.5 us
    dynamic_slice x3, local copies, waits for them, and re-layouts, half(): return lax.dynamic_slice_in_dim(x, other, NS, 0)  16.9 us
    dynamic_update_slice x2, local copies, waits for them, and re-layouts, place(): return lax.dynamic_update_slice_in_dim(mine, got, other, 0)  15.8 us
    ppermute x12, starting transfers between devices, backward_hop(): return lax.ppermute(x, 'cp', [(k + hop, k) for k in range(n_dev - hop)])  15.6 us
    pallas_call x1, Pallas kernels, finish(): pl.pallas_call(functools.partial(finish_kernel, n_t, n_alias, scale), in_...  14.7 us
  transfers between devices with their start and end apart: 30, of which 11 were waited for; matrix products, arithmetic and copies ran while one was open for 3% of the time, Pallas kernels for 19%

profile of v2, /device:TPU:0, one launch (start us, length us, event | category | flops | bytes accessed | tf_op | source)
XLA Modules:
  0.0 656.9 jit_solution(2184874938881149451)
XLA Ops:
  0.6 1.9 dynamic-slice_bitcast_fusion
  2.6 1.5 pad_maximum_fusion
  4.9 9.7 %docs.1 = (s32[8,32,128]{2,1,0:T(8,128)S(1)}, s32[32,128]{1,0:T(8,128)S(1)}) custom-call(s32[32,128]{1,0:T(8,128)} %doc.1), custom_call_target="tpu_custom_call" | custom-call | tf_op jit(solution)/shard_map/docs/pallas_call | solution.py:576
  15.2 3.9 tables.2
  20.4 635.1 %conditional.1 = (bf16[32,128,8,256]{3,2,1,0:T(8,128)(2,1)}, bf16[32,128,8,256]{3,2,1,0:T(8,128)(2,1)}, bf16[32,128,1,256]{3,1,2,0:T(8,128)(2,1)}, bf16[32,128,1,256]{3,1,2,0:T(8,128)(2,1)}) conditional(s32[]{:T(128)} %bitcast.24, (s32[]{:T(128)}, bf16[32,1024,256]{2,1,0:T(8,128)(2,1)}, bf16[32,1024,256]{2,1,0:T(8,128)(2,1)}, s32[]{:T(128)}, ...), branch_computations={%region_0.0_spmd, %region_3.0_spmd} | conditional | flops 60000002048 | bytes 542541696 | solution.py:725
  29.0 7.5 %constant_dynamic-slice_fusion.2 = bf16[16,1024,256]{2,1,0:T(8,128)(2,1)} fusion(bf16[32,1024,256]{2,1,0:T(8,128)(2,1)} %get-tuple-element.370.g_all, s32[]{:T(128)S(6)} %select_n.1), kind=kLoop, calls=%fused_computation.15 | loop fusion | bytes 16777220 | tf_op jit(solution)/shard_map/cond/branch_1_fun/dynamic_slice | solution.py:573
  36.6 7.5 %constant_dynamic-slice_fusion.3 = bf16[16,1024,256]{2,1,0:T(8,128)(2,1)} fusion(bf16[32,1024,256]{2,1,0:T(8,128)(2,1)} %get-tuple-element.368.q_all, s32[]{:T(128)S(6)} %select_n.1), kind=kLoop, calls=%fused_computation.16 | loop fusion | bytes 16777220 | tf_op jit(solution)/shard_map/cond/branch_1_fun/dynamic_slice | solution.py:573
  44.5 12.6 %pack.6 = (bf16[16,8,32,512]{3,2,1,0:T(8,128)(2,1)}, bf16[24,32,512]{2,1,0:T(8,128)(2,1)}, bf16[34,32,512]{2,1,0:T(8,128)(2,1)}, bf16[34,32,512]{2,1,0:T(8,128)(...) custom-call(s32[848]{0:T(1024)S(1)} %get-tuple-element.366.tab, ...), custom_call_target="tpu_custom_call" | custom-call | tf_op jit(solution)/shard_map/cond/branch_1_fun/pack/pallas_call | solution.py:599
  57.1 2.8 collective-permute-start.2
  59.9 2.6 collective-permute-start.6
  63.8 21.9 %collective-permute-done.10.rest_2_.rest_4_.rest_6_.rest_8_ = bf16[12,32,512]{2,1,0:T(8,128)(2,1)S(1)} collective-permute-done((bf16[12,32,512]{2,1,0:T(8,128)(2,1)}, bf16[12,32,512]{2,1,0:T(8,128)(2,1)S(1)}, u32[]{:S(2)}, u32[]{:S(2)}) %collective-permute-start.10) | collective-permute-done | bytes 393248 | tf_op jit(solution)/shard_map/cond/branch_1_fun/ppermute | solution.py:613
  85.7 5.2 collective-permute-start.12
  92.2 2.0 collective-permute-start.13
  95.6 3.1 collective-permute-start.7
  98.7 1.4 collective-permute-start.3
  100.1 79.4 %branch_1_fun.4 = (bf16[32,1024,256]{2,1,0:T(8,128)(2,1)}, bf16[16,1024,256]{2,1,0:T(8,128)(2,1)}, bf16[32,1024,256]{2,1,0:T(8,128)(2,1)}, bf16[16,1024,256]{2,1...) custom-call(s32[848]{0:T(1024)S(1)} %get-tuple-element.366.tab, ...), custom_call_target="tpu_custom_call" | custom-call | flops 15000000512 | bytes 25000000 | tf_op jit(solution)/shard_map/cond/branch_1_fun/pallas_call | solution.py:625
  179.5 2.2 collective-permute-start.9
  185.6 35.4 %collective-permute-start.5 = (bf16[32,32,512]{2,1,0:T(8,128)(2,1)}, bf16[32,32,512]{2,1,0:T(8,128)(2,1)S(1)}, u32[]{:S(2)}, u32[]{:S(2)}) collective-permute-start(bf16[32,32,512]{2,1,0:T(8,128)(2,1)} %get-tuple-element.378), channel_id=1, source_target_pairs={{0,2},{1,3},{2,4},{3,5},{4,6},{5,7}} | collective-permute-start | bytes 3145736 | tf_op jit(solution)/shard_map/cond/branch_1_fun/ppermute | solution.py:613
  223.2 10.3 %collective-permute-done.5.rest_3_ = bf16[32,32,512]{2,1,0:T(8,128)(2,1)S(1)} collective-permute-done((bf16[32,32,512]{2,1,0:T(8,128)(2,1)}, bf16[32,32,512]{2,1,0:T(8,128)(2,1)S(1)}, u32[]{:S(2)}, u32[]{:S(2)}) %collective-permute-start.5) | collective-permute-done | bytes 1048608 | tf_op jit(solution)/shard_map/cond/branch_1_fun/ppermute | solution.py:613
  235.9 1.4 collective-permute-start.25
  240.3 99.4 %collective-permute-done.24.rest_8_ = f32[6,32,512]{2,1,0:T(8,128)S(1)} collective-permute-done((f32[6,32,512]{2,1,0:T(8,128)}, f32[6,32,512]{2,1,0:T(8,128)S(1)}, u32[]{:S(2)}, u32[]{:S(2)}) %collective-permute-start.24) | collective-permute-done | bytes 393248 | tf_op jit(solution)/shard_map/cond/branch_1_fun/ppermute | solution.py:617
  343.7 20.2 %collective-permute-done.20.rest_4_ = f32[12,32,512]{2,1,0:T(8,128)S(1)} collective-permute-done((f32[12,32,512]{2,1,0:T(8,128)}, f32[12,32,512]{2,1,0:T(8,128)S(1)}, u32[]{:S(2)}, u32[]{:S(2)}) %collective-permute-start.20) | collective-permute-done | bytes 786464 | tf_op jit(solution)/shard_map/cond/branch_1_fun/ppermute | solution.py:617
  365.2 29.9 %collective-permute-done.27.rest_11_ = f32[18,32,512]{2,1,0:T(8,128)S(1)} collective-permute-done((f32[18,32,512]{2,1,0:T(8,128)}, f32[18,32,512]{2,1,0:T(8,128)S(1)}, u32[]{:S(2)}, u32[]{:S(2)}) %collective-permute-start.27) | collective-permute-done | bytes 1179680 | tf_op jit(solution)/shard_map/cond/branch_1_fun/ppermute | solution.py:617
  399.8 25.5 %collective-permute-done.21.rest_5_ = f32[22,32,512]{2,1,0:T(8,128)S(1)} collective-permute-done((f32[22,32,512]{2,1,0:T(8,128)S(1)}, f32[22,32,512]{2,1,0:T(8,128)S(1)}, u32[]{:S(2)}, u32[]{:S(2)}) %collective-permute-start.21) | collective-permute-done | bytes 1441824 | tf_op jit(solution)/shard_map/cond/branch_1_fun/ppermute | solution.py:617
  427.8 31.3 %collective-permute-done.23.rest_7_ = f32[24,32,512]{2,1,0:T(8,128)S(1)} collective-permute-done((f32[24,32,512]{2,1,0:T(8,128)}, f32[24,32,512]{2,1,0:T(8,128)S(1)}, u32[]{:S(2)}, u32[]{:S(2)}) %collective-permute-start.23) | collective-permute-done | bytes 1572896 | tf_op jit(solution)/shard_map/cond/branch_1_fun/ppermute | solution.py:617
  461.5 29.5 %collective-permute-done.22.rest_6_ = f32[24,32,512]{2,1,0:T(8,128)S(1)} collective-permute-done((f32[24,32,512]{2,1,0:T(8,128)S(1)}, f32[24,32,512]{2,1,0:T(8,128)S(1)}, u32[]{:S(2)}, u32[]{:S(2)}) %collective-permute-start.22) | collective-permute-done | bytes 1572896 | tf_op jit(solution)/shard_map/cond/branch_1_fun/ppermute | solution.py:617
  493.5 122.2 %collective-permute-done.17.rest_1_ = f32[32,32,512]{2,1,0:T(8,128)S(1)} collective-permute-done((f32[32,32,512]{2,1,0:T(8,128)}, f32[32,32,512]{2,1,0:T(8,128)S(1)}, u32[]{:S(2)}, u32[]{:S(2)}) %collective-permute-start.17) | collective-permute-done | bytes 2097184 | tf_op jit(solution)/shard_map/cond/branch_1_fun/ppermute | solution.py:617
  617.7 1.4 copy-done.13
  619.1 14.7 %finish.6 = (bf16[32,128,256]{2,1,0:T(8,128)(2,1)}, bf16[32,128,256]{2,1,0:T(8,128)(2,1)S(1)}, bf16[16,128,512]{2,1,0:T(8,128)(2,1)}) custom-call(s32[848]{0:T(1024)S(1)} %copy-done.32, f32[16,8,32,512]{3,2,1,0:T(8,128)} %get-tuple-element.424.acc, f32[20,32,512]{2,1,0:T(8,128)} %copy-done.21, f32[32,32,512]{2,1,0:T(8,128)} %copy-done.15, ...), custom_call_target="tpu_custom_call" | custom-call | tf_op jit(solution)/shard_map/cond/branch_1_fun/finish/pallas_call | solution.py:652
  633.9 4.4 collective-permute-done.28
  639.5 8.3 %constant_dynamic-update-slice_fusion.3 = bf16[32,1024,256]{2,1,0:T(8,128)(2,1)} fusion(bf16[32,1024,256]{2,1,0:T(8,128)(2,1)} %get-tuple-element.420, bf16[16,1024,256]{2,1,0:T(8,128)(2,1)} %collective-permute-done.14, s32[]{:T(128)S(6)} %select_n.1), kind=kLoop, calls=%fused_computation.14 | loop fusion | bytes 16777220 | tf_op jit(solution)/shard_map/cond/branch_1_fun/dynamic_update_slice | solution.py:668
  647.7 7.5 %constant_dynamic-update-slice_fusion.2 = bf16[32,1024,256]{2,1,0:T(8,128)(2,1)} fusion(bf16[32,1024,256]{2,1,0:T(8,128)(2,1)} %get-tuple-element.422, bf16[16,1024,256]{2,1,0:T(8,128)(2,1)} %collective-permute-done.15, s32[]{:T(128)S(6)} %select_n.1), kind=kLoop, calls=%fused_computation.13 | loop fusion | bytes 16777220 | tf_op jit(solution)/shard_map/cond/branch_1_fun/dynamic_update_slice | solution.py:668
  (110 shorter events, 38.2 us)
Async XLA Ops:
  4.1 16.3 %collective-permute-start.40 = (bf16[16,128,512]{2,1,0:T(8,128)(2,1)}, bf16[16,128,512]{2,1,0:T(8,128)(2,1)}, u32[]{:S(2)}, u32[]{:S(2)}) collective-permute-start(bf16[16,128,512]{2,1,0:T(8,128)(2,1)} %pad_maximum_fusion), channel_id=1, source_target_pairs={{0,1},{1,0},{2,3},{3,2},{4,5},{5,4},{6,7},{7,6}} | collective-permute-start | bytes 6291464 | tf_op jit(solution)/shard_map/ppermute | solution.py:575
  36.5 59.0 %collective-permute-start.1 = (bf16[16,1024,256]{2,1,0:T(8,128)(2,1)}, bf16[16,1024,256]{2,1,0:T(8,128)(2,1)}, u32[]{:S(2)}, u32[]{:S(2)}) collective-permute-start(bf16[16,1024,256]{2,1,0:T(8,128)(2,1)} %constant_dynamic-slice_fusion.2), channel_id=1, source_target_pairs={{0,1},{1,0},{2,3},{3,2},{4,5},{5,4},{6,7},{7,6}} | collective-permute-start | bytes 25165832 | tf_op jit(solution)/shard_map/cond/branch_1_fun/ppermute | solution.py:677
  44.1 54.5 %collective-permute-start = (bf16[16,1024,256]{2,1,0:T(8,128)(2,1)}, bf16[16,1024,256]{2,1,0:T(8,128)(2,1)}, u32[]{:S(2)}, u32[]{:S(2)}) collective-permute-start(bf16[16,1024,256]{2,1,0:T(8,128)(2,1)} %constant_dynamic-slice_fusion.3), channel_id=1, source_target_pairs={{0,1},{1,0},{2,3},{3,2},{4,5},{5,4},{6,7},{7,6}} | collective-permute-start | bytes 25165832 | tf_op jit(solution)/shard_map/cond/branch_1_fun/ppermute | solution.py:676
  57.1 37.1 %collective-permute-start.2 = (bf16[24,32,512]{2,1,0:T(8,128)(2,1)}, bf16[24,32,512]{2,1,0:T(8,128)(2,1)S(1)}, u32[]{:S(2)}, u32[]{:S(2)}) collective-permute-start(bf16[24,32,512]{2,1,0:T(8,128)(2,1)} %get-tuple-element.375), channel_id=1, source_target_pairs={{0,2},{1,3},{2,4},{3,5},{4,6},{5,7}} | collective-permute-start | bytes 2359304 | tf_op jit(solution)/shard_map/cond/branch_1_fun/ppermute | solution.py:613
  59.9 32.3 %collective-permute-start.6 = (bf16[20,32,512]{2,1,0:T(8,128)(2,1)}, bf16[20,32,512]{2,1,0:T(8,128)(2,1)S(1)}, u32[]{:S(2)}, u32[]{:S(2)}) collective-permute-start(bf16[20,32,512]{2,1,0:T(8,128)(2,1)} %get-tuple-element.379), channel_id=1, source_target_pairs={{0,4},{1,5},{2,6},{3,7}} | collective-permute-start | bytes 1966088 | tf_op jit(solution)/shard_map/cond/branch_1_fun/ppermute | solution.py:613
  62.5 23.2 %collective-permute-start.10 = (bf16[12,32,512]{2,1,0:T(8,128)(2,1)}, bf16[12,32,512]{2,1,0:T(8,128)(2,1)S(1)}, u32[]{:S(2)}, u32[]{:S(2)}) collective-permute-start(bf16[12,32,512]{2,1,0:T(8,128)(2,1)} %get-tuple-element.383), channel_id=1, source_target_pairs={{0,6},{1,7}} | collective-permute-start | bytes 1179656 | tf_op jit(solution)/shard_map/cond/branch_1_fun/ppermute | solution.py:613
  85.7 99.8 %collective-permute-start.12 = (bf16[12,32,512]{2,1,0:T(8,128)(2,1)}, bf16[12,32,512]{2,1,0:T(8,128)(2,1)S(1)}, u32[]{:S(2)}, u32[]{:S(2)}) collective-permute-start(bf16[12,32,512]{2,1,0:T(8,128)(2,1)} %get-tuple-element.385), channel_id=1, source_target_pairs={{0,6},{1,7}} | collective-permute-start | bytes 1179656 | tf_op jit(solution)/shard_map/cond/branch_1_fun/ppermute | solution.py:613
  92.2 131.0 %collective-permute-start.13 = (bf16[12,32,512]{2,1,0:T(8,128)(2,1)}, bf16[12,32,512]{2,1,0:T(8,128)(2,1)}, u32[]{:S(2)}, u32[]{:S(2)}) collective-permute-start(bf16[12,32,512]{2,1,0:T(8,128)(2,1)} %get-tuple-element.386), channel_id=1, source_target_pairs={{0,6},{1,7}} | collective-permute-start | bytes 1179656 | tf_op jit(solution)/shard_map/cond/branch_1_fun/ppermute | solution.py:613
  94.2 85.2 %collective-permute-start.11 = (bf16[14,32,512]{2,1,0:T(8,128)(2,1)}, bf16[14,32,512]{2,1,0:T(8,128)(2,1)S(1)}, u32[]{:S(2)}, u32[]{:S(2)}) collective-permute-start(bf16[14,32,512]{2,1,0:T(8,128)(2,1)} %get-tuple-element.384), channel_id=1, source_target_pairs={{0,6},{1,7}} | collective-permute-start | bytes 1376264 | tf_op jit(solution)/shard_map/cond/branch_1_fun/ppermute | solution.py:613
  95.6 86.1 %collective-permute-start.7 = (bf16[24,32,512]{2,1,0:T(8,128)(2,1)}, bf16[24,32,512]{2,1,0:T(8,128)(2,1)S(1)}, u32[]{:S(2)}, u32[]{:S(2)}) collective-permute-start(bf16[24,32,512]{2,1,0:T(8,128)(2,1)} %get-tuple-element.380), channel_id=1, source_target_pairs={{0,4},{1,5},{2,6},{3,7}} | collective-permute-start | bytes 2359304 | tf_op jit(solution)/shard_map/cond/branch_1_fun/ppermute | solution.py:613
  98.7 84.3 %collective-permute-start.3 = (bf16[34,32,512]{2,1,0:T(8,128)(2,1)}, bf16[34,32,512]{2,1,0:T(8,128)(2,1)S(1)}, u32[]{:S(2)}, u32[]{:S(2)}) collective-permute-start(bf16[34,32,512]{2,1,0:T(8,128)(2,1)} %get-tuple-element.376), channel_id=1, source_target_pairs={{0,2},{1,3},{2,4},{3,5},{4,6},{5,7}} | collective-permute-start | bytes 3342344 | tf_op jit(solution)/shard_map/cond/branch_1_fun/ppermute | solution.py:613
  179.5 43.8 %collective-permute-start.9 = (bf16[20,32,512]{2,1,0:T(8,128)(2,1)}, bf16[20,32,512]{2,1,0:T(8,128)(2,1)}, u32[]{:S(2)}, u32[]{:S(2)}) collective-permute-start(bf16[20,32,512]{2,1,0:T(8,128)(2,1)} %get-tuple-element.382), channel_id=1, source_target_pairs={{0,4},{1,5},{2,6},{3,7}} | collective-permute-start | bytes 1966088 | tf_op jit(solution)/shard_map/cond/branch_1_fun/ppermute | solution.py:613
  181.6 39.4 %collective-permute-start.8 = (bf16[22,32,512]{2,1,0:T(8,128)(2,1)}, bf16[22,32,512]{2,1,0:T(8,128)(2,1)S(1)}, u32[]{:S(2)}, u32[]{:S(2)}) collective-permute-start(bf16[22,32,512]{2,1,0:T(8,128)(2,1)} %get-tuple-element.381), channel_id=1, source_target_pairs={{0,4},{1,5},{2,6},{3,7}} | collective-permute-start | bytes 2162696 | tf_op jit(solution)/shard_map/cond/branch_1_fun/ppermute | solution.py:613
  183.0 38.0 %collective-permute-start.4 = (bf16[34,32,512]{2,1,0:T(8,128)(2,1)}, bf16[34,32,512]{2,1,0:T(8,128)(2,1)S(1)}, u32[]{:S(2)}, u32[]{:S(2)}) collective-permute-start(bf16[34,32,512]{2,1,0:T(8,128)(2,1)} %get-tuple-element.377), channel_id=1, source_target_pairs={{0,2},{1,3},{2,4},{3,5},{4,6},{5,7}} | collective-permute-start | bytes 3342344 | tf_op jit(solution)/shard_map/cond/branch_1_fun/ppermute | solution.py:613
  185.6 48.0 %collective-permute-start.5 = (bf16[32,32,512]{2,1,0:T(8,128)(2,1)}, bf16[32,32,512]{2,1,0:T(8,128)(2,1)S(1)}, u32[]{:S(2)}, u32[]{:S(2)}) collective-permute-start(bf16[32,32,512]{2,1,0:T(8,128)(2,1)} %get-tuple-element.378), channel_id=1, source_target_pairs={{0,2},{1,3},{2,4},{3,5},{4,6},{5,7}} | collective-permute-start | bytes 3145736 | tf_op jit(solution)/shard_map/cond/branch_1_fun/ppermute | solution.py:613
  234.5 384.6 %copy-start.32 = (s32[848]{0:T(1024)S(1)}, s32[848]{0:T(1024)}, u32[]{:S(2)}) copy-start(s32[848]{0:T(1024)} %copy-done.30) | copy-start | bytes 10180 | tf_op jit(solution)/shard_map/cond
  235.9 403.6 %collective-permute-start.14 = (bf16[16,1024,256]{2,1,0:T(8,128)(2,1)}, bf16[16,1024,256]{2,1,0:T(8,128)(2,1)}, u32[]{:S(2)}, u32[]{:S(2)}) collective-permute-start(bf16[16,1024,256]{2,1,0:T(8,128)(2,1)} %get-tuple-element.421), channel_id=1, source_target_pairs={{0,1},{1,0},{2,3},{3,2},{4,5},{5,4},{6,7},{7,6}} | collective-permute-start | bytes 25165832 | tf_op jit(solution)/shard_map/cond/branch_1_fun/ppermute | solution.py:667
  235.9 105.1 %collective-permute-start.25 = (f32[10,32,512]{2,1,0:T(8,128)}, f32[10,32,512]{2,1,0:T(8,128)S(1)}, u32[]{:S(2)}, u32[]{:S(2)}) collective-permute-start(f32[10,32,512]{2,1,0:T(8,128)} %get-tuple-element.434), channel_id=1, source_target_pairs={{6,0},{7,1}} | collective-permute-start | bytes 1966088 | tf_op jit(solution)/shard_map/cond/branch_1_fun/ppermute | solution.py:617
  237.4 105.0 %collective-permute-start.26 = (f32[12,32,512]{2,1,0:T(8,128)S(1)}, f32[12,32,512]{2,1,0:T(8,128)S(1)}, u32[]{:S(2)}, u32[]{:S(2)}) collective-permute-start(f32[12,32,512]{2,1,0:T(8,128)S(1)} %copy-done.11), channel_id=1, source_target_pairs={{6,0},{7,1}} | collective-permute-start | bytes 2359304 | tf_op jit(solution)/shard_map/cond/branch_1_fun/ppermute | solution.py:617
  238.7 409.1 %collective-permute-start.15 = (bf16[16,1024,256]{2,1,0:T(8,128)(2,1)}, bf16[16,1024,256]{2,1,0:T(8,128)(2,1)}, u32[]{:S(2)}, u32[]{:S(2)}) collective-permute-start(bf16[16,1024,256]{2,1,0:T(8,128)(2,1)} %get-tuple-element.423), channel_id=1, source_target_pairs={{0,1},{1,0},{2,3},{3,2},{4,5},{5,4},{6,7},{7,6}} | collective-permute-start | bytes 25165832 | tf_op jit(solution)/shard_map/cond/branch_1_fun/ppermute | solution.py:667
  239.0 100.7 %collective-permute-start.24 = (f32[6,32,512]{2,1,0:T(8,128)}, f32[6,32,512]{2,1,0:T(8,128)S(1)}, u32[]{:S(2)}, u32[]{:S(2)}) collective-permute-start(f32[6,32,512]{2,1,0:T(8,128)} %get-tuple-element.433), channel_id=1, source_target_pairs={{6,0},{7,1}} | collective-permute-start | bytes 1179656 | tf_op jit(solution)/shard_map/cond/branch_1_fun/ppermute | solution.py:617
  339.8 57.7 %collective-permute-start.16 = (f32[20,32,512]{2,1,0:T(8,128)}, f32[20,32,512]{2,1,0:T(8,128)S(1)}, u32[]{:S(2)}, u32[]{:S(2)}) collective-permute-start(f32[20,32,512]{2,1,0:T(8,128)} %get-tuple-element.425), channel_id=1, source_target_pairs={{2,0},{3,1},{4,2},{5,3},{6,4},{7,5}} | collective-permute-start | bytes 3932168 | tf_op jit(solution)/shard_map/cond/branch_1_fun/ppermute | solution.py:617
  341.1 54.0 %collective-permute-start.27 = (f32[18,32,512]{2,1,0:T(8,128)}, f32[18,32,512]{2,1,0:T(8,128)S(1)}, u32[]{:S(2)}, u32[]{:S(2)}) collective-permute-start(f32[18,32,512]{2,1,0:T(8,128)} %get-tuple-element.436), channel_id=1, source_target_pairs={{6,0},{7,1}} | collective-permute-start | bytes 3538952 | tf_op jit(solution)/shard_map/cond/branch_1_fun/ppermute | solution.py:617
  342.4 21.5 %collective-permute-start.20 = (f32[12,32,512]{2,1,0:T(8,128)}, f32[12,32,512]{2,1,0:T(8,128)S(1)}, u32[]{:S(2)}, u32[]{:S(2)}) collective-permute-start(f32[12,32,512]{2,1,0:T(8,128)} %get-tuple-element.429), channel_id=1, source_target_pairs={{4,0},{5,1},{6,2},{7,3}} | collective-permute-start | bytes 2359304 | tf_op jit(solution)/shard_map/cond/branch_1_fun/ppermute | solution.py:617
  363.9 251.8 %copy-start.25 = (f32[12,32,512]{2,1,0:T(8,128)}, f32[12,32,512]{2,1,0:T(8,128)S(1)}, u32[]{:S(2)}) copy-start(f32[12,32,512]{2,1,0:T(8,128)S(1)} %collective-permute-done.20.rest_4_) | copy-start | bytes 2359300 | tf_op jit(solution)/shard_map/cond
  363.9 61.4 %collective-permute-start.21 = (f32[22,32,512]{2,1,0:T(8,128)S(1)}, f32[22,32,512]{2,1,0:T(8,128)S(1)}, u32[]{:S(2)}, u32[]{:S(2)}) collective-permute-start(f32[22,32,512]{2,1,0:T(8,128)S(1)} %copy-done.19), channel_id=1, source_target_pairs={{4,0},{5,1},{6,2},{7,3}} | collective-permute-start | bytes 4325384 | tf_op jit(solution)/shard_map/cond/branch_1_fun/ppermute | solution.py:617
  396.1 62.9 %collective-permute-start.23 = (f32[24,32,512]{2,1,0:T(8,128)}, f32[24,32,512]{2,1,0:T(8,128)S(1)}, u32[]{:S(2)}, u32[]{:S(2)}) collective-permute-start(f32[24,32,512]{2,1,0:T(8,128)} %get-tuple-element.432), channel_id=1, source_target_pairs={{4,0},{5,1},{6,2},{7,3}} | collective-permute-start | bytes 4718600 | tf_op jit(solution)/shard_map/cond/branch_1_fun/ppermute | solution.py:617
  398.5 92.5 %collective-permute-start.22 = (f32[24,32,512]{2,1,0:T(8,128)S(1)}, f32[24,32,512]{2,1,0:T(8,128)S(1)}, u32[]{:S(2)}, u32[]{:S(2)}) collective-permute-start(f32[24,32,512]{2,1,0:T(8,128)S(1)} %copy-done.7), channel_id=1, source_target_pairs={{4,0},{5,1},{6,2},{7,3}} | collective-permute-start | bytes 4718600 | tf_op jit(solution)/shard_map/cond/branch_1_fun/ppermute | solution.py:617
  426.5 189.2 %collective-permute-start.19 = (f32[38,32,512]{2,1,0:T(8,128)}, f32[38,32,512]{2,1,0:T(8,128)S(1)}, u32[]{:S(2)}, u32[]{:S(2)}) collective-permute-start(f32[38,32,512]{2,1,0:T(8,128)} %get-tuple-element.428), channel_id=1, source_target_pairs={{2,0},{3,1},{4,2},{5,3},{6,4},{7,5}} | collective-permute-start | bytes 7471112 | tf_op jit(solution)/shard_map/cond/branch_1_fun/ppermute | solution.py:617
  460.2 155.5 %collective-permute-start.18 = (f32[34,32,512]{2,1,0:T(8,128)S(1)}, f32[34,32,512]{2,1,0:T(8,128)S(1)}, u32[]{:S(2)}, u32[]{:S(2)}) collective-permute-start(f32[34,32,512]{2,1,0:T(8,128)S(1)} %copy-done.5), channel_id=1, source_target_pairs={{2,0},{3,1},{4,2},{5,3},{6,4},{7,5}} | collective-permute-start | bytes 6684680 | tf_op jit(solution)/shard_map/cond/branch_1_fun/ppermute | solution.py:617
  492.2 123.5 %collective-permute-start.17 = (f32[32,32,512]{2,1,0:T(8,128)}, f32[32,32,512]{2,1,0:T(8,128)S(1)}, u32[]{:S(2)}, u32[]{:S(2)}) collective-permute-start(f32[32,32,512]{2,1,0:T(8,128)} %get-tuple-element.426), channel_id=1, source_target_pairs={{2,0},{3,1},{4,2},{5,3},{6,4},{7,5}} | collective-permute-start | bytes 6291464 | tf_op jit(solution)/shard_map/cond/branch_1_fun/ppermute | solution.py:617
  633.9 4.4 collective-permute-start.28
  (30 other events, 796.0 us)

commit v3 on v2

--- a/solution.py
+++ b/solution.py
@@ -15,11 +15,15 @@
 NCH = 4
 
 FAST = (
-    ((24, 34, 34, 32), (20, 24, 22, 20), (12, 14, 12, 12)),
-    ((20, 32, 34, 38), (12, 22, 24, 24), (6, 10, 12, 18)),
+    ((28, 34, 34, 30), (22, 24, 22, 18), (14, 14, 12, 10)),
+    ((20, 28, 30, 46), (12, 18, 22, 34), (6, 8, 10, 24)),
+    (4, 8, 12, 16),
 )
+RELAY_F = (1, 2)
+RELAY_B = (1, 2)
+QA = 4
 SLOW_SEQS = 4
-SLOW = (((8 * SLOW_SEQS,),) * 3,) * 2
+SLOW = (((8 * SLOW_SEQS,),) * 3,) * 2 + ((NS,),)
 
 CNT, OFF, DM, ST, SG, CE, FIT = 0, 336, 672, 704, 712, 840, 844
 NTAB = 848
@@ -65,7 +69,7 @@
 
 
 def table_kernel(plan, ks, me, tab):
-    f_cap, b_cap = plan
+    f_cap, b_cap, quota = plan
     n_t = len(f_cap[0])
     f_lo = [bounds(cap) for cap in f_cap]
     c, e, lo, hi = me[0], me[1], me[2], me[3]
@@ -104,6 +108,8 @@
                         tab[at(OFF, cc, d, s)] = off[d]
                     off[d] = off[d] + n
                 for t in range(n_t):
+                    if s >= quota[t]:
+                        continue
                     ok = s < hi
                     for d in range(min(cc, 3)):
                         ok = ok & (off[d] <= f_lo[d][t + 1])
@@ -150,70 +156,50 @@
             wait(size)
 
 
-def pack_kernel(n_t, f_lo, tab, k_all, v_all, mate, kvcol, *rest):
+def pack_kernel(n_t, n, f_lo, tab, k_all, v_all, mate, kvcol, *rest):
     chunks = [rest[d * n_t:(d + 1) * n_t] for d in range(3)]
     inb, stage, isem, sem, csem = rest[3 * n_t:]
     lo = tab[ST]
-    n = tab[ST + n_t] if n_t == 1 else NS
-    n = n - lo
     c, e = tab[CE], tab[CE + 1]
-
-    def inputs(s, sl):
-        return [
-            pltpu.make_async_copy(k_all.at[e * NS + s], inb.at[sl, 0], isem.at[sl]),
-            pltpu.make_async_copy(v_all.at[e * NS + s], inb.at[sl, 1], isem.at[sl]),
-            pltpu.make_async_copy(mate.at[s], stage.at[sl, pl.ds(4 - 4 * e, 4)], isem.at[sl]),
-        ]
-
-    def out_copy(s, sl):
-        return pltpu.make_async_copy(stage.at[sl], kvcol.at[s], csem.at[sl])
-
-    def drain(s, sl):
-        out_copy(s, sl).wait()
-        for d in range(3):
-            run_waits(tab[at(CNT, c + d + 1, d, s)],
-                      lambda size: pltpu.make_async_copy(stage.at[sl, pl.ds(0, size)], kvcol.at[s, pl.ds(0, size)], sem.at[sl]).wait())
-
-    @pl.when(n > 0)
-    def _():
-        for copy in inputs(lo, 0):
+    part = n // 4
+    loads = []
+    for i in range(4):
+        rows = pl.ds(i * part, part)
+        loads.append([
+            pltpu.make_async_copy(k_all.at[pl.ds(e * NS + lo + i * part, part)], inb.at[0, rows], isem.at[i]),
+            pltpu.make_async_copy(v_all.at[pl.ds(e * NS + lo + i * part, part)], inb.at[1, rows], isem.at[i]),
+            pltpu.make_async_copy(mate.at[pl.ds(lo + i * part, part)], stage.at[rows, pl.ds(4 - 4 * e, 4)], isem.at[i]),
+        ])
+        for copy in loads[-1]:
             copy.start()
-
-    def step(i, _):
-        s = lo + i
-        sl = lax.rem(i, 3)
-        nx = lax.rem(i + 1, 3)
-
-        @pl.when(i >= 2)
-        def _():
-            drain(s - 2, nx)
-
-        @pl.when(i + 1 < n)
-        def _():
-            for copy in inputs(s + 1, nx):
-                copy.start()
-
-        for copy in inputs(s, sl):
+    for i in range(4):
+        for copy in loads[i]:
             copy.wait()
-        stage[sl, pl.ds(4 * e, 4)] = jnp.concatenate([inb[sl, 0], inb[sl, 1]], axis=1).reshape(4, G, 512)
-        out_copy(s, sl).start()
-        for d in range(3):
-            cnt = tab[at(CNT, c + d + 1, d, s)]
-            off = tab[at(OFF, c + d + 1, d, s)]
-            run_copies(lambda v: f_lo[d][v], n_t, off, cnt,
-                       lambda v, slot, k, size: pltpu.make_async_copy(
-                           stage.at[sl, pl.ds(8 - cnt + k, size)], chunks[d][v].at[pl.ds(slot, size)], sem.at[sl]).start())
+
+        def step(j, _):
+            s = lo + j
+            stage[j, pl.ds(4 * e, 4), :, :256] = inb[0, j].reshape(4, G, 256)
+            stage[j, pl.ds(4 * e, 4), :, 256:] = inb[1, j].reshape(4, G, 256)
+            pltpu.make_async_copy(stage.at[j], kvcol.at[s], csem).start()
+            for d in range(3):
+                cnt = tab[at(CNT, c + d + 1, d, s)]
+                off = tab[at(OFF, c + d + 1, d, s)]
+                run_copies(lambda v: f_lo[d][v], n_t, off, cnt,
+                           lambda v, slot, k, size: pltpu.make_async_copy(
+                               stage.at[j, pl.ds(8 - cnt + k, size)], chunks[d][v].at[pl.ds(slot, size)], sem).start())
+            return 0
+
+        lax.fori_loop(i * part, (i + 1) * part, step, 0)
+
+    def drain(j, _):
+        pltpu.make_async_copy(stage.at[j], kvcol.at[lo + j], csem).wait()
+        for d in range(3):
+            run_waits(tab[at(CNT, c + d + 1, d, lo + j)],
+                      lambda size: pltpu.make_async_copy(
+                          stage.at[j, pl.ds(0, size)], kvcol.at[lo + j, pl.ds(0, size)], sem).wait())
         return 0
 
-    lax.fori_loop(0, n, step, 0)
-
-    @pl.when(n >= 2)
-    def _():
-        drain(lo + n - 2, lax.rem(n + 1, 3))
-
-    @pl.when(n >= 1)
-    def _():
-        drain(lo + n - 1, lax.rem(n + 2, 3))
+    lax.fori_loop(0, n, drain, 0)
 
 
 def dot_nt(a, b):
@@ -228,9 +214,20 @@
     return lax.dot_general(a, b, (((0,), (0,)), ((), ())), preferred_element_type=jnp.float32)
 
 
-def compute_kernel(t, n_t, f_lo, n_alias, scale, tab, docs, q_all, q_mate, g_all, g_mate, kvcol, *rest):
-    fbuf = [rest[d * (t + 1):(d + 1) * (t + 1)] for d in range(3)]
-    rest = rest[3 * (t + 1) + n_alias:]
+def split(refs, counts):
+    out = []
+    for k in counts:
+        out.append(refs[:k])
+        refs = refs[k:]
+    return out, refs
+
+
+def compute_kernel(t, n_t, f_lo, n_mate, ways, n_alias, scale, tab, docs, q_all, g_all, kvcol, *rest):
+    q_mates, rest = rest[:n_mate], rest[n_mate:]
+    g_mates, rest = rest[:n_mate], rest[n_mate:]
+    fbuf, rest = split(rest, ways)
+    fbuf = [fbuf[d * (t + 1):(d + 1) * (t + 1)] for d in range(3)]
+    rest = rest[n_alias:]
     o_all, o_send, dq_all, dq_send, acc = rest[:5]
     rest = rest[5:]
     live = n_t - t
@@ -247,10 +244,14 @@
         return [
             pltpu.make_async_copy(src, dst, isem.at[sl])
             for src, dst in (
-                (kvcol.at[ss], kvs.at[sl, 0]),
-                (q_all.at[own], qg.at[sl, 0]), (q_mate.at[ss], qg.at[sl, 1]),
-                (g_all.at[own], qg.at[sl, 2]), (g_mate.at[ss], qg.at[sl, 3]),
+                (kvcol.at[ss], kvs.at[sl, 0]), (q_all.at[own], qg.at[sl, 0]), (g_all.at[own], qg.at[sl, 2]),
             )
+        ]
+
+    def mate_inputs(refs, row, sl):
+        return [
+            pltpu.make_async_copy(refs[0].at[row], qg.at[sl, 1], isem.at[sl]),
+            pltpu.make_async_copy(refs[1].at[row], qg.at[sl, 3], isem.at[sl]),
         ]
 
     def outputs(ss, sl):
@@ -267,15 +268,37 @@
     def fetch(ss, sl):
         for copy in inputs(ss, sl):
             copy.start()
+        if n_mate == 1:
+            for copy in mate_inputs((q_mates[0], g_mates[0]), ss, sl):
+                copy.start()
+        else:
+            @pl.when(ss < QA)
+            def _():
+                for copy in mate_inputs((q_mates[0], g_mates[0]), ss, sl):
+                    copy.start()
+
+            @pl.when(ss >= QA)
+            def _():
+                for copy in mate_inputs((q_mates[1], g_mates[1]), ss - QA, sl):
+                    copy.start()
         for d in range(3):
             cnt = tab[at(CNT, c, d, ss)]
             off = tab[at(OFF, c, d, ss)]
-            run_copies(lambda v: f_lo[d][v], t + 1, off, cnt,
-                       lambda v, slot, k, size: pltpu.make_async_copy(
-                           fbuf[d][v].at[pl.ds(slot, size)], kvs.at[sl, d + 1, pl.ds(8 - cnt + k, size)], isem.at[sl]).start())
+
+            def issue(v, slot, k, size):
+                def go(ref):
+                    pltpu.make_async_copy(ref.at[pl.ds(slot, size)], kvs.at[sl, d + 1, pl.ds(8 - cnt + k, size)], isem.at[sl]).start()
+
+                if len(fbuf[d][v]) == 1:
+                    go(fbuf[d][v][0])
+                else:
+                    pl.when(c != 2)(lambda: go(fbuf[d][v][0]))
+                    pl.when(c == 2)(lambda: go(fbuf[d][v][1]))
+
+            run_copies(lambda v: f_lo[d][v], t + 1, off, cnt, issue)
 
     def fetch_wait(ss, sl):
-        for copy in inputs(ss, sl):
+        for copy in inputs(ss, sl) + mate_inputs((q_mates[0], g_mates[0]), 0, sl):
             copy.wait()
         for d in range(3):
             run_waits(tab[at(CNT, c, d, ss)],
@@ -328,11 +351,11 @@
                 if causal:
                     vis = vis & (lane + 128 * j <= row_tok + 128 * h)
                 xs.append(jnp.where(vis, sc[:, 128 * j:128 * (j + 1)], NEG_BIG))
-            top = jnp.max(jnp.maximum(xs[0], xs[1]), axis=1, keepdims=True)
+            top = jnp.maximum(xs[0], xs[1])
             es = [jnp.exp2(x - top) for x in xs]
             e_scr[d, :, :128] = es[0]
             e_scr[d, :, 128:] = es[1]
-            m_scr[d] = jnp.broadcast_to(top, (1024, 128))
+            m_scr[d] = top
             l_scr[d] = es[0] + es[1]
 
         scores(0, True)
@@ -345,17 +368,26 @@
 
         @pl.when(dm == 0)
         def _():
-            f_scr[0] = jnp.broadcast_to(1.0 / jnp.sum(l_scr[0], axis=1, keepdims=True), (1024, 128))
+            m = m_scr[0]
+            f = jnp.exp2(m - jnp.max(m, axis=1, keepdims=True))
+            f_scr[0] = f * (1.0 / jnp.sum(l_scr[0] * f, axis=1, keepdims=True))
 
         @pl.when(dm > 0)
         def _():
-            def top_of(d, m):
+            o_acc[:, :128] = jnp.maximum(m_scr[0], m_scr[1])
+
+            def top_of(d, x):
                 o_acc[:, :128] = jnp.maximum(o_acc[:, :128], m_scr[d])
-                return m
-
-            o_acc[:, :128] = m_scr[0]
-            lax.fori_loop(1, dm + 1, top_of, 0)
-            o_acc[:, 128:] = jnp.zeros((1024, 128), jnp.float32)
+                return x
+
+            lax.fori_loop(2, dm + 1, top_of, 0)
+            top = jnp.broadcast_to(jnp.max(o_acc[:, :128], axis=1, keepdims=True), (1024, 128))
+            o_acc[:, :128] = top
+            f0 = jnp.exp2(m_scr[0] - top)
+            f1 = jnp.exp2(m_scr[1] - top)
+            f_scr[0] = f0
+            f_scr[1] = f1
+            o_acc[:, 128:] = l_scr[0] * f0 + l_scr[1] * f1
 
             def sum_of(d, x):
                 f = jnp.exp2(m_scr[d] - o_acc[:, :128])
@@ -363,14 +395,17 @@
                 o_acc[:, 128:] = o_acc[:, 128:] + l_scr[d] * f
                 return x
 
-            lax.fori_loop(0, dm + 1, sum_of, 0)
-            o_acc[:, 128:] = jnp.broadcast_to(1.0 / jnp.sum(o_acc[:, 128:], axis=1, keepdims=True), (1024, 128))
+            lax.fori_loop(2, dm + 1, sum_of, 0)
+            inv = jnp.broadcast_to(1.0 / jnp.sum(o_acc[:, 128:], axis=1, keepdims=True), (1024, 128))
+            o_acc[:, 128:] = inv
+            f_scr[0] = f_scr[0] * inv
+            f_scr[1] = f_scr[1] * inv
 
             def scale_of(d, x):
                 f_scr[d] = f_scr[d] * o_acc[:, 128:]
                 return x
 
-            lax.fori_loop(0, dm + 1, scale_of, 0)
+            lax.fori_loop(2, dm + 1, scale_of, 0)
 
         def weighted(d):
             for j in range(2):
@@ -461,9 +496,10 @@
         put_wait(base + n - 1, lax.rem(n + 1, 2))
 
 
-def finish_kernel(n_t, n_alias, scale, tab, acc, *rest):
-    bufs = [rest[d * n_t:(d + 1) * n_t] for d in range(3)]
-    dk_all, dv_all, dkv_send, own, got, kb, vb, sb, sem, osem = rest[3 * n_t + n_alias:]
+def finish_kernel(n_t, ways, n_alias, scale, tab, acc, *rest):
+    bufs, rest = split(rest, ways)
+    bufs = [bufs[d * n_t:(d + 1) * n_t] for d in range(3)]
+    dk_all, dv_all, dkv_send, own, got, kb, vb, sb, sem, osem = rest[n_alias:]
     lo = tab[ST]
     n = tab[ST + n_t] if n_t == 1 else NS
     n = n - lo
@@ -474,9 +510,18 @@
         for d in range(3):
             cnt = tab[at(CNT, c + d + 1, d, ss)]
             off = tab[at(OFF, c + d + 1, d, ss)]
-            run_copies(lambda v: tab[sg(c + d + 1, d, v)], n_t, off, cnt,
-                       lambda v, slot, k, size: pltpu.make_async_copy(
-                           bufs[d][v].at[pl.ds(slot, size)], got.at[sl, d, pl.ds(8 - cnt + k, size)], sem.at[sl]).start())
+
+            def issue(v, slot, k, size):
+                def go(ref):
+                    pltpu.make_async_copy(ref.at[pl.ds(slot, size)], got.at[sl, d, pl.ds(8 - cnt + k, size)], sem.at[sl]).start()
+
+                if len(bufs[d][v]) == 1:
+                    go(bufs[d][v][0])
+                else:
+                    pl.when(c != 1)(lambda: go(bufs[d][v][0]))
+                    pl.when(c == 1)(lambda: go(bufs[d][v][1]))
+
+            run_copies(lambda v: tab[sg(c + d + 1, d, v)], n_t, off, cnt, issue)
 
     def fetch_wait(ss, sl):
         pltpu.make_async_copy(acc.at[ss], own.at[sl], sem.at[sl]).wait()
@@ -593,38 +638,42 @@
                 name="tables",
             )(ks, me)
 
-        def pack(plan, tab):
+        def pack(plan, tab, n):
             f_cap = plan[0]
             n_t = len(f_cap[0])
             return pl.pallas_call(
-                functools.partial(pack_kernel, n_t, [bounds(cap) for cap in f_cap]),
+                functools.partial(pack_kernel, n_t, n, [bounds(cap) for cap in f_cap]),
                 in_specs=[SMEM] + [ANY] * 3,
                 out_specs=[ANY] * (1 + 3 * n_t),
                 out_shape=[shape((NS, 8, G, 512), bf)] + [shape((f_cap[d][t], G, 512), bf) for d in range(3) for t in range(n_t)],
                 scratch_shapes=[
-                    pltpu.VMEM((3, 2, piece, hd), bf), pltpu.VMEM((3, 8, G, 512), bf),
-                    pltpu.SemaphoreType.DMA((3,)), pltpu.SemaphoreType.DMA((3,)), pltpu.SemaphoreType.DMA((3,)),
+                    pltpu.VMEM((2, n, piece, hd), bf), pltpu.VMEM((n, 8, G, 512), bf),
+                    pltpu.SemaphoreType.DMA((4,)), pltpu.SemaphoreType.DMA, pltpu.SemaphoreType.DMA,
                 ],
                 name="pack",
             )(tab, k3, v3, kv_mate.reshape(NS, 4, G, 512))
 
+        def chip_hop(x, *moves):
+            return lax.ppermute(x, 'cp', [(2 * a + k, 2 * b + k) for a, b in moves for k in range(2)])
+
         def forward_hop(x, d):
-            hop = 2 * (d + 1)
-            return lax.ppermute(x, 'cp', [(k, k + hop) for k in range(n_dev - hop)])
+            return chip_hop(x, *[(k, k + d + 1) for k in range(NCH - d - 1)])
 
         def backward_hop(x, d):
-            hop = 2 * (d + 1)
-            return lax.ppermute(x, 'cp', [(k + hop, k) for k in range(n_dev - hop)])
-
-        def attend(plan, t, tab, q_mate, g_mate, kvcol, frecv, state):
-            f_cap, b_cap = plan
+            return chip_hop(x, *[(k + d + 1, k) for k in range(NCH - d - 1)])
+
+        def attend(plan, t, tab, mates, kvcol, frecv, state):
+            f_cap, b_cap = plan[:2]
             n_t = len(f_cap[0])
             live = n_t - t
             n_alias = 0 if state is None else len(state)
-            n_in = 7 + 3 * (t + 1)
+            mates = mates[:1] if n_t > 1 and t == 0 else mates
+            got = [frecv[d][u] for d in range(3) for u in range(t + 1)]
+            flat = [x for way in got for x in way]
+            n_in = 5 + 2 * len(mates) + len(flat)
             return pl.pallas_call(
-                functools.partial(compute_kernel, t, n_t, [bounds(cap) for cap in f_cap], n_alias, scale),
-                in_specs=[SMEM, VMEM] + [ANY] * (5 + 3 * (t + 1) + n_alias),
+                functools.partial(compute_kernel, t, n_t, [bounds(cap) for cap in f_cap], len(mates), [len(way) for way in got], n_alias, scale),
+                in_specs=[SMEM, VMEM] + [ANY] * (n_in - 2 + n_alias),
                 out_specs=[ANY] * (5 + 3 * live),
                 scratch_shapes=[
                     pltpu.VMEM((2, 4, rows, hd), bf), pltpu.VMEM((2, 4, rows, hd), bf),
@@ -643,15 +692,16 @@
                 input_output_aliases={n_in + k: k for k in range(n_alias)},
                 compiler_params=BIG,
                 cost_estimate=pl.CostEstimate(flops=60_000_000_000 // n_t, bytes_accessed=100_000_000 // n_t, transcendentals=0),
-            )(tab, docs, q3, q_mate, g3, g_mate, kvcol, *[frecv[d][u] for d in range(3) for u in range(t + 1)],
-              *([] if state is None else state))
+            )(tab, docs, q3, g3, kvcol, *[m[0] for m in mates], *[m[1] for m in mates], *flat, *([] if state is None else state))
 
         def finish(plan, tab, acc, brecv, state):
             n_t = len(plan[0][0])
             n_alias = 0 if state is None else 3
+            got = [way for row in brecv for way in row]
+            flat = [x for way in got for x in way]
             return pl.pallas_call(
-                functools.partial(finish_kernel, n_t, n_alias, scale),
-                in_specs=[SMEM] + [ANY] * (1 + 3 * n_t + n_alias),
+                functools.partial(finish_kernel, n_t, [len(way) for way in got], n_alias, scale),
+                in_specs=[SMEM] + [ANY] * (1 + len(flat) + n_alias),
                 out_specs=[ANY] * 3,
                 out_shape=[shape((nb, piece, hd), bf), shape((nb, piece, hd), bf), shape((NS, piece, 512), bf)],
                 scratch_shapes=[
@@ -659,9 +709,9 @@
                     pltpu.VMEM((2, piece, hd), bf), pltpu.VMEM((2, piece, hd), bf), pltpu.VMEM((2, piece, 512), bf),
                     pltpu.SemaphoreType.DMA((2,)), pltpu.SemaphoreType.DMA((2,)),
                 ],
-                input_output_aliases={2 + 3 * n_t + k: k for k in range(n_alias)},
+                input_output_aliases={2 + len(flat) + k: k for k in range(n_alias)},
                 name="finish",
-            )(tab, acc, *[b for row in brecv for b in row], *([] if state is None else state))
+            )(tab, acc, *flat, *([] if state is None else state))
 
         def place(mine, send):
             got = lax.ppermute(send, 'cp', swap)
@@ -672,37 +722,48 @@
             return (lax.dynamic_update_slice_in_dim(dk_all, got[:, :, :hd], other, 0),
                     lax.dynamic_update_slice_in_dim(dv_all, got[:, :, hd:], other, 0))
 
-        def mates():
-            q_mate = lax.ppermute(half(q3), 'cp', swap)
-            g_mate = lax.ppermute(half(g3), 'cp', swap)
-            return q_mate, g_mate
+        def swap_part(x, lo, n):
+            return lax.ppermute(lax.dynamic_slice_in_dim(x, other + lo, n, 0), 'cp', swap)
 
         tab = tables(FAST, jnp.int32(0), jnp.int32(NS))
 
         def fast():
             n_t = len(FAST[0][0])
-            packed = pack(FAST, tab)
+            packed = pack(FAST, tab, NS)
             kvcol, fsend = packed[0], packed[1:]
             frecv = [[None] * n_t for _ in range(3)]
             for t in range(n_t):
                 for d in range(3):
-                    frecv[d][t] = forward_hop(fsend[d * n_t + t], d)
-            q_mate, g_mate = mates()
+                    x = fsend[d * n_t + t]
+                    if d == 0 and t in RELAY_F:
+                        across = chip_hop(x, (0, 1), (2, 3))
+                        mid = chip_hop(x, (1, 3))
+                        frecv[0][t] = (across, chip_hop(mid, (3, 2)))
+                    else:
+                        frecv[d][t] = (forward_hop(x, d),)
+            mates = [(swap_part(q3, 0, QA), swap_part(g3, 0, QA)),
+                     (swap_part(q3, QA, NS - QA), swap_part(g3, QA, NS - QA))]
             state = None
             brecv = [[None] * n_t for _ in range(3)]
             for t in range(n_t):
                 live = n_t - t
-                outs = attend(FAST, t, tab, q_mate, g_mate, kvcol, frecv, state)
+                outs = attend(FAST, t, tab, mates, kvcol, frecv, state)
                 state = list(outs[:5]) + [outs[5 + d * live + k] for d in range(3) for k in range(1, live)]
                 for d in range(3):
-                    brecv[d][t] = backward_hop(outs[5 + d * live], d)
+                    x = outs[5 + d * live]
+                    if d == 0 and t in RELAY_B:
+                        across = chip_hop(x, (1, 0), (3, 2))
+                        mid = chip_hop(x, (2, 0))
+                        brecv[0][t] = (across, chip_hop(mid, (0, 1)))
+                    else:
+                        brecv[d][t] = (backward_hop(x, d),)
             o_all, o_send, dq_all, dq_send, acc = state
             attn_out = place(o_all, o_send)
             grad_query = place(dq_all, dq_send)
             return (attn_out, grad_query) + place_kv(*finish(FAST, tab, acc, brecv, None))
 
         def slow():
-            q_mate, g_mate = mates()
+            mates = [(swap_part(q3, 0, NS), swap_part(g3, 0, NS))]
 
             def blank():
                 outs = [shape((nb, rows, hd), bf), shape((NS, rows, hd), bf), shape((nb, rows, hd), bf), shape((NS, rows, hd), bf),
@@ -712,11 +773,11 @@
             def one_round(i, carry):
                 state, grads = list(carry[:5]), list(carry[5:])
                 tab = tables(SLOW, i * SLOW_SEQS, (i + 1) * SLOW_SEQS)
-                packed = pack(SLOW, tab)
-                frecv = [[forward_hop(packed[1 + d], d)] for d in range(3)]
+                packed = pack(SLOW, tab, SLOW_SEQS)
+                frecv = [[(forward_hop(packed[1 + d], d),)] for d in range(3)]
                 blank_b = [jnp.zeros((SLOW[1][0][0], G, 512), f32) for _ in range(3)]
-                outs = attend(SLOW, 0, tab, q_mate, g_mate, packed[0], frecv, state + blank_b)
-                brecv = [[backward_hop(outs[5 + d], d)] for d in range(3)]
+                outs = attend(SLOW, 0, tab, mates, packed[0], frecv, state + blank_b)
+                brecv = [[(backward_hop(outs[5 + d], d),)] for d in range(3)]
                 return tuple(outs[:5]) + tuple(finish(SLOW, tab, outs[4], brecv, grads))
 
             out = lax.fori_loop(0, NS // SLOW_SEQS, one_round, tuple(blank()))

time: 663 us -> 655 us (0.988)
  starting transfers between devices: 77.3 us -> 149 us
  waiting for transfers between devices: 396 us -> 326 us
  local copies, waits for them, and re-layouts: 45.7 us -> 38.1 us
    ppermute x26 -> x36, starting transfers between devices: 76 us -> 147 us  [the longest x32 147 us: chip_hop(): lax.ppermute(x, 'cp', [(2 * a + k, 2 * b + k) for a, b in moves for k in...]
    ppermute x26 -> x36, waiting for transfers between devices: 392 us -> 322 us  [the longest x32 322 us: chip_hop(): lax.ppermute(x, 'cp', [(2 * a + k, 2 * b + k) for a, b in moves for k in...]
    dynamic_slice x0 -> x4, local copies, waits for them, and re-layouts: none -> 15.3 us  [swap_part(): lax.dynamic_slice_in_dim(x, other + lo, n, 0)]
    dynamic_slice x3 -> x1, local copies, waits for them, and re-layouts: 16.9 us -> 1.75 us  [half(): return lax.dynamic_slice_in_dim(x, other, NS, 0)]
    pallas_call x4, Pallas kernels: 82.8 us -> 92 us  [attend(): pl.pallas_call(functools.partial(compute_kernel, t, n_t, [bounds(cap) for...]
    cond x60 -> x66, local copies, waits for them, and re-layouts: 11.2 us -> 3.4 us
  transfers between devices with their start and end apart: 30 -> 40, of which waited for: 11 -> 14; matrix products, arithmetic and copies ran while one was open for 3% -> 3% of each run, Pallas kernels for 19% -> 19%
where the time goes in v3:
time: 655 us; the launch traced here: 648 us
  waiting for transfers between devices  326 us (50%)
  starting transfers between devices  149 us (23%)
  Pallas kernels  126 us (19%)
  local copies, waits for them, and re-layouts  38.1 us (6%)
    ppermute x32, waiting for transfers between devices, chip_hop(): lax.ppermute(x, 'cp', [(2 * a + k, 2 * b + k) for a, b in moves for k in...  322 us
    ppermute x32, starting transfers between devices, chip_hop(): lax.ppermute(x, 'cp', [(2 * a + k, 2 * b + k) for a, b in moves for k in...  147 us
    pallas_call x4, Pallas kernels, attend(): pl.pallas_call(functools.partial(compute_kernel, t, n_t, [bounds(cap) for...  92 us
    dynamic_update_slice x2, local copies, waits for them, and re-layouts, place(): return lax.dynamic_update_slice_in_dim(mine, got, other, 0)  15.8 us
    dynamic_slice x4, local copies, waits for them, and re-layouts, swap_part(): lax.dynamic_slice_in_dim(x, other + lo, n, 0)  15.3 us
    pallas_call x1, Pallas kernels, finish(): pl.pallas_call(functools.partial(finish_kernel, n_t, [len(way) for way in...  14.9 us
  transfers between devices with their start and end apart: 40, of which 14 were waited for; matrix products, arithmetic and copies ran while one was open for 3% of the time, Pallas kernels for 19%

profile of v3, /device:TPU:0, one launch (start us, length us, event | category | flops | bytes accessed | tf_op | source)
XLA Modules:
  0.0 648.2 jit_solution(15408481119594473195)
XLA Ops:
  4.8 9.7 %docs.1 = (s32[8,32,128]{2,1,0:T(8,128)S(1)}, s32[32,128]{1,0:T(8,128)S(1)}) custom-call(s32[32,128]{1,0:T(8,128)} %doc.1), custom_call_target="tpu_custom_call" | custom-call | tf_op jit(solution)/shard_map/docs/pallas_call | solution.py:621
  19.8 627.1 %conditional.1 = (bf16[32,128,8,256]{3,2,1,0:T(8,128)(2,1)}, bf16[32,128,8,256]{3,2,1,0:T(8,128)(2,1)}, bf16[32,128,1,256]{3,1,2,0:T(8,128)(2,1)}, bf16[32,128,1,256]{3,1,2,0:T(8,128)(2,1)}) conditional(s32[]{:T(128)} %bitcast.24, (s32[]{:T(128)}, bf16[32,1024,256]{2,1,0:T(8,128)(2,1)}, bf16[32,1024,256]{2,1,0:T(8,128)(2,1)}, s32[]{:T(128)}, ...), branch_computations={%region_0.0_spmd, %region_3.0_spmd} | conditional | flops 60000002048 | bytes 614617728 | solution.py:786
  23.3 5.9 constant_dynamic-slice_fusion.4
  29.3 5.8 constant_dynamic-slice_fusion.2
  35.5 6.4 pack.6
  49.2 6.1 collective-permute-done.16.rest_4_.rest_9_.rest_12_.rest_14_
  55.3 5.4 collective-permute-start.17
  62.4 7.7 %collective-permute-done.17.rest_10_.rest_13_.rest_15_ = bf16[14,32,512]{2,1,0:T(8,128)(2,1)S(1)} collective-permute-done((bf16[14,32,512]{2,1,0:T(8,128)(2,1)}, bf16[14,32,512]{2,1,0:T(8,128)(2,1)S(1)}, u32[]{:S(2)}, u32[]{:S(2)}) %collective-permute-start.17) | collective-permute-done | bytes 458784 | tf_op jit(solution)/shard_map/cond/branch_1_fun/ppermute | solution.py:657
  72.0 7.8 %collective-permute-done.12.rest_3_.rest_7_.rest_9_.rest_10_ = bf16[22,32,512]{2,1,0:T(8,128)(2,1)} collective-permute-done((bf16[22,32,512]{2,1,0:T(8,128)(2,1)}, bf16[22,32,512]{2,1,0:T(8,128)(2,1)}, u32[]{:S(2)}, u32[]{:S(2)}) %collective-permute-start.12) | collective-permute-done | bytes 720928 | tf_op jit(solution)/shard_map/cond/branch_1_fun/ppermute | solution.py:657
  79.8 21.1 %collective-permute-start.4 = (bf16[28,32,512]{2,1,0:T(8,128)(2,1)S(1)}, bf16[28,32,512]{2,1,0:T(8,128)(2,1)S(1)}, u32[]{:S(2)}, u32[]{:S(2)}) collective-permute-start(bf16[28,32,512]{2,1,0:T(8,128)(2,1)S(1)} %copy-done.38), channel_id=1, source_target_pairs={{0,2},{1,3},{2,4},{3,5},{4,6},{5,7}} | collective-permute-start | bytes 2752520 | tf_op jit(solution)/shard_map/cond/branch_1_fun/ppermute | solution.py:657
  100.9 20.2 %collective-permute-done.4.rest_2_.rest_4_ = bf16[28,32,512]{2,1,0:T(8,128)(2,1)S(1)} collective-permute-done((bf16[28,32,512]{2,1,0:T(8,128)(2,1)S(1)}, bf16[28,32,512]{2,1,0:T(8,128)(2,1)S(1)}, u32[]{:S(2)}, u32[]{:S(2)}) %collective-permute-start.4) | collective-permute-done | bytes 917536 | tf_op jit(solution)/shard_map/cond/branch_1_fun/ppermute | solution.py:657
  122.7 31.1 %collective-permute-start.5 = (bf16[34,32,512]{2,1,0:T(8,128)(2,1)}, bf16[34,32,512]{2,1,0:T(8,128)(2,1)S(1)}, u32[]{:S(2)}, u32[]{:S(2)}) collective-permute-start(bf16[34,32,512]{2,1,0:T(8,128)(2,1)} %get-tuple-element.376), channel_id=1, source_target_pairs={{0,2},{1,3},{4,6},{5,7}} | collective-permute-start | bytes 3342344 | tf_op jit(solution)/shard_map/cond/branch_1_fun/ppermute | solution.py:657
  157.2 23.1 %branch_1_fun.4 = (bf16[32,1024,256]{2,1,0:T(8,128)(2,1)}, bf16[16,1024,256]{2,1,0:T(8,128)(2,1)}, bf16[32,1024,256]{2,1,0:T(8,128)(2,1)}, bf16[16,1024,256]{2,1...) custom-call(s32[848]{0:T(1024)} %copy-done.33, ...), custom_call_target="tpu_custom_call" | custom-call | flops 15000000512 | bytes 25000000 | tf_op jit(solution)/shard_map/cond/branch_1_fun/pallas_call | solution.py:674
  180.3 20.0 %collective-permute-start.8 = (bf16[34,32,512]{2,1,0:T(8,128)(2,1)}, bf16[34,32,512]{2,1,0:T(8,128)(2,1)S(1)}, u32[]{:S(2)}, u32[]{:S(2)}) collective-permute-start(bf16[34,32,512]{2,1,0:T(8,128)(2,1)} %get-tuple-element.377), channel_id=1, source_target_pairs={{0,2},{1,3},{4,6},{5,7}} | collective-permute-start | bytes 3342344 | tf_op jit(solution)/shard_map/cond/branch_1_fun/ppermute | solution.py:657
  200.3 6.6 %collective-permute-start.14 = (bf16[22,32,512]{2,1,0:T(8,128)(2,1)}, bf16[22,32,512]{2,1,0:T(8,128)(2,1)S(1)}, u32[]{:S(2)}, u32[]{:S(2)}) collective-permute-start(bf16[22,32,512]{2,1,0:T(8,128)(2,1)} %get-tuple-element.381), channel_id=1, source_target_pairs={{0,4},{1,5},{2,6},{3,7}} | collective-permute-start | bytes 2162696 | tf_op jit(solution)/shard_map/cond/branch_1_fun/ppermute | solution.py:657
  210.4 23.1 %branch_1_fun.5 = (bf16[32,1024,256]{2,1,0:T(8,128)(2,1)}, bf16[16,1024,256]{2,1,0:T(8,128)(2,1)}, bf16[32,1024,256]{2,1,0:T(8,128)(2,1)}, bf16[16,1024,256]{2,1...) custom-call(s32[848]{0:T(1024)} %copy-done.33, ...), custom_call_target="tpu_custom_call", output_to_operand_aliasing={{0}: (16, {}), {1}: (17, {}), {2}: (18, {}), {3}: (19, {}),... | custom-call | flops 15000000512 | bytes 25000000 | tf_op jit(solution)/shard_map/cond/branch_1_fun/pallas_call | solution.py:674
  233.9 16.7 %collective-permute-start.15 = (bf16[18,32,512]{2,1,0:T(8,128)(2,1)}, bf16[18,32,512]{2,1,0:T(8,128)(2,1)S(1)}, u32[]{:S(2)}, u32[]{:S(2)}) collective-permute-start(bf16[18,32,512]{2,1,0:T(8,128)(2,1)} %get-tuple-element.382), channel_id=1, source_target_pairs={{0,4},{1,5},{2,6},{3,7}} | collective-permute-start | bytes 1769480 | tf_op jit(solution)/shard_map/cond/branch_1_fun/ppermute | solution.py:657
  250.7 9.2 %collective-permute-start.19 = (bf16[10,32,512]{2,1,0:T(8,128)(2,1)}, bf16[10,32,512]{2,1,0:T(8,128)(2,1)S(1)}, u32[]{:S(2)}, u32[]{:S(2)}) collective-permute-start(bf16[10,32,512]{2,1,0:T(8,128)(2,1)} %get-tuple-element.386), channel_id=1, source_target_pairs={{0,6},{1,7}} | collective-permute-start | bytes 983048 | tf_op jit(solution)/shard_map/cond/branch_1_fun/ppermute | solution.py:657
  262.6 22.7 %branch_1_fun.6 = (bf16[32,1024,256]{2,1,0:T(8,128)(2,1)}, bf16[16,1024,256]{2,1,0:T(8,128)(2,1)}, bf16[32,1024,256]{2,1,0:T(8,128)(2,1)}, bf16[16,1024,256]{2,1...) custom-call(s32[848]{0:T(1024)S(1)} %copy-done.34, ...), custom_call_target="tpu_custom_call", output_to_operand_aliasing={{0}: (20, {}), {1}: (21, {}), {2}: (22, {}), {3}: (23, {}),... | custom-call | flops 15000000512 | bytes 25000000 | tf_op jit(solution)/shard_map/cond/branch_1_fun/pallas_call | solution.py:674
  290.1 23.1 %branch_1_fun.7 = (bf16[32,1024,256]{2,1,0:T(8,128)(2,1)}, bf16[16,1024,256]{2,1,0:T(8,128)(2,1)}, bf16[32,1024,256]{2,1,0:T(8,128)(2,1)}, bf16[16,1024,256]{2,1...) custom-call(s32[848]{0:T(1024)S(1)} %copy-done.34, ...), custom_call_target="tpu_custom_call", output_to_operand_aliasing={{0}: (23, {}), {1}: (24, {}), {2}: (25, {}), {3}: (26, {}),... | custom-call | flops 15000000512 | bytes 25000000 | tf_op jit(solution)/shard_map/cond/branch_1_fun/pallas_call | solution.py:674
  313.2 19.6 %collective-permute-done.34.rest_10_ = f32[6,32,512]{2,1,0:T(8,128)} collective-permute-done((f32[6,32,512]{2,1,0:T(8,128)}, f32[6,32,512]{2,1,0:T(8,128)}, u32[]{:S(2)}, u32[]{:S(2)}) %collective-permute-start.34) | collective-permute-done | bytes 393248 | tf_op jit(solution)/shard_map/cond/branch_1_fun/ppermute | solution.py:657
  336.8 96.2 %collective-permute-done.35.rest_11_ = f32[8,32,512]{2,1,0:T(8,128)S(1)} collective-permute-done((f32[8,32,512]{2,1,0:T(8,128)}, f32[8,32,512]{2,1,0:T(8,128)S(1)}, u32[]{:S(2)}, u32[]{:S(2)}) %collective-permute-start.35) | collective-permute-done | bytes 524320 | tf_op jit(solution)/shard_map/cond/branch_1_fun/ppermute | solution.py:657
  437.5 40.3 %collective-permute-done.24 = f32[28,32,512]{2,1,0:T(8,128)S(1)} collective-permute-done((f32[28,32,512]{2,1,0:T(8,128)S(1)}, f32[28,32,512]{2,1,0:T(8,128)S(1)}, u32[]{:S(2)}, u32[]{:S(2)}) %collective-permute-start.24) | collective-permute-done | bytes 1835040 | tf_op jit(solution)/shard_map/cond/branch_1_fun/ppermute | solution.py:657
  480.4 39.5 %collective-permute-done.27 = f32[30,32,512]{2,1,0:T(8,128)S(1)} collective-permute-done((f32[30,32,512]{2,1,0:T(8,128)S(1)}, f32[30,32,512]{2,1,0:T(8,128)S(1)}, u32[]{:S(2)}, u32[]{:S(2)}) %collective-permute-start.27) | collective-permute-done | bytes 1966112 | tf_op jit(solution)/shard_map/cond/branch_1_fun/ppermute | solution.py:657
  521.2 4.8 collective-permute-done.26.rest_3_
  527.6 39.6 %collective-permute-done.33.rest_9_ = f32[34,32,512]{2,1,0:T(8,128)S(1)} collective-permute-done((f32[34,32,512]{2,1,0:T(8,128)}, f32[34,32,512]{2,1,0:T(8,128)S(1)}, u32[]{:S(2)}, u32[]{:S(2)}) %collective-permute-start.33) | collective-permute-done | bytes 2228256 | tf_op jit(solution)/shard_map/cond/branch_1_fun/ppermute | solution.py:657
  568.6 20.9 %collective-permute-done.29.rest_5_ = f32[46,32,512]{2,1,0:T(8,128)S(1)} collective-permute-done((f32[46,32,512]{2,1,0:T(8,128)}, f32[46,32,512]{2,1,0:T(8,128)S(1)}, u32[]{:S(2)}, u32[]{:S(2)}) %collective-permute-start.29) | collective-permute-done | bytes 3014688 | tf_op jit(solution)/shard_map/cond/branch_1_fun/ppermute | solution.py:657
  589.5 18.3 %collective-permute-done.25.rest_2_ = f32[28,32,512]{2,1,0:T(8,128)S(1)} collective-permute-done((f32[28,32,512]{2,1,0:T(8,128)S(1)}, f32[28,32,512]{2,1,0:T(8,128)S(1)}, u32[]{:S(2)}, u32[]{:S(2)}) %collective-permute-start.25) | collective-permute-done | bytes 1835040 | tf_op jit(solution)/shard_map/cond/branch_1_fun/ppermute | solution.py:657
  610.3 14.9 %finish.6 = (bf16[32,128,256]{2,1,0:T(8,128)(2,1)S(1)}, bf16[32,128,256]{2,1,0:T(8,128)(2,1)}, bf16[16,128,512]{2,1,0:T(8,128)(2,1)}) custom-call(s32[848]{0:T(1024)S(1)} %copy-done.34, f32[16,8,32,512]{3,2,1,0:T(8,128)} %get-tuple-element.424.acc, f32[20,32,512]{2,1,0:T(8,128)} %collective-permute-done.22.rest_0_, f32[28,32,512]{2,1,0:T(8,128)} %copy-done.18, ...), custom_call_target="tpu_custom_call" | custom-call | tf_op jit(solution)/shard_map/cond/branch_1_fun/finish/pallas_call | solution.py:702
  625.2 4.4 collective-permute-done.38
  630.8 8.3 %constant_dynamic-update-slice_fusion.2 = bf16[32,1024,256]{2,1,0:T(8,128)(2,1)} fusion(bf16[32,1024,256]{2,1,0:T(8,128)(2,1)} %get-tuple-element.422, bf16[16,1024,256]{2,1,0:T(8,128)(2,1)} %collective-permute-done.21, s32[]{:T(128)S(6)} %select_n.1), kind=kLoop, calls=%fused_computation.13 | loop fusion | bytes 16777220 | tf_op jit(solution)/shard_map/cond/branch_1_fun/dynamic_update_slice | solution.py:718
  639.0 7.5 %constant_dynamic-update-slice_fusion.3 = bf16[32,1024,256]{2,1,0:T(8,128)(2,1)} fusion(bf16[32,1024,256]{2,1,0:T(8,128)(2,1)} %get-tuple-element.420, bf16[16,1024,256]{2,1,0:T(8,128)(2,1)} %collective-permute-done.20, s32[]{:T(128)S(6)} %select_n.1), kind=kLoop, calls=%fused_computation.14 | loop fusion | bytes 16777220 | tf_op jit(solution)/shard_map/cond/branch_1_fun/dynamic_update_slice | solution.py:718
  (138 shorter events, 55.0 us)
Async XLA Ops:
  29.2 179.1 %collective-permute-start.1 = (bf16[12,1024,256]{2,1,0:T(8,128)(2,1)}, bf16[12,1024,256]{2,1,0:T(8,128)(2,1)}, u32[]{:S(2)}, u32[]{:S(2)}) collective-permute-start(bf16[12,1024,256]{2,1,0:T(8,128)(2,1)} %constant_dynamic-slice_fusion.4), channel_id=1, source_target_pairs={{0,1},{1,0},{2,3},{3,2},{4,5},{5,4},{6,7},{7,6}} | collective-permute-start | bytes 18874376 | tf_op jit(solution)/shard_map/cond/branch_1_fun/ppermute | solution.py:726
  35.1 174.5 %collective-permute-start.3 = (bf16[12,1024,256]{2,1,0:T(8,128)(2,1)}, bf16[12,1024,256]{2,1,0:T(8,128)(2,1)}, u32[]{:S(2)}, u32[]{:S(2)}) collective-permute-start(bf16[12,1024,256]{2,1,0:T(8,128)(2,1)} %constant_dynamic-slice_fusion.2), channel_id=1, source_target_pairs={{0,1},{1,0},{2,3},{3,2},{4,5},{5,4},{6,7},{7,6}} | collective-permute-start | bytes 18874376 | tf_op jit(solution)/shard_map/cond/branch_1_fun/ppermute | solution.py:726
  70.1 83.7 %collective-permute-start = (bf16[4,1024,256]{2,1,0:T(8,128)(2,1)S(1)}, bf16[4,1024,256]{2,1,0:T(8,128)(2,1)S(1)}, u32[]{:S(2)}, u32[]{:S(2)}) collective-permute-start(bf16[4,1024,256]{2,1,0:T(8,128)(2,1)S(1)} %constant_dynamic-slice_fusion.5), channel_id=1, source_target_pairs={{0,1},{1,0},{2,3},{3,2},{4,5},{5,4},{6,7},{7,6}} | collective-permute-start | bytes 6291464 | tf_op jit(solution)/shard_map/cond/branch_1_fun/ppermute | solution.py:726
  79.8 75.7 %collective-permute-start.2 = (bf16[4,1024,256]{2,1,0:T(8,128)(2,1)S(1)}, bf16[4,1024,256]{2,1,0:T(8,128)(2,1)S(1)}, u32[]{:S(2)}, u32[]{:S(2)}) collective-permute-start(bf16[4,1024,256]{2,1,0:T(8,128)(2,1)S(1)} %constant_dynamic-slice_fusion.3), channel_id=1, source_target_pairs={{0,1},{1,0},{2,3},{3,2},{4,5},{5,4},{6,7},{7,6}} | collective-permute-start | bytes 6291464 | tf_op jit(solution)/shard_map/cond/branch_1_fun/ppermute | solution.py:726
  79.8 41.2 %collective-permute-start.4 = (bf16[28,32,512]{2,1,0:T(8,128)(2,1)S(1)}, bf16[28,32,512]{2,1,0:T(8,128)(2,1)S(1)}, u32[]{:S(2)}, u32[]{:S(2)}) collective-permute-start(bf16[28,32,512]{2,1,0:T(8,128)(2,1)S(1)} %copy-done.38), channel_id=1, source_target_pairs={{0,2},{1,3},{2,4},{3,5},{4,6},{5,7}} | collective-permute-start | bytes 2752520 | tf_op jit(solution)/shard_map/cond/branch_1_fun/ppermute | solution.py:657
  122.7 57.6 %collective-permute-start.5 = (bf16[34,32,512]{2,1,0:T(8,128)(2,1)}, bf16[34,32,512]{2,1,0:T(8,128)(2,1)S(1)}, u32[]{:S(2)}, u32[]{:S(2)}) collective-permute-start(bf16[34,32,512]{2,1,0:T(8,128)(2,1)} %get-tuple-element.376), channel_id=1, source_target_pairs={{0,2},{1,3},{4,6},{5,7}} | collective-permute-start | bytes 3342344 | tf_op jit(solution)/shard_map/cond/branch_1_fun/ppermute | solution.py:657
  153.8 46.5 %collective-permute-start.9 = (bf16[34,32,512]{2,1,0:T(8,128)(2,1)}, bf16[34,32,512]{2,1,0:T(8,128)(2,1)}, u32[]{:S(2)}, u32[]{:S(2)}) collective-permute-start(bf16[34,32,512]{2,1,0:T(8,128)(2,1)} %get-tuple-element.377), channel_id=1, source_target_pairs={{2,6},{3,7}} | collective-permute-start | bytes 3342344 | tf_op jit(solution)/shard_map/cond/branch_1_fun/ppermute | solution.py:657
  155.5 51.5 %collective-permute-start.7 = (bf16[34,32,512]{2,1,0:T(8,128)(2,1)}, bf16[34,32,512]{2,1,0:T(8,128)(2,1)}, u32[]{:S(2)}, u32[]{:S(2)}) collective-permute-start(bf16[34,32,512]{2,1,0:T(8,128)(2,1)} %collective-permute-done.6), channel_id=1, source_target_pairs={{6,4},{7,5}} | collective-permute-start | bytes 3342344 | tf_op jit(solution)/shard_map/cond/branch_1_fun/ppermute | solution.py:657
  180.3 79.6 %collective-permute-start.8 = (bf16[34,32,512]{2,1,0:T(8,128)(2,1)}, bf16[34,32,512]{2,1,0:T(8,128)(2,1)S(1)}, u32[]{:S(2)}, u32[]{:S(2)}) collective-permute-start(bf16[34,32,512]{2,1,0:T(8,128)(2,1)} %get-tuple-element.377), channel_id=1, source_target_pairs={{0,2},{1,3},{4,6},{5,7}} | collective-permute-start | bytes 3342344 | tf_op jit(solution)/shard_map/cond/branch_1_fun/ppermute | solution.py:657
  200.3 50.3 %collective-permute-start.14 = (bf16[22,32,512]{2,1,0:T(8,128)(2,1)}, bf16[22,32,512]{2,1,0:T(8,128)(2,1)S(1)}, u32[]{:S(2)}, u32[]{:S(2)}) collective-permute-start(bf16[22,32,512]{2,1,0:T(8,128)(2,1)} %get-tuple-element.381), channel_id=1, source_target_pairs={{0,4},{1,5},{2,6},{3,7}} | collective-permute-start | bytes 2162696 | tf_op jit(solution)/shard_map/cond/branch_1_fun/ppermute | solution.py:657
  208.3 80.4 %collective-permute-start.11 = (bf16[30,32,512]{2,1,0:T(8,128)(2,1)}, bf16[30,32,512]{2,1,0:T(8,128)(2,1)S(1)}, u32[]{:S(2)}, u32[]{:S(2)}) collective-permute-start(bf16[30,32,512]{2,1,0:T(8,128)(2,1)} %get-tuple-element.378), channel_id=1, source_target_pairs={{0,2},{1,3},{2,4},{3,5},{4,6},{5,7}} | collective-permute-start | bytes 2949128 | tf_op jit(solution)/shard_map/cond/branch_1_fun/ppermute | solution.py:657
  209.7 51.5 %collective-permute-start.10 = (bf16[34,32,512]{2,1,0:T(8,128)(2,1)}, bf16[34,32,512]{2,1,0:T(8,128)(2,1)S(1)}, u32[]{:S(2)}, u32[]{:S(2)}) collective-permute-start(bf16[34,32,512]{2,1,0:T(8,128)(2,1)} %collective-permute-done.9), channel_id=1, source_target_pairs={{6,4},{7,5}} | collective-permute-start | bytes 3342344 | tf_op jit(solution)/shard_map/cond/branch_1_fun/ppermute | solution.py:657
  233.9 52.7 %collective-permute-start.15 = (bf16[18,32,512]{2,1,0:T(8,128)(2,1)}, bf16[18,32,512]{2,1,0:T(8,128)(2,1)S(1)}, u32[]{:S(2)}, u32[]{:S(2)}) collective-permute-start(bf16[18,32,512]{2,1,0:T(8,128)(2,1)} %get-tuple-element.382), channel_id=1, source_target_pairs={{0,4},{1,5},{2,6},{3,7}} | collective-permute-start | bytes 1769480 | tf_op jit(solution)/shard_map/cond/branch_1_fun/ppermute | solution.py:657
  250.7 34.6 %collective-permute-start.19 = (bf16[10,32,512]{2,1,0:T(8,128)(2,1)}, bf16[10,32,512]{2,1,0:T(8,128)(2,1)S(1)}, u32[]{:S(2)}, u32[]{:S(2)}) collective-permute-start(bf16[10,32,512]{2,1,0:T(8,128)(2,1)} %get-tuple-element.386), channel_id=1, source_target_pairs={{0,6},{1,7}} | collective-permute-start | bytes 983048 | tf_op jit(solution)/shard_map/cond/branch_1_fun/ppermute | solution.py:657
  259.9 75.5 %collective-permute-start.22 = (f32[20,32,512]{2,1,0:T(8,128)}, f32[20,32,512]{2,1,0:T(8,128)}, u32[]{:S(2)}, u32[]{:S(2)}) collective-permute-start(f32[20,32,512]{2,1,0:T(8,128)} %get-tuple-element.425), channel_id=1, source_target_pairs={{2,0},{3,1},{4,2},{5,3},{6,4},{7,5}} | collective-permute-start | bytes 3932168 | tf_op jit(solution)/shard_map/cond/branch_1_fun/ppermute | solution.py:657
  261.2 72.9 %collective-permute-start.30 = (f32[12,32,512]{2,1,0:T(8,128)}, f32[12,32,512]{2,1,0:T(8,128)}, u32[]{:S(2)}, u32[]{:S(2)}) collective-permute-start(f32[12,32,512]{2,1,0:T(8,128)} %get-tuple-element.429), channel_id=1, source_target_pairs={{4,0},{5,1},{6,2},{7,3}} | collective-permute-start | bytes 2359304 | tf_op jit(solution)/shard_map/cond/branch_1_fun/ppermute | solution.py:657
  285.3 47.5 %collective-permute-start.34 = (f32[6,32,512]{2,1,0:T(8,128)}, f32[6,32,512]{2,1,0:T(8,128)}, u32[]{:S(2)}, u32[]{:S(2)}) collective-permute-start(f32[6,32,512]{2,1,0:T(8,128)} %get-tuple-element.433), channel_id=1, source_target_pairs={{6,0},{7,1}} | collective-permute-start | bytes 1179656 | tf_op jit(solution)/shard_map/cond/branch_1_fun/ppermute | solution.py:657
  287.5 148.2 %collective-permute-start.32 = (f32[22,32,512]{2,1,0:T(8,128)}, f32[22,32,512]{2,1,0:T(8,128)S(1)}, u32[]{:S(2)}, u32[]{:S(2)}) collective-permute-start(f32[22,32,512]{2,1,0:T(8,128)} %get-tuple-element.431), channel_id=1, source_target_pairs={{4,0},{5,1},{6,2},{7,3}} | collective-permute-start | bytes 4325384 | tf_op jit(solution)/shard_map/cond/branch_1_fun/ppermute | solution.py:657
  288.8 145.6 %collective-permute-start.31 = (f32[18,32,512]{2,1,0:T(8,128)}, f32[18,32,512]{2,1,0:T(8,128)}, u32[]{:S(2)}, u32[]{:S(2)}) collective-permute-start(f32[18,32,512]{2,1,0:T(8,128)} %get-tuple-element.430), channel_id=1, source_target_pairs={{4,0},{5,1},{6,2},{7,3}} | collective-permute-start | bytes 3538952 | tf_op jit(solution)/shard_map/cond/branch_1_fun/ppermute | solution.py:657
  332.8 103.3 %collective-permute-start.37 = (f32[24,32,512]{2,1,0:T(8,128)}, f32[24,32,512]{2,1,0:T(8,128)S(1)}, u32[]{:S(2)}, u32[]{:S(2)}) collective-permute-start(f32[24,32,512]{2,1,0:T(8,128)} %get-tuple-element.436), channel_id=1, source_target_pairs={{6,0},{7,1}} | collective-permute-start | bytes 4718600 | tf_op jit(solution)/shard_map/cond/branch_1_fun/ppermute | solution.py:657
  334.1 98.8 %collective-permute-start.36 = (f32[10,32,512]{2,1,0:T(8,128)S(1)}, f32[10,32,512]{2,1,0:T(8,128)S(1)}, u32[]{:S(2)}, u32[]{:S(2)}) collective-permute-start(f32[10,32,512]{2,1,0:T(8,128)S(1)} %copy-done.13), channel_id=1, source_target_pairs={{6,0},{7,1}} | collective-permute-start | bytes 1966088 | tf_op jit(solution)/shard_map/cond/branch_1_fun/ppermute | solution.py:657
  335.5 97.5 %collective-permute-start.35 = (f32[8,32,512]{2,1,0:T(8,128)}, f32[8,32,512]{2,1,0:T(8,128)S(1)}, u32[]{:S(2)}, u32[]{:S(2)}) collective-permute-start(f32[8,32,512]{2,1,0:T(8,128)} %get-tuple-element.434), channel_id=1, source_target_pairs={{6,0},{7,1}} | collective-permute-start | bytes 1572872 | tf_op jit(solution)/shard_map/cond/branch_1_fun/ppermute | solution.py:657
  433.0 197.8 %collective-permute-start.21 = (bf16[16,1024,256]{2,1,0:T(8,128)(2,1)}, bf16[16,1024,256]{2,1,0:T(8,128)(2,1)}, u32[]{:S(2)}, u32[]{:S(2)}) collective-permute-start(bf16[16,1024,256]{2,1,0:T(8,128)(2,1)} %get-tuple-element.423), channel_id=1, source_target_pairs={{0,1},{1,0},{2,3},{3,2},{4,5},{5,4},{6,7},{7,6}} | collective-permute-start | bytes 25165832 | tf_op jit(solution)/shard_map/cond/branch_1_fun/ppermute | solution.py:717
  433.0 44.8 %collective-permute-start.24 = (f32[28,32,512]{2,1,0:T(8,128)S(1)}, f32[28,32,512]{2,1,0:T(8,128)S(1)}, u32[]{:S(2)}, u32[]{:S(2)}) collective-permute-start(f32[28,32,512]{2,1,0:T(8,128)S(1)} %copy-done.17), channel_id=1, source_target_pairs={{4,0},{5,1}} | collective-permute-start | bytes 5505032 | tf_op jit(solution)/shard_map/cond/branch_1_fun/ppermute | solution.py:657
  434.3 44.7 %collective-permute-start.23 = (f32[28,32,512]{2,1,0:T(8,128)S(1)}, f32[28,32,512]{2,1,0:T(8,128)S(1)}, u32[]{:S(2)}, u32[]{:S(2)}) collective-permute-start(f32[28,32,512]{2,1,0:T(8,128)S(1)} %copy-done.17), channel_id=1, source_target_pairs={{2,0},{3,1},{6,4},{7,5}} | collective-permute-start | bytes 5505032 | tf_op jit(solution)/shard_map/cond/branch_1_fun/ppermute | solution.py:657
  435.7 203.4 %collective-permute-start.20 = (bf16[16,1024,256]{2,1,0:T(8,128)(2,1)}, bf16[16,1024,256]{2,1,0:T(8,128)(2,1)}, u32[]{:S(2)}, u32[]{:S(2)}) collective-permute-start(bf16[16,1024,256]{2,1,0:T(8,128)(2,1)} %get-tuple-element.421), channel_id=1, source_target_pairs={{0,1},{1,0},{2,3},{3,2},{4,5},{5,4},{6,7},{7,6}} | collective-permute-start | bytes 25165832 | tf_op jit(solution)/shard_map/cond/branch_1_fun/ppermute | solution.py:717
  436.2 83.7 %collective-permute-start.27 = (f32[30,32,512]{2,1,0:T(8,128)S(1)}, f32[30,32,512]{2,1,0:T(8,128)S(1)}, u32[]{:S(2)}, u32[]{:S(2)}) collective-permute-start(f32[30,32,512]{2,1,0:T(8,128)S(1)} %copy-done.6), channel_id=1, source_target_pairs={{4,0},{5,1}} | collective-permute-start | bytes 5898248 | tf_op jit(solution)/shard_map/cond/branch_1_fun/ppermute | solution.py:657
  477.8 89.4 %collective-permute-start.33 = (f32[34,32,512]{2,1,0:T(8,128)}, f32[34,32,512]{2,1,0:T(8,128)S(1)}, u32[]{:S(2)}, u32[]{:S(2)}) collective-permute-start(f32[34,32,512]{2,1,0:T(8,128)} %get-tuple-element.432), channel_id=1, source_target_pairs={{4,0},{5,1},{6,2},{7,3}} | collective-permute-start | bytes 6684680 | tf_op jit(solution)/shard_map/cond/branch_1_fun/ppermute | solution.py:657
  479.1 46.9 %collective-permute-start.26 = (f32[30,32,512]{2,1,0:T(8,128)S(1)}, f32[30,32,512]{2,1,0:T(8,128)S(1)}, u32[]{:S(2)}, u32[]{:S(2)}) collective-permute-start(f32[30,32,512]{2,1,0:T(8,128)S(1)} %copy-done.6), channel_id=1, source_target_pairs={{2,0},{3,1},{6,4},{7,5}} | collective-permute-start | bytes 5898248 | tf_op jit(solution)/shard_map/cond/branch_1_fun/ppermute | solution.py:657
  519.9 69.6 %collective-permute-start.29 = (f32[46,32,512]{2,1,0:T(8,128)}, f32[46,32,512]{2,1,0:T(8,128)S(1)}, u32[]{:S(2)}, u32[]{:S(2)}) collective-permute-start(f32[46,32,512]{2,1,0:T(8,128)} %get-tuple-element.428), channel_id=1, source_target_pairs={{2,0},{3,1},{4,2},{5,3},{6,4},{7,5}} | collective-permute-start | bytes 9043976 | tf_op jit(solution)/shard_map/cond/branch_1_fun/ppermute | solution.py:657
  526.0 81.8 %collective-permute-start.28 = (f32[30,32,512]{2,1,0:T(8,128)S(1)}, f32[30,32,512]{2,1,0:T(8,128)S(1)}, u32[]{:S(2)}, u32[]{:S(2)}) collective-permute-start(f32[30,32,512]{2,1,0:T(8,128)S(1)} %collective-permute-done.27), channel_id=1, source_target_pairs={{0,2},{1,3}} | collective-permute-start | bytes 5898248 | tf_op jit(solution)/shard_map/cond/branch_1_fun/ppermute | solution.py:657
  567.2 40.6 %collective-permute-start.25 = (f32[28,32,512]{2,1,0:T(8,128)S(1)}, f32[28,32,512]{2,1,0:T(8,128)S(1)}, u32[]{:S(2)}, u32[]{:S(2)}) collective-permute-start(f32[28,32,512]{2,1,0:T(8,128)S(1)} %collective-permute-done.24), channel_id=1, source_target_pairs={{0,2},{1,3}} | collective-permute-start | bytes 5505032 | tf_op jit(solution)/shard_map/cond/branch_1_fun/ppermute | solution.py:657
  (43 other events, 1245.7 us)

commit v4 on v3

--- a/solution.py
+++ b/solution.py
@@ -232,7 +232,7 @@
     rest = rest[5:]
     live = n_t - t
     bbuf = [rest[d * live:(d + 1) * live] for d in range(3)]
-    qg, outb, kvs, dkv, e_scr, p_scr, m_scr, l_scr, f_scr, docr, o_acc, dq_acc, isem, osem = rest[3 * live:]
+    qg, outb, kvs, dkv, e_scr, dp_scr, p_scr, l_scr, f_scr, t_scr, docr, o_acc, isem, osem = rest[3 * live:]
 
     base = tab[ST + t]
     n = tab[ST + t + 1] - base
@@ -326,6 +326,7 @@
     row_tok = lax.broadcasted_iota(jnp.int32, (1024, 128), 0) >> 3
     lane = lax.broadcasted_iota(jnp.int32, (1024, 128), 1)
     cs = scale * LOG2E
+    lo_half, hi_half = slice(0, 128), slice(128, 256)
 
     def keys_of(slot, d):
         return kvs[slot, d, :, :, :256].reshape(256, 256)
@@ -333,127 +334,125 @@
     def values_of(slot, d):
         return kvs[slot, d, :, :, 256:].reshape(256, 256)
 
-    def attend(role, s, slot):
-        q_ref, g_ref = qg.at[slot, role], qg.at[slot, 2 + role]
-        h = e if role == 0 else 1 - e
-        dm = tab[DM + s * 2 + h]
+    def attend(s, slot):
         row = e * NS + s
-        dq_row = docs[2 * c + h, pl.ds(row, 1), :]
-        d_t = jnp.transpose(jnp.broadcast_to(dq_row, (128, 128)))
-        docr[...] = jnp.broadcast_to(d_t[:, None, :], (128, 8, 128)).reshape(1024, 128)
-
-        def scores(d, causal):
-            sc = dot_nt(q_ref[...], keys_of(slot, d)) * cs
+        dm = jnp.maximum(tab[DM + s * 2], tab[DM + s * 2 + 1])
+        piece = (e, 1 - e)
+        for role in range(2):
+            dq_row = docs[2 * c + piece[role], pl.ds(row, 1), :]
+            d_t = jnp.transpose(jnp.broadcast_to(dq_row, (128, 128)))
+            docr[role] = jnp.broadcast_to(d_t[:, None, :], (128, 8, 128)).reshape(1024, 128)
+
+        def scores(role, d, causal):
+            sc = dot_nt(qg[slot, role], keys_of(slot, d)) * cs
             xs = []
             for j in range(2):
                 dk = docs[2 * (c - d) + j, pl.ds(row, 1), :]
-                vis = docr[...] == dk
+                vis = docr[role] == dk
                 if causal:
-                    vis = vis & (lane + 128 * j <= row_tok + 128 * h)
+                    vis = vis & (lane + 128 * j <= row_tok + 128 * piece[role])
                 xs.append(jnp.where(vis, sc[:, 128 * j:128 * (j + 1)], NEG_BIG))
             top = jnp.maximum(xs[0], xs[1])
             es = [jnp.exp2(x - top) for x in xs]
-            e_scr[d, :, :128] = es[0]
-            e_scr[d, :, 128:] = es[1]
-            m_scr[d] = top
-            l_scr[d] = es[0] + es[1]
-
-        scores(0, True)
-
-        def more_scores(d, _):
-            scores(d, False)
-            return 0
-
-        lax.fori_loop(1, dm + 1, more_scores, 0)
-
-        @pl.when(dm == 0)
-        def _():
-            m = m_scr[0]
-            f = jnp.exp2(m - jnp.max(m, axis=1, keepdims=True))
-            f_scr[0] = f * (1.0 / jnp.sum(l_scr[0] * f, axis=1, keepdims=True))
-
-        @pl.when(dm > 0)
-        def _():
-            o_acc[:, :128] = jnp.maximum(m_scr[0], m_scr[1])
-
-            def top_of(d, x):
-                o_acc[:, :128] = jnp.maximum(o_acc[:, :128], m_scr[d])
-                return x
-
-            lax.fori_loop(2, dm + 1, top_of, 0)
-            top = jnp.broadcast_to(jnp.max(o_acc[:, :128], axis=1, keepdims=True), (1024, 128))
-            o_acc[:, :128] = top
-            f0 = jnp.exp2(m_scr[0] - top)
-            f1 = jnp.exp2(m_scr[1] - top)
-            f_scr[0] = f0
-            f_scr[1] = f1
-            o_acc[:, 128:] = l_scr[0] * f0 + l_scr[1] * f1
-
-            def sum_of(d, x):
-                f = jnp.exp2(m_scr[d] - o_acc[:, :128])
-                f_scr[d] = f
-                o_acc[:, 128:] = o_acc[:, 128:] + l_scr[d] * f
-                return x
-
-            lax.fori_loop(2, dm + 1, sum_of, 0)
-            inv = jnp.broadcast_to(1.0 / jnp.sum(o_acc[:, 128:], axis=1, keepdims=True), (1024, 128))
-            o_acc[:, 128:] = inv
-            f_scr[0] = f_scr[0] * inv
-            f_scr[1] = f_scr[1] * inv
-
-            def scale_of(d, x):
-                f_scr[d] = f_scr[d] * o_acc[:, 128:]
-                return x
-
-            lax.fori_loop(2, dm + 1, scale_of, 0)
-
-        def weighted(d):
-            for j in range(2):
-                p = e_scr[d, :, 128 * j:128 * (j + 1)] * f_scr[d]
-                p_scr[d, :, 128 * j:128 * (j + 1)] = p.astype(jnp.bfloat16)
-            return dot_nn(p_scr[d], values_of(slot, d))
-
-        o_acc[...] = weighted(0)
-
-        def more_weighted(d, _):
-            o_acc[...] = o_acc[...] + weighted(d)
-            return 0
-
-        lax.fori_loop(1, dm + 1, more_weighted, 0)
-        o_low = o_acc[...].astype(jnp.bfloat16)
-        outb[slot, role] = o_low
-        delta = jnp.sum(g_ref[...].astype(jnp.float32) * o_low.astype(jnp.float32), axis=1, keepdims=True)
-        m_scr[0] = jnp.broadcast_to(delta, (1024, 128))
-
-        def grads(d):
-            dp = dot_nt(g_ref[...], values_of(slot, d))
-            ds = []
-            for j in range(2):
-                p = e_scr[d, :, 128 * j:128 * (j + 1)] * f_scr[d]
-                ds.append((p * (dp[:, 128 * j:128 * (j + 1)] - m_scr[0])).astype(jnp.bfloat16))
-            ds = jnp.concatenate(ds, axis=1)
-            dk = dot_tn(ds, q_ref[...]).reshape(8, G, 256)
-            dv = dot_tn(p_scr[d], g_ref[...]).reshape(8, G, 256)
-            return dot_nn(ds, keys_of(slot, d)), dk, dv
-
-        dq0, dk0, dv0 = grads(0)
-        dq_acc[...] = dq0
-        if role == 0:
-            dkv[slot, 0, :, :, :256] = dk0
-            dkv[slot, 0, :, :, 256:] = dv0
-        else:
-            dkv[slot, 0, :, :, :256] = dkv[slot, 0, :, :, :256] + dk0
-            dkv[slot, 0, :, :, 256:] = dkv[slot, 0, :, :, 256:] + dv0
-
-        def more_grads(d, _):
-            dq1, dk1, dv1 = grads(d)
-            dq_acc[...] = dq_acc[...] + dq1
-            dkv[slot, d, :, :, :256] = dkv[slot, d, :, :, :256] + dk1
-            dkv[slot, d, :, :, 256:] = dkv[slot, d, :, :, 256:] + dv1
-            return 0
-
-        lax.fori_loop(1, dm + 1, more_grads, 0)
-        outb[slot, 2 + role] = (dq_acc[...] * scale).astype(jnp.bfloat16)
+            e_scr[d, role, :, lo_half] = es[0]
+            e_scr[d, role, :, hi_half] = es[1]
+            f_scr[d, role] = top
+            l_scr[d, role] = es[0] + es[1]
+            return top
+
+        def dprob(role, d):
+            dp_scr[d, role] = dot_nt(g_of(role), values_of(slot, d))
+
+        def g_of(role):
+            return qg[slot, 2 + role]
+
+        for role in range(2):
+            t_scr[role] = scores(role, 0, True)
+
+        def far_scores(d, x):
+            for role in range(2):
+                t_scr[role] = jnp.maximum(t_scr[role], scores(role, d, False))
+            for role in range(2):
+                dprob(role, d)
+            return x
+
+        lax.fori_loop(1, dm + 1, far_scores, 0)
+
+        for role in range(2):
+            top = jnp.broadcast_to(jnp.max(t_scr[role], axis=1, keepdims=True), (1024, 128))
+            t_scr[role] = top
+            f = jnp.exp2(f_scr[0, role] - top)
+            f_scr[0, role] = f
+            l_scr[0, role] = l_scr[0, role] * f
+        dprob(0, 0)
+
+        def far_sums(d, x):
+            for role in range(2):
+                f = jnp.exp2(f_scr[d, role] - t_scr[role])
+                f_scr[d, role] = f
+                l_scr[0, role] = l_scr[0, role] + l_scr[d, role] * f
+            return x
+
+        lax.fori_loop(1, dm + 1, far_sums, 0)
+
+        for role in range(2):
+            t_scr[role] = jnp.broadcast_to(1.0 / jnp.sum(l_scr[0, role], axis=1, keepdims=True), (1024, 128))
+        dprob(1, 0)
+
+        def weighted(role, d):
+            f = f_scr[d, role] * t_scr[role]
+            f_scr[d, role] = f
+            for half in (lo_half, hi_half):
+                p_scr[d, role, :, half] = (e_scr[d, role, :, half] * f).astype(jnp.bfloat16)
+            return dot_nn(p_scr[d, role], values_of(slot, d))
+
+        def value_grads(d):
+            dv = dot_tn(p_scr[d, 0], g_of(0)) + dot_tn(p_scr[d, 1], g_of(1))
+            dkv[slot, d, :, :, 256:] = dv.reshape(8, G, 256)
+
+        for role in range(2):
+            o_acc[role] = weighted(role, 0)
+
+        def far_weighted(d, x):
+            for role in range(2):
+                o_acc[role] = o_acc[role] + weighted(role, d)
+            value_grads(d)
+            return x
+
+        lax.fori_loop(1, dm + 1, far_weighted, 0)
+
+        for role in range(2):
+            o_low = o_acc[role].astype(jnp.bfloat16)
+            outb[slot, role] = o_low
+            delta = jnp.sum(g_of(role).astype(jnp.float32) * o_low.astype(jnp.float32), axis=1, keepdims=True)
+            t_scr[role] = jnp.broadcast_to(delta, (1024, 128))
+        value_grads(0)
+
+        def score_grads(d):
+            out = []
+            for role in range(2):
+                ds = [
+                    (e_scr[d, role, :, half] * f_scr[d, role] * (dp_scr[d, role, :, half] - t_scr[role])).astype(jnp.bfloat16)
+                    for half in (lo_half, hi_half)
+                ]
+                out.append(jnp.concatenate(ds, axis=1))
+            dk = dot_tn(out[0], qg[slot, 0]) + dot_tn(out[1], qg[slot, 1])
+            dkv[slot, d, :, :, :256] = dk.reshape(8, G, 256)
+            return [dot_nn(ds, keys_of(slot, d)) for ds in out]
+
+        dq = score_grads(0)
+        for role in range(2):
+            o_acc[role] = dq[role]
+
+        def far_grads(d, x):
+            dq = score_grads(d)
+            for role in range(2):
+                o_acc[role] = o_acc[role] + dq[role]
+            return x
+
+        lax.fori_loop(1, dm + 1, far_grads, 0)
+        for role in range(2):
+            outb[slot, 2 + role] = (o_acc[role] * scale).astype(jnp.bfloat16)
 
     @pl.when(n > 0)
     def _():
@@ -473,15 +472,7 @@
             put_wait(s - 2, slot)
 
         fetch_wait(s, slot)
-        any_dm = jnp.maximum(tab[DM + s * 2], tab[DM + s * 2 + 1])
-
-        def clear(d, _):
-            dkv[slot, d] = jnp.zeros((8, G, 512), jnp.float32)
-            return 0
-
-        lax.fori_loop(1, any_dm + 1, clear, 0)
-        attend(0, s, slot)
-        attend(1, s, slot)
+        attend(s, slot)
         put(s, slot)
         return 0
 
@@ -678,10 +669,9 @@
                 scratch_shapes=[
                     pltpu.VMEM((2, 4, rows, hd), bf), pltpu.VMEM((2, 4, rows, hd), bf),
                     pltpu.VMEM((2, 4, 8, G, 512), bf), pltpu.VMEM((2, 4, 8, G, 512), f32),
-                    pltpu.VMEM((4, rows, 256), f32), pltpu.VMEM((4, rows, 256), bf),
-                    pltpu.VMEM((4, rows, 128), f32), pltpu.VMEM((4, rows, 128), f32), pltpu.VMEM((4, rows, 128), f32),
-                    pltpu.VMEM((rows, 128), jnp.int32),
-                    pltpu.VMEM((rows, hd), f32), pltpu.VMEM((rows, hd), f32),
+                    pltpu.VMEM((4, 2, rows, 256), f32), pltpu.VMEM((4, 2, rows, 256), f32), pltpu.VMEM((4, 2, rows, 256), bf),
+                    pltpu.VMEM((4, 2, rows, 128), f32), pltpu.VMEM((4, 2, rows, 128), f32), pltpu.VMEM((2, rows, 128), f32),
+                    pltpu.VMEM((2, rows, 128), jnp.int32), pltpu.VMEM((2, rows, hd), f32),
                     pltpu.SemaphoreType.DMA((2,)), pltpu.SemaphoreType.DMA((2,)),
                 ],
                 out_shape=[

time: 655 us -> 649 us (level)
  waiting for transfers between devices: 326 us -> 313 us
    ppermute x32, waiting for transfers between devices: 322 us -> 308 us  [chip_hop(): lax.ppermute(x, 'cp', [(2 * a + k, 2 * b + k) for a, b in moves for k in...]
  transfers between devices with their start and end apart: 40 -> 40, of which waited for: 14 -> 14; matrix products, arithmetic and copies ran while one was open for 3% -> 3% of each run, Pallas kernels for 19% -> 20%
where the time goes in v4:
time: 649 us; the launch traced here: 643 us
  waiting for transfers between devices  313 us (48%)
  starting transfers between devices  151 us (23%)
  Pallas kernels  127 us (20%)
  local copies, waits for them, and re-layouts  38.1 us (6%)
  loops' own time  9.4 us (1%)
    ppermute x32, waiting for transfers between devices, chip_hop(): lax.ppermute(x, 'cp', [(2 * a + k, 2 * b + k) for a, b in moves for k in...  308 us
    ppermute x32, starting transfers between devices, chip_hop(): lax.ppermute(x, 'cp', [(2 * a + k, 2 * b + k) for a, b in moves for k in...  150 us
    pallas_call x4, Pallas kernels, attend(): pl.pallas_call(functools.partial(compute_kernel, t, n_t, [bounds(cap) for...  92.5 us
    dynamic_update_slice x2, local copies, waits for them, and re-layouts, place(): return lax.dynamic_update_slice_in_dim(mine, got, other, 0)  15.8 us
    dynamic_slice x4, local copies, waits for them, and re-layouts, swap_part(): lax.dynamic_slice_in_dim(x, other + lo, n, 0)  15.3 us
    pallas_call x1, Pallas kernels, finish(): pl.pallas_call(functools.partial(finish_kernel, n_t, [len(way) for way in...  14.9 us
  transfers between devices with their start and end apart: 40, of which 14 were waited for; matrix products, arithmetic and copies ran while one was open for 3% of the time, Pallas kernels for 20%

profile of v4, /device:TPU:0, one launch (start us, length us, event | category | flops | bytes accessed | tf_op | source)
XLA Modules:
  0.0 642.8 jit_solution(15867670401027255798)
XLA Ops:
  4.8 9.7 %docs.1 = (s32[8,32,128]{2,1,0:T(8,128)S(1)}, s32[32,128]{1,0:T(8,128)S(1)}) custom-call(s32[32,128]{1,0:T(8,128)} %doc.1), custom_call_target="tpu_custom_call" | custom-call | tf_op jit(solution)/shard_map/docs/pallas_call | solution.py:612
  19.8 621.9 %conditional.1 = (bf16[32,128,8,256]{3,2,1,0:T(8,128)(2,1)}, bf16[32,128,8,256]{3,2,1,0:T(8,128)(2,1)}, bf16[32,128,1,256]{3,1,2,0:T(8,128)(2,1)}, bf16[32,128,1,256]{3,1,2,0:T(8,128)(2,1)}) conditional(s32[]{:T(128)} %bitcast.24, (s32[]{:T(128)}, bf16[32,1024,256]{2,1,0:T(8,128)(2,1)}, bf16[32,1024,256]{2,1,0:T(8,128)(2,1)}, s32[]{:T(128)}, ...), branch_computations={%region_0.0_spmd, %region_3.0_spmd} | conditional | flops 60000002048 | bytes 614617728 | solution.py:776
  28.2 5.9 constant_dynamic-slice_fusion.4
  34.2 5.8 constant_dynamic-slice_fusion.2
  40.4 6.4 %pack.6 = (bf16[16,8,32,512]{3,2,1,0:T(8,128)(2,1)}, bf16[28,32,512]{2,1,0:T(8,128)(2,1)}, bf16[34,32,512]{2,1,0:T(8,128)(2,1)}, bf16[34,32,512]{2,1,0:T(8,128)(...) custom-call(s32[848]{0:T(1024)S(1)} %get-tuple-element.366.tab, ...), custom_call_target="tpu_custom_call" | custom-call | tf_op jit(solution)/shard_map/cond/branch_1_fun/pack/pallas_call | solution.py:635
  54.1 6.1 collective-permute-done.16.rest_4_.rest_9_.rest_12_.rest_14_
  60.2 5.4 collective-permute-start.17
  67.3 7.7 %collective-permute-done.17.rest_10_.rest_13_.rest_15_ = bf16[14,32,512]{2,1,0:T(8,128)(2,1)S(1)} collective-permute-done((bf16[14,32,512]{2,1,0:T(8,128)(2,1)}, bf16[14,32,512]{2,1,0:T(8,128)(2,1)S(1)}, u32[]{:S(2)}, u32[]{:S(2)}) %collective-permute-start.17) | collective-permute-done | bytes 458784 | tf_op jit(solution)/shard_map/cond/branch_1_fun/ppermute | solution.py:648
  76.9 7.8 %collective-permute-done.12.rest_3_.rest_7_.rest_9_.rest_10_ = bf16[22,32,512]{2,1,0:T(8,128)(2,1)} collective-permute-done((bf16[22,32,512]{2,1,0:T(8,128)(2,1)}, bf16[22,32,512]{2,1,0:T(8,128)(2,1)}, u32[]{:S(2)}, u32[]{:S(2)}) %collective-permute-start.12) | collective-permute-done | bytes 720928 | tf_op jit(solution)/shard_map/cond/branch_1_fun/ppermute | solution.py:648
  84.7 21.1 %collective-permute-start.4 = (bf16[28,32,512]{2,1,0:T(8,128)(2,1)S(1)}, bf16[28,32,512]{2,1,0:T(8,128)(2,1)S(1)}, u32[]{:S(2)}, u32[]{:S(2)}) collective-permute-start(bf16[28,32,512]{2,1,0:T(8,128)(2,1)S(1)} %copy-done.38), channel_id=1, source_target_pairs={{0,2},{1,3},{2,4},{3,5},{4,6},{5,7}} | collective-permute-start | bytes 2752520 | tf_op jit(solution)/shard_map/cond/branch_1_fun/ppermute | solution.py:648
  105.8 20.2 %collective-permute-done.4.rest_2_.rest_4_ = bf16[28,32,512]{2,1,0:T(8,128)(2,1)S(1)} collective-permute-done((bf16[28,32,512]{2,1,0:T(8,128)(2,1)S(1)}, bf16[28,32,512]{2,1,0:T(8,128)(2,1)S(1)}, u32[]{:S(2)}, u32[]{:S(2)}) %collective-permute-start.4) | collective-permute-done | bytes 917536 | tf_op jit(solution)/shard_map/cond/branch_1_fun/ppermute | solution.py:648
  127.6 31.1 %collective-permute-start.5 = (bf16[34,32,512]{2,1,0:T(8,128)(2,1)}, bf16[34,32,512]{2,1,0:T(8,128)(2,1)S(1)}, u32[]{:S(2)}, u32[]{:S(2)}) collective-permute-start(bf16[34,32,512]{2,1,0:T(8,128)(2,1)} %get-tuple-element.376), channel_id=1, source_target_pairs={{0,2},{1,3},{4,6},{5,7}} | collective-permute-start | bytes 3342344 | tf_op jit(solution)/shard_map/cond/branch_1_fun/ppermute | solution.py:648
  162.0 20.9 %branch_1_fun.4 = (bf16[32,1024,256]{2,1,0:T(8,128)(2,1)}, bf16[16,1024,256]{2,1,0:T(8,128)(2,1)}, bf16[32,1024,256]{2,1,0:T(8,128)(2,1)}, bf16[16,1024,256]{2,1...) custom-call(s32[848]{0:T(1024)} %copy-done.33, ...), custom_call_target="tpu_custom_call" | custom-call | flops 15000000512 | bytes 25000000 | tf_op jit(solution)/shard_map/cond/branch_1_fun/pallas_call | solution.py:665
  182.9 17.0 %collective-permute-start.8 = (bf16[34,32,512]{2,1,0:T(8,128)(2,1)}, bf16[34,32,512]{2,1,0:T(8,128)(2,1)S(1)}, u32[]{:S(2)}, u32[]{:S(2)}) collective-permute-start(bf16[34,32,512]{2,1,0:T(8,128)(2,1)} %get-tuple-element.377), channel_id=1, source_target_pairs={{0,2},{1,3},{4,6},{5,7}} | collective-permute-start | bytes 3342344 | tf_op jit(solution)/shard_map/cond/branch_1_fun/ppermute | solution.py:648
  199.9 10.5 %collective-permute-start.14 = (bf16[22,32,512]{2,1,0:T(8,128)(2,1)}, bf16[22,32,512]{2,1,0:T(8,128)(2,1)S(1)}, u32[]{:S(2)}, u32[]{:S(2)}) collective-permute-start(bf16[22,32,512]{2,1,0:T(8,128)(2,1)} %get-tuple-element.381), channel_id=1, source_target_pairs={{0,4},{1,5},{2,6},{3,7}} | collective-permute-start | bytes 2162696 | tf_op jit(solution)/shard_map/cond/branch_1_fun/ppermute | solution.py:648
  213.9 30.3 %branch_1_fun.5 = (bf16[32,1024,256]{2,1,0:T(8,128)(2,1)}, bf16[16,1024,256]{2,1,0:T(8,128)(2,1)}, bf16[32,1024,256]{2,1,0:T(8,128)(2,1)}, bf16[16,1024,256]{2,1...) custom-call(s32[848]{0:T(1024)} %copy-done.33, ...), custom_call_target="tpu_custom_call", output_to_operand_aliasing={{0}: (16, {}), {1}: (17, {}), {2}: (18, {}), {3}: (19, {}),... | custom-call | flops 15000000512 | bytes 25000000 | tf_op jit(solution)/shard_map/cond/branch_1_fun/pallas_call | solution.py:665
  244.3 16.8 %collective-permute-start.15 = (bf16[18,32,512]{2,1,0:T(8,128)(2,1)}, bf16[18,32,512]{2,1,0:T(8,128)(2,1)S(1)}, u32[]{:S(2)}, u32[]{:S(2)}) collective-permute-start(bf16[18,32,512]{2,1,0:T(8,128)(2,1)} %get-tuple-element.382), channel_id=1, source_target_pairs={{0,4},{1,5},{2,6},{3,7}} | collective-permute-start | bytes 1769480 | tf_op jit(solution)/shard_map/cond/branch_1_fun/ppermute | solution.py:648
  261.0 9.3 %collective-permute-start.19 = (bf16[10,32,512]{2,1,0:T(8,128)(2,1)}, bf16[10,32,512]{2,1,0:T(8,128)(2,1)S(1)}, u32[]{:S(2)}, u32[]{:S(2)}) collective-permute-start(bf16[10,32,512]{2,1,0:T(8,128)(2,1)} %get-tuple-element.386), channel_id=1, source_target_pairs={{0,6},{1,7}} | collective-permute-start | bytes 983048 | tf_op jit(solution)/shard_map/cond/branch_1_fun/ppermute | solution.py:648
  273.1 20.5 %branch_1_fun.6 = (bf16[32,1024,256]{2,1,0:T(8,128)(2,1)}, bf16[16,1024,256]{2,1,0:T(8,128)(2,1)}, bf16[32,1024,256]{2,1,0:T(8,128)(2,1)}, bf16[16,1024,256]{2,1...) custom-call(s32[848]{0:T(1024)S(1)} %copy-done.34, ...), custom_call_target="tpu_custom_call", output_to_operand_aliasing={{0}: (20, {}), {1}: (21, {}), {2}: (22, {}), {3}: (23, {}),... | custom-call | flops 15000000512 | bytes 25000000 | tf_op jit(solution)/shard_map/cond/branch_1_fun/pallas_call | solution.py:665
  298.4 20.8 %branch_1_fun.7 = (bf16[32,1024,256]{2,1,0:T(8,128)(2,1)}, bf16[16,1024,256]{2,1,0:T(8,128)(2,1)}, bf16[32,1024,256]{2,1,0:T(8,128)(2,1)}, bf16[16,1024,256]{2,1...) custom-call(s32[848]{0:T(1024)S(1)} %copy-done.34, ...), custom_call_target="tpu_custom_call", output_to_operand_aliasing={{0}: (23, {}), {1}: (24, {}), {2}: (25, {}), {3}: (26, {}),... | custom-call | flops 15000000512 | bytes 25000000 | tf_op jit(solution)/shard_map/cond/branch_1_fun/pallas_call | solution.py:665
  319.2 14.2 %collective-permute-done.34.rest_10_ = f32[6,32,512]{2,1,0:T(8,128)} collective-permute-done((f32[6,32,512]{2,1,0:T(8,128)}, f32[6,32,512]{2,1,0:T(8,128)}, u32[]{:S(2)}, u32[]{:S(2)}) %collective-permute-start.34) | collective-permute-done | bytes 393248 | tf_op jit(solution)/shard_map/cond/branch_1_fun/ppermute | solution.py:648
  337.3 90.1 %collective-permute-done.35.rest_11_ = f32[8,32,512]{2,1,0:T(8,128)S(1)} collective-permute-done((f32[8,32,512]{2,1,0:T(8,128)}, f32[8,32,512]{2,1,0:T(8,128)S(1)}, u32[]{:S(2)}, u32[]{:S(2)}) %collective-permute-start.35) | collective-permute-done | bytes 524320 | tf_op jit(solution)/shard_map/cond/branch_1_fun/ppermute | solution.py:648
  428.7 8.6 %collective-permute-done.31.rest_7_ = f32[18,32,512]{2,1,0:T(8,128)} collective-permute-done((f32[18,32,512]{2,1,0:T(8,128)}, f32[18,32,512]{2,1,0:T(8,128)}, u32[]{:S(2)}, u32[]{:S(2)}) %collective-permute-start.31) | collective-permute-done | bytes 1179680 | tf_op jit(solution)/shard_map/cond/branch_1_fun/ppermute | solution.py:648
  440.0 36.5 %collective-permute-done.24 = f32[28,32,512]{2,1,0:T(8,128)S(1)} collective-permute-done((f32[28,32,512]{2,1,0:T(8,128)S(1)}, f32[28,32,512]{2,1,0:T(8,128)S(1)}, u32[]{:S(2)}, u32[]{:S(2)}) %collective-permute-start.24) | collective-permute-done | bytes 1835040 | tf_op jit(solution)/shard_map/cond/branch_1_fun/ppermute | solution.py:648
  479.1 39.5 %collective-permute-done.27 = f32[30,32,512]{2,1,0:T(8,128)S(1)} collective-permute-done((f32[30,32,512]{2,1,0:T(8,128)S(1)}, f32[30,32,512]{2,1,0:T(8,128)S(1)}, u32[]{:S(2)}, u32[]{:S(2)}) %collective-permute-start.27) | collective-permute-done | bytes 1966112 | tf_op jit(solution)/shard_map/cond/branch_1_fun/ppermute | solution.py:648
  524.6 39.4 %collective-permute-done.33.rest_9_ = f32[34,32,512]{2,1,0:T(8,128)S(1)} collective-permute-done((f32[34,32,512]{2,1,0:T(8,128)}, f32[34,32,512]{2,1,0:T(8,128)S(1)}, u32[]{:S(2)}, u32[]{:S(2)}) %collective-permute-start.33) | collective-permute-done | bytes 2228256 | tf_op jit(solution)/shard_map/cond/branch_1_fun/ppermute | solution.py:648
  565.4 18.9 %collective-permute-done.29.rest_5_ = f32[46,32,512]{2,1,0:T(8,128)S(1)} collective-permute-done((f32[46,32,512]{2,1,0:T(8,128)}, f32[46,32,512]{2,1,0:T(8,128)S(1)}, u32[]{:S(2)}, u32[]{:S(2)}) %collective-permute-start.29) | collective-permute-done | bytes 3014688 | tf_op jit(solution)/shard_map/cond/branch_1_fun/ppermute | solution.py:648
  584.4 18.3 %collective-permute-done.25.rest_2_ = f32[28,32,512]{2,1,0:T(8,128)S(1)} collective-permute-done((f32[28,32,512]{2,1,0:T(8,128)S(1)}, f32[28,32,512]{2,1,0:T(8,128)S(1)}, u32[]{:S(2)}, u32[]{:S(2)}) %collective-permute-start.25) | collective-permute-done | bytes 1835040 | tf_op jit(solution)/shard_map/cond/branch_1_fun/ppermute | solution.py:648
  605.2 14.9 %finish.6 = (bf16[32,128,256]{2,1,0:T(8,128)(2,1)S(1)}, bf16[32,128,256]{2,1,0:T(8,128)(2,1)}, bf16[16,128,512]{2,1,0:T(8,128)(2,1)}) custom-call(s32[848]{0:T(1024)S(1)} %copy-done.34, f32[16,8,32,512]{3,2,1,0:T(8,128)} %get-tuple-element.424.acc, f32[20,32,512]{2,1,0:T(8,128)} %collective-permute-done.22.rest_0_, f32[28,32,512]{2,1,0:T(8,128)} %copy-done.18, ...), custom_call_target="tpu_custom_call" | custom-call | tf_op jit(solution)/shard_map/cond/branch_1_fun/finish/pallas_call | solution.py:692
  620.1 4.4 collective-permute-done.38
  625.6 8.3 %constant_dynamic-update-slice_fusion.2 = bf16[32,1024,256]{2,1,0:T(8,128)(2,1)} fusion(bf16[32,1024,256]{2,1,0:T(8,128)(2,1)} %get-tuple-element.422, bf16[16,1024,256]{2,1,0:T(8,128)(2,1)} %collective-permute-done.21, s32[]{:T(128)S(6)} %select_n.1), kind=kLoop, calls=%fused_computation.13 | loop fusion | bytes 16777220 | tf_op jit(solution)/shard_map/cond/branch_1_fun/dynamic_update_slice | solution.py:708
  633.9 7.5 %constant_dynamic-update-slice_fusion.3 = bf16[32,1024,256]{2,1,0:T(8,128)(2,1)} fusion(bf16[32,1024,256]{2,1,0:T(8,128)(2,1)} %get-tuple-element.420, bf16[16,1024,256]{2,1,0:T(8,128)(2,1)} %collective-permute-done.20, s32[]{:T(128)S(6)} %select_n.1), kind=kLoop, calls=%fused_computation.14 | loop fusion | bytes 16777220 | tf_op jit(solution)/shard_map/cond/branch_1_fun/dynamic_update_slice | solution.py:708
  (138 shorter events, 57.3 us)
Async XLA Ops:
  34.1 177.6 %collective-permute-start.1 = (bf16[12,1024,256]{2,1,0:T(8,128)(2,1)}, bf16[12,1024,256]{2,1,0:T(8,128)(2,1)}, u32[]{:S(2)}, u32[]{:S(2)}) collective-permute-start(bf16[12,1024,256]{2,1,0:T(8,128)(2,1)} %constant_dynamic-slice_fusion.4), channel_id=1, source_target_pairs={{0,1},{1,0},{2,3},{3,2},{4,5},{5,4},{6,7},{7,6}} | collective-permute-start | bytes 18874376 | tf_op jit(solution)/shard_map/cond/branch_1_fun/ppermute | solution.py:716
  40.0 173.1 %collective-permute-start.3 = (bf16[12,1024,256]{2,1,0:T(8,128)(2,1)}, bf16[12,1024,256]{2,1,0:T(8,128)(2,1)}, u32[]{:S(2)}, u32[]{:S(2)}) collective-permute-start(bf16[12,1024,256]{2,1,0:T(8,128)(2,1)} %constant_dynamic-slice_fusion.2), channel_id=1, source_target_pairs={{0,1},{1,0},{2,3},{3,2},{4,5},{5,4},{6,7},{7,6}} | collective-permute-start | bytes 18874376 | tf_op jit(solution)/shard_map/cond/branch_1_fun/ppermute | solution.py:716
  50.6 34.1 %collective-permute-start.13 = (bf16[24,32,512]{2,1,0:T(8,128)(2,1)}, bf16[24,32,512]{2,1,0:T(8,128)(2,1)S(1)}, u32[]{:S(2)}, u32[]{:S(2)}) collective-permute-start(bf16[24,32,512]{2,1,0:T(8,128)(2,1)} %get-tuple-element.380), channel_id=1, source_target_pairs={{0,4},{1,5},{2,6},{3,7}} | collective-permute-start | bytes 2359304 | tf_op jit(solution)/shard_map/cond/branch_1_fun/ppermute | solution.py:648
  75.0 83.7 %collective-permute-start = (bf16[4,1024,256]{2,1,0:T(8,128)(2,1)S(1)}, bf16[4,1024,256]{2,1,0:T(8,128)(2,1)S(1)}, u32[]{:S(2)}, u32[]{:S(2)}) collective-permute-start(bf16[4,1024,256]{2,1,0:T(8,128)(2,1)S(1)} %constant_dynamic-slice_fusion.5), channel_id=1, source_target_pairs={{0,1},{1,0},{2,3},{3,2},{4,5},{5,4},{6,7},{7,6}} | collective-permute-start | bytes 6291464 | tf_op jit(solution)/shard_map/cond/branch_1_fun/ppermute | solution.py:716
  84.7 75.7 %collective-permute-start.2 = (bf16[4,1024,256]{2,1,0:T(8,128)(2,1)S(1)}, bf16[4,1024,256]{2,1,0:T(8,128)(2,1)S(1)}, u32[]{:S(2)}, u32[]{:S(2)}) collective-permute-start(bf16[4,1024,256]{2,1,0:T(8,128)(2,1)S(1)} %constant_dynamic-slice_fusion.3), channel_id=1, source_target_pairs={{0,1},{1,0},{2,3},{3,2},{4,5},{5,4},{6,7},{7,6}} | collective-permute-start | bytes 6291464 | tf_op jit(solution)/shard_map/cond/branch_1_fun/ppermute | solution.py:716
  84.7 41.2 %collective-permute-start.4 = (bf16[28,32,512]{2,1,0:T(8,128)(2,1)S(1)}, bf16[28,32,512]{2,1,0:T(8,128)(2,1)S(1)}, u32[]{:S(2)}, u32[]{:S(2)}) collective-permute-start(bf16[28,32,512]{2,1,0:T(8,128)(2,1)S(1)} %copy-done.38), channel_id=1, source_target_pairs={{0,2},{1,3},{2,4},{3,5},{4,6},{5,7}} | collective-permute-start | bytes 2752520 | tf_op jit(solution)/shard_map/cond/branch_1_fun/ppermute | solution.py:648
  127.6 55.3 %collective-permute-start.5 = (bf16[34,32,512]{2,1,0:T(8,128)(2,1)}, bf16[34,32,512]{2,1,0:T(8,128)(2,1)S(1)}, u32[]{:S(2)}, u32[]{:S(2)}) collective-permute-start(bf16[34,32,512]{2,1,0:T(8,128)(2,1)} %get-tuple-element.376), channel_id=1, source_target_pairs={{0,2},{1,3},{4,6},{5,7}} | collective-permute-start | bytes 3342344 | tf_op jit(solution)/shard_map/cond/branch_1_fun/ppermute | solution.py:648
  158.7 41.2 %collective-permute-start.9 = (bf16[34,32,512]{2,1,0:T(8,128)(2,1)}, bf16[34,32,512]{2,1,0:T(8,128)(2,1)}, u32[]{:S(2)}, u32[]{:S(2)}) collective-permute-start(bf16[34,32,512]{2,1,0:T(8,128)(2,1)} %get-tuple-element.377), channel_id=1, source_target_pairs={{2,6},{3,7}} | collective-permute-start | bytes 3342344 | tf_op jit(solution)/shard_map/cond/branch_1_fun/ppermute | solution.py:648
  160.4 50.0 %collective-permute-start.7 = (bf16[34,32,512]{2,1,0:T(8,128)(2,1)}, bf16[34,32,512]{2,1,0:T(8,128)(2,1)}, u32[]{:S(2)}, u32[]{:S(2)}) collective-permute-start(bf16[34,32,512]{2,1,0:T(8,128)(2,1)} %collective-permute-done.6), channel_id=1, source_target_pairs={{6,4},{7,5}} | collective-permute-start | bytes 3342344 | tf_op jit(solution)/shard_map/cond/branch_1_fun/ppermute | solution.py:648
  182.9 87.4 %collective-permute-start.8 = (bf16[34,32,512]{2,1,0:T(8,128)(2,1)}, bf16[34,32,512]{2,1,0:T(8,128)(2,1)S(1)}, u32[]{:S(2)}, u32[]{:S(2)}) collective-permute-start(bf16[34,32,512]{2,1,0:T(8,128)(2,1)} %get-tuple-element.377), channel_id=1, source_target_pairs={{0,2},{1,3},{4,6},{5,7}} | collective-permute-start | bytes 3342344 | tf_op jit(solution)/shard_map/cond/branch_1_fun/ppermute | solution.py:648
  199.9 61.1 %collective-permute-start.14 = (bf16[22,32,512]{2,1,0:T(8,128)(2,1)}, bf16[22,32,512]{2,1,0:T(8,128)(2,1)S(1)}, u32[]{:S(2)}, u32[]{:S(2)}) collective-permute-start(bf16[22,32,512]{2,1,0:T(8,128)(2,1)} %get-tuple-element.381), channel_id=1, source_target_pairs={{0,4},{1,5},{2,6},{3,7}} | collective-permute-start | bytes 2162696 | tf_op jit(solution)/shard_map/cond/branch_1_fun/ppermute | solution.py:648
  211.8 85.2 %collective-permute-start.11 = (bf16[30,32,512]{2,1,0:T(8,128)(2,1)}, bf16[30,32,512]{2,1,0:T(8,128)(2,1)S(1)}, u32[]{:S(2)}, u32[]{:S(2)}) collective-permute-start(bf16[30,32,512]{2,1,0:T(8,128)(2,1)} %get-tuple-element.378), channel_id=1, source_target_pairs={{0,2},{1,3},{2,4},{3,5},{4,6},{5,7}} | collective-permute-start | bytes 2949128 | tf_op jit(solution)/shard_map/cond/branch_1_fun/ppermute | solution.py:648
  213.1 58.6 %collective-permute-start.10 = (bf16[34,32,512]{2,1,0:T(8,128)(2,1)}, bf16[34,32,512]{2,1,0:T(8,128)(2,1)S(1)}, u32[]{:S(2)}, u32[]{:S(2)}) collective-permute-start(bf16[34,32,512]{2,1,0:T(8,128)(2,1)} %collective-permute-done.9), channel_id=1, source_target_pairs={{6,4},{7,5}} | collective-permute-start | bytes 3342344 | tf_op jit(solution)/shard_map/cond/branch_1_fun/ppermute | solution.py:648
  244.3 50.6 %collective-permute-start.15 = (bf16[18,32,512]{2,1,0:T(8,128)(2,1)}, bf16[18,32,512]{2,1,0:T(8,128)(2,1)S(1)}, u32[]{:S(2)}, u32[]{:S(2)}) collective-permute-start(bf16[18,32,512]{2,1,0:T(8,128)(2,1)} %get-tuple-element.382), channel_id=1, source_target_pairs={{0,4},{1,5},{2,6},{3,7}} | collective-permute-start | bytes 1769480 | tf_op jit(solution)/shard_map/cond/branch_1_fun/ppermute | solution.py:648
  270.4 65.6 %collective-permute-start.22 = (f32[20,32,512]{2,1,0:T(8,128)}, f32[20,32,512]{2,1,0:T(8,128)}, u32[]{:S(2)}, u32[]{:S(2)}) collective-permute-start(f32[20,32,512]{2,1,0:T(8,128)} %get-tuple-element.425), channel_id=1, source_target_pairs={{2,0},{3,1},{4,2},{5,3},{6,4},{7,5}} | collective-permute-start | bytes 3932168 | tf_op jit(solution)/shard_map/cond/branch_1_fun/ppermute | solution.py:648
  271.7 63.0 %collective-permute-start.30 = (f32[12,32,512]{2,1,0:T(8,128)}, f32[12,32,512]{2,1,0:T(8,128)}, u32[]{:S(2)}, u32[]{:S(2)}) collective-permute-start(f32[12,32,512]{2,1,0:T(8,128)} %get-tuple-element.429), channel_id=1, source_target_pairs={{4,0},{5,1},{6,2},{7,3}} | collective-permute-start | bytes 2359304 | tf_op jit(solution)/shard_map/cond/branch_1_fun/ppermute | solution.py:648
  293.6 39.8 %collective-permute-start.34 = (f32[6,32,512]{2,1,0:T(8,128)}, f32[6,32,512]{2,1,0:T(8,128)}, u32[]{:S(2)}, u32[]{:S(2)}) collective-permute-start(f32[6,32,512]{2,1,0:T(8,128)} %get-tuple-element.433), channel_id=1, source_target_pairs={{6,0},{7,1}} | collective-permute-start | bytes 1179656 | tf_op jit(solution)/shard_map/cond/branch_1_fun/ppermute | solution.py:648
  295.7 142.9 %collective-permute-start.32 = (f32[22,32,512]{2,1,0:T(8,128)}, f32[22,32,512]{2,1,0:T(8,128)S(1)}, u32[]{:S(2)}, u32[]{:S(2)}) collective-permute-start(f32[22,32,512]{2,1,0:T(8,128)} %get-tuple-element.431), channel_id=1, source_target_pairs={{4,0},{5,1},{6,2},{7,3}} | collective-permute-start | bytes 4325384 | tf_op jit(solution)/shard_map/cond/branch_1_fun/ppermute | solution.py:648
  297.0 140.3 %collective-permute-start.31 = (f32[18,32,512]{2,1,0:T(8,128)}, f32[18,32,512]{2,1,0:T(8,128)}, u32[]{:S(2)}, u32[]{:S(2)}) collective-permute-start(f32[18,32,512]{2,1,0:T(8,128)} %get-tuple-element.430), channel_id=1, source_target_pairs={{4,0},{5,1},{6,2},{7,3}} | collective-permute-start | bytes 3538952 | tf_op jit(solution)/shard_map/cond/branch_1_fun/ppermute | solution.py:648
  333.4 105.3 %collective-permute-start.37 = (f32[24,32,512]{2,1,0:T(8,128)}, f32[24,32,512]{2,1,0:T(8,128)S(1)}, u32[]{:S(2)}, u32[]{:S(2)}) collective-permute-start(f32[24,32,512]{2,1,0:T(8,128)} %get-tuple-element.436), channel_id=1, source_target_pairs={{6,0},{7,1}} | collective-permute-start | bytes 4718600 | tf_op jit(solution)/shard_map/cond/branch_1_fun/ppermute | solution.py:648
  334.7 92.7 %collective-permute-start.36 = (f32[10,32,512]{2,1,0:T(8,128)S(1)}, f32[10,32,512]{2,1,0:T(8,128)S(1)}, u32[]{:S(2)}, u32[]{:S(2)}) collective-permute-start(f32[10,32,512]{2,1,0:T(8,128)S(1)} %copy-done.13), channel_id=1, source_target_pairs={{6,0},{7,1}} | collective-permute-start | bytes 1966088 | tf_op jit(solution)/shard_map/cond/branch_1_fun/ppermute | solution.py:648
  336.0 91.4 %collective-permute-start.35 = (f32[8,32,512]{2,1,0:T(8,128)}, f32[8,32,512]{2,1,0:T(8,128)S(1)}, u32[]{:S(2)}, u32[]{:S(2)}) collective-permute-start(f32[8,32,512]{2,1,0:T(8,128)} %get-tuple-element.434), channel_id=1, source_target_pairs={{6,0},{7,1}} | collective-permute-start | bytes 1572872 | tf_op jit(solution)/shard_map/cond/branch_1_fun/ppermute | solution.py:648
  427.4 198.3 %collective-permute-start.21 = (bf16[16,1024,256]{2,1,0:T(8,128)(2,1)}, bf16[16,1024,256]{2,1,0:T(8,128)(2,1)}, u32[]{:S(2)}, u32[]{:S(2)}) collective-permute-start(bf16[16,1024,256]{2,1,0:T(8,128)(2,1)} %get-tuple-element.423), channel_id=1, source_target_pairs={{0,1},{1,0},{2,3},{3,2},{4,5},{5,4},{6,7},{7,6}} | collective-permute-start | bytes 25165832 | tf_op jit(solution)/shard_map/cond/branch_1_fun/ppermute | solution.py:707
  427.4 49.1 %collective-permute-start.24 = (f32[28,32,512]{2,1,0:T(8,128)S(1)}, f32[28,32,512]{2,1,0:T(8,128)S(1)}, u32[]{:S(2)}, u32[]{:S(2)}) collective-permute-start(f32[28,32,512]{2,1,0:T(8,128)S(1)} %copy-done.17), channel_id=1, source_target_pairs={{4,0},{5,1}} | collective-permute-start | bytes 5505032 | tf_op jit(solution)/shard_map/cond/branch_1_fun/ppermute | solution.py:648
  437.3 40.5 %collective-permute-start.23 = (f32[28,32,512]{2,1,0:T(8,128)S(1)}, f32[28,32,512]{2,1,0:T(8,128)S(1)}, u32[]{:S(2)}, u32[]{:S(2)}) collective-permute-start(f32[28,32,512]{2,1,0:T(8,128)S(1)} %copy-done.17), channel_id=1, source_target_pairs={{2,0},{3,1},{6,4},{7,5}} | collective-permute-start | bytes 5505032 | tf_op jit(solution)/shard_map/cond/branch_1_fun/ppermute | solution.py:648
  438.6 195.3 %collective-permute-start.20 = (bf16[16,1024,256]{2,1,0:T(8,128)(2,1)}, bf16[16,1024,256]{2,1,0:T(8,128)(2,1)}, u32[]{:S(2)}, u32[]{:S(2)}) collective-permute-start(bf16[16,1024,256]{2,1,0:T(8,128)(2,1)} %get-tuple-element.421), channel_id=1, source_target_pairs={{0,1},{1,0},{2,3},{3,2},{4,5},{5,4},{6,7},{7,6}} | collective-permute-start | bytes 25165832 | tf_op jit(solution)/shard_map/cond/branch_1_fun/ppermute | solution.py:707
  438.7 80.0 %collective-permute-start.27 = (f32[30,32,512]{2,1,0:T(8,128)S(1)}, f32[30,32,512]{2,1,0:T(8,128)S(1)}, u32[]{:S(2)}, u32[]{:S(2)}) collective-permute-start(f32[30,32,512]{2,1,0:T(8,128)S(1)} %copy-done.6), channel_id=1, source_target_pairs={{4,0},{5,1}} | collective-permute-start | bytes 5898248 | tf_op jit(solution)/shard_map/cond/branch_1_fun/ppermute | solution.py:648
  476.5 87.5 %collective-permute-start.33 = (f32[34,32,512]{2,1,0:T(8,128)}, f32[34,32,512]{2,1,0:T(8,128)S(1)}, u32[]{:S(2)}, u32[]{:S(2)}) collective-permute-start(f32[34,32,512]{2,1,0:T(8,128)} %get-tuple-element.432), channel_id=1, source_target_pairs={{4,0},{5,1},{6,2},{7,3}} | collective-permute-start | bytes 6684680 | tf_op jit(solution)/shard_map/cond/branch_1_fun/ppermute | solution.py:648
  477.8 43.0 %collective-permute-start.26 = (f32[30,32,512]{2,1,0:T(8,128)S(1)}, f32[30,32,512]{2,1,0:T(8,128)S(1)}, u32[]{:S(2)}, u32[]{:S(2)}) collective-permute-start(f32[30,32,512]{2,1,0:T(8,128)S(1)} %copy-done.6), channel_id=1, source_target_pairs={{2,0},{3,1},{6,4},{7,5}} | collective-permute-start | bytes 5898248 | tf_op jit(solution)/shard_map/cond/branch_1_fun/ppermute | solution.py:648
  518.7 65.7 %collective-permute-start.29 = (f32[46,32,512]{2,1,0:T(8,128)}, f32[46,32,512]{2,1,0:T(8,128)S(1)}, u32[]{:S(2)}, u32[]{:S(2)}) collective-permute-start(f32[46,32,512]{2,1,0:T(8,128)} %get-tuple-element.428), channel_id=1, source_target_pairs={{2,0},{3,1},{4,2},{5,3},{6,4},{7,5}} | collective-permute-start | bytes 9043976 | tf_op jit(solution)/shard_map/cond/branch_1_fun/ppermute | solution.py:648
  520.9 81.8 %collective-permute-start.28 = (f32[30,32,512]{2,1,0:T(8,128)S(1)}, f32[30,32,512]{2,1,0:T(8,128)S(1)}, u32[]{:S(2)}, u32[]{:S(2)}) collective-permute-start(f32[30,32,512]{2,1,0:T(8,128)S(1)} %collective-permute-done.27), channel_id=1, source_target_pairs={{0,2},{1,3}} | collective-permute-start | bytes 5898248 | tf_op jit(solution)/shard_map/cond/branch_1_fun/ppermute | solution.py:648
  564.0 38.7 %collective-permute-start.25 = (f32[28,32,512]{2,1,0:T(8,128)S(1)}, f32[28,32,512]{2,1,0:T(8,128)S(1)}, u32[]{:S(2)}, u32[]{:S(2)}) collective-permute-start(f32[28,32,512]{2,1,0:T(8,128)S(1)} %collective-permute-done.24), channel_id=1, source_target_pairs={{0,2},{1,3}} | collective-permute-start | bytes 5505032 | tf_op jit(solution)/shard_map/cond/branch_1_fun/ppermute | solution.py:648
  (43 other events, 1222.9 us)

commit v5 on v4

--- a/solution.py
+++ b/solution.py
@@ -15,17 +15,18 @@
 NCH = 4
 
 FAST = (
-    ((28, 34, 34, 30), (22, 24, 22, 18), (14, 14, 12, 10)),
-    ((20, 28, 30, 46), (12, 18, 22, 34), (6, 8, 10, 24)),
-    (4, 8, 12, 16),
+    ((22, 44, 60), (18, 34, 36), (12, 20, 18)),
+    ((14, 34, 34, 42), (10, 22, 24, 32), (4, 10, 12, 24)),
+    (3, 8, 13, 16),
 )
-RELAY_F = (1, 2)
+LEVELS = ((22, 15, 9), (28, 21, 15), (42, 32, 24))
+RELAY_F = (2,)
 RELAY_B = (1, 2)
-QA = 4
+QA = 3
 SLOW_SEQS = 4
 SLOW = (((8 * SLOW_SEQS,),) * 3,) * 2 + ((NS,),)
 
-CNT, OFF, DM, ST, SG, CE, FIT = 0, 336, 672, 704, 712, 840, 844
+CNT, OFF, DM, ST, SG, CE, FIT, LEVEL, SPLIT = 0, 336, 672, 704, 712, 840, 844, 845, 846
 NTAB = 848
 
 
@@ -70,7 +71,7 @@
 
 def table_kernel(plan, ks, me, tab):
     f_cap, b_cap, quota = plan
-    n_t = len(f_cap[0])
+    n_f, n_t = len(f_cap[0]), len(b_cap[0])
     f_lo = [bounds(cap) for cap in f_cap]
     c, e, lo, hi = me[0], me[1], me[2], me[3]
     zero = jnp.int32(0)
@@ -91,6 +92,7 @@
             tab[DM + s * 2 + h] = (need + 255) >> 8
 
     fit = jnp.bool_(True)
+    last = [zero] * 3
     for col in range(2):
         row0 = jnp.where(e == 0, col, 1 - col) * NS
         for cc in range(NCH):
@@ -112,7 +114,7 @@
                         continue
                     ok = s < hi
                     for d in range(min(cc, 3)):
-                        ok = ok & (off[d] <= f_lo[d][t + 1])
+                        ok = ok & (off[d] <= f_lo[d][min(t, n_f - 1) + 1])
                     ready[t] = ready[t] + jnp.where(ok, 1, 0)
                     for d in range(min(cc, 3)):
                         avail[t][d] = jnp.where(ok, off[d], avail[t][d])
@@ -127,11 +129,26 @@
                 if col == 0:
                     tab[sg(cc, d, 0)] = sent
                 for v in range(n_t):
+                    if v == n_t - 1:
+                        last[d] = jnp.maximum(last[d], off[d] - sent)
                     sent = jnp.minimum(sent + b_cap[d][v], avail[v][d])
                     if col == 0:
                         tab[sg(cc, d, v + 1)] = sent
                 fit = fit & (sent == off[d])
     tab[FIT] = jnp.where(fit, 1, 0)
+    level = zero
+    for size in LEVELS[:-1]:
+        over = (last[0] > size[0]) | (last[1] > size[1]) | (last[2] > size[2])
+        level = level + jnp.where(over, 1, 0)
+    tab[LEVEL] = level
+    done = zero
+    for s in range(NS):
+        ok = jnp.bool_(True)
+        for d in range(3):
+            cc = c + d + 1
+            ok = ok & (tab[at(OFF, cc, d, s)] + tab[at(CNT, cc, d, s)] <= tab[sg(cc, d, n_t - 1)])
+        done = done + jnp.where(ok, 1, 0)
+    tab[SPLIT] = done
 
 
 def run_copies(lo_of, n_chunks, off, n, issue):
@@ -222,11 +239,11 @@
     return out, refs
 
 
-def compute_kernel(t, n_t, f_lo, n_mate, ways, n_alias, scale, tab, docs, q_all, g_all, kvcol, *rest):
+def compute_kernel(t, n_t, n_got, f_lo, n_mate, ways, n_alias, scale, tab, docs, q_all, g_all, kvcol, *rest):
     q_mates, rest = rest[:n_mate], rest[n_mate:]
     g_mates, rest = rest[:n_mate], rest[n_mate:]
     fbuf, rest = split(rest, ways)
-    fbuf = [fbuf[d * (t + 1):(d + 1) * (t + 1)] for d in range(3)]
+    fbuf = [fbuf[d * n_got:(d + 1) * n_got] for d in range(3)]
     rest = rest[n_alias:]
     o_all, o_send, dq_all, dq_send, acc = rest[:5]
     rest = rest[5:]
@@ -295,7 +312,7 @@
                     pl.when(c != 2)(lambda: go(fbuf[d][v][0]))
                     pl.when(c == 2)(lambda: go(fbuf[d][v][1]))
 
-            run_copies(lambda v: f_lo[d][v], t + 1, off, cnt, issue)
+            run_copies(lambda v: f_lo[d][v], n_got, off, cnt, issue)
 
     def fetch_wait(ss, sl):
         for copy in inputs(ss, sl) + mate_inputs((q_mates[0], g_mates[0]), 0, sl):
@@ -487,13 +504,12 @@
         put_wait(base + n - 1, lax.rem(n + 1, 2))
 
 
-def finish_kernel(n_t, ways, n_alias, scale, tab, acc, *rest):
+def finish_kernel(part, n_t, ways, n_alias, scale, tab, acc, *rest):
     bufs, rest = split(rest, ways)
     bufs = [bufs[d * n_t:(d + 1) * n_t] for d in range(3)]
     dk_all, dv_all, dkv_send, own, got, kb, vb, sb, sem, osem = rest[n_alias:]
-    lo = tab[ST]
-    n = tab[ST + n_t] if n_t == 1 else NS
-    n = n - lo
+    lo, hi = ((tab[ST], tab[ST + 1]), (0, tab[SPLIT]), (tab[SPLIT], NS))[part]
+    n = hi - lo
     c, e = tab[CE], tab[CE + 1]
 
     def fetch(ss, sl):
@@ -655,15 +671,16 @@
 
         def attend(plan, t, tab, mates, kvcol, frecv, state):
             f_cap, b_cap = plan[:2]
-            n_t = len(f_cap[0])
+            n_t = len(b_cap[0])
             live = n_t - t
             n_alias = 0 if state is None else len(state)
             mates = mates[:1] if n_t > 1 and t == 0 else mates
-            got = [frecv[d][u] for d in range(3) for u in range(t + 1)]
+            n_got = min(t + 1, len(f_cap[0]))
+            got = [frecv[d][u] for d in range(3) for u in range(n_got)]
             flat = [x for way in got for x in way]
             n_in = 5 + 2 * len(mates) + len(flat)
             return pl.pallas_call(
-                functools.partial(compute_kernel, t, n_t, [bounds(cap) for cap in f_cap], len(mates), [len(way) for way in got], n_alias, scale),
+                functools.partial(compute_kernel, t, n_t, n_got, [bounds(cap) for cap in f_cap], len(mates), [len(way) for way in got], n_alias, scale),
                 in_specs=[SMEM, VMEM] + [ANY] * (n_in - 2 + n_alias),
                 out_specs=[ANY] * (5 + 3 * live),
                 scratch_shapes=[
@@ -684,13 +701,13 @@
                 cost_estimate=pl.CostEstimate(flops=60_000_000_000 // n_t, bytes_accessed=100_000_000 // n_t, transcendentals=0),
             )(tab, docs, q3, g3, kvcol, *[m[0] for m in mates], *[m[1] for m in mates], *flat, *([] if state is None else state))
 
-        def finish(plan, tab, acc, brecv, state):
-            n_t = len(plan[0][0])
+        def finish(part, tab, acc, brecv, state):
+            n_t = len(brecv[0])
             n_alias = 0 if state is None else 3
             got = [way for row in brecv for way in row]
             flat = [x for way in got for x in way]
             return pl.pallas_call(
-                functools.partial(finish_kernel, n_t, [len(way) for way in got], n_alias, scale),
+                functools.partial(finish_kernel, part, n_t, [len(way) for way in got], n_alias, scale),
                 in_specs=[SMEM] + [ANY] * (1 + len(flat) + n_alias),
                 out_specs=[ANY] * 3,
                 out_shape=[shape((nb, piece, hd), bf), shape((nb, piece, hd), bf), shape((NS, piece, 512), bf)],
@@ -700,7 +717,6 @@
                     pltpu.SemaphoreType.DMA((2,)), pltpu.SemaphoreType.DMA((2,)),
                 ],
                 input_output_aliases={2 + len(flat) + k: k for k in range(n_alias)},
-                name="finish",
             )(tab, acc, *flat, *([] if state is None else state))
 
         def place(mine, send):
@@ -718,13 +734,13 @@
         tab = tables(FAST, jnp.int32(0), jnp.int32(NS))
 
         def fast():
-            n_t = len(FAST[0][0])
+            n_f, n_t = len(FAST[0][0]), len(FAST[1][0])
             packed = pack(FAST, tab, NS)
             kvcol, fsend = packed[0], packed[1:]
-            frecv = [[None] * n_t for _ in range(3)]
-            for t in range(n_t):
+            frecv = [[None] * n_f for _ in range(3)]
+            for t in range(n_f):
                 for d in range(3):
-                    x = fsend[d * n_t + t]
+                    x = fsend[d * n_f + t]
                     if d == 0 and t in RELAY_F:
                         across = chip_hop(x, (0, 1), (2, 3))
                         mid = chip_hop(x, (1, 3))
@@ -734,11 +750,13 @@
             mates = [(swap_part(q3, 0, QA), swap_part(g3, 0, QA)),
                      (swap_part(q3, QA, NS - QA), swap_part(g3, QA, NS - QA))]
             state = None
-            brecv = [[None] * n_t for _ in range(3)]
+            brecv = [[None] * (n_t - 1) for _ in range(3)]
             for t in range(n_t):
                 live = n_t - t
                 outs = attend(FAST, t, tab, mates, kvcol, frecv, state)
                 state = list(outs[:5]) + [outs[5 + d * live + k] for d in range(3) for k in range(1, live)]
+                if t == n_t - 1:
+                    break
                 for d in range(3):
                     x = outs[5 + d * live]
                     if d == 0 and t in RELAY_B:
@@ -748,9 +766,22 @@
                     else:
                         brecv[d][t] = (backward_hop(x, d),)
             o_all, o_send, dq_all, dq_send, acc = state
-            attn_out = place(o_all, o_send)
-            grad_query = place(dq_all, dq_send)
-            return (attn_out, grad_query) + place_kv(*finish(FAST, tab, acc, brecv, None))
+            last = outs[5:]
+
+            def tail(k):
+                def run():
+                    got = []
+                    for d in range(3):
+                        got.append((backward_hop(last[d][:LEVELS[k][d]], d),))
+                    attn_out = place(o_all, o_send)
+                    grad_query = place(dq_all, dq_send)
+                    grads = finish(1, tab, acc, brecv, None)
+                    grads = finish(2, tab, acc, [row + [x] for row, x in zip(brecv, got)], grads)
+                    return (attn_out, grad_query) + place_kv(*grads)
+
+                return run
+
+            return lax.switch(tab[LEVEL], [tail(k) for k in range(len(LEVELS))])
 
         def slow():
             mates = [(swap_part(q3, 0, NS), swap_part(g3, 0, NS))]
@@ -768,7 +799,7 @@
                 blank_b = [jnp.zeros((SLOW[1][0][0], G, 512), f32) for _ in range(3)]
                 outs = attend(SLOW, 0, tab, mates, packed[0], frecv, state + blank_b)
                 brecv = [[(backward_hop(outs[5 + d], d),)] for d in range(3)]
-                return tuple(outs[:5]) + tuple(finish(SLOW, tab, outs[4], brecv, grads))
+                return tuple(outs[:5]) + tuple(finish(0, tab, outs[4], brecv, grads))
 
             out = lax.fori_loop(0, NS // SLOW_SEQS, one_round, tuple(blank()))
             return (place(out[0], out[1]), place(out[2], out[3])) + place_kv(*out[5:])

time: 649 us -> 620 us (0.955)
  the two profiles are of different devices: /device:TPU:0 before, /device:TPU:3 now
where the time goes in v5:
time: 620 us; the launch traced here: 613 us
  waiting for transfers between devices  234 us (38%)
  Pallas kernels  163 us (26%)
  starting transfers between devices  154 us (25%)
  local copies, waits for them, and re-layouts  47.7 us (8%)
  loops' own time  9.64 us (2%)
    ppermute x27, waiting for transfers between devices, chip_hop(): lax.ppermute(x, 'cp', [(2 * a + k, 2 * b + k) for a, b in moves for k in...  229 us
    ppermute x27, starting transfers between devices, chip_hop(): lax.ppermute(x, 'cp', [(2 * a + k, 2 * b + k) for a, b in moves for k in...  145 us
    pallas_call x4, Pallas kernels, attend(): pl.pallas_call(functools.partial(compute_kernel, t, n_t, n_got, [bounds(c...  130 us
    dynamic_slice x4, local copies, waits for them, and re-layouts, swap_part(): lax.dynamic_slice_in_dim(x, other + lo, n, 0)  16.4 us
    pallas_call x2, Pallas kernels, finish(): pl.pallas_call(functools.partial(finish_kernel, part, n_t, [len(way) for...  15.9 us
    dynamic_update_slice x2, local copies, waits for them, and re-layouts, place(): return lax.dynamic_update_slice_in_dim(mine, got, other, 0)  15.8 us
  transfers between devices with their start and end apart: 35, of which 12 were waited for; matrix products, arithmetic and copies ran while one was open for 5% of the time, Pallas kernels for 20%

profile of v5, /device:TPU:3, one launch (start us, length us, event | category | flops | bytes accessed | tf_op | source)
XLA Modules:
  0.0 613.4 jit_solution(4812513835563875234)
XLA Ops:
  4.6 7.7 %docs.1 = (s32[8,32,128]{2,1,0:T(8,128)S(1)}, s32[32,128]{1,0:T(8,128)S(1)}) custom-call(s32[32,128]{1,0:T(8,128)} %doc.1), custom_call_target="tpu_custom_call" | custom-call | tf_op jit(solution)/shard_map/docs/pallas_call | solution.py:628
  12.9 3.3 tables.2
  17.5 594.6 %conditional.2 = (bf16[32,128,8,256]{3,2,1,0:T(8,128)(2,1)}, bf16[32,128,8,256]{3,2,1,0:T(8,128)(2,1)}, bf16[32,128,1,256]{3,1,2,0:T(8,128)(2,1)}, bf16[32,128,1,256]{3,1,2,0:T(8,128)(2,1)}) conditional(s32[]{:T(128)} %bitcast.37, (s32[]{:T(128)}, bf16[32,1024,256]{2,1,0:T(8,128)(2,1)}, bf16[32,1024,256]{2,1,0:T(8,128)(2,1)}, s32[]{:T(128)}, ...), branch_computations={%region_0.0_spmd, %region_3.0_spmd} | conditional | flops 60000002048 | bytes 559333248 | solution.py:807
  25.7 7.0 %constant_dynamic-slice_fusion.4 = bf16[13,1024,256]{2,1,0:T(8,128)(2,1)} fusion(bf16[32,1024,256]{2,1,0:T(8,128)(2,1)} %get-tuple-element.583.q_all, s32[]{:T(128)S(6)} %select_n.18), kind=kLoop, calls=%fused_computation.29 | loop fusion | bytes 13631492 | tf_op jit(solution)/shard_map/cond/branch_1_fun/dynamic_slice | solution.py:732
  33.1 6.3 %constant_dynamic-slice_fusion.2 = bf16[13,1024,256]{2,1,0:T(8,128)(2,1)} fusion(bf16[32,1024,256]{2,1,0:T(8,128)(2,1)} %get-tuple-element.584.g_all, s32[]{:T(128)S(6)} %select_n.18), kind=kLoop, calls=%fused_computation.27 | loop fusion | bytes 13631492 | tf_op jit(solution)/shard_map/cond/branch_1_fun/dynamic_slice | solution.py:732
  39.6 5.5 pack.6
  50.8 31.7 %collective-permute-done.27.rest_3_.rest_6_.rest_8_ = bf16[18,32,512]{2,1,0:T(8,128)(2,1)S(1)} collective-permute-done((bf16[18,32,512]{2,1,0:T(8,128)(2,1)}, bf16[18,32,512]{2,1,0:T(8,128)(2,1)S(1)}, u32[]{:S(2)}, u32[]{:S(2)}) %collective-permute-start.27) | collective-permute-done | bytes 589856 | tf_op jit(solution)/shard_map/cond/branch_1_fun/ppermute | solution.py:664
  84.4 4.7 collective-permute-start.25
  90.6 9.5 %collective-permute-done.22.rest_2_.rest_4_ = bf16[22,32,512]{2,1,0:T(8,128)(2,1)S(1)} collective-permute-done((bf16[22,32,512]{2,1,0:T(8,128)(2,1)}, bf16[22,32,512]{2,1,0:T(8,128)(2,1)S(1)}, u32[]{:S(2)}, u32[]{:S(2)}) %collective-permute-start.22) | collective-permute-done | bytes 720928 | tf_op jit(solution)/shard_map/cond/branch_1_fun/ppermute | solution.py:664
  100.2 3.0 collective-permute-start.18
  112.8 35.7 %collective-permute-done.25 = bf16[60,32,512]{2,1,0:T(8,128)(2,1)} collective-permute-done((bf16[60,32,512]{2,1,0:T(8,128)(2,1)}, bf16[60,32,512]{2,1,0:T(8,128)(2,1)}, u32[]{:S(2)}, u32[]{:S(2)}) %collective-permute-start.25) | collective-permute-done | bytes 1966112 | tf_op jit(solution)/shard_map/cond/branch_1_fun/ppermute | solution.py:664
  150.5 25.4 %branch_1_fun.8 = (bf16[32,1024,256]{2,1,0:T(8,128)(2,1)}, bf16[16,1024,256]{2,1,0:T(8,128)(2,1)}, bf16[32,1024,256]{2,1,0:T(8,128)(2,1)}, bf16[16,1024,256]{2,1...) custom-call(s32[848]{0:T(1024)} %copy-done.27, ...), custom_call_target="tpu_custom_call" | custom-call | flops 15000000512 | bytes 25000000 | tf_op jit(solution)/shard_map/cond/branch_1_fun/pallas_call | solution.py:682
  175.8 4.8 collective-permute-start.29
  181.4 39.9 %branch_1_fun.9 = (bf16[32,1024,256]{2,1,0:T(8,128)(2,1)}, bf16[16,1024,256]{2,1,0:T(8,128)(2,1)}, bf16[32,1024,256]{2,1,0:T(8,128)(2,1)}, bf16[16,1024,256]{2,1...) custom-call(s32[848]{0:T(1024)} %copy-done.27, ...), custom_call_target="tpu_custom_call", output_to_operand_aliasing={{0}: (15, {}), {1}: (16, {}), {2}: (17, {}), {3}: (18, {}),... | custom-call | flops 15000000512 | bytes 25000000 | tf_op jit(solution)/shard_map/cond/branch_1_fun/pallas_call | solution.py:682
  222.6 39.8 %branch_1_fun.10 = (bf16[32,1024,256]{2,1,0:T(8,128)(2,1)}, bf16[16,1024,256]{2,1,0:T(8,128)(2,1)}, bf16[32,1024,256]{2,1,0:T(8,128)(2,1)}, bf16[16,1024,256]{2,...) custom-call(s32[848]{0:T(1024)S(1)} %copy-done.28, ...), custom_call_target="tpu_custom_call", output_to_operand_aliasing={{0}: (19, {}), {1}: (20, {}), {2}: (21, {}), {3}: (22, {}),... | custom-call | flops 15000000512 | bytes 25000000 | tf_op jit(solution)/shard_map/cond/branch_1_fun/pallas_call | solution.py:682
  271.7 29.5 %collective-permute-done.40 = f32[10,32,512]{2,1,0:T(8,128)S(1)} collective-permute-done((f32[10,32,512]{2,1,0:T(8,128)}, f32[10,32,512]{2,1,0:T(8,128)S(1)}, u32[]{:S(2)}, u32[]{:S(2)}) %collective-permute-start.40) | collective-permute-done | bytes 655392 | tf_op jit(solution)/shard_map/cond/branch_1_fun/ppermute | solution.py:664
  303.4 100.1 %collective-permute-start.37 = (f32[34,32,512]{2,1,0:T(8,128)}, f32[34,32,512]{2,1,0:T(8,128)}, u32[]{:S(2)}, u32[]{:S(2)}) collective-permute-start(f32[34,32,512]{2,1,0:T(8,128)} %get-tuple-element.642), channel_id=1, source_target_pairs={{2,0},{3,1},{6,4},{7,5}} | collective-permute-start | bytes 6684680 | tf_op jit(solution)/shard_map/cond/branch_1_fun/ppermute | solution.py:664
  411.4 25.4 %branch_1_fun.11 = (bf16[32,1024,256]{2,1,0:T(8,128)(2,1)}, bf16[16,1024,256]{2,1,0:T(8,128)(2,1)}, bf16[32,1024,256]{2,1,0:T(8,128)(2,1)}, bf16[16,1024,256]{2,...) custom-call(s32[848]{0:T(1024)S(1)} %copy-done.28, ...), custom_call_target="tpu_custom_call", output_to_operand_aliasing={{0}: (19, {}), {1}: (20, {}), {2}: (21, {}), {3}: (22, {}),... | custom-call | flops 15000000512 | bytes 25000000 | tf_op jit(solution)/shard_map/cond/branch_1_fun/pallas_call | solution.py:682
  436.8 8.3 %collective-permute-done.42 = f32[24,32,512]{2,1,0:T(8,128)} collective-permute-done((f32[24,32,512]{2,1,0:T(8,128)}, f32[24,32,512]{2,1,0:T(8,128)}, u32[]{:S(2)}, u32[]{:S(2)}) %collective-permute-start.42) | collective-permute-done | bytes 1572896 | tf_op jit(solution)/shard_map/cond/branch_1_fun/ppermute | solution.py:664
  445.1 3.5 collective-permute-done.37
  448.6 47.6 %collective-permute-done.34 = f32[34,32,512]{2,1,0:T(8,128)} collective-permute-done((f32[34,32,512]{2,1,0:T(8,128)S(1)}, f32[34,32,512]{2,1,0:T(8,128)}, u32[]{:S(2)}, u32[]{:S(2)}) %collective-permute-start.34) | collective-permute-done | bytes 2228256 | tf_op jit(solution)/shard_map/cond/branch_1_fun/ppermute | solution.py:664
  496.2 8.0 %collective-permute-done.36 = f32[34,32,512]{2,1,0:T(8,128)} collective-permute-done((f32[34,32,512]{2,1,0:T(8,128)}, f32[34,32,512]{2,1,0:T(8,128)}, u32[]{:S(2)}, u32[]{:S(2)}) %collective-permute-start.36) | collective-permute-done | bytes 2228256 | tf_op jit(solution)/shard_map/cond/branch_1_fun/ppermute | solution.py:664
  504.2 107.6 %conditional = (bf16[32,128,8,256]{3,2,1,0:T(8,128)(2,1)}, bf16[32,128,8,256]{3,2,1,0:T(8,128)(2,1)}, bf16[32,128,1,256]{3,1,0,2:T(8,128)(2,1)}, bf16[32,128,1,256]{3,1,0,2:T(8,128)(2,1)}) conditional(s32[]{:T(128)} %bitcast.31, (bf16[16,1024,256]{2,1,0:T(8,128)(2,1)}, s32[]{:T(128)}, bf16[32,1024,256]{2,1,0:T(8,128)(2,1)}, ...), branch_computations={%region_4.0_spmd, %region_5.0_spmd, %region_6.0_spmd} | conditional | flops 3 | bytes 147352448 | solution.py:784
  504.2 2.8 collective-permute-start.6
  507.0 2.9 slice.39
  519.7 11.7 %branch_1_fun.6 = (bf16[32,128,256]{2,1,0:T(8,128)(2,1)S(1)}, bf16[32,128,256]{2,1,0:T(8,128)(2,1)}, bf16[16,128,512]{2,1,0:T(8,128)(2,1)}) custom-call(s32[848]{0:T(1024)} %copy-done.31, f32[16,8,32,512]{3,2,1,0:T(8,128)} %get-tuple-element.533.acc, f32[14,32,512]{2,1,0:T(8,128)} %get-tuple-element.534.rest_0_, f32[34,32,512]{2,1,0:T(8,128)} %get-tuple-element.535.rest_1_, ...), custom_call_target="tpu_custom_call" | custom-call | tf_op jit(solution)/shard_map/cond/branch_1_fun/cond/branch_1_fun/pallas_call | solution.py:709
  531.3 53.1 %collective-permute-done.9.rest_9_ = f32[21,32,512]{2,1,0:T(8,128)} collective-permute-done((f32[21,32,512]{2,1,0:T(8,128)}, f32[21,32,512]{2,1,0:T(8,128)}, u32[]{:S(2)}, u32[]{:S(2)}) %collective-permute-start.9) | collective-permute-done | bytes 1376288 | tf_op jit(solution)/shard_map/cond/branch_1_fun/cond/branch_1_fun/ppermute | solution.py:664
  584.5 4.3 branch_1_fun.7
  589.0 4.3 collective-permute-done.11
  593.3 2.7 fusion.4
  596.0 8.3 %constant_dynamic-update-slice_fusion.5 = bf16[32,1024,256]{2,1,0:T(8,128)(2,1)} fusion(bf16[32,1024,256]{2,1,0:T(8,128)(2,1)} %get-tuple-element.527, bf16[16,1024,256]{2,1,0:T(8,128)(2,1)} %collective-permute-done.6, s32[]{:T(128)S(6)} %select_n.15), kind=kLoop, calls=%fused_computation.20 | loop fusion | bytes 16777220 | tf_op jit(solution)/shard_map/cond/branch_1_fun/cond/branch_1_fun/dynamic_update_slice | solution.py:724
  604.3 7.5 %constant_dynamic-update-slice_fusion.4 = bf16[32,1024,256]{2,1,0:T(8,128)(2,1)} fusion(bf16[32,1024,256]{2,1,0:T(8,128)(2,1)} %get-tuple-element.530, bf16[16,1024,256]{2,1,0:T(8,128)(2,1)} %collective-permute-done.7, s32[]{:T(128)S(6)} %select_n.15), kind=kLoop, calls=%fused_computation.19 | loop fusion | bytes 16777220 | tf_op jit(solution)/shard_map/cond/branch_1_fun/cond/branch_1_fun/dynamic_update_slice | solution.py:724
  (118 shorter events, 56.8 us)
Async XLA Ops:
  3.9 13.6 %collective-permute-start.57 = (bf16[16,128,512]{2,1,0:T(8,128)(2,1)}, bf16[16,128,512]{2,1,0:T(8,128)(2,1)S(1)}, u32[]{:S(2)}, u32[]{:S(2)}) collective-permute-start(bf16[16,128,512]{2,1,0:T(8,128)(2,1)} %pad_maximum_fusion), channel_id=1, source_target_pairs={{0,1},{1,0},{2,3},{3,2},{4,5},{5,4},{6,7},{7,6}} | collective-permute-start | bytes 6291464 | tf_op jit(solution)/shard_map/ppermute | solution.py:627
  32.7 147.9 %collective-permute-start.19 = (bf16[13,1024,256]{2,1,0:T(8,128)(2,1)}, bf16[13,1024,256]{2,1,0:T(8,128)(2,1)}, u32[]{:S(2)}, u32[]{:S(2)}) collective-permute-start(bf16[13,1024,256]{2,1,0:T(8,128)(2,1)} %constant_dynamic-slice_fusion.4), channel_id=1, source_target_pairs={{0,1},{1,0},{2,3},{3,2},{4,5},{5,4},{6,7},{7,6}} | collective-permute-start | bytes 20447240 | tf_op jit(solution)/shard_map/cond/branch_1_fun/ppermute | solution.py:732
  39.5 141.9 %collective-permute-start.21 = (bf16[13,1024,256]{2,1,0:T(8,128)(2,1)}, bf16[13,1024,256]{2,1,0:T(8,128)(2,1)}, u32[]{:S(2)}, u32[]{:S(2)}) collective-permute-start(bf16[13,1024,256]{2,1,0:T(8,128)(2,1)} %constant_dynamic-slice_fusion.2), channel_id=1, source_target_pairs={{0,1},{1,0},{2,3},{3,2},{4,5},{5,4},{6,7},{7,6}} | collective-permute-start | bytes 20447240 | tf_op jit(solution)/shard_map/cond/branch_1_fun/ppermute | solution.py:732
  45.1 37.4 %collective-permute-start.27 = (bf16[18,32,512]{2,1,0:T(8,128)(2,1)}, bf16[18,32,512]{2,1,0:T(8,128)(2,1)S(1)}, u32[]{:S(2)}, u32[]{:S(2)}) collective-permute-start(bf16[18,32,512]{2,1,0:T(8,128)(2,1)} %get-tuple-element.593), channel_id=1, source_target_pairs={{0,4},{1,5},{2,6},{3,7}} | collective-permute-start | bytes 1769480 | tf_op jit(solution)/shard_map/cond/branch_1_fun/ppermute | solution.py:664
  48.1 58.2 %collective-permute-start.28 = (bf16[34,32,512]{2,1,0:T(8,128)(2,1)}, bf16[34,32,512]{2,1,0:T(8,128)(2,1)S(1)}, u32[]{:S(2)}, u32[]{:S(2)}) collective-permute-start(bf16[34,32,512]{2,1,0:T(8,128)(2,1)} %get-tuple-element.594), channel_id=1, source_target_pairs={{0,4},{1,5},{2,6},{3,7}} | collective-permute-start | bytes 3342344 | tf_op jit(solution)/shard_map/cond/branch_1_fun/ppermute | solution.py:664
  50.1 34.3 %collective-permute-start.31 = (bf16[20,32,512]{2,1,0:T(8,128)(2,1)}, bf16[20,32,512]{2,1,0:T(8,128)(2,1)S(1)}, u32[]{:S(2)}, u32[]{:S(2)}) collective-permute-start(bf16[20,32,512]{2,1,0:T(8,128)(2,1)} %get-tuple-element.597), channel_id=1, source_target_pairs={{0,6},{1,7}} | collective-permute-start | bytes 1966088 | tf_op jit(solution)/shard_map/cond/branch_1_fun/ppermute | solution.py:664
  82.5 17.7 %collective-permute-start.22 = (bf16[22,32,512]{2,1,0:T(8,128)(2,1)}, bf16[22,32,512]{2,1,0:T(8,128)(2,1)S(1)}, u32[]{:S(2)}, u32[]{:S(2)}) collective-permute-start(bf16[22,32,512]{2,1,0:T(8,128)(2,1)} %get-tuple-element.590), channel_id=1, source_target_pairs={{0,2},{1,3},{2,4},{3,5},{4,6},{5,7}} | collective-permute-start | bytes 2162696 | tf_op jit(solution)/shard_map/cond/branch_1_fun/ppermute | solution.py:664
  84.4 64.1 %collective-permute-start.25 = (bf16[60,32,512]{2,1,0:T(8,128)(2,1)}, bf16[60,32,512]{2,1,0:T(8,128)(2,1)}, u32[]{:S(2)}, u32[]{:S(2)}) collective-permute-start(bf16[60,32,512]{2,1,0:T(8,128)(2,1)} %get-tuple-element.592), channel_id=1, source_target_pairs={{2,6},{3,7}} | collective-permute-start | bytes 5898248 | tf_op jit(solution)/shard_map/cond/branch_1_fun/ppermute | solution.py:664
  100.2 8.3 %collective-permute-start.18 = (bf16[3,1024,256]{2,1,0:T(8,128)(2,1)S(1)}, bf16[3,1024,256]{2,1,0:T(8,128)(2,1)S(1)}, u32[]{:S(2)}, u32[]{:S(2)}) collective-permute-start(bf16[3,1024,256]{2,1,0:T(8,128)(2,1)S(1)} %constant_dynamic-slice_fusion.5), channel_id=1, source_target_pairs={{0,1},{1,0},{2,3},{3,2},{4,5},{5,4},{6,7},{7,6}} | collective-permute-start | bytes 4718600 | tf_op jit(solution)/shard_map/cond/branch_1_fun/ppermute | solution.py:732
  106.4 5.1 collective-permute-start.20
  108.5 67.4 %collective-permute-start.23 = (bf16[44,32,512]{2,1,0:T(8,128)(2,1)}, bf16[44,32,512]{2,1,0:T(8,128)(2,1)S(1)}, u32[]{:S(2)}, u32[]{:S(2)}) collective-permute-start(bf16[44,32,512]{2,1,0:T(8,128)(2,1)} %get-tuple-element.591), channel_id=1, source_target_pairs={{0,2},{1,3},{2,4},{3,5},{4,6},{5,7}} | collective-permute-start | bytes 4325384 | tf_op jit(solution)/shard_map/cond/branch_1_fun/ppermute | solution.py:664
  111.5 109.9 %collective-permute-start.24 = (bf16[60,32,512]{2,1,0:T(8,128)(2,1)}, bf16[60,32,512]{2,1,0:T(8,128)(2,1)}, u32[]{:S(2)}, u32[]{:S(2)}) collective-permute-start(bf16[60,32,512]{2,1,0:T(8,128)(2,1)} %get-tuple-element.592), channel_id=1, source_target_pairs={{0,2},{1,3},{4,6},{5,7}} | collective-permute-start | bytes 5898248 | tf_op jit(solution)/shard_map/cond/branch_1_fun/ppermute | solution.py:664
  148.5 72.9 %collective-permute-start.26 = (bf16[60,32,512]{2,1,0:T(8,128)(2,1)}, bf16[60,32,512]{2,1,0:T(8,128)(2,1)}, u32[]{:S(2)}, u32[]{:S(2)}) collective-permute-start(bf16[60,32,512]{2,1,0:T(8,128)(2,1)} %collective-permute-done.25), channel_id=1, source_target_pairs={{6,4},{7,5}} | collective-permute-start | bytes 5898248 | tf_op jit(solution)/shard_map/cond/branch_1_fun/ppermute | solution.py:664
  175.8 45.5 %collective-permute-start.29 = (bf16[36,32,512]{2,1,0:T(8,128)(2,1)}, bf16[36,32,512]{2,1,0:T(8,128)(2,1)S(1)}, u32[]{:S(2)}, u32[]{:S(2)}) collective-permute-start(bf16[36,32,512]{2,1,0:T(8,128)(2,1)} %get-tuple-element.595), channel_id=1, source_target_pairs={{0,4},{1,5},{2,6},{3,7}} | collective-permute-start | bytes 3538952 | tf_op jit(solution)/shard_map/cond/branch_1_fun/ppermute | solution.py:664
  180.7 40.7 %collective-permute-start.32 = (bf16[18,32,512]{2,1,0:T(8,128)(2,1)}, bf16[18,32,512]{2,1,0:T(8,128)(2,1)S(1)}, u32[]{:S(2)}, u32[]{:S(2)}) collective-permute-start(bf16[18,32,512]{2,1,0:T(8,128)(2,1)} %get-tuple-element.598), channel_id=1, source_target_pairs={{0,6},{1,7}} | collective-permute-start | bytes 1769480 | tf_op jit(solution)/shard_map/cond/branch_1_fun/ppermute | solution.py:664
  262.3 143.8 %collective-permute-start.38 = (f32[34,32,512]{2,1,0:T(8,128)}, f32[34,32,512]{2,1,0:T(8,128)}, u32[]{:S(2)}, u32[]{:S(2)}) collective-permute-start(f32[34,32,512]{2,1,0:T(8,128)} %get-tuple-element.642), channel_id=1, source_target_pairs={{4,0},{5,1}} | collective-permute-start | bytes 6684680 | tf_op jit(solution)/shard_map/cond/branch_1_fun/ppermute | solution.py:664
  264.4 143.1 %collective-permute-start.35 = (f32[34,32,512]{2,1,0:T(8,128)S(1)}, f32[34,32,512]{2,1,0:T(8,128)}, u32[]{:S(2)}, u32[]{:S(2)}) collective-permute-start(f32[34,32,512]{2,1,0:T(8,128)S(1)} %copy-done.22), channel_id=1, source_target_pairs={{4,0},{5,1}} | collective-permute-start | bytes 6684680 | tf_op jit(solution)/shard_map/cond/branch_1_fun/ppermute | solution.py:664
  266.4 36.2 %collective-permute-start.33 = (f32[14,32,512]{2,1,0:T(8,128)}, f32[14,32,512]{2,1,0:T(8,128)S(1)}, u32[]{:S(2)}, u32[]{:S(2)}) collective-permute-start(f32[14,32,512]{2,1,0:T(8,128)} %get-tuple-element.640), channel_id=1, source_target_pairs={{2,0},{3,1},{4,2},{5,3},{6,4},{7,5}} | collective-permute-start | bytes 2752520 | tf_op jit(solution)/shard_map/cond/branch_1_fun/ppermute | solution.py:664
  268.3 32.8 %collective-permute-start.40 = (f32[10,32,512]{2,1,0:T(8,128)}, f32[10,32,512]{2,1,0:T(8,128)S(1)}, u32[]{:S(2)}, u32[]{:S(2)}) collective-permute-start(f32[10,32,512]{2,1,0:T(8,128)} %get-tuple-element.643), channel_id=1, source_target_pairs={{4,0},{5,1},{6,2},{7,3}} | collective-permute-start | bytes 1966088 | tf_op jit(solution)/shard_map/cond/branch_1_fun/ppermute | solution.py:664
  270.4 138.4 %collective-permute-start.41 = (f32[22,32,512]{2,1,0:T(8,128)}, f32[22,32,512]{2,1,0:T(8,128)S(1)}, u32[]{:S(2)}, u32[]{:S(2)}) collective-permute-start(f32[22,32,512]{2,1,0:T(8,128)} %get-tuple-element.644), channel_id=1, source_target_pairs={{4,0},{5,1},{6,2},{7,3}} | collective-permute-start | bytes 4325384 | tf_op jit(solution)/shard_map/cond/branch_1_fun/ppermute | solution.py:664
  302.0 101.5 %collective-permute-start.45 = (f32[12,32,512]{2,1,0:T(8,128)}, f32[12,32,512]{2,1,0:T(8,128)S(1)}, u32[]{:S(2)}, u32[]{:S(2)}) collective-permute-start(f32[12,32,512]{2,1,0:T(8,128)} %get-tuple-element.648), channel_id=1, source_target_pairs={{6,0},{7,1}} | collective-permute-start | bytes 2359304 | tf_op jit(solution)/shard_map/cond/branch_1_fun/ppermute | solution.py:664
  303.4 145.1 %collective-permute-start.37 = (f32[34,32,512]{2,1,0:T(8,128)}, f32[34,32,512]{2,1,0:T(8,128)}, u32[]{:S(2)}, u32[]{:S(2)}) collective-permute-start(f32[34,32,512]{2,1,0:T(8,128)} %get-tuple-element.642), channel_id=1, source_target_pairs={{2,0},{3,1},{6,4},{7,5}} | collective-permute-start | bytes 6684680 | tf_op jit(solution)/shard_map/cond/branch_1_fun/ppermute | solution.py:664
  403.5 92.7 %collective-permute-start.34 = (f32[34,32,512]{2,1,0:T(8,128)S(1)}, f32[34,32,512]{2,1,0:T(8,128)}, u32[]{:S(2)}, u32[]{:S(2)}) collective-permute-start(f32[34,32,512]{2,1,0:T(8,128)S(1)} %copy-done.22), channel_id=1, source_target_pairs={{2,0},{3,1},{6,4},{7,5}} | collective-permute-start | bytes 6684680 | tf_op jit(solution)/shard_map/cond/branch_1_fun/ppermute | solution.py:664
  406.2 90.0 %collective-permute-start.39 = (f32[34,32,512]{2,1,0:T(8,128)}, f32[34,32,512]{2,1,0:T(8,128)}, u32[]{:S(2)}, u32[]{:S(2)}) collective-permute-start(f32[34,32,512]{2,1,0:T(8,128)} %collective-permute-done.38), channel_id=1, source_target_pairs={{0,2},{1,3}} | collective-permute-start | bytes 6684680 | tf_op jit(solution)/shard_map/cond/branch_1_fun/ppermute | solution.py:664
  407.5 96.7 %collective-permute-start.36 = (f32[34,32,512]{2,1,0:T(8,128)}, f32[34,32,512]{2,1,0:T(8,128)}, u32[]{:S(2)}, u32[]{:S(2)}) collective-permute-start(f32[34,32,512]{2,1,0:T(8,128)} %collective-permute-done.35), channel_id=1, source_target_pairs={{0,2},{1,3}} | collective-permute-start | bytes 6684680 | tf_op jit(solution)/shard_map/cond/branch_1_fun/ppermute | solution.py:664
  408.8 36.2 %collective-permute-start.42 = (f32[24,32,512]{2,1,0:T(8,128)}, f32[24,32,512]{2,1,0:T(8,128)}, u32[]{:S(2)}, u32[]{:S(2)}) collective-permute-start(f32[24,32,512]{2,1,0:T(8,128)} %get-tuple-element.645), channel_id=1, source_target_pairs={{4,0},{5,1},{6,2},{7,3}} | collective-permute-start | bytes 4718600 | tf_op jit(solution)/shard_map/cond/branch_1_fun/ppermute | solution.py:664
  504.2 91.8 %collective-permute-start.6 = (bf16[16,1024,256]{2,1,0:T(8,128)(2,1)}, bf16[16,1024,256]{2,1,0:T(8,128)(2,1)}, u32[]{:S(2)}, u32[]{:S(2)}) collective-permute-start(bf16[16,1024,256]{2,1,0:T(8,128)(2,1)} %get-tuple-element.528), channel_id=1, source_target_pairs={{0,1},{1,0},{2,3},{3,2},{4,5},{5,4},{6,7},{7,6}} | collective-permute-start | bytes 25165832 | tf_op jit(solution)/shard_map/cond/branch_1_fun/cond/branch_1_fun/ppermute | solution.py:723
  507.0 97.3 %collective-permute-start.7 = (bf16[16,1024,256]{2,1,0:T(8,128)(2,1)}, bf16[16,1024,256]{2,1,0:T(8,128)(2,1)}, u32[]{:S(2)}, u32[]{:S(2)}) collective-permute-start(bf16[16,1024,256]{2,1,0:T(8,128)(2,1)} %get-tuple-element.531), channel_id=1, source_target_pairs={{0,1},{1,0},{2,3},{3,2},{4,5},{5,4},{6,7},{7,6}} | collective-permute-start | bytes 25165832 | tf_op jit(solution)/shard_map/cond/branch_1_fun/cond/branch_1_fun/ppermute | solution.py:723
  509.9 74.5 %collective-permute-start.8 = (f32[28,32,512]{2,1,0:T(8,128)}, f32[28,32,512]{2,1,0:T(8,128)}, u32[]{:S(2)}, u32[]{:S(2)}) collective-permute-start(f32[28,32,512]{2,1,0:T(8,128)} %slice.39), channel_id=1, source_target_pairs={{2,0},{3,1},{4,2},{5,3},{6,4},{7,5}} | collective-permute-start | bytes 5505032 | tf_op jit(solution)/shard_map/cond/branch_1_fun/cond/branch_1_fun/ppermute | solution.py:664
  514.5 70.0 %collective-permute-start.9 = (f32[21,32,512]{2,1,0:T(8,128)}, f32[21,32,512]{2,1,0:T(8,128)}, u32[]{:S(2)}, u32[]{:S(2)}) collective-permute-start(f32[21,32,512]{2,1,0:T(8,128)} %slice.40), channel_id=1, source_target_pairs={{4,0},{5,1},{6,2},{7,3}} | collective-permute-start | bytes 4128776 | tf_op jit(solution)/shard_map/cond/branch_1_fun/cond/branch_1_fun/ppermute | solution.py:664
  518.0 13.3 %collective-permute-start.10 = (f32[15,32,512]{2,1,0:T(8,128)}, f32[15,32,512]{2,1,0:T(8,128)}, u32[]{:S(2)}, u32[]{:S(2)}) collective-permute-start(f32[15,32,512]{2,1,0:T(8,128)} %slice.41), channel_id=1, source_target_pairs={{6,0},{7,1}} | collective-permute-start | bytes 2949128 | tf_op jit(solution)/shard_map/cond/branch_1_fun/cond/branch_1_fun/ppermute | solution.py:664
  588.7 4.5 collective-permute-start.11
  (30 other events, 1059.4 us)

commit v6 on v5

--- a/solution.py
+++ b/solution.py
@@ -15,18 +15,17 @@
 NCH = 4
 
 FAST = (
-    ((22, 44, 60), (18, 34, 36), (12, 20, 18)),
-    ((14, 34, 34, 42), (10, 22, 24, 32), (4, 10, 12, 24)),
-    (3, 8, 13, 16),
+    ((28, 34, 34, 30), (22, 24, 22, 18), (14, 14, 12, 10)),
+    ((22, 32, 34, 36), (14, 22, 24, 30), (8, 10, 12, 20)),
+    (4, 8, 12, 16),
 )
-LEVELS = ((22, 15, 9), (28, 21, 15), (42, 32, 24))
-RELAY_F = (2,)
+RELAY_F = ()
 RELAY_B = (1, 2)
-QA = 3
+QA = 4
 SLOW_SEQS = 4
 SLOW = (((8 * SLOW_SEQS,),) * 3,) * 2 + ((NS,),)
 
-CNT, OFF, DM, ST, SG, CE, FIT, LEVEL, SPLIT = 0, 336, 672, 704, 712, 840, 844, 845, 846
+CNT, OFF, DM, ST, SG, CE, FIT, SPLIT = 0, 336, 672, 704, 712, 840, 844, 845
 NTAB = 848
 
 
@@ -92,7 +91,6 @@
             tab[DM + s * 2 + h] = (need + 255) >> 8
 
     fit = jnp.bool_(True)
-    last = [zero] * 3
     for col in range(2):
         row0 = jnp.where(e == 0, col, 1 - col) * NS
         for cc in range(NCH):
@@ -129,18 +127,11 @@
                 if col == 0:
                     tab[sg(cc, d, 0)] = sent
                 for v in range(n_t):
-                    if v == n_t - 1:
-                        last[d] = jnp.maximum(last[d], off[d] - sent)
                     sent = jnp.minimum(sent + b_cap[d][v], avail[v][d])
                     if col == 0:
                         tab[sg(cc, d, v + 1)] = sent
                 fit = fit & (sent == off[d])
     tab[FIT] = jnp.where(fit, 1, 0)
-    level = zero
-    for size in LEVELS[:-1]:
-        over = (last[0] > size[0]) | (last[1] > size[1]) | (last[2] > size[2])
-        level = level + jnp.where(over, 1, 0)
-    tab[LEVEL] = level
     done = zero
     for s in range(NS):
         ok = jnp.bool_(True)
@@ -296,7 +287,7 @@
 
             @pl.when(ss >= QA)
             def _():
-                for copy in mate_inputs((q_mates[1], g_mates[1]), ss - QA, sl):
+                for copy in mate_inputs((q_mates[1], g_mates[1]), e * NS + ss, sl):
                     copy.start()
         for d in range(3):
             cnt = tab[at(CNT, c, d, ss)]
@@ -731,6 +722,9 @@
         def swap_part(x, lo, n):
             return lax.ppermute(lax.dynamic_slice_in_dim(x, other + lo, n, 0), 'cp', swap)
 
+        def swap_all(x):
+            return lax.ppermute(x, 'cp', swap)
+
         tab = tables(FAST, jnp.int32(0), jnp.int32(NS))
 
         def fast():
@@ -748,15 +742,13 @@
                     else:
                         frecv[d][t] = (forward_hop(x, d),)
             mates = [(swap_part(q3, 0, QA), swap_part(g3, 0, QA)),
-                     (swap_part(q3, QA, NS - QA), swap_part(g3, QA, NS - QA))]
+                     (swap_all(q3), swap_all(g3))]
             state = None
-            brecv = [[None] * (n_t - 1) for _ in range(3)]
+            brecv = [[None] * n_t for _ in range(3)]
             for t in range(n_t):
                 live = n_t - t
                 outs = attend(FAST, t, tab, mates, kvcol, frecv, state)
                 state = list(outs[:5]) + [outs[5 + d * live + k] for d in range(3) for k in range(1, live)]
-                if t == n_t - 1:
-                    break
                 for d in range(3):
                     x = outs[5 + d * live]
                     if d == 0 and t in RELAY_B:
@@ -766,22 +758,11 @@
                     else:
                         brecv[d][t] = (backward_hop(x, d),)
             o_all, o_send, dq_all, dq_send, acc = state
-            last = outs[5:]
-
-            def tail(k):
-                def run():
-                    got = []
-                    for d in range(3):
-                        got.append((backward_hop(last[d][:LEVELS[k][d]], d),))
-                    attn_out = place(o_all, o_send)
-                    grad_query = place(dq_all, dq_send)
-                    grads = finish(1, tab, acc, brecv, None)
-                    grads = finish(2, tab, acc, [row + [x] for row, x in zip(brecv, got)], grads)
-                    return (attn_out, grad_query) + place_kv(*grads)
-
-                return run
-
-            return lax.switch(tab[LEVEL], [tail(k) for k in range(len(LEVELS))])
+            attn_out = place(o_all, o_send)
+            grad_query = place(dq_all, dq_send)
+            grads = finish(1, tab, acc, [row[:-1] for row in brecv], None)
+            grads = finish(2, tab, acc, brecv, grads)
+            return (attn_out, grad_query) + place_kv(*grads)
 
         def slow():
             mates = [(swap_part(q3, 0, NS), swap_part(g3, 0, NS))]

time: 620 us -> 554 us (0.89)
  waiting for transfers between devices: 234 us -> 199 us
  local copies, waits for them, and re-layouts: 47.7 us -> 24 us
  starting transfers between devices: 154 us -> 147 us
    ppermute x27 -> x28, waiting for transfers between devices: 229 us -> 195 us  [chip_hop(): lax.ppermute(x, 'cp', [(2 * a + k, 2 * b + k) for a, b in moves for k in...]
    dynamic_slice x4 -> x2, local copies, waits for them, and re-layouts: 16.4 us -> 3.46 us  [swap_part(): lax.dynamic_slice_in_dim(x, other + lo, n, 0)]
    slice x4 -> x0, local copies, waits for them, and re-layouts: 8.4 us -> none  [the longest x3 7.82 us: run(): got.append((backward_hop(last[d][:LEVELS[k][d]], d),))]
    ppermute x27 -> x28, starting transfers between devices: 145 us -> 138 us  [chip_hop(): lax.ppermute(x, 'cp', [(2 * a + k, 2 * b + k) for a, b in moves for k in...]
  transfers between devices with their start and end apart: 35 -> 36, of which waited for: 12 -> 8; matrix products, arithmetic and copies ran while one was open for 5% -> 3% of each run, Pallas kernels for 20% -> 30%
where the time goes in v6:
time: 554 us; the launch traced here: 548 us
  waiting for transfers between devices  199 us (36%)
  Pallas kernels  164 us (30%)
  starting transfers between devices  147 us (27%)
  local copies, waits for them, and re-layouts  24 us (4%)
  loops' own time  8.58 us (2%)
    ppermute x28, waiting for transfers between devices, chip_hop(): lax.ppermute(x, 'cp', [(2 * a + k, 2 * b + k) for a, b in moves for k in...  195 us
    ppermute x28, starting transfers between devices, chip_hop(): lax.ppermute(x, 'cp', [(2 * a + k, 2 * b + k) for a, b in moves for k in...  138 us
    pallas_call x4, Pallas kernels, attend(): pl.pallas_call(functools.partial(compute_kernel, t, n_t, n_got, [bounds(c...  131 us
    pallas_call x2, Pallas kernels, finish(): pl.pallas_call(functools.partial(finish_kernel, part, n_t, [len(way) for...  16 us
    dynamic_update_slice x2, local copies, waits for them, and re-layouts, place(): return lax.dynamic_update_slice_in_dim(mine, got, other, 0)  15.8 us
  transfers between devices with their start and end apart: 36, of which 8 were waited for; matrix products, arithmetic and copies ran while one was open for 3% of the time, Pallas kernels for 30%

profile of v6, /device:TPU:3, one launch (start us, length us, event | category | flops | bytes accessed | tf_op | source)
XLA Modules:
  0.0 548.3 jit_solution(10341852032152792285)
XLA Ops:
  4.6 7.7 %docs.1 = (s32[8,32,128]{2,1,0:T(8,128)S(1)}, s32[32,128]{1,0:T(8,128)S(1)}) custom-call(s32[32,128]{1,0:T(8,128)} %doc.1), custom_call_target="tpu_custom_call" | custom-call | tf_op jit(solution)/shard_map/docs/pallas_call | solution.py:619
  12.9 3.5 tables.2
  17.7 529.5 %conditional.1 = (bf16[32,128,8,256]{3,2,1,0:T(8,128)(2,1)}, bf16[32,128,8,256]{3,2,1,0:T(8,128)(2,1)}, bf16[32,128,1,256]{3,1,2,0:T(8,128)(2,1)}, bf16[32,128,1,256]{3,1,2,0:T(8,128)(2,1)}) conditional(s32[]{:T(128)} %bitcast.24, (s32[]{:T(128)}, bf16[32,1024,256]{2,1,0:T(8,128)(2,1)}, bf16[32,1024,256]{2,1,0:T(8,128)(2,1)}, s32[]{:T(128)}, ...), branch_computations={%region_0.0_spmd, %region_3.0_spmd} | conditional | flops 60000002048 | bytes 633491712 | solution.py:788
  26.0 6.3 %pack.6 = (bf16[16,8,32,512]{3,2,1,0:T(8,128)(2,1)}, bf16[28,32,512]{2,1,0:T(8,128)(2,1)}, bf16[34,32,512]{2,1,0:T(8,128)(2,1)}, bf16[34,32,512]{2,1,0:T(8,128)(...) custom-call(s32[848]{0:T(1024)S(1)} %get-tuple-element.366.tab, ...), custom_call_target="tpu_custom_call" | custom-call | tf_op jit(solution)/shard_map/cond/branch_1_fun/pack/pallas_call | solution.py:642
  38.8 17.8 %collective-permute-start.8 = (bf16[22,32,512]{2,1,0:T(8,128)(2,1)S(1)}, bf16[22,32,512]{2,1,0:T(8,128)(2,1)S(1)}, u32[]{:S(2)}, u32[]{:S(2)}) collective-permute-start(bf16[22,32,512]{2,1,0:T(8,128)(2,1)S(1)} %copy-done.36), channel_id=1, source_target_pairs={{0,4},{1,5},{2,6},{3,7}} | collective-permute-start | bytes 2162696 | tf_op jit(solution)/shard_map/cond/branch_1_fun/ppermute | solution.py:655
  56.5 14.2 %collective-permute-done.8.rest_3_.rest_6_.rest_7_.rest_8_ = bf16[22,32,512]{2,1,0:T(8,128)(2,1)S(1)} collective-permute-done((bf16[22,32,512]{2,1,0:T(8,128)(2,1)S(1)}, bf16[22,32,512]{2,1,0:T(8,128)(2,1)S(1)}, u32[]{:S(2)}, u32[]{:S(2)}) %collective-permute-start.8) | collective-permute-done | bytes 720928 | tf_op jit(solution)/shard_map/cond/branch_1_fun/ppermute | solution.py:655
  70.7 1.9 collective-permute-start.4
  72.6 19.8 %collective-permute-done.4.rest_2_.rest_4_ = bf16[28,32,512]{2,1,0:T(8,128)(2,1)S(1)} collective-permute-done((bf16[28,32,512]{2,1,0:T(8,128)(2,1)S(1)}, bf16[28,32,512]{2,1,0:T(8,128)(2,1)S(1)}, u32[]{:S(2)}, u32[]{:S(2)}) %collective-permute-start.4) | collective-permute-done | bytes 917536 | tf_op jit(solution)/shard_map/cond/branch_1_fun/ppermute | solution.py:655
  93.8 4.9 collective-permute-start.9
  98.7 1.9 collective-permute-start.5
  100.7 32.9 %branch_1_fun.6 = (bf16[32,1024,256]{2,1,0:T(8,128)(2,1)}, bf16[16,1024,256]{2,1,0:T(8,128)(2,1)}, bf16[32,1024,256]{2,1,0:T(8,128)(2,1)}, bf16[16,1024,256]{2,1...) custom-call(s32[848]{0:T(1024)} %copy-done.29, ...), custom_call_target="tpu_custom_call" | custom-call | flops 15000000512 | bytes 25000000 | tf_op jit(solution)/shard_map/cond/branch_1_fun/pallas_call | solution.py:673
  134.3 6.7 %collective-permute-start.11 = (bf16[18,32,512]{2,1,0:T(8,128)(2,1)}, bf16[18,32,512]{2,1,0:T(8,128)(2,1)S(1)}, u32[]{:S(2)}, u32[]{:S(2)}) collective-permute-start(bf16[18,32,512]{2,1,0:T(8,128)(2,1)} %get-tuple-element.382), channel_id=1, source_target_pairs={{0,4},{1,5},{2,6},{3,7}} | collective-permute-start | bytes 1769480 | tf_op jit(solution)/shard_map/cond/branch_1_fun/ppermute | solution.py:655
  142.5 3.1 collective-permute-start.6
  145.6 2.3 collective-permute-start.18
  148.0 33.1 %branch_1_fun.7 = (bf16[32,1024,256]{2,1,0:T(8,128)(2,1)}, bf16[16,1024,256]{2,1,0:T(8,128)(2,1)}, bf16[32,1024,256]{2,1,0:T(8,128)(2,1)}, bf16[16,1024,256]{2,1...) custom-call(s32[848]{0:T(1024)} %copy-done.29, ...), custom_call_target="tpu_custom_call", output_to_operand_aliasing={{0}: (15, {}), {1}: (16, {}), {2}: (17, {}), {3}: (18, {}),... | custom-call | flops 15000000512 | bytes 25000000 | tf_op jit(solution)/shard_map/cond/branch_1_fun/pallas_call | solution.py:673
  181.1 12.8 %collective-permute-start.7 = (bf16[30,32,512]{2,1,0:T(8,128)(2,1)}, bf16[30,32,512]{2,1,0:T(8,128)(2,1)}, u32[]{:S(2)}, u32[]{:S(2)}) collective-permute-start(bf16[30,32,512]{2,1,0:T(8,128)(2,1)} %get-tuple-element.378), channel_id=1, source_target_pairs={{0,2},{1,3},{2,4},{3,5},{4,6},{5,7}} | collective-permute-start | bytes 2949128 | tf_op jit(solution)/shard_map/cond/branch_1_fun/ppermute | solution.py:655
  197.7 32.5 %branch_1_fun.8 = (bf16[32,1024,256]{2,1,0:T(8,128)(2,1)}, bf16[16,1024,256]{2,1,0:T(8,128)(2,1)}, bf16[32,1024,256]{2,1,0:T(8,128)(2,1)}, bf16[16,1024,256]{2,1...) custom-call(s32[848]{0:T(1024)S(1)} %copy-done.30, ...), custom_call_target="tpu_custom_call", output_to_operand_aliasing={{0}: (18, {}), {1}: (19, {}), {2}: (20, {}), {3}: (21, {}),... | custom-call | flops 15000000512 | bytes 25000000 | tf_op jit(solution)/shard_map/cond/branch_1_fun/pallas_call | solution.py:673
  230.3 2.0 collective-permute-start.20
  238.7 32.3 %branch_1_fun.9 = (bf16[32,1024,256]{2,1,0:T(8,128)(2,1)}, bf16[16,1024,256]{2,1,0:T(8,128)(2,1)}, bf16[32,1024,256]{2,1,0:T(8,128)(2,1)}, bf16[16,1024,256]{2,1...) custom-call(s32[848]{0:T(1024)S(1)} %copy-done.30, ...), custom_call_target="tpu_custom_call", output_to_operand_aliasing={{0}: (21, {}), {1}: (22, {}), {2}: (23, {}), {3}: (24, {}),... | custom-call | flops 15000000512 | bytes 25000000 | tf_op jit(solution)/shard_map/cond/branch_1_fun/pallas_call | solution.py:673
  271.0 3.2 collective-permute-done.27.rest_6_.rest_7_
  275.1 32.8 %collective-permute-done.28.rest_7_.rest_8_ = f32[24,32,512]{2,1,0:T(8,128)S(1)} collective-permute-done((f32[24,32,512]{2,1,0:T(8,128)}, f32[24,32,512]{2,1,0:T(8,128)S(1)}, u32[]{:S(2)}, u32[]{:S(2)}) %collective-permute-start.28) | collective-permute-done | bytes 1572896 | tf_op jit(solution)/shard_map/cond/branch_1_fun/ppermute | solution.py:655
  307.9 7.3 %collective-permute-start.17 = (bf16[16,1024,256]{2,1,0:T(8,128)(2,1)}, bf16[16,1024,256]{2,1,0:T(8,128)(2,1)}, u32[]{:S(2)}, u32[]{:S(2)}) collective-permute-start(bf16[16,1024,256]{2,1,0:T(8,128)(2,1)} %get-tuple-element.423), channel_id=1, source_target_pairs={{0,1},{1,0},{2,3},{3,2},{4,5},{5,4},{6,7},{7,6}} | collective-permute-start | bytes 25165832 | tf_op jit(solution)/shard_map/cond/branch_1_fun/ppermute | solution.py:714
  315.2 59.3 %collective-permute-start.22 = (f32[34,32,512]{2,1,0:T(8,128)S(1)}, f32[34,32,512]{2,1,0:T(8,128)S(1)}, u32[]{:S(2)}, u32[]{:S(2)}) collective-permute-start(f32[34,32,512]{2,1,0:T(8,128)S(1)} %copy-done.9), channel_id=1, source_target_pairs={{2,0},{3,1},{6,4},{7,5}} | collective-permute-start | bytes 6684680 | tf_op jit(solution)/shard_map/cond/branch_1_fun/ppermute | solution.py:655
  377.1 45.0 %collective-permute-done.22.rest_3_ = f32[34,32,512]{2,1,0:T(8,128)S(1)} collective-permute-done((f32[34,32,512]{2,1,0:T(8,128)S(1)}, f32[34,32,512]{2,1,0:T(8,128)S(1)}, u32[]{:S(2)}, u32[]{:S(2)}) %collective-permute-start.22) | collective-permute-done | bytes 2228256 | tf_op jit(solution)/shard_map/cond/branch_1_fun/ppermute | solution.py:655
  422.1 4.1 collective-permute-start.25
  427.5 43.8 %collective-permute-done.24.rest_4_ = f32[34,32,512]{2,1,0:T(8,128)S(1)} collective-permute-done((f32[34,32,512]{2,1,0:T(8,128)S(1)}, f32[34,32,512]{2,1,0:T(8,128)S(1)}, u32[]{:S(2)}, u32[]{:S(2)}) %collective-permute-start.24) | collective-permute-done | bytes 2228256 | tf_op jit(solution)/shard_map/cond/branch_1_fun/ppermute | solution.py:655
  473.3 11.0 %branch_1_fun.10 = (bf16[32,128,256]{2,1,0:T(8,128)(2,1)}, bf16[32,128,256]{2,1,0:T(8,128)(2,1)S(1)}, bf16[16,128,512]{2,1,0:T(8,128)(2,1)}) custom-call(s32[848]{0:T(1024)S(1)} %copy-done.30, f32[16,8,32,512]{3,2,1,0:T(8,128)} %get-tuple-element.424.acc, f32[22,32,512]{2,1,0:T(8,128)} %copy-done.17, f32[32,32,512]{2,1,0:T(8,128)} %copy-done.12, ...), custom_call_target="tpu_custom_call" | custom-call | tf_op jit(solution)/shard_map/cond/branch_1_fun/pallas_call | solution.py:700
  484.3 36.2 %collective-permute-done.29.rest_9_ = f32[30,32,512]{2,1,0:T(8,128)} collective-permute-done((f32[30,32,512]{2,1,0:T(8,128)}, f32[30,32,512]{2,1,0:T(8,128)}, u32[]{:S(2)}, u32[]{:S(2)}) %collective-permute-start.29) | collective-permute-done | bytes 1966112 | tf_op jit(solution)/shard_map/cond/branch_1_fun/ppermute | solution.py:655
  520.5 5.0 branch_1_fun.11
  525.6 4.4 collective-permute-done.34
  531.2 8.3 %constant_dynamic-update-slice_fusion.3 = bf16[32,1024,256]{2,1,0:T(8,128)(2,1)} fusion(bf16[32,1024,256]{2,1,0:T(8,128)(2,1)} %get-tuple-element.420, bf16[16,1024,256]{2,1,0:T(8,128)(2,1)} %collective-permute-done.16, s32[]{:T(128)S(6)} %select_n.1), kind=kLoop, calls=%fused_computation.14 | loop fusion | bytes 16777220 | tf_op jit(solution)/shard_map/cond/branch_1_fun/dynamic_update_slice | solution.py:715
  539.4 7.5 %constant_dynamic-update-slice_fusion.2 = bf16[32,1024,256]{2,1,0:T(8,128)(2,1)} fusion(bf16[32,1024,256]{2,1,0:T(8,128)(2,1)} %get-tuple-element.422, bf16[16,1024,256]{2,1,0:T(8,128)(2,1)} %collective-permute-done.17, s32[]{:T(128)S(6)} %select_n.1), kind=kLoop, calls=%fused_computation.13 | loop fusion | bytes 16777220 | tf_op jit(solution)/shard_map/cond/branch_1_fun/dynamic_update_slice | solution.py:715
  (117 shorter events, 33.6 us)
Async XLA Ops:
  3.9 13.8 %collective-permute-start.46 = (bf16[16,128,512]{2,1,0:T(8,128)(2,1)}, bf16[16,128,512]{2,1,0:T(8,128)(2,1)S(1)}, u32[]{:S(2)}, u32[]{:S(2)}) collective-permute-start(bf16[16,128,512]{2,1,0:T(8,128)(2,1)} %pad_maximum_fusion), channel_id=1, source_target_pairs={{0,1},{1,0},{2,3},{3,2},{4,5},{5,4},{6,7},{7,6}} | collective-permute-start | bytes 6291464 | tf_op jit(solution)/shard_map/ppermute | solution.py:618
  25.4 117.0 %collective-permute-start.1 = (bf16[32,1024,256]{2,1,0:T(8,128)(2,1)}, bf16[32,1024,256]{2,1,0:T(8,128)(2,1)}, u32[]{:S(2)}, u32[]{:S(2)}) collective-permute-start(bf16[32,1024,256]{2,1,0:T(8,128)(2,1)} %get-tuple-element.368.q_all), channel_id=1, source_target_pairs={{0,1},{1,0},{2,3},{3,2},{4,5},{5,4},{6,7},{7,6}} | collective-permute-start | bytes 50331656 | tf_op jit(solution)/shard_map/cond/branch_1_fun/ppermute | solution.py:726
  25.9 119.7 %collective-permute-start.3 = (bf16[32,1024,256]{2,1,0:T(8,128)(2,1)}, bf16[32,1024,256]{2,1,0:T(8,128)(2,1)}, u32[]{:S(2)}, u32[]{:S(2)}) collective-permute-start(bf16[32,1024,256]{2,1,0:T(8,128)(2,1)} %get-tuple-element.369.g_all), channel_id=1, source_target_pairs={{0,1},{1,0},{2,3},{3,2},{4,5},{5,4},{6,7},{7,6}} | collective-permute-start | bytes 50331656 | tf_op jit(solution)/shard_map/cond/branch_1_fun/ppermute | solution.py:726
  35.6 58.2 %collective-permute-start.2 = (bf16[4,1024,256]{2,1,0:T(8,128)(2,1)S(1)}, bf16[4,1024,256]{2,1,0:T(8,128)(2,1)S(1)}, u32[]{:S(2)}, u32[]{:S(2)}) collective-permute-start(bf16[4,1024,256]{2,1,0:T(8,128)(2,1)S(1)} %constant_dynamic-slice_fusion.2), channel_id=1, source_target_pairs={{0,1},{1,0},{2,3},{3,2},{4,5},{5,4},{6,7},{7,6}} | collective-permute-start | bytes 6291464 | tf_op jit(solution)/shard_map/cond/branch_1_fun/ppermute | solution.py:723
  38.6 60.1 %collective-permute-start = (bf16[4,1024,256]{2,1,0:T(8,128)(2,1)S(1)}, bf16[4,1024,256]{2,1,0:T(8,128)(2,1)S(1)}, u32[]{:S(2)}, u32[]{:S(2)}) collective-permute-start(bf16[4,1024,256]{2,1,0:T(8,128)(2,1)S(1)} %constant_dynamic-slice_fusion.3), channel_id=1, source_target_pairs={{0,1},{1,0},{2,3},{3,2},{4,5},{5,4},{6,7},{7,6}} | collective-permute-start | bytes 6291464 | tf_op jit(solution)/shard_map/cond/branch_1_fun/ppermute | solution.py:723
  38.8 31.9 %collective-permute-start.8 = (bf16[22,32,512]{2,1,0:T(8,128)(2,1)S(1)}, bf16[22,32,512]{2,1,0:T(8,128)(2,1)S(1)}, u32[]{:S(2)}, u32[]{:S(2)}) collective-permute-start(bf16[22,32,512]{2,1,0:T(8,128)(2,1)S(1)} %copy-done.36), channel_id=1, source_target_pairs={{0,4},{1,5},{2,6},{3,7}} | collective-permute-start | bytes 2162696 | tf_op jit(solution)/shard_map/cond/branch_1_fun/ppermute | solution.py:655
  70.7 21.7 %collective-permute-start.4 = (bf16[28,32,512]{2,1,0:T(8,128)(2,1)S(1)}, bf16[28,32,512]{2,1,0:T(8,128)(2,1)S(1)}, u32[]{:S(2)}, u32[]{:S(2)}) collective-permute-start(bf16[28,32,512]{2,1,0:T(8,128)(2,1)S(1)} %copy-done.35), channel_id=1, source_target_pairs={{0,2},{1,3},{2,4},{3,5},{4,6},{5,7}} | collective-permute-start | bytes 2752520 | tf_op jit(solution)/shard_map/cond/branch_1_fun/ppermute | solution.py:655
  92.4 41.2 %collective-permute-start.13 = (bf16[14,32,512]{2,1,0:T(8,128)(2,1)}, bf16[14,32,512]{2,1,0:T(8,128)(2,1)}, u32[]{:S(2)}, u32[]{:S(2)}) collective-permute-start(bf16[14,32,512]{2,1,0:T(8,128)(2,1)} %get-tuple-element.384), channel_id=1, source_target_pairs={{0,6},{1,7}} | collective-permute-start | bytes 1376264 | tf_op jit(solution)/shard_map/cond/branch_1_fun/ppermute | solution.py:655
  93.8 40.5 %collective-permute-start.9 = (bf16[24,32,512]{2,1,0:T(8,128)(2,1)}, bf16[24,32,512]{2,1,0:T(8,128)(2,1)}, u32[]{:S(2)}, u32[]{:S(2)}) collective-permute-start(bf16[24,32,512]{2,1,0:T(8,128)(2,1)} %get-tuple-element.380), channel_id=1, source_target_pairs={{0,4},{1,5},{2,6},{3,7}} | collective-permute-start | bytes 2359304 | tf_op jit(solution)/shard_map/cond/branch_1_fun/ppermute | solution.py:655
  98.7 42.4 %collective-permute-start.5 = (bf16[34,32,512]{2,1,0:T(8,128)(2,1)}, bf16[34,32,512]{2,1,0:T(8,128)(2,1)S(1)}, u32[]{:S(2)}, u32[]{:S(2)}) collective-permute-start(bf16[34,32,512]{2,1,0:T(8,128)(2,1)} %get-tuple-element.376), channel_id=1, source_target_pairs={{0,2},{1,3},{2,4},{3,5},{4,6},{5,7}} | collective-permute-start | bytes 3342344 | tf_op jit(solution)/shard_map/cond/branch_1_fun/ppermute | solution.py:655
  133.6 47.4 %collective-permute-start.14 = (bf16[12,32,512]{2,1,0:T(8,128)(2,1)}, bf16[12,32,512]{2,1,0:T(8,128)(2,1)S(1)}, u32[]{:S(2)}, u32[]{:S(2)}) collective-permute-start(bf16[12,32,512]{2,1,0:T(8,128)(2,1)} %get-tuple-element.385), channel_id=1, source_target_pairs={{0,6},{1,7}} | collective-permute-start | bytes 1179656 | tf_op jit(solution)/shard_map/cond/branch_1_fun/ppermute | solution.py:655
  134.3 59.5 %collective-permute-start.11 = (bf16[18,32,512]{2,1,0:T(8,128)(2,1)}, bf16[18,32,512]{2,1,0:T(8,128)(2,1)S(1)}, u32[]{:S(2)}, u32[]{:S(2)}) collective-permute-start(bf16[18,32,512]{2,1,0:T(8,128)(2,1)} %get-tuple-element.382), channel_id=1, source_target_pairs={{0,4},{1,5},{2,6},{3,7}} | collective-permute-start | bytes 1769480 | tf_op jit(solution)/shard_map/cond/branch_1_fun/ppermute | solution.py:655
  141.1 54.3 %collective-permute-start.10 = (bf16[22,32,512]{2,1,0:T(8,128)(2,1)}, bf16[22,32,512]{2,1,0:T(8,128)(2,1)S(1)}, u32[]{:S(2)}, u32[]{:S(2)}) collective-permute-start(bf16[22,32,512]{2,1,0:T(8,128)(2,1)} %get-tuple-element.381), channel_id=1, source_target_pairs={{0,4},{1,5},{2,6},{3,7}} | collective-permute-start | bytes 2162696 | tf_op jit(solution)/shard_map/cond/branch_1_fun/ppermute | solution.py:655
  142.5 54.2 %collective-permute-start.6 = (bf16[34,32,512]{2,1,0:T(8,128)(2,1)}, bf16[34,32,512]{2,1,0:T(8,128)(2,1)S(1)}, u32[]{:S(2)}, u32[]{:S(2)}) collective-permute-start(bf16[34,32,512]{2,1,0:T(8,128)(2,1)} %get-tuple-element.377), channel_id=1, source_target_pairs={{0,2},{1,3},{2,4},{3,5},{4,6},{5,7}} | collective-permute-start | bytes 3342344 | tf_op jit(solution)/shard_map/cond/branch_1_fun/ppermute | solution.py:655
  145.6 89.7 %collective-permute-start.18 = (f32[22,32,512]{2,1,0:T(8,128)}, f32[22,32,512]{2,1,0:T(8,128)S(1)}, u32[]{:S(2)}, u32[]{:S(2)}) collective-permute-start(f32[22,32,512]{2,1,0:T(8,128)} %get-tuple-element.425), channel_id=1, source_target_pairs={{2,0},{3,1},{4,2},{5,3},{6,4},{7,5}} | collective-permute-start | bytes 4325384 | tf_op jit(solution)/shard_map/cond/branch_1_fun/ppermute | solution.py:655
  181.1 49.2 %collective-permute-start.7 = (bf16[30,32,512]{2,1,0:T(8,128)(2,1)}, bf16[30,32,512]{2,1,0:T(8,128)(2,1)}, u32[]{:S(2)}, u32[]{:S(2)}) collective-permute-start(bf16[30,32,512]{2,1,0:T(8,128)(2,1)} %get-tuple-element.378), channel_id=1, source_target_pairs={{0,2},{1,3},{2,4},{3,5},{4,6},{5,7}} | collective-permute-start | bytes 2949128 | tf_op jit(solution)/shard_map/cond/branch_1_fun/ppermute | solution.py:655
  193.9 38.4 %collective-permute-start.30 = (f32[8,32,512]{2,1,0:T(8,128)S(1)}, f32[8,32,512]{2,1,0:T(8,128)}, u32[]{:S(2)}, u32[]{:S(2)}) collective-permute-start(f32[8,32,512]{2,1,0:T(8,128)S(1)} %copy-done.37), channel_id=1, source_target_pairs={{6,0},{7,1}} | collective-permute-start | bytes 1572872 | tf_op jit(solution)/shard_map/cond/branch_1_fun/ppermute | solution.py:655
  195.4 38.3 %collective-permute-start.26 = (f32[14,32,512]{2,1,0:T(8,128)}, f32[14,32,512]{2,1,0:T(8,128)S(1)}, u32[]{:S(2)}, u32[]{:S(2)}) collective-permute-start(f32[14,32,512]{2,1,0:T(8,128)} %get-tuple-element.429), channel_id=1, source_target_pairs={{4,0},{5,1},{6,2},{7,3}} | collective-permute-start | bytes 2752520 | tf_op jit(solution)/shard_map/cond/branch_1_fun/ppermute | solution.py:655
  196.7 39.8 %collective-permute-start.31 = (f32[10,32,512]{2,1,0:T(8,128)}, f32[10,32,512]{2,1,0:T(8,128)S(1)}, u32[]{:S(2)}, u32[]{:S(2)}) collective-permute-start(f32[10,32,512]{2,1,0:T(8,128)} %get-tuple-element.434), channel_id=1, source_target_pairs={{6,0},{7,1}} | collective-permute-start | bytes 1966088 | tf_op jit(solution)/shard_map/cond/branch_1_fun/ppermute | solution.py:655
  230.3 84.9 %collective-permute-start.20 = (f32[32,32,512]{2,1,0:T(8,128)}, f32[32,32,512]{2,1,0:T(8,128)}, u32[]{:S(2)}, u32[]{:S(2)}) collective-permute-start(f32[32,32,512]{2,1,0:T(8,128)} %get-tuple-element.426), channel_id=1, source_target_pairs={{4,0},{5,1}} | collective-permute-start | bytes 6291464 | tf_op jit(solution)/shard_map/cond/branch_1_fun/ppermute | solution.py:655
  232.3 142.2 %collective-permute-start.19 = (f32[32,32,512]{2,1,0:T(8,128)}, f32[32,32,512]{2,1,0:T(8,128)S(1)}, u32[]{:S(2)}, u32[]{:S(2)}) collective-permute-start(f32[32,32,512]{2,1,0:T(8,128)} %get-tuple-element.426), channel_id=1, source_target_pairs={{2,0},{3,1},{6,4},{7,5}} | collective-permute-start | bytes 6291464 | tf_op jit(solution)/shard_map/cond/branch_1_fun/ppermute | solution.py:655
  233.7 37.3 %collective-permute-start.32 = (f32[12,32,512]{2,1,0:T(8,128)}, f32[12,32,512]{2,1,0:T(8,128)}, u32[]{:S(2)}, u32[]{:S(2)}) collective-permute-start(f32[12,32,512]{2,1,0:T(8,128)} %get-tuple-element.435), channel_id=1, source_target_pairs={{6,0},{7,1}} | collective-permute-start | bytes 2359304 | tf_op jit(solution)/shard_map/cond/branch_1_fun/ppermute | solution.py:655
  235.3 39.0 %collective-permute-start.27 = (f32[22,32,512]{2,1,0:T(8,128)}, f32[22,32,512]{2,1,0:T(8,128)}, u32[]{:S(2)}, u32[]{:S(2)}) collective-permute-start(f32[22,32,512]{2,1,0:T(8,128)} %get-tuple-element.430), channel_id=1, source_target_pairs={{4,0},{5,1},{6,2},{7,3}} | collective-permute-start | bytes 4325384 | tf_op jit(solution)/shard_map/cond/branch_1_fun/ppermute | solution.py:655
  237.4 70.4 %collective-permute-start.28 = (f32[24,32,512]{2,1,0:T(8,128)}, f32[24,32,512]{2,1,0:T(8,128)S(1)}, u32[]{:S(2)}, u32[]{:S(2)}) collective-permute-start(f32[24,32,512]{2,1,0:T(8,128)} %get-tuple-element.431), channel_id=1, source_target_pairs={{4,0},{5,1},{6,2},{7,3}} | collective-permute-start | bytes 4718600 | tf_op jit(solution)/shard_map/cond/branch_1_fun/ppermute | solution.py:655
  271.0 260.1 %collective-permute-start.16 = (bf16[16,1024,256]{2,1,0:T(8,128)(2,1)}, bf16[16,1024,256]{2,1,0:T(8,128)(2,1)}, u32[]{:S(2)}, u32[]{:S(2)}) collective-permute-start(bf16[16,1024,256]{2,1,0:T(8,128)(2,1)} %get-tuple-element.421), channel_id=1, source_target_pairs={{0,1},{1,0},{2,3},{3,2},{4,5},{5,4},{6,7},{7,6}} | collective-permute-start | bytes 25165832 | tf_op jit(solution)/shard_map/cond/branch_1_fun/ppermute | solution.py:714
  274.3 101.6 %collective-permute-start.23 = (f32[34,32,512]{2,1,0:T(8,128)S(1)}, f32[34,32,512]{2,1,0:T(8,128)S(1)}, u32[]{:S(2)}, u32[]{:S(2)}) collective-permute-start(f32[34,32,512]{2,1,0:T(8,128)S(1)} %copy-done.9), channel_id=1, source_target_pairs={{4,0},{5,1}} | collective-permute-start | bytes 6684680 | tf_op jit(solution)/shard_map/cond/branch_1_fun/ppermute | solution.py:655
  307.9 231.6 %collective-permute-start.17 = (bf16[16,1024,256]{2,1,0:T(8,128)(2,1)}, bf16[16,1024,256]{2,1,0:T(8,128)(2,1)}, u32[]{:S(2)}, u32[]{:S(2)}) collective-permute-start(bf16[16,1024,256]{2,1,0:T(8,128)(2,1)} %get-tuple-element.423), channel_id=1, source_target_pairs={{0,1},{1,0},{2,3},{3,2},{4,5},{5,4},{6,7},{7,6}} | collective-permute-start | bytes 25165832 | tf_op jit(solution)/shard_map/cond/branch_1_fun/ppermute | solution.py:714
  315.2 106.9 %collective-permute-start.22 = (f32[34,32,512]{2,1,0:T(8,128)S(1)}, f32[34,32,512]{2,1,0:T(8,128)S(1)}, u32[]{:S(2)}, u32[]{:S(2)}) collective-permute-start(f32[34,32,512]{2,1,0:T(8,128)S(1)} %copy-done.9), channel_id=1, source_target_pairs={{2,0},{3,1},{6,4},{7,5}} | collective-permute-start | bytes 6684680 | tf_op jit(solution)/shard_map/cond/branch_1_fun/ppermute | solution.py:655
  374.5 51.7 %collective-permute-start.21 = (f32[32,32,512]{2,1,0:T(8,128)}, f32[32,32,512]{2,1,0:T(8,128)S(1)}, u32[]{:S(2)}, u32[]{:S(2)}) collective-permute-start(f32[32,32,512]{2,1,0:T(8,128)} %collective-permute-done.20), channel_id=1, source_target_pairs={{0,2},{1,3}} | collective-permute-start | bytes 6291464 | tf_op jit(solution)/shard_map/cond/branch_1_fun/ppermute | solution.py:655
  375.8 95.5 %collective-permute-start.24 = (f32[34,32,512]{2,1,0:T(8,128)S(1)}, f32[34,32,512]{2,1,0:T(8,128)S(1)}, u32[]{:S(2)}, u32[]{:S(2)}) collective-permute-start(f32[34,32,512]{2,1,0:T(8,128)S(1)} %collective-permute-done.23), channel_id=1, source_target_pairs={{0,2},{1,3}} | collective-permute-start | bytes 6684680 | tf_op jit(solution)/shard_map/cond/branch_1_fun/ppermute | solution.py:655
  422.1 98.4 %collective-permute-start.25 = (f32[36,32,512]{2,1,0:T(8,128)}, f32[36,32,512]{2,1,0:T(8,128)}, u32[]{:S(2)}, u32[]{:S(2)}) collective-permute-start(f32[36,32,512]{2,1,0:T(8,128)} %get-tuple-element.428), channel_id=1, source_target_pairs={{2,0},{3,1},{4,2},{5,3},{6,4},{7,5}} | collective-permute-start | bytes 7077896 | tf_op jit(solution)/shard_map/cond/branch_1_fun/ppermute | solution.py:655
  426.2 94.3 %collective-permute-start.29 = (f32[30,32,512]{2,1,0:T(8,128)}, f32[30,32,512]{2,1,0:T(8,128)}, u32[]{:S(2)}, u32[]{:S(2)}) collective-permute-start(f32[30,32,512]{2,1,0:T(8,128)} %get-tuple-element.432), channel_id=1, source_target_pairs={{4,0},{5,1},{6,2},{7,3}} | collective-permute-start | bytes 5898248 | tf_op jit(solution)/shard_map/cond/branch_1_fun/ppermute | solution.py:655
  (33 other events, 782.3 us)

commit v7 on v0

v7 whole, which is shorter than its diff:
```python
import functools

import jax
import jax.numpy as jnp
from jax import lax
from jax.experimental import pallas as pl
from jax.experimental.pallas import tpu as pltpu
from jax.sharding import PartitionSpec as P

NEG_BIG = -1e30
LOG2E = 1.4426950408889634
NS = 16
CH = 2
NJ = NS // CH
AHEAD = 2


def dot_nt(a, b):
    return lax.dot_general(a, b, (((1,), (1,)), ((), ())), preferred_element_type=jnp.float32)


def dot_nn(a, b):
    return lax.dot_general(a, b, (((1,), (0,)), ((), ())), preferred_element_type=jnp.float32)


def dot_tn(a, b):
    return lax.dot_general(a, b, (((0,), (0,)), ((), ())), preferred_element_type=jnp.float32)


def remote(src, dst, send, recv, dev):
    return pltpu.make_async_remote_copy(src_ref=src, dst_ref=dst, send_sem=send, recv_sem=recv,
                                        device_id={'cp': dev}, device_id_type=pl.DeviceIdType.MESH)


def fused_kernel(scale, doc, q, g, k, v, o, dq, dk, dv, qgm, kvr, part, hold,
                 docs, kvs, qg, outb, dkv, tmp, fin, e_scr, dp_scr, p_scr, l_scr, f_scr, t_scr, docr, o_acc,
                 doc_s, doc_r, isem, osem, osend_r, q_s, q_r, kv_s, kv_r, hop_s, part_r, tsem, fsem, dsend_r, lsem, xsem, rel_s):
    rank = lax.axis_index('cp')
    n_dev = docs.shape[0]
    c = rank // 2
    e = lax.rem(rank, 2)
    mate = 2 * c + 1 - e
    other = NS * (1 - e)
    mine = NS * e

    def dev(chip):
        return 2 * chip + e

    docs[rank] = doc[...]

    def doc_copy(i):
        return remote(doc, docs.at[rank], doc_s.at[i], doc_r.at[i], lax.rem(rank + i, n_dev))

    for i in range(1, n_dev):
        doc_copy(i).start()

    def kv_parts(chip, way, j, cols):
        out = []
        for col in cols:
            for which, ref in ((0, k), (1, v)):
                out.append(remote(ref.at[pl.ds(col * NS + CH * j, CH)], kvr.at[c, pl.ds(CH * j, CH), which, pl.ds(128 * e, 128)],
                                  kv_s.at[way, which], kv_r.at[c, j], 2 * chip + col))
        return out

    def send_kv(chip, way, j):
        for copy in kv_parts(chip, way, j, (0, 1)):
            copy.start()

    def kv_forward(a, chip, j):
        return remote(kvr.at[a, pl.ds(CH * j, CH)], kvr.at[a, pl.ds(CH * j, CH)], hop_s, kv_r.at[a, j], dev(chip))

    def stream_kv(j):
        @pl.when(c == 0)
        def _():
            send_kv(1, 0, j)
            send_kv(2, 1, j)

        @pl.when(c == 1)
        def _():
            send_kv(3, 0, j)
            send_kv(0, 1, j)

        @pl.when(c == 2)
        def _():
            send_kv(3, 0, j)

    def to_mate(j):
        for which, ref in ((0, k), (1, v)):
            remote(ref.at[pl.ds(other + CH * j, CH)], kvr.at[c, pl.ds(CH * j, CH), which, pl.ds(128 * e, 128)],
                   kv_s.at[2, which], kv_r.at[c, j], mate).start()

    def rows_to_mate(j):
        for which, ref in ((0, q), (1, g)):
            remote(ref.at[pl.ds(other + CH * j, CH)], qgm.at[pl.ds(CH * j, CH), which], q_s.at[which], q_r.at[j], mate).start()

    stream_kv(0)
    to_mate(0)
    rows_to_mate(0)
    for j in range(1, AHEAD):
        stream_kv(j)
    for j in range(1, NJ):
        to_mate(j)
        rows_to_mate(j)
    for i in range(1, n_dev):
        doc_copy(i).wait()

    def arrive(j):
        remote(kvr.at[c, pl.ds(CH * j, CH), :, pl.ds(0, 128)], kvr.at[c, pl.ds(CH * j, CH), :, pl.ds(0, 128)],
               hop_s, kv_r.at[c, j], mate).wait_recv()
        remote(qgm.at[pl.ds(CH * j, CH)], qgm.at[pl.ds(CH * j, CH)], hop_s, q_r.at[j], mate).wait_recv()
        for a in range(3):
            @pl.when(a < c)
            def _():
                kv_forward(a, a, j).wait_recv()

        @pl.when(c == 1)
        def _():
            kv_forward(0, 3, j).start()

        @pl.when(c == 0)
        def _():
            kv_forward(1, 1, j).wait_recv()
            kv_forward(1, 2, j).start()

        @pl.when(j + AHEAD < NJ)
        def _():
            stream_kv(j + AHEAD)

    def inputs(s, sl):
        row = mine + s
        rows = pl.ds(128 * e, 128)
        rest = pl.ds(128 - 128 * e, 128)
        pairs = [
            (q.at[row], qg.at[sl, 0]), (g.at[row], qg.at[sl, 2]), (qgm.at[s, 0], qg.at[sl, 1]), (qgm.at[s, 1], qg.at[sl, 3]),
            (k.at[row], kvs.at[sl, 0, 0, rows]), (v.at[row], kvs.at[sl, 0, 1, rows]),
            (kvr.at[c, s, :, rest], kvs.at[sl, 0, :, rest]),
        ]
        return [pltpu.make_async_copy(src, dst, isem.at[sl, i]) for i, (src, dst) in enumerate(pairs)]

    def far_input(s, sl, d):
        return pltpu.make_async_copy(kvr.at[c - d, s], kvs.at[sl, d], isem.at[sl, 6 + d])

    def fetch(s, sl):
        for copy in inputs(s, sl):
            copy.start()
        for d in range(1, 4):
            @pl.when(d <= c)
            def _():
                far_input(s, sl, d).start()

    def fetch_wait(s, sl):
        for copy in inputs(s, sl):
            copy.wait()
        for d in range(1, 4):
            @pl.when(d <= c)
            def _():
                far_input(s, sl, d).wait()

    def row_outputs(s, sl):
        row = mine + s
        here = [pltpu.make_async_copy(outb.at[sl, 0], o.at[row], osem.at[sl, 0]),
                pltpu.make_async_copy(outb.at[sl, 2], dq.at[row], osem.at[sl, 1])]
        there = [remote(outb.at[sl, 1], o.at[row], osem.at[sl, 2], osend_r.at[0], mate),
                 remote(outb.at[sl, 3], dq.at[row], osem.at[sl, 3], osend_r.at[1], mate)]
        return here, there

    def keep(sl, d, slot, s):
        return pltpu.make_async_copy(dkv.at[sl, d], hold.at[slot, s], osem.at[sl, 4 + d])

    def give(sl, d, chip, slot, s):
        return remote(dkv.at[sl, d], part.at[slot, s], osem.at[sl, 4 + d], part_r.at[slot, s], dev(chip))

    def grads_out(s, sl, start):
        even = lax.rem(s, 2) == 0

        def local(d, slot):
            copy = keep(sl, d, slot, s)
            copy.start() if start else copy.wait()

        def away(d, chip, slot):
            copy = give(sl, d, chip, slot, s)
            copy.start() if start else copy.wait_send()

        @pl.when(c < 3)
        def _():
            local(0, 1)

        @pl.when(c == 1)
        def _():
            local(1, 0)

        @pl.when(c == 2)
        def _():
            away(2, 0, 1)
            pl.when(even)(lambda: away(1, 3, 0))
            pl.when(jnp.logical_not(even))(lambda: local(1, 0))

        @pl.when(c == 3)
        def _():
            away(3, 1, 0)
            away(1, 2, 1)
            pl.when(even)(lambda: away(2, 1, 1))
            pl.when(jnp.logical_not(even))(lambda: away(2, 2, 0))

    def put(s, sl):
        here, there = row_outputs(s, sl)
        for copy in here + there:
            copy.start()
        grads_out(s, sl, True)

    def put_wait(s, sl):
        here, there = row_outputs(s, sl)
        for copy in here:
            copy.wait()
        for copy in there:
            copy.wait_send()
        grads_out(s, sl, False)

    def final_copies(s, sl):
        row = mine + s
        rows, rest = pl.ds(128 * e, 128), pl.ds(128 - 128 * e, 128)
        here = [pltpu.make_async_copy(fin.at[sl, 0, rows], dk.at[row], fsem.at[sl, 0]),
                pltpu.make_async_copy(fin.at[sl, 1, rows], dv.at[row], fsem.at[sl, 1])]
        there = [remote(fin.at[sl, 0, rest], dk.at[row], fsem.at[sl, 2], dsend_r.at[0], mate),
                 remote(fin.at[sl, 1, rest], dv.at[row], fsem.at[sl, 3], dsend_r.at[1], mate)]
        return here, there

    def final_wait(s, sl):
        here, there = final_copies(s, sl)
        for copy in here:
            copy.wait()
        for copy in there:
            copy.wait_send()

    def finalize(s, total):
        sl = lax.rem(s, 2)

        @pl.when(s >= 2)
        def _():
            final_wait(s - 2, sl)
        fin[sl, 0] = (total[:, :256] * scale).astype(jnp.bfloat16)
        fin[sl, 1] = total[:, 256:].astype(jnp.bfloat16)
        here, there = final_copies(s, sl)
        for copy in here + there:
            copy.start()

    row_tok = lax.broadcasted_iota(jnp.int32, (1024, 128), 0) >> 3
    lane = lax.broadcasted_iota(jnp.int32, (1024, 128), 1)
    cs = scale * LOG2E
    lo_half, hi_half = slice(0, 128), slice(128, 256)

    def attend(s, slot):
        row = mine + s
        piece = (e, 1 - e)
        for role in range(2):
            dq_row = docs[2 * c + piece[role], pl.ds(row, 1), :]
            d_t = jnp.transpose(jnp.broadcast_to(dq_row, (128, 128)))
            docr[role] = jnp.broadcast_to(d_t[:, None, :], (128, 8, 128)).reshape(1024, 128)

        def g_of(role):
            return qg[slot, 2 + role]

        def scores(role, d, causal):
            sc = dot_nt(qg[slot, role], kvs[slot, d, 0]) * cs
            xs = []
            for j in range(2):
                dk_row = docs[2 * (c - d) + j, pl.ds(row, 1), :]
                vis = docr[role] == dk_row
                if causal:
                    vis = vis & (lane + 128 * j <= row_tok + 128 * piece[role])
                xs.append(jnp.where(vis, sc[:, 128 * j:128 * (j + 1)], NEG_BIG))
            top = jnp.maximum(xs[0], xs[1])
            es = [jnp.exp2(x - top) for x in xs]
            e_scr[d, role, :, lo_half] = es[0]
            e_scr[d, role, :, hi_half] = es[1]
            f_scr[d, role] = top
            l_scr[d, role] = es[0] + es[1]
            return top

        def dprob(role, d):
            dp_scr[d, role] = dot_nt(g_of(role), kvs[slot, d, 1])

        for role in range(2):
            t_scr[role] = scores(role, 0, True)

        def far_scores(d, x):
            for role in range(2):
                t_scr[role] = jnp.maximum(t_scr[role], scores(role, d, False))
            for role in range(2):
                dprob(role, d)
            return x
        lax.fori_loop(1, c + 1, far_scores, 0)

        for role in range(2):
            top = jnp.broadcast_to(jnp.max(t_scr[role], axis=1, keepdims=True), (1024, 128))
            t_scr[role] = top
            f = jnp.exp2(f_scr[0, role] - top)
            f_scr[0, role] = f
            l_scr[0, role] = l_scr[0, role] * f
        dprob(0, 0)

        def far_sums(d, x):
            for role in range(2):
                f = jnp.exp2(f_scr[d, role] - t_scr[role])
                f_scr[d, role] = f
                l_scr[0, role] = l_scr[0, role] + l_scr[d, role] * f
            return x
        lax.fori_loop(1, c + 1, far_sums, 0)

        for role in range(2):
            t_scr[role] = jnp.broadcast_to(1.0 / jnp.sum(l_scr[0, role], axis=1, keepdims=True), (1024, 128))
        dprob(1, 0)

        def weighted(role, d):
            f = f_scr[d, role] * t_scr[role]
            f_scr[d, role] = f
            for half in (lo_half, hi_half):
                p_scr[d, role, :, half] = (e_scr[d, role, :, half] * f).astype(jnp.bfloat16)
            return dot_nn(p_scr[d, role], kvs[slot, d, 1])

        def value_grads(d):
            dkv[slot, d, :, 256:] = dot_tn(p_scr[d, 0], g_of(0)) + dot_tn(p_scr[d, 1], g_of(1))

        for role in range(2):
            o_acc[role] = weighted(role, 0)

        def far_weighted(d, x):
            for role in range(2):
                o_acc[role] = o_acc[role] + weighted(role, d)
            value_grads(d)
            return x
        lax.fori_loop(1, c + 1, far_weighted, 0)

        for role in range(2):
            o_low = o_acc[role].astype(jnp.bfloat16)
            outb[slot, role] = o_low
            delta = jnp.sum(g_of(role).astype(jnp.float32) * o_low.astype(jnp.float32), axis=1, keepdims=True)
            t_scr[role] = jnp.broadcast_to(delta, (1024, 128))
        value_grads(0)

        def score_grads(d):
            out = []
            for role in range(2):
                ds = [
                    (e_scr[d, role, :, half] * f_scr[d, role] * (dp_scr[d, role, :, half] - t_scr[role])).astype(jnp.bfloat16)
                    for half in (lo_half, hi_half)
                ]
                out.append(jnp.concatenate(ds, axis=1))
            dkv[slot, d, :, :256] = dot_tn(out[0], qg[slot, 0]) + dot_tn(out[1], qg[slot, 1])
            return [dot_nn(ds, kvs[slot, d, 0]) for ds in out]

        got = score_grads(0)
        for role in range(2):
            o_acc[role] = got[role]

        def far_grads(d, x):
            got = score_grads(d)
            for role in range(2):
                o_acc[role] = o_acc[role] + got[role]
            return x
        lax.fori_loop(1, c + 1, far_grads, 0)
        for role in range(2):
            outb[slot, 2 + role] = (o_acc[role] * scale).astype(jnp.bfloat16)

    def part_wait(slot, s):
        remote(part.at[slot, s], part.at[slot, s], hop_s, part_r.at[slot, s], mate).wait_recv()

    arrive(0)
    fetch(0, 0)

    def step(s, x):
        slot = lax.rem(s, 2)

        @pl.when(s + 1 < NS)
        def _():
            @pl.when(lax.rem(s + 1, CH) == 0)
            def _():
                arrive((s + 1) // CH)
            fetch(s + 1, 1 - slot)

        @pl.when(s >= 2)
        def _():
            put_wait(s - 2, slot)
        fetch_wait(s, slot)
        attend(s, slot)

        @pl.when(c == 3)
        def _():
            @pl.when(lax.rem(s, 2) == 0)
            def _():
                part_wait(0, s)
                copy = pltpu.make_async_copy(part.at[0, s], tmp, tsem)
                copy.start()
                copy.wait()
                dkv[slot, 2] = dkv[slot, 2] + tmp[...]
        put(s, slot)

        @pl.when(c == 3)
        def _():
            finalize(s, dkv[slot, 0])
        return x

    lax.fori_loop(0, NS, step, 0)
    put_wait(NS - 2, 0)
    put_wait(NS - 1, 1)

    def load(src, i):
        return pltpu.make_async_copy(src, dkv.at[0, i], lsem.at[i])

    def passed(s, sl, chip, slot):
        return remote(dkv.at[1, sl], part.at[slot, s], xsem.at[sl], part_r.at[slot, s], dev(chip))

    def relay(s):
        return remote(part.at[2, s], part.at[1, s], rel_s.at[s], part_r.at[1, s], dev(1))

    def home(i, x):
        @pl.when(c == 0)
        def _():
            @pl.when((i < NS) & (lax.rem(i, 2) == 1))
            def _():
                part_wait(2, i)
                relay(i).start()

            @pl.when(i >= 2)
            def _():
                s = i - 2
                load(hold.at[1, s], 0).start()
                part_wait(1, s)
                load(part.at[1, s], 1).start()
                part_wait(0, s)
                load(part.at[0, s], 2).start()
                for n, src in enumerate((hold.at[1, s], part.at[1, s], part.at[0, s])):
                    load(src, n).wait()
                finalize(s, dkv[0, 0] + dkv[0, 1] + dkv[0, 2])

        @pl.when(c == 1)
        def _():
            @pl.when(i < NS)
            def _():
                sl = lax.rem(i, 2)
                load(hold.at[0, i], 0).start()
                part_wait(0, i)
                load(part.at[0, i], 1).start()

                @pl.when(i >= 2)
                def _():
                    passed(i - 2, sl, 0, 0).wait_send()
                load(hold.at[0, i], 0).wait()
                load(part.at[0, i], 1).wait()
                dkv[1, sl] = dkv[0, 0] + dkv[0, 1]
                passed(i, sl, 0, 0).start()

            @pl.when(i >= 2)
            def _():
                s = i - 2
                load(hold.at[1, s], 2).start()
                part_wait(1, s)
                load(part.at[1, s], 3).start()
                load(hold.at[1, s], 2).wait()
                load(part.at[1, s], 3).wait()
                finalize(s, dkv[0, 2] + dkv[0, 3])

        @pl.when((c == 2) & (i < NS))
        def _():
            @pl.when(lax.rem(i, 2) == 1)
            def _():
                sl = lax.rem(i // 2, 2)
                load(hold.at[0, i], 0).start()
                part_wait(0, i)
                load(part.at[0, i], 1).start()

                @pl.when(i >= 4)
                def _():
                    passed(i - 4, sl, 0, 2).wait_send()
                load(hold.at[0, i], 0).wait()
                load(part.at[0, i], 1).wait()
                dkv[1, sl] = dkv[0, 0] + dkv[0, 1]
                passed(i, sl, 0, 2).start()
            load(hold.at[1, i], 2).start()
            part_wait(1, i)
            load(part.at[1, i], 3).start()
            load(hold.at[1, i], 2).wait()
            load(part.at[1, i], 3).wait()
            finalize(i, dkv[0, 2] + dkv[0, 3])
        return x

    @pl.when(c < 3)
    def _():
        lax.fori_loop(0, NS + 2, home, 0)

    @pl.when(c == 0)
    def _():
        for s in range(1, NS, 2):
            relay(s).wait_send()
        remote(kvr.at[1], kvr.at[1], hop_s, kv_r.at[0, 0], mate).wait_send()

    @pl.when(c == 1)
    def _():
        passed(NS - 2, 0, 0, 0).wait_send()
        passed(NS - 1, 1, 0, 0).wait_send()
        remote(kvr.at[0], kvr.at[0], hop_s, kv_r.at[0, 0], mate).wait_send()

    @pl.when(c == 2)
    def _():
        passed(NS - 3, (NS - 3) // 2 % 2, 0, 2).wait_send()
        passed(NS - 1, (NS - 1) // 2 % 2, 0, 2).wait_send()
    final_wait(NS - 2, 0)
    final_wait(NS - 1, 1)
    for which, ref in ((0, k), (1, v)):
        for way in range(2):
            @pl.when((c < 2) | ((c == 2) & (way == 0)))
            def _():
                remote(ref, ref, kv_s.at[way, which], kv_r.at[0, 0], mate).wait_send()
        half = ref.at[pl.ds(other, NS)]
        remote(half, half, kv_s.at[2, which], kv_r.at[0, 0], mate).wait_send()
    for which, ref in ((0, q), (1, g)):
        half = ref.at[pl.ds(other, NS)]
        remote(half, half, q_s.at[which], q_r.at[0], mate).wait_send()
    for which, ref in ((0, o), (1, dq)):
        half = ref.at[pl.ds(other, NS)]
        remote(half, half, hop_s, osend_r.at[which], mate).wait_recv()
    for which, ref in ((0, dk), (1, dv)):
        half = ref.at[pl.ds(other, NS)]
        remote(half, half, hop_s, dsend_r.at[which], mate).wait_recv()


ANY = pl.BlockSpec(memory_space=pl.ANY)
VMEM = pl.BlockSpec(memory_space=pltpu.VMEM)


def solution(mesh):
    n_dev = mesh.shape['cp']
    seq_spec = P('dp', 'cp', None, None)
    id_spec = P('dp', 'cp')
    bf, f32 = jnp.bfloat16, jnp.float32
    shape = jax.ShapeDtypeStruct
    dma = pltpu.SemaphoreType.DMA

    def per_device(query, keys, values, grad_out, doc_id):
        nb, piece, heads, hd = query.shape
        rows = piece * heads
        outs = pl.pallas_call(
            functools.partial(fused_kernel, hd ** -0.5),
            in_specs=[VMEM] + [ANY] * 4,
            out_specs=[ANY] * 8,
            out_shape=[
                shape((nb, rows, hd), bf), shape((nb, rows, hd), bf), shape((nb, piece, hd), bf), shape((nb, piece, hd), bf),
                shape((NS, 2, rows, hd), bf), shape((4, NS, 2, 256, 256), bf),
                shape((3, NS, 256, 512), f32), shape((2, NS, 256, 512), f32),
            ],
            scratch_shapes=[
                pltpu.VMEM((n_dev, nb, piece), jnp.int32), pltpu.VMEM((2, 4, 2, 256, 256), bf), pltpu.VMEM((2, 4, rows, hd), bf),
                pltpu.VMEM((2, 4, rows, hd), bf), pltpu.VMEM((2, 4, 256, 512), f32), pltpu.VMEM((256, 512), f32),
                pltpu.VMEM((2, 2, 256, 256), bf),
                pltpu.VMEM((4, 2, rows, 256), f32), pltpu.VMEM((4, 2, rows, 256), f32), pltpu.VMEM((4, 2, rows, 256), bf),
                pltpu.VMEM((4, 2, rows, 128), f32), pltpu.VMEM((4, 2, rows, 128), f32), pltpu.VMEM((2, rows, 128), f32),
                pltpu.VMEM((2, rows, 128), jnp.int32), pltpu.VMEM((2, rows, hd), f32),
                dma((n_dev,)), dma((n_dev,)), dma((2, 10)), dma((2, 8)), dma((2,)), dma((2,)), dma((NJ,)), dma((3, 2)), dma((4, NJ)),
                dma, dma((3, NS)), dma, dma((2, 4)), dma((2,)), dma((4,)), dma((2,)), dma((NS,)),
            ],
            compiler_params=pltpu.CompilerParams(has_side_effects=True, vmem_limit_bytes=62 * 1024 * 1024),
            name="attend",
        )(doc_id, query.reshape(nb, rows, hd), grad_out.reshape(nb, rows, hd), keys.reshape(nb, piece, hd), values.reshape(nb, piece, hd))
        o, dq, dk, dv = outs[:4]
        return o.reshape(query.shape), dq.reshape(query.shape), dk.reshape(keys.shape), dv.reshape(values.shape)

    return jax.shard_map(per_device, mesh=mesh, in_specs=(seq_spec, seq_spec, seq_spec, seq_spec, id_spec),
                         out_specs=(seq_spec, seq_spec, seq_spec, seq_spec), check_vma=False)
```

time: 2310 us -> 439 us (0.19)
  matrix products: 1040 us -> 0 us
  waiting for transfers between devices: 941 us -> 0 us
  Pallas kernels: 0 us -> 411 us
  other arithmetic: 155 us -> 0 us
  local copies, waits for them, and re-layouts: 128 us -> 26.6 us
  starting transfers between devices: 37.4 us -> 0 us
    dot_general x55 -> x0, matrix products: 1040 us -> none  [the longest x8 235 us: out_update(): jnp.einsum('cril,cle->crie', prob_bf16, val_cur, preferred_element_type=j...]
    ppermute x72 -> x0, waiting for transfers between devices: 941 us -> none  [the longest x7 338 us: out_body(): doc_cur = lax.ppermute(doc_cur, 'cp', to_next)]
    pallas_call x0 -> x1, Pallas kernels: none -> 411 us  [per_device(): pl.pallas_call(functools.partial(fused_kernel, hd ** (-0.5)), in_specs=[V...]
    while x105 -> x0, local copies, waits for them, and re-layouts: 85.1 us -> none
    reduce_sum x8 -> x0, other arithmetic: 68.5 us -> none  [stats_update(): jnp.sum(exp_scores, axis=-1)]
    ppermute x72 -> x0, starting transfers between devices: 37.4 us -> none  [the longest x7 23.8 us: grad_body(): dv_acc = lax.ppermute(dv_acc, 'cp', to_next)]
    unnamed x3 -> x0, other arithmetic: 35.3 us -> none
    convert_element_type x1 -> x0, other arithmetic: 31 us -> none  [per_device(): grad_query = (grads[3] * score_scale).astype(jnp.bfloat16)]
  transfers between devices with their start and end apart: 72 -> 0, of which waited for: 36 -> 0; matrix products, arithmetic and copies ran while one was open for 27% -> 0% of each run, Pallas kernels for 0% -> 0%
where the time goes in v7:
time: 439 us; the launch traced here: 438 us
  Pallas kernels  411 us (94%)
  local copies, waits for them, and re-layouts  26.6 us (6%)
    pallas_call x1, Pallas kernels, per_device(): pl.pallas_call(functools.partial(fused_kernel, hd ** (-0.5)), in_specs=[V...  411 us
    unnamed x10, local copies, waits for them, and re-layouts  26.6 us

profile of v7, /device:TPU:0, one launch (start us, length us, event | category | flops | bytes accessed | tf_op | source)
XLA Modules:
  0.0 437.9 jit_solution(14950502394562514850)
XLA Ops:
  0.6 410.7 %attend.1 = (bf16[32,1024,256]{2,1,0:T(8,128)(2,1)}, bf16[32,1024,256]{2,1,0:T(8,128)(2,1)}, bf16[32,128,256]{2,1,0:T(8,128)(2,1)}, bf16[32,128,256]{2,1,0:T(8,1...) custom-call(s32[32,128]{1,0:T(8,128)} %doc.1, ...), custom_call_target="tpu_custom_call" | custom-call | tf_op jit(solution)/shard_map/attend/pallas_call | solution.py:542
  411.3 0.0 copy-start
  411.3 14.6 %copy.15 = bf16[32,128,8,256]{3,2,1,0:T(8,128)(2,1)} copy(bf16[32,128,8,256]{3,2,1,0:T(8,128)(2,1)} %bitcast.15) | data formatting | bytes 33554432
  425.9 2.3 copy-done
  428.2 0.0 copy-start.2
  428.2 0.0 copy-start.1
  428.2 7.1 %copy.16 = bf16[32,128,8,256]{3,2,1,0:T(8,128)(2,1)} copy(bf16[32,128,8,256]{3,2,1,0:T(8,128)(2,1)S(1)} %bitcast.14) | data formatting | bytes 33554432
  435.2 0.0 copy-done.2
  435.2 1.3 copy.17
  436.6 0.0 copy-done.1
  436.6 1.3 copy.18
Async XLA Ops:
  411.3 16.9 %copy-start = (bf16[32,1024,256]{2,1,0:T(8,128)(2,1)S(1)}, bf16[32,1024,256]{2,1,0:T(8,128)(2,1)}, u32[]{:S(2)}) copy-start(bf16[32,1024,256]{2,1,0:T(8,128)(2,1)} %get-tuple-element.9) | copy-start | bytes 50331652
  428.2 7.1 %copy-start.2 = (bf16[32,128,256]{2,1,0:T(8,128)(2,1)S(1)}, bf16[32,128,256]{2,1,0:T(8,128)(2,1)}, u32[]{:S(2)}) copy-start(bf16[32,128,256]{2,1,0:T(8,128)(2,1)} %get-tuple-element.10) | copy-start | bytes 6291460
  428.2 8.4 %copy-start.1 = (bf16[32,128,256]{2,1,0:T(8,128)(2,1)S(1)}, bf16[32,128,256]{2,1,0:T(8,128)(2,1)}, u32[]{:S(2)}) copy-start(bf16[32,128,256]{2,1,0:T(8,128)(2,1)} %get-tuple-element.11) | copy-start | bytes 6291460

commit v8 on v7

--- a/solution.py
+++ b/solution.py
@@ -13,6 +13,8 @@
 CH = 2
 NJ = NS // CH
 AHEAD = 2
+NG = 4
+ROUND = (0, 2, 4, 6, 8, 10, 11, 12)
 
 
 def dot_nt(a, b):
@@ -34,7 +36,7 @@
 
 def fused_kernel(scale, doc, q, g, k, v, o, dq, dk, dv, qgm, kvr, part, hold,
                  docs, kvs, qg, outb, dkv, tmp, fin, e_scr, dp_scr, p_scr, l_scr, f_scr, t_scr, docr, o_acc,
-                 doc_s, doc_r, isem, osem, osend_r, q_s, q_r, kv_s, kv_r, hop_s, part_r, tsem, fsem, dsend_r, lsem, xsem, rel_s):
+                 doc_s, doc_r, isem, osem, gsem, osend_r, q_s, q_r, kv_s, kv_r, hop_s, part_r, tsem, fsem, dsend_r, lsem, xsem, rel_s):
     rank = lax.axis_index('cp')
     n_dev = docs.shape[0]
     c = rank // 2
@@ -165,13 +167,20 @@
         return here, there
 
     def keep(sl, d, slot, s):
-        return pltpu.make_async_copy(dkv.at[sl, d], hold.at[slot, s], osem.at[sl, 4 + d])
+        return pltpu.make_async_copy(dkv.at[sl, d], hold.at[slot, s], gsem.at[sl, d])
 
     def give(sl, d, chip, slot, s):
-        return remote(dkv.at[sl, d], part.at[slot, s], osem.at[sl, 4 + d], part_r.at[slot, s], dev(chip))
-
-    def grads_out(s, sl, start):
-        even = lax.rem(s, 2) == 0
+        return remote(dkv.at[sl, d], part.at[slot, s], gsem.at[sl, d], part_r.at[slot, s], dev(chip))
+
+    def around(s):
+        out = jnp.bool_(False)
+        for one in ROUND:
+            out = out | (s == one)
+        return out
+
+    def grads_out(s, start):
+        even = jnp.logical_not(around(s))
+        sl = lax.rem(s, NG)
 
         def local(d, slot):
             copy = keep(sl, d, slot, s)
@@ -206,7 +215,7 @@
         here, there = row_outputs(s, sl)
         for copy in here + there:
             copy.start()
-        grads_out(s, sl, True)
+        grads_out(s, True)
 
     def put_wait(s, sl):
         here, there = row_outputs(s, sl)
@@ -214,7 +223,6 @@
             copy.wait()
         for copy in there:
             copy.wait_send()
-        grads_out(s, sl, False)
 
     def final_copies(s, sl):
         row = mine + s
@@ -251,6 +259,7 @@
 
     def attend(s, slot):
         row = mine + s
+        gslot = lax.rem(s, NG)
         piece = (e, 1 - e)
         for role in range(2):
             dq_row = docs[2 * c + piece[role], pl.ds(row, 1), :]
@@ -319,7 +328,7 @@
             return dot_nn(p_scr[d, role], kvs[slot, d, 1])
 
         def value_grads(d):
-            dkv[slot, d, :, 256:] = dot_tn(p_scr[d, 0], g_of(0)) + dot_tn(p_scr[d, 1], g_of(1))
+            dkv[gslot, d, :, 256:] = dot_tn(p_scr[d, 0], g_of(0)) + dot_tn(p_scr[d, 1], g_of(1))
 
         for role in range(2):
             o_acc[role] = weighted(role, 0)
@@ -346,7 +355,7 @@
                     for half in (lo_half, hi_half)
                 ]
                 out.append(jnp.concatenate(ds, axis=1))
-            dkv[slot, d, :, :256] = dot_tn(out[0], qg[slot, 0]) + dot_tn(out[1], qg[slot, 1])
+            dkv[gslot, d, :, :256] = dot_tn(out[0], qg[slot, 0]) + dot_tn(out[1], qg[slot, 1])
             return [dot_nn(ds, kvs[slot, d, 0]) for ds in out]
 
         got = score_grads(0)
@@ -381,28 +390,33 @@
         @pl.when(s >= 2)
         def _():
             put_wait(s - 2, slot)
+
+        @pl.when(s >= NG)
+        def _():
+            grads_out(s - NG, False)
         fetch_wait(s, slot)
         attend(s, slot)
 
         @pl.when(c == 3)
         def _():
-            @pl.when(lax.rem(s, 2) == 0)
+            gslot = lax.rem(s, NG)
+
+            @pl.when(jnp.logical_not(around(s)))
             def _():
                 part_wait(0, s)
                 copy = pltpu.make_async_copy(part.at[0, s], tmp, tsem)
                 copy.start()
                 copy.wait()
-                dkv[slot, 2] = dkv[slot, 2] + tmp[...]
+                dkv[gslot, 2] = dkv[gslot, 2] + tmp[...]
+            finalize(s, dkv[gslot, 0])
         put(s, slot)
-
-        @pl.when(c == 3)
-        def _():
-            finalize(s, dkv[slot, 0])
         return x
 
     lax.fori_loop(0, NS, step, 0)
     put_wait(NS - 2, 0)
     put_wait(NS - 1, 1)
+    for s in range(NS - NG, NS):
+        grads_out(s, False)
 
     def load(src, i):
         return pltpu.make_async_copy(src, dkv.at[0, i], lsem.at[i])
@@ -416,7 +430,7 @@
     def home(i, x):
         @pl.when(c == 0)
         def _():
-            @pl.when((i < NS) & (lax.rem(i, 2) == 1))
+            @pl.when(around(i))
             def _():
                 part_wait(2, i)
                 relay(i).start()
@@ -462,14 +476,14 @@
 
         @pl.when((c == 2) & (i < NS))
         def _():
-            @pl.when(lax.rem(i, 2) == 1)
-            def _():
-                sl = lax.rem(i // 2, 2)
+            @pl.when(around(i))
+            def _():
+                sl = lax.rem(i, 4)
                 load(hold.at[0, i], 0).start()
                 part_wait(0, i)
                 load(part.at[0, i], 1).start()
 
-                @pl.when(i >= 4)
+                @pl.when((i >= 4) & around(i - 4))
                 def _():
                     passed(i - 4, sl, 0, 2).wait_send()
                 load(hold.at[0, i], 0).wait()
@@ -490,7 +504,7 @@
 
     @pl.when(c == 0)
     def _():
-        for s in range(1, NS, 2):
+        for s in ROUND:
             relay(s).wait_send()
         remote(kvr.at[1], kvr.at[1], hop_s, kv_r.at[0, 0], mate).wait_send()
 
@@ -502,8 +516,9 @@
 
     @pl.when(c == 2)
     def _():
-        passed(NS - 3, (NS - 3) // 2 % 2, 0, 2).wait_send()
-        passed(NS - 1, (NS - 1) // 2 % 2, 0, 2).wait_send()
+        for s in ROUND:
+            if s + 4 not in ROUND:
+                passed(s, s % 4, 0, 2).wait_send()
     final_wait(NS - 2, 0)
     final_wait(NS - 1, 1)
     for which, ref in ((0, k), (1, v)):
@@ -550,13 +565,13 @@
             ],
             scratch_shapes=[
                 pltpu.VMEM((n_dev, nb, piece), jnp.int32), pltpu.VMEM((2, 4, 2, 256, 256), bf), pltpu.VMEM((2, 4, rows, hd), bf),
-                pltpu.VMEM((2, 4, rows, hd), bf), pltpu.VMEM((2, 4, 256, 512), f32), pltpu.VMEM((256, 512), f32),
+                pltpu.VMEM((2, 4, rows, hd), bf), pltpu.VMEM((NG, 4, 256, 512), f32), pltpu.VMEM((256, 512), f32),
                 pltpu.VMEM((2, 2, 256, 256), bf),
                 pltpu.VMEM((4, 2, rows, 256), f32), pltpu.VMEM((4, 2, rows, 256), f32), pltpu.VMEM((4, 2, rows, 256), bf),
                 pltpu.VMEM((4, 2, rows, 128), f32), pltpu.VMEM((4, 2, rows, 128), f32), pltpu.VMEM((2, rows, 128), f32),
                 pltpu.VMEM((2, rows, 128), jnp.int32), pltpu.VMEM((2, rows, hd), f32),
-                dma((n_dev,)), dma((n_dev,)), dma((2, 10)), dma((2, 8)), dma((2,)), dma((2,)), dma((NJ,)), dma((3, 2)), dma((4, NJ)),
-                dma, dma((3, NS)), dma, dma((2, 4)), dma((2,)), dma((4,)), dma((2,)), dma((NS,)),
+                dma((n_dev,)), dma((n_dev,)), dma((2, 10)), dma((2, 4)), dma((NG, 4)), dma((2,)), dma((2,)), dma((NJ,)), dma((3, 2)), dma((4, NJ)),
+                dma, dma((3, NS)), dma, dma((2, 4)), dma((2,)), dma((4,)), dma((4,)), dma((NS,)),
             ],
             compiler_params=pltpu.CompilerParams(has_side_effects=True, vmem_limit_bytes=62 * 1024 * 1024),
             name="attend",

time: 439 us -> 449 us (1.023)
  Pallas kernels: 411 us -> 421 us
    pallas_call x1, Pallas kernels: 411 us -> 421 us  [per_device(): pl.pallas_call(functools.partial(fused_kernel, hd ** (-0.5)), in_specs=[V...]
where the time goes in v8:
time: 449 us; the launch traced here: 448 us
  Pallas kernels  421 us (94%)
  local copies, waits for them, and re-layouts  26.6 us (6%)
    pallas_call x1, Pallas kernels, per_device(): pl.pallas_call(functools.partial(fused_kernel, hd ** (-0.5)), in_specs=[V...  421 us
    unnamed x10, local copies, waits for them, and re-layouts  26.6 us

profile of v8, /device:TPU:0, one launch (start us, length us, event | category | flops | bytes accessed | tf_op | source)
XLA Modules:
  0.0 448.0 jit_solution(1771247800892589015)
XLA Ops:
  0.6 420.8 %attend.1 = (bf16[32,1024,256]{2,1,0:T(8,128)(2,1)}, bf16[32,1024,256]{2,1,0:T(8,128)(2,1)}, bf16[32,128,256]{2,1,0:T(8,128)(2,1)}, bf16[32,128,256]{2,1,0:T(8,1...) custom-call(s32[32,128]{1,0:T(8,128)} %doc.1, ...), custom_call_target="tpu_custom_call" | custom-call | tf_op jit(solution)/shard_map/attend/pallas_call | solution.py:557
  421.4 0.0 copy-start
  421.4 14.6 %copy.15 = bf16[32,128,8,256]{3,2,1,0:T(8,128)(2,1)} copy(bf16[32,128,8,256]{3,2,1,0:T(8,128)(2,1)} %bitcast.15) | data formatting | bytes 33554432
  436.0 2.3 copy-done
  438.3 0.0 copy-start.2
  438.3 0.0 copy-start.1
  438.3 7.1 %copy.16 = bf16[32,128,8,256]{3,2,1,0:T(8,128)(2,1)} copy(bf16[32,128,8,256]{3,2,1,0:T(8,128)(2,1)S(1)} %bitcast.14) | data formatting | bytes 33554432
  445.4 0.0 copy-done.2
  445.4 1.3 copy.17
  446.7 0.0 copy-done.1
  446.7 1.3 copy.18
Async XLA Ops:
  421.4 16.9 %copy-start = (bf16[32,1024,256]{2,1,0:T(8,128)(2,1)S(1)}, bf16[32,1024,256]{2,1,0:T(8,128)(2,1)}, u32[]{:S(2)}) copy-start(bf16[32,1024,256]{2,1,0:T(8,128)(2,1)} %get-tuple-element.9) | copy-start | bytes 50331652
  438.3 7.1 %copy-start.2 = (bf16[32,128,256]{2,1,0:T(8,128)(2,1)S(1)}, bf16[32,128,256]{2,1,0:T(8,128)(2,1)}, u32[]{:S(2)}) copy-start(bf16[32,128,256]{2,1,0:T(8,128)(2,1)} %get-tuple-element.10) | copy-start | bytes 6291460
  438.3 8.4 %copy-start.1 = (bf16[32,128,256]{2,1,0:T(8,128)(2,1)S(1)}, bf16[32,128,256]{2,1,0:T(8,128)(2,1)}, u32[]{:S(2)}) copy-start(bf16[32,128,256]{2,1,0:T(8,128)(2,1)} %get-tuple-element.11) | copy-start | bytes 6291460

commit v9 on v8

--- a/solution.py
+++ b/solution.py
@@ -10,11 +10,13 @@
 NEG_BIG = -1e30
 LOG2E = 1.4426950408889634
 NS = 16
-CH = 2
-NJ = NS // CH
+NJ = NS
 AHEAD = 2
 NG = 4
-ROUND = (0, 2, 4, 6, 8, 10, 11, 12)
+ROUND = (0, 1, 4, 7, 8, 9, 10, 14)
+EARLY_X = {12: 0, 15: 1}
+EARLY_Y = {4: 0, 6: 1, 9: 4, 12: 7, 15: 8}
+LAG = (2, 5, 6)
 
 
 def dot_nt(a, b):
@@ -35,8 +37,8 @@
 
 
 def fused_kernel(scale, doc, q, g, k, v, o, dq, dk, dv, qgm, kvr, part, hold,
-                 docs, kvs, qg, outb, dkv, tmp, fin, e_scr, dp_scr, p_scr, l_scr, f_scr, t_scr, docr, o_acc,
-                 doc_s, doc_r, isem, osem, gsem, osend_r, q_s, q_r, kv_s, kv_r, hop_s, part_r, tsem, fsem, dsend_r, lsem, xsem, rel_s):
+                 docs, kvs, qg, outb, dkv, sums, fin, e_scr, dp_scr, p_scr, l_scr, f_scr, t_scr, docr, o_acc,
+                 doc_s, doc_r, isem, osem, gsem, osend_r, q_s, q_r, kv_s, kv_r, hop_s, part_r, fsem, dsend_r, lsem, xsem, rel_s):
     rank = lax.axis_index('cp')
     n_dev = docs.shape[0]
     c = rank // 2
@@ -60,7 +62,7 @@
         out = []
         for col in cols:
             for which, ref in ((0, k), (1, v)):
-                out.append(remote(ref.at[pl.ds(col * NS + CH * j, CH)], kvr.at[c, pl.ds(CH * j, CH), which, pl.ds(128 * e, 128)],
+                out.append(remote(ref.at[pl.ds(col * NS + j, 1)], kvr.at[c, pl.ds(j, 1), which, pl.ds(128 * e, 128)],
                                   kv_s.at[way, which], kv_r.at[c, j], 2 * chip + col))
         return out
 
@@ -69,7 +71,7 @@
             copy.start()
 
     def kv_forward(a, chip, j):
-        return remote(kvr.at[a, pl.ds(CH * j, CH)], kvr.at[a, pl.ds(CH * j, CH)], hop_s, kv_r.at[a, j], dev(chip))
+        return remote(kvr.at[a, pl.ds(j, 1)], kvr.at[a, pl.ds(j, 1)], hop_s, kv_r.at[a, j], dev(chip))
 
     def stream_kv(j):
         @pl.when(c == 0)
@@ -79,7 +81,6 @@
 
         @pl.when(c == 1)
         def _():
-            send_kv(3, 0, j)
             send_kv(0, 1, j)
 
         @pl.when(c == 2)
@@ -88,14 +89,18 @@
 
     def to_mate(j):
         for which, ref in ((0, k), (1, v)):
-            remote(ref.at[pl.ds(other + CH * j, CH)], kvr.at[c, pl.ds(CH * j, CH), which, pl.ds(128 * e, 128)],
+            remote(ref.at[pl.ds(other + j, 1)], kvr.at[c, pl.ds(j, 1), which, pl.ds(128 * e, 128)],
                    kv_s.at[2, which], kv_r.at[c, j], mate).start()
 
     def rows_to_mate(j):
         for which, ref in ((0, q), (1, g)):
-            remote(ref.at[pl.ds(other + CH * j, CH)], qgm.at[pl.ds(CH * j, CH), which], q_s.at[which], q_r.at[j], mate).start()
+            remote(ref.at[pl.ds(other + j, 1)], qgm.at[pl.ds(j, 1), which], q_s.at[which], q_r.at[j], mate).start()
 
     stream_kv(0)
+
+    @pl.when(c == 1)
+    def _():
+        send_kv(3, 0, 0)
     to_mate(0)
     rows_to_mate(0)
     for j in range(1, AHEAD):
@@ -107,9 +112,9 @@
         doc_copy(i).wait()
 
     def arrive(j):
-        remote(kvr.at[c, pl.ds(CH * j, CH), :, pl.ds(0, 128)], kvr.at[c, pl.ds(CH * j, CH), :, pl.ds(0, 128)],
+        remote(kvr.at[c, pl.ds(j, 1), :, pl.ds(0, 128)], kvr.at[c, pl.ds(j, 1), :, pl.ds(0, 128)],
                hop_s, kv_r.at[c, j], mate).wait_recv()
-        remote(qgm.at[pl.ds(CH * j, CH)], qgm.at[pl.ds(CH * j, CH)], hop_s, q_r.at[j], mate).wait_recv()
+        remote(qgm.at[pl.ds(j, 1)], qgm.at[pl.ds(j, 1)], hop_s, q_r.at[j], mate).wait_recv()
         for a in range(3):
             @pl.when(a < c)
             def _():
@@ -118,6 +123,10 @@
         @pl.when(c == 1)
         def _():
             kv_forward(0, 3, j).start()
+
+            @pl.when(j + 1 < NJ)
+            def _():
+                send_kv(3, 0, j + 1)
 
         @pl.when(c == 0)
         def _():
@@ -206,10 +215,11 @@
 
         @pl.when(c == 3)
         def _():
-            away(3, 1, 0)
-            away(1, 2, 1)
+            if not start:
+                away(3, 1, 0)
             pl.when(even)(lambda: away(2, 1, 1))
             pl.when(jnp.logical_not(even))(lambda: away(2, 2, 0))
+            away(1, 2, 1)
 
     def put(s, sl):
         here, there = row_outputs(s, sl)
@@ -374,6 +384,48 @@
     def part_wait(slot, s):
         remote(part.at[slot, s], part.at[slot, s], hop_s, part_r.at[slot, s], mate).wait_recv()
 
+    def load(src, i):
+        return pltpu.make_async_copy(src, sums.at[i], lsem.at[i])
+
+    def passed(s, sl, slot):
+        return remote(sums.at[4 + sl], part.at[slot, s], xsem.at[sl], part_r.at[slot, s], dev(0))
+
+    def relay(s):
+        return remote(part.at[2, s], part.at[1, s], rel_s.at[s], part_r.at[1, s], dev(1))
+
+    def pass_on(i, count, slot):
+        sl = lax.rem(count, 2)
+        load(hold.at[0, i], 0).start()
+        part_wait(0, i)
+        load(part.at[0, i], 1).start()
+
+        @pl.when(count >= 2)
+        def _():
+            passed(i, sl, slot).wait_send()
+        load(hold.at[0, i], 0).wait()
+        load(part.at[0, i], 1).wait()
+        sums[4 + sl] = sums[0] + sums[1]
+        passed(i, sl, slot).start()
+
+    def pass_x(i):
+        pass_on(i, jnp.int32(i), 0)
+
+    def pass_y(i):
+        count = jnp.int32(0)
+        for one in ROUND:
+            count = count + jnp.where(one < i, 1, 0)
+        pass_on(i, count, 2)
+
+    def total(s, terms):
+        for n, src in enumerate(terms):
+            load(src, n).start()
+        for n, src in enumerate(terms):
+            load(src, n).wait()
+        value = sums[0]
+        for n in range(1, len(terms)):
+            value = value + sums[n]
+        finalize(s, value)
+
     arrive(0)
     fetch(0, 0)
 
@@ -382,9 +434,7 @@
 
         @pl.when(s + 1 < NS)
         def _():
-            @pl.when(lax.rem(s + 1, CH) == 0)
-            def _():
-                arrive((s + 1) // CH)
+            arrive(s + 1)
             fetch(s + 1, 1 - slot)
 
         @pl.when(s >= 2)
@@ -400,16 +450,20 @@
         @pl.when(c == 3)
         def _():
             gslot = lax.rem(s, NG)
+            give(gslot, 3, 1, 0, s).start()
 
             @pl.when(jnp.logical_not(around(s)))
             def _():
                 part_wait(0, s)
-                copy = pltpu.make_async_copy(part.at[0, s], tmp, tsem)
-                copy.start()
-                copy.wait()
-                dkv[gslot, 2] = dkv[gslot, 2] + tmp[...]
+                load(part.at[0, s], 0).start()
+                load(part.at[0, s], 0).wait()
+                dkv[gslot, 2] = dkv[gslot, 2] + sums[0]
             finalize(s, dkv[gslot, 0])
         put(s, slot)
+        for at, i in EARLY_X.items():
+            pl.when((c == 1) & (s == at))(lambda: pass_x(i))
+        for at, i in EARLY_Y.items():
+            pl.when((c == 2) & (s == at))(lambda: pass_y(i))
         return x
 
     lax.fori_loop(0, NS, step, 0)
@@ -418,15 +472,6 @@
     for s in range(NS - NG, NS):
         grads_out(s, False)
 
-    def load(src, i):
-        return pltpu.make_async_copy(src, dkv.at[0, i], lsem.at[i])
-
-    def passed(s, sl, chip, slot):
-        return remote(dkv.at[1, sl], part.at[slot, s], xsem.at[sl], part_r.at[slot, s], dev(chip))
-
-    def relay(s):
-        return remote(part.at[2, s], part.at[1, s], rel_s.at[s], part_r.at[1, s], dev(1))
-
     def home(i, x):
         @pl.when(c == 0)
         def _():
@@ -434,73 +479,38 @@
             def _():
                 part_wait(2, i)
                 relay(i).start()
-
-            @pl.when(i >= 2)
-            def _():
-                s = i - 2
-                load(hold.at[1, s], 0).start()
+            s = i - LAG[0]
+
+            @pl.when((s >= 0) & (s < NS))
+            def _():
                 part_wait(1, s)
-                load(part.at[1, s], 1).start()
                 part_wait(0, s)
-                load(part.at[0, s], 2).start()
-                for n, src in enumerate((hold.at[1, s], part.at[1, s], part.at[0, s])):
-                    load(src, n).wait()
-                finalize(s, dkv[0, 0] + dkv[0, 1] + dkv[0, 2])
+                total(s, (hold.at[1, s], part.at[1, s], part.at[0, s]))
 
         @pl.when(c == 1)
         def _():
-            @pl.when(i < NS)
-            def _():
-                sl = lax.rem(i, 2)
-                load(hold.at[0, i], 0).start()
-                part_wait(0, i)
-                load(part.at[0, i], 1).start()
-
-                @pl.when(i >= 2)
-                def _():
-                    passed(i - 2, sl, 0, 0).wait_send()
-                load(hold.at[0, i], 0).wait()
-                load(part.at[0, i], 1).wait()
-                dkv[1, sl] = dkv[0, 0] + dkv[0, 1]
-                passed(i, sl, 0, 0).start()
-
-            @pl.when(i >= 2)
-            def _():
-                s = i - 2
-                load(hold.at[1, s], 2).start()
+            pl.when((i >= len(EARLY_X)) & (i < NS))(lambda: pass_x(i))
+            s = i - LAG[1]
+
+            @pl.when((s >= 0) & (s < NS))
+            def _():
                 part_wait(1, s)
-                load(part.at[1, s], 3).start()
-                load(hold.at[1, s], 2).wait()
-                load(part.at[1, s], 3).wait()
-                finalize(s, dkv[0, 2] + dkv[0, 3])
-
-        @pl.when((c == 2) & (i < NS))
-        def _():
-            @pl.when(around(i))
-            def _():
-                sl = lax.rem(i, 4)
-                load(hold.at[0, i], 0).start()
-                part_wait(0, i)
-                load(part.at[0, i], 1).start()
-
-                @pl.when((i >= 4) & around(i - 4))
-                def _():
-                    passed(i - 4, sl, 0, 2).wait_send()
-                load(hold.at[0, i], 0).wait()
-                load(part.at[0, i], 1).wait()
-                dkv[1, sl] = dkv[0, 0] + dkv[0, 1]
-                passed(i, sl, 0, 2).start()
-            load(hold.at[1, i], 2).start()
-            part_wait(1, i)
-            load(part.at[1, i], 3).start()
-            load(hold.at[1, i], 2).wait()
-            load(part.at[1, i], 3).wait()
-            finalize(i, dkv[0, 2] + dkv[0, 3])
+                total(s, (hold.at[1, s], part.at[1, s]))
+
+        @pl.when(c == 2)
+        def _():
+            pl.when(around(i) & (i > max(EARLY_Y.values())))(lambda: pass_y(i))
+            s = i - LAG[2]
+
+            @pl.when((s >= 0) & (s < NS))
+            def _():
+                part_wait(1, s)
+                total(s, (hold.at[1, s], part.at[1, s]))
         return x
 
     @pl.when(c < 3)
     def _():
-        lax.fori_loop(0, NS + 2, home, 0)
+        lax.fori_loop(0, NS + max(LAG), home, 0)
 
     @pl.when(c == 0)
     def _():
@@ -510,15 +520,14 @@
 
     @pl.when(c == 1)
     def _():
-        passed(NS - 2, 0, 0, 0).wait_send()
-        passed(NS - 1, 1, 0, 0).wait_send()
+        for sl in range(2):
+            passed(0, sl, 0).wait_send()
         remote(kvr.at[0], kvr.at[0], hop_s, kv_r.at[0, 0], mate).wait_send()
 
     @pl.when(c == 2)
     def _():
-        for s in ROUND:
-            if s + 4 not in ROUND:
-                passed(s, s % 4, 0, 2).wait_send()
+        for sl in range(2):
+            passed(0, sl, 2).wait_send()
     final_wait(NS - 2, 0)
     final_wait(NS - 1, 1)
     for which, ref in ((0, k), (1, v)):
@@ -565,13 +574,13 @@
             ],
             scratch_shapes=[
                 pltpu.VMEM((n_dev, nb, piece), jnp.int32), pltpu.VMEM((2, 4, 2, 256, 256), bf), pltpu.VMEM((2, 4, rows, hd), bf),
-                pltpu.VMEM((2, 4, rows, hd), bf), pltpu.VMEM((NG, 4, 256, 512), f32), pltpu.VMEM((256, 512), f32),
+                pltpu.VMEM((2, 4, rows, hd), bf), pltpu.VMEM((NG, 4, 256, 512), f32), pltpu.VMEM((6, 256, 512), f32),
                 pltpu.VMEM((2, 2, 256, 256), bf),
                 pltpu.VMEM((4, 2, rows, 256), f32), pltpu.VMEM((4, 2, rows, 256), f32), pltpu.VMEM((4, 2, rows, 256), bf),
                 pltpu.VMEM((4, 2, rows, 128), f32), pltpu.VMEM((4, 2, rows, 128), f32), pltpu.VMEM((2, rows, 128), f32),
                 pltpu.VMEM((2, rows, 128), jnp.int32), pltpu.VMEM((2, rows, hd), f32),
                 dma((n_dev,)), dma((n_dev,)), dma((2, 10)), dma((2, 4)), dma((NG, 4)), dma((2,)), dma((2,)), dma((NJ,)), dma((3, 2)), dma((4, NJ)),
-                dma, dma((3, NS)), dma, dma((2, 4)), dma((2,)), dma((4,)), dma((4,)), dma((NS,)),
+                dma, dma((3, NS)), dma((2, 4)), dma((2,)), dma((3,)), dma((2,)), dma((NS,)),
             ],
             compiler_params=pltpu.CompilerParams(has_side_effects=True, vmem_limit_bytes=62 * 1024 * 1024),
             name="attend",

time: 449 us -> 363 us (0.81)
  Pallas kernels: 421 us -> 331 us
    pallas_call x1, Pallas kernels: 421 us -> 331 us  [per_device(): pl.pallas_call(functools.partial(fused_kernel, hd ** (-0.5)), in_specs=[V...]
where the time goes in v9:
time: 363 us; the launch traced here: 359 us
  Pallas kernels  331 us (91%)
  local copies, waits for them, and re-layouts  26.6 us (7%)
    pallas_call x1, Pallas kernels, per_device(): pl.pallas_call(functools.partial(fused_kernel, hd ** (-0.5)), in_specs=[V...  331 us
    unnamed x10, local copies, waits for them, and re-layouts  26.6 us

profile of v9, /device:TPU:0, one launch (start us, length us, event | category | flops | bytes accessed | tf_op | source)
XLA Modules:
  0.0 358.6 jit_solution(14009295856343584755)
XLA Ops:
  0.6 331.4 %attend.1 = (bf16[32,1024,256]{2,1,0:T(8,128)(2,1)}, bf16[32,1024,256]{2,1,0:T(8,128)(2,1)}, bf16[32,128,256]{2,1,0:T(8,128)(2,1)}, bf16[32,128,256]{2,1,0:T(8,1...) custom-call(s32[32,128]{1,0:T(8,128)} %doc.1, ...), custom_call_target="tpu_custom_call" | custom-call | tf_op jit(solution)/shard_map/attend/pallas_call | solution.py:566
  332.0 0.0 copy-start
  332.0 14.6 %copy.15 = bf16[32,128,8,256]{3,2,1,0:T(8,128)(2,1)} copy(bf16[32,128,8,256]{3,2,1,0:T(8,128)(2,1)} %bitcast.15) | data formatting | bytes 33554432
  346.6 2.3 copy-done
  348.9 0.0 copy-start.2
  348.9 0.0 copy-start.1
  348.9 7.1 %copy.16 = bf16[32,128,8,256]{3,2,1,0:T(8,128)(2,1)} copy(bf16[32,128,8,256]{3,2,1,0:T(8,128)(2,1)S(1)} %bitcast.14) | data formatting | bytes 33554432
  355.9 0.0 copy-done.2
  355.9 1.3 copy.17
  357.3 0.0 copy-done.1
  357.3 1.3 copy.18
Async XLA Ops:
  332.0 16.9 %copy-start = (bf16[32,1024,256]{2,1,0:T(8,128)(2,1)S(1)}, bf16[32,1024,256]{2,1,0:T(8,128)(2,1)}, u32[]{:S(2)}) copy-start(bf16[32,1024,256]{2,1,0:T(8,128)(2,1)} %get-tuple-element.9) | copy-start | bytes 50331652
  348.9 7.1 %copy-start.2 = (bf16[32,128,256]{2,1,0:T(8,128)(2,1)S(1)}, bf16[32,128,256]{2,1,0:T(8,128)(2,1)}, u32[]{:S(2)}) copy-start(bf16[32,128,256]{2,1,0:T(8,128)(2,1)} %get-tuple-element.10) | copy-start | bytes 6291460
  348.9 8.4 %copy-start.1 = (bf16[32,128,256]{2,1,0:T(8,128)(2,1)S(1)}, bf16[32,128,256]{2,1,0:T(8,128)(2,1)}, u32[]{:S(2)}) copy-start(bf16[32,128,256]{2,1,0:T(8,128)(2,1)} %get-tuple-element.11) | copy-start | bytes 6291460

commit v10 on v9

--- a/solution.py
+++ b/solution.py
@@ -13,10 +13,10 @@
 NJ = NS
 AHEAD = 2
 NG = 4
-ROUND = (0, 1, 4, 7, 8, 9, 10, 14)
-EARLY_X = {12: 0, 15: 1}
-EARLY_Y = {4: 0, 6: 1, 9: 4, 12: 7, 15: 8}
-LAG = (2, 5, 6)
+ROUND = (0, 2, 4, 8, 9, 11, 13, 14)
+EARLY_X = {7: 0, 10: 1, 13: 2, 15: 3}
+EARLY_Y = {7: 0, 9: 2, 12: 4, 15: 8}
+LAG = (4, 5, 7)
 
 
 def dot_nt(a, b):
@@ -278,6 +278,13 @@
 
         def g_of(role):
             return qg[slot, 2 + role]
+
+        def far_loop(body):
+            for chip in range(1, 4):
+                @pl.when(c == chip)
+                def _():
+                    for d in range(1, chip + 1):
+                        body(d, 0)
 
         def scores(role, d, causal):
             sc = dot_nt(qg[slot, role], kvs[slot, d, 0]) * cs
@@ -308,30 +315,22 @@
             for role in range(2):
                 dprob(role, d)
             return x
-        lax.fori_loop(1, c + 1, far_scores, 0)
-
-        for role in range(2):
-            top = jnp.broadcast_to(jnp.max(t_scr[role], axis=1, keepdims=True), (1024, 128))
-            t_scr[role] = top
-            f = jnp.exp2(f_scr[0, role] - top)
-            f_scr[0, role] = f
-            l_scr[0, role] = l_scr[0, role] * f
+        far_loop(far_scores)
+
+        for role in range(2):
+            t_scr[role] = jnp.broadcast_to(jnp.max(t_scr[role], axis=1, keepdims=True), (1024, 128))
         dprob(0, 0)
 
-        def far_sums(d, x):
-            for role in range(2):
-                f = jnp.exp2(f_scr[d, role] - t_scr[role])
-                f_scr[d, role] = f
-                l_scr[0, role] = l_scr[0, role] + l_scr[d, role] * f
-            return x
-        lax.fori_loop(1, c + 1, far_sums, 0)
-
-        for role in range(2):
-            t_scr[role] = jnp.broadcast_to(1.0 / jnp.sum(l_scr[0, role], axis=1, keepdims=True), (1024, 128))
+        for role in range(2):
+            top = t_scr[role]
+            norm = l_scr[0, role] * jnp.exp2(f_scr[0, role] - top)
+            for d in range(1, 4):
+                norm = norm + l_scr[d, role] * jnp.exp2(f_scr[d, role] - top)
+            t_scr[role] = top + jnp.log2(jnp.broadcast_to(jnp.sum(norm, axis=1, keepdims=True), (1024, 128)))
         dprob(1, 0)
 
         def weighted(role, d):
-            f = f_scr[d, role] * t_scr[role]
+            f = jnp.exp2(f_scr[d, role] - t_scr[role])
             f_scr[d, role] = f
             for half in (lo_half, hi_half):
                 p_scr[d, role, :, half] = (e_scr[d, role, :, half] * f).astype(jnp.bfloat16)
@@ -348,7 +347,7 @@
                 o_acc[role] = o_acc[role] + weighted(role, d)
             value_grads(d)
             return x
-        lax.fori_loop(1, c + 1, far_weighted, 0)
+        far_loop(far_weighted)
 
         for role in range(2):
             o_low = o_acc[role].astype(jnp.bfloat16)
@@ -377,7 +376,7 @@
             for role in range(2):
                 o_acc[role] = o_acc[role] + got[role]
             return x
-        lax.fori_loop(1, c + 1, far_grads, 0)
+        far_loop(far_grads)
         for role in range(2):
             outb[slot, 2 + role] = (o_acc[role] * scale).astype(jnp.bfloat16)
 
@@ -426,6 +425,9 @@
             value = value + sums[n]
         finalize(s, value)
 
+    for d in range(1, 4):
+        f_scr[d] = jnp.full((2, 1024, 128), NEG_BIG, jnp.float32)
+        l_scr[d] = jnp.zeros((2, 1024, 128), jnp.float32)
     arrive(0)
     fetch(0, 0)
 

time: 363 us -> 362 us (level)
  no operation moved by 1% of the time
where the time goes in v10:
time: 362 us; the launch traced here: 357 us
  Pallas kernels  330 us (91%)
  local copies, waits for them, and re-layouts  26.6 us (7%)
    pallas_call x1, Pallas kernels, per_device(): pl.pallas_call(functools.partial(fused_kernel, hd ** (-0.5)), in_specs=[V...  330 us
    unnamed x10, local copies, waits for them, and re-layouts  26.6 us

profile of v10, /device:TPU:0, one launch (start us, length us, event | category | flops | bytes accessed | tf_op | source)
XLA Modules:
  0.0 357.2 jit_solution(14145047732754732964)
XLA Ops:
  0.6 330.0 %attend.1 = (bf16[32,1024,256]{2,1,0:T(8,128)(2,1)}, bf16[32,1024,256]{2,1,0:T(8,128)(2,1)}, bf16[32,128,256]{2,1,0:T(8,128)(2,1)}, bf16[32,128,256]{2,1,0:T(8,1...) custom-call(s32[32,128]{1,0:T(8,128)} %doc.1, ...), custom_call_target="tpu_custom_call" | custom-call | tf_op jit(solution)/shard_map/attend/pallas_call | solution.py:568
  330.6 0.0 copy-start
  330.6 14.6 %copy.15 = bf16[32,128,8,256]{3,2,1,0:T(8,128)(2,1)} copy(bf16[32,128,8,256]{3,2,1,0:T(8,128)(2,1)} %bitcast.15) | data formatting | bytes 33554432
  345.2 2.3 copy-done
  347.5 0.0 copy-start.2
  347.5 0.0 copy-start.1
  347.5 7.1 %copy.16 = bf16[32,128,8,256]{3,2,1,0:T(8,128)(2,1)} copy(bf16[32,128,8,256]{3,2,1,0:T(8,128)(2,1)S(1)} %bitcast.14) | data formatting | bytes 33554432
  354.6 0.0 copy-done.2
  354.6 1.3 copy.17
  355.9 0.0 copy-done.1
  355.9 1.3 copy.18
Async XLA Ops:
  330.6 16.9 %copy-start = (bf16[32,1024,256]{2,1,0:T(8,128)(2,1)S(1)}, bf16[32,1024,256]{2,1,0:T(8,128)(2,1)}, u32[]{:S(2)}) copy-start(bf16[32,1024,256]{2,1,0:T(8,128)(2,1)} %get-tuple-element.9) | copy-start | bytes 50331652
  347.5 7.1 %copy-start.2 = (bf16[32,128,256]{2,1,0:T(8,128)(2,1)S(1)}, bf16[32,128,256]{2,1,0:T(8,128)(2,1)}, u32[]{:S(2)}) copy-start(bf16[32,128,256]{2,1,0:T(8,128)(2,1)} %get-tuple-element.10) | copy-start | bytes 6291460
  347.5 8.4 %copy-start.1 = (bf16[32,128,256]{2,1,0:T(8,128)(2,1)S(1)}, bf16[32,128,256]{2,1,0:T(8,128)(2,1)}, u32[]{:S(2)}) copy-start(bf16[32,128,256]{2,1,0:T(8,128)(2,1)} %get-tuple-element.11) | copy-start | bytes 6291460

commit v11 on v10

--- a/solution.py
+++ b/solution.py
@@ -384,7 +384,15 @@
         remote(part.at[slot, s], part.at[slot, s], hop_s, part_r.at[slot, s], mate).wait_recv()
 
     def load(src, i):
-        return pltpu.make_async_copy(src, sums.at[i], lsem.at[i])
+        return [pltpu.make_async_copy(src.at[pl.ds(64 * n, 64)], sums.at[i, pl.ds(64 * n, 64)], lsem.at[i, n]) for n in range(4)]
+
+    def start(copies):
+        for copy in copies:
+            copy.start()
+
+    def finish(copies):
+        for copy in copies:
+            copy.wait()
 
     def passed(s, sl, slot):
         return remote(sums.at[4 + sl], part.at[slot, s], xsem.at[sl], part_r.at[slot, s], dev(0))
@@ -394,15 +402,15 @@
 
     def pass_on(i, count, slot):
         sl = lax.rem(count, 2)
-        load(hold.at[0, i], 0).start()
+        start(load(hold.at[0, i], 0))
         part_wait(0, i)
-        load(part.at[0, i], 1).start()
+        start(load(part.at[0, i], 1))
 
         @pl.when(count >= 2)
         def _():
             passed(i, sl, slot).wait_send()
-        load(hold.at[0, i], 0).wait()
-        load(part.at[0, i], 1).wait()
+        finish(load(hold.at[0, i], 0))
+        finish(load(part.at[0, i], 1))
         sums[4 + sl] = sums[0] + sums[1]
         passed(i, sl, slot).start()
 
@@ -417,9 +425,9 @@
 
     def total(s, terms):
         for n, src in enumerate(terms):
-            load(src, n).start()
+            start(load(src, n))
         for n, src in enumerate(terms):
-            load(src, n).wait()
+            finish(load(src, n))
         value = sums[0]
         for n in range(1, len(terms)):
             value = value + sums[n]
@@ -457,8 +465,8 @@
             @pl.when(jnp.logical_not(around(s)))
             def _():
                 part_wait(0, s)
-                load(part.at[0, s], 0).start()
-                load(part.at[0, s], 0).wait()
+                start(load(part.at[0, s], 0))
+                finish(load(part.at[0, s], 0))
                 dkv[gslot, 2] = dkv[gslot, 2] + sums[0]
             finalize(s, dkv[gslot, 0])
         put(s, slot)
@@ -474,6 +482,17 @@
     for s in range(NS - NG, NS):
         grads_out(s, False)
 
+    def finals(i, lag):
+        def end(k):
+            return jnp.clip(k + 1 - lag + jnp.maximum(k - (NS - 1 - lag), 0), 0, NS)
+
+        def deco(body):
+            def one(s, x):
+                body(s)
+                return x
+            lax.fori_loop(end(i - 1), end(i), one, 0)
+        return deco
+
     def home(i, x):
         @pl.when(c == 0)
         def _():
@@ -481,10 +500,8 @@
             def _():
                 part_wait(2, i)
                 relay(i).start()
-            s = i - LAG[0]
-
-            @pl.when((s >= 0) & (s < NS))
-            def _():
+            @finals(i, LAG[0])
+            def _(s):
                 part_wait(1, s)
                 part_wait(0, s)
                 total(s, (hold.at[1, s], part.at[1, s], part.at[0, s]))
@@ -492,27 +509,23 @@
         @pl.when(c == 1)
         def _():
             pl.when((i >= len(EARLY_X)) & (i < NS))(lambda: pass_x(i))
-            s = i - LAG[1]
-
-            @pl.when((s >= 0) & (s < NS))
-            def _():
+            @finals(i, LAG[1])
+            def _(s):
                 part_wait(1, s)
                 total(s, (hold.at[1, s], part.at[1, s]))
 
         @pl.when(c == 2)
         def _():
             pl.when(around(i) & (i > max(EARLY_Y.values())))(lambda: pass_y(i))
-            s = i - LAG[2]
-
-            @pl.when((s >= 0) & (s < NS))
-            def _():
+            @finals(i, LAG[2])
+            def _(s):
                 part_wait(1, s)
                 total(s, (hold.at[1, s], part.at[1, s]))
         return x
 
     @pl.when(c < 3)
     def _():
-        lax.fori_loop(0, NS + max(LAG), home, 0)
+        lax.fori_loop(0, NS + 1, home, 0)
 
     @pl.when(c == 0)
     def _():
@@ -582,7 +595,7 @@
                 pltpu.VMEM((4, 2, rows, 128), f32), pltpu.VMEM((4, 2, rows, 128), f32), pltpu.VMEM((2, rows, 128), f32),
                 pltpu.VMEM((2, rows, 128), jnp.int32), pltpu.VMEM((2, rows, hd), f32),
                 dma((n_dev,)), dma((n_dev,)), dma((2, 10)), dma((2, 4)), dma((NG, 4)), dma((2,)), dma((2,)), dma((NJ,)), dma((3, 2)), dma((4, NJ)),
-                dma, dma((3, NS)), dma((2, 4)), dma((2,)), dma((3,)), dma((2,)), dma((NS,)),
+                dma, dma((3, NS)), dma((2, 4)), dma((2,)), dma((3, 4)), dma((2,)), dma((NS,)),
             ],
             compiler_params=pltpu.CompilerParams(has_side_effects=True, vmem_limit_bytes=62 * 1024 * 1024),
             name="attend",

time: 362 us -> 365 us (level); the launches traced: 357 us -> 364 us
  Pallas kernels: 330 us -> 337 us
    pallas_call x1, Pallas kernels: 330 us -> 337 us  [per_device(): pl.pallas_call(functools.partial(fused_kernel, hd ** (-0.5)), in_specs=[V...]
where the time goes in v11:
time: 365 us; the launch traced here: 364 us
  Pallas kernels  337 us (92%)
  local copies, waits for them, and re-layouts  26.6 us (7%)
    pallas_call x1, Pallas kernels, per_device(): pl.pallas_call(functools.partial(fused_kernel, hd ** (-0.5)), in_specs=[V...  337 us
    unnamed x10, local copies, waits for them, and re-layouts  26.6 us

profile of v11, /device:TPU:0, one launch (start us, length us, event | category | flops | bytes accessed | tf_op | source)
XLA Modules:
  0.0 364.1 jit_solution(15287079861797713937)
XLA Ops:
  0.6 336.9 %attend.1 = (bf16[32,1024,256]{2,1,0:T(8,128)(2,1)}, bf16[32,1024,256]{2,1,0:T(8,128)(2,1)}, bf16[32,128,256]{2,1,0:T(8,128)(2,1)}, bf16[32,128,256]{2,1,0:T(8,1...) custom-call(s32[32,128]{1,0:T(8,128)} %doc.1, ...), custom_call_target="tpu_custom_call" | custom-call | tf_op jit(solution)/shard_map/attend/pallas_call | solution.py:581
  337.5 0.0 copy-start
  337.5 14.6 %copy.15 = bf16[32,128,8,256]{3,2,1,0:T(8,128)(2,1)} copy(bf16[32,128,8,256]{3,2,1,0:T(8,128)(2,1)} %bitcast.15) | data formatting | bytes 33554432
  352.1 2.3 copy-done
  354.4 0.0 copy-start.2
  354.4 0.0 copy-start.1
  354.4 7.1 %copy.16 = bf16[32,128,8,256]{3,2,1,0:T(8,128)(2,1)} copy(bf16[32,128,8,256]{3,2,1,0:T(8,128)(2,1)S(1)} %bitcast.14) | data formatting | bytes 33554432
  361.4 0.0 copy-done.2
  361.4 1.3 copy.17
  362.7 0.0 copy-done.1
  362.7 1.3 copy.18
Async XLA Ops:
  337.5 16.9 %copy-start = (bf16[32,1024,256]{2,1,0:T(8,128)(2,1)S(1)}, bf16[32,1024,256]{2,1,0:T(8,128)(2,1)}, u32[]{:S(2)}) copy-start(bf16[32,1024,256]{2,1,0:T(8,128)(2,1)} %get-tuple-element.9) | copy-start | bytes 50331652
  354.4 7.1 %copy-start.2 = (bf16[32,128,256]{2,1,0:T(8,128)(2,1)S(1)}, bf16[32,128,256]{2,1,0:T(8,128)(2,1)}, u32[]{:S(2)}) copy-start(bf16[32,128,256]{2,1,0:T(8,128)(2,1)} %get-tuple-element.10) | copy-start | bytes 6291460
  354.4 8.4 %copy-start.1 = (bf16[32,128,256]{2,1,0:T(8,128)(2,1)S(1)}, bf16[32,128,256]{2,1,0:T(8,128)(2,1)}, u32[]{:S(2)}) copy-start(bf16[32,128,256]{2,1,0:T(8,128)(2,1)} %get-tuple-element.11) | copy-start | bytes 6291460

commit v12 on v11

--- a/solution.py
+++ b/solution.py
@@ -13,10 +13,25 @@
 NJ = NS
 AHEAD = 2
 NG = 4
-ROUND = (0, 2, 4, 8, 9, 11, 13, 14)
-EARLY_X = {7: 0, 10: 1, 13: 2, 15: 3}
-EARLY_Y = {7: 0, 9: 2, 12: 4, 15: 8}
-LAG = (4, 5, 7)
+PLAN1 = 'RRMMRFRRFRFFRRMM'
+PLAN0 = 'ANNNAAANCCCNNCNN'
+LAST2 = (7, 8, 12)
+EARLY_X = {7: 1, 9: 2, 10: 3, 12: 7, 13: 8, 14: 9, 15: 10}
+EARLY_Y = {5: 0, 6: 1, 8: 4, 10: 6, 11: 7, 13: 9}
+LAG = (4, 7, 7)
+
+
+def where_plan(plan, kinds):
+    return tuple(s for s in range(NS) if plan[s] in kinds)
+
+
+ROUND, MERGE, FAR1 = (where_plan(PLAN1, x) for x in 'RMF')
+HERE0, ON1, ON2 = (where_plan(PLAN0, x) for x in 'NAC')
+OWN1 = where_plan(PLAN1, 'RM')
+OWN2 = tuple(s for s in range(NS) if s not in LAST2)
+OWN3 = tuple(range(NS))
+PASS_X = where_plan(PLAN0, 'NC')
+PASS_0 = where_plan(PLAN0, 'AC')
 
 
 def dot_nt(a, b):
@@ -38,7 +53,7 @@
 
 def fused_kernel(scale, doc, q, g, k, v, o, dq, dk, dv, qgm, kvr, part, hold,
                  docs, kvs, qg, outb, dkv, sums, fin, e_scr, dp_scr, p_scr, l_scr, f_scr, t_scr, docr, o_acc,
-                 doc_s, doc_r, isem, osem, gsem, osend_r, q_s, q_r, kv_s, kv_r, hop_s, part_r, fsem, dsend_r, lsem, xsem, rel_s):
+                 doc_s, doc_r, isem, osem, gsem, osend_r, q_s, q_r, kv_s, kv_r, hop_s, part_r, fsem, dsend_r, lsem, xsem, rel_s, down_r):
     rank = lax.axis_index('cp')
     n_dev = docs.shape[0]
     c = rank // 2
@@ -181,45 +196,55 @@
     def give(sl, d, chip, slot, s):
         return remote(dkv.at[sl, d], part.at[slot, s], gsem.at[sl, d], part_r.at[slot, s], dev(chip))
 
-    def around(s):
+    def member(s, group):
         out = jnp.bool_(False)
-        for one in ROUND:
+        for one in group:
             out = out | (s == one)
         return out
 
-    def grads_out(s, start):
-        even = jnp.logical_not(around(s))
+    def rank_in(s, group):
+        count = jnp.int32(0)
+        for one in group:
+            count = count + jnp.where(one < s, 1, 0)
+        return count
+
+    def choose(cond, yes, no):
+        pl.when(cond)(yes)
+        pl.when(jnp.logical_not(cond))(no)
+
+    def grads_out(s, begin):
         sl = lax.rem(s, NG)
 
         def local(d, slot):
             copy = keep(sl, d, slot, s)
-            copy.start() if start else copy.wait()
+            copy.start() if begin else copy.wait()
 
         def away(d, chip, slot):
             copy = give(sl, d, chip, slot, s)
-            copy.start() if start else copy.wait_send()
-
-        @pl.when(c < 3)
+            copy.start() if begin else copy.wait_send()
+
+        @pl.when(c == 0)
         def _():
             local(0, 1)
 
         @pl.when(c == 1)
         def _():
+            choose(member(s, FAR1), lambda: away(0, 3, 2), lambda: local(0, 1))
             local(1, 0)
 
         @pl.when(c == 2)
         def _():
-            away(2, 0, 1)
-            pl.when(even)(lambda: away(1, 3, 0))
-            pl.when(jnp.logical_not(even))(lambda: local(1, 0))
-
-        @pl.when(c == 3)
-        def _():
-            if not start:
+            choose(member(s, ROUND), lambda: local(1, 0), lambda: away(1, 3, 0))
+            choose(member(s, LAST2), lambda: away(0, 3, 1), lambda: local(0, 1))
+            choose(member(s, ON2), lambda: local(2, 2), lambda: away(2, 0, 1))
+
+        if not begin:
+            @pl.when(c == 3)
+            def _():
                 away(3, 1, 0)
-            pl.when(even)(lambda: away(2, 1, 1))
-            pl.when(jnp.logical_not(even))(lambda: away(2, 2, 0))
-            away(1, 2, 1)
+                pl.when(member(s, ROUND))(lambda: away(2, 2, 0))
+                pl.when(member(s, MERGE))(lambda: away(2, 1, 1))
+                pl.when(jnp.logical_not(member(s, LAST2)))(lambda: away(1, 2, 1))
 
     def put(s, sl):
         here, there = row_outputs(s, sl)
@@ -234,33 +259,39 @@
         for copy in there:
             copy.wait_send()
 
-    def final_copies(s, sl):
+    def final_copies(kind, sl, s, chip):
         row = mine + s
-        rows, rest = pl.ds(128 * e, 128), pl.ds(128 - 128 * e, 128)
-        here = [pltpu.make_async_copy(fin.at[sl, 0, rows], dk.at[row], fsem.at[sl, 0]),
-                pltpu.make_async_copy(fin.at[sl, 1, rows], dv.at[row], fsem.at[sl, 1])]
-        there = [remote(fin.at[sl, 0, rest], dk.at[row], fsem.at[sl, 2], dsend_r.at[0], mate),
-                 remote(fin.at[sl, 1, rest], dv.at[row], fsem.at[sl, 3], dsend_r.at[1], mate)]
-        return here, there
-
-    def final_wait(s, sl):
-        here, there = final_copies(s, sl)
-        for copy in here:
-            copy.wait()
-        for copy in there:
-            copy.wait_send()
-
-    def finalize(s, total):
-        sl = lax.rem(s, 2)
-
-        @pl.when(s >= 2)
-        def _():
-            final_wait(s - 2, sl)
-        fin[sl, 0] = (total[:, :256] * scale).astype(jnp.bfloat16)
-        fin[sl, 1] = total[:, 256:].astype(jnp.bfloat16)
-        here, there = final_copies(s, sl)
-        for copy in here + there:
+        out = []
+        for which, ref in ((0, dk), (1, dv)):
+            for far, rows in ((0, pl.ds(128 * e, 128)), (1, pl.ds(128 - 128 * e, 128))):
+                src, sem = fin.at[kind, sl, which, rows], fsem.at[kind, sl, 2 * which + far]
+                if far:
+                    out.append(remote(src, ref.at[row], sem, dsend_r.at[which], mate if chip is None else 2 * chip + 1 - e))
+                elif chip is None:
+                    out.append(pltpu.make_async_copy(src, ref.at[row], sem))
+                else:
+                    out.append(remote(src, ref.at[row], sem, down_r.at[which], dev(chip)))
+        return out
+
+    def final_wait(kind, sl, chip):
+        for i, copy in enumerate(final_copies(kind, sl, 0, chip)):
+            if chip is None and i % 2 == 0:
+                copy.wait()
+            else:
+                copy.wait_send()
+
+    def finalize(kind, group, s, value, chip):
+        count = rank_in(s, group)
+        sl = lax.rem(count, 2)
+        pl.when(count >= 2)(lambda: final_wait(kind, sl, chip))
+        fin[kind, sl, 0] = (value[:, :256] * scale).astype(jnp.bfloat16)
+        fin[kind, sl, 1] = value[:, 256:].astype(jnp.bfloat16)
+        for copy in final_copies(kind, sl, s, chip):
             copy.start()
+
+    def final_drain(kind, group, chip):
+        for n in range(max(0, len(group) - 2), len(group)):
+            final_wait(kind, n % 2, chip)
 
     row_tok = lax.broadcasted_iota(jnp.int32, (1024, 128), 0) >> 3
     lane = lax.broadcasted_iota(jnp.int32, (1024, 128), 1)
@@ -394,36 +425,34 @@
         for copy in copies:
             copy.wait()
 
-    def passed(s, sl, slot):
-        return remote(sums.at[4 + sl], part.at[slot, s], xsem.at[sl], part_r.at[slot, s], dev(0))
+    def passed(s, sl, chip, slot):
+        return remote(sums.at[4 + sl], part.at[slot, s], xsem.at[sl], part_r.at[slot, s], dev(chip))
 
     def relay(s):
         return remote(part.at[2, s], part.at[1, s], rel_s.at[s], part_r.at[1, s], dev(1))
 
-    def pass_on(i, count, slot):
+    def pass_on(i, group, held, slot_in, chip, slot_out):
+        count = rank_in(i, group)
         sl = lax.rem(count, 2)
-        start(load(hold.at[0, i], 0))
-        part_wait(0, i)
-        start(load(part.at[0, i], 1))
-
-        @pl.when(count >= 2)
-        def _():
-            passed(i, sl, slot).wait_send()
-        finish(load(hold.at[0, i], 0))
-        finish(load(part.at[0, i], 1))
+        start(load(hold.at[held, i], 0))
+        part_wait(slot_in, i)
+        start(load(part.at[slot_in, i], 1))
+        pl.when(count >= 2)(lambda: passed(i, sl, chip, slot_out).wait_send())
+        finish(load(hold.at[held, i], 0))
+        finish(load(part.at[slot_in, i], 1))
         sums[4 + sl] = sums[0] + sums[1]
-        passed(i, sl, slot).start()
+        passed(i, sl, chip, slot_out).start()
 
     def pass_x(i):
-        pass_on(i, jnp.int32(i), 0)
+        pass_on(i, PASS_X, 0, 0, 0, 0)
 
     def pass_y(i):
-        count = jnp.int32(0)
-        for one in ROUND:
-            count = count + jnp.where(one < i, 1, 0)
-        pass_on(i, count, 2)
-
-    def total(s, terms):
+        pass_on(i, ROUND, 0, 0, 0, 2)
+
+    def total(kind, group, s, held, slots, chip):
+        terms = [hold.at[held, s]] + [part.at[slot, s] for slot in slots]
+        for slot in slots:
+            part_wait(slot, s)
         for n, src in enumerate(terms):
             start(load(src, n))
         for n, src in enumerate(terms):
@@ -431,7 +460,7 @@
         value = sums[0]
         for n in range(1, len(terms)):
             value = value + sums[n]
-        finalize(s, value)
+        finalize(kind, group, s, value, chip)
 
     for d in range(1, 4):
         f_scr[d] = jnp.full((2, 1024, 128), NEG_BIG, jnp.float32)
@@ -461,14 +490,33 @@
         def _():
             gslot = lax.rem(s, NG)
             give(gslot, 3, 1, 0, s).start()
-
-            @pl.when(jnp.logical_not(around(s)))
+            pl.when(member(s, ROUND))(lambda: give(gslot, 2, 2, 0, s).start())
+
+            @pl.when(member(s, MERGE))
             def _():
                 part_wait(0, s)
                 start(load(part.at[0, s], 0))
                 finish(load(part.at[0, s], 0))
                 dkv[gslot, 2] = dkv[gslot, 2] + sums[0]
-            finalize(s, dkv[gslot, 0])
+
+            @pl.when(member(s, FAR1))
+            def _():
+                part_wait(0, s)
+                start(load(part.at[0, s], 0))
+                part_wait(2, s)
+                start(load(part.at[2, s], 1))
+                finish(load(part.at[0, s], 0))
+                finish(load(part.at[2, s], 1))
+                finalize(1, FAR1, s, dkv[gslot, 2] + sums[0] + sums[1], 1)
+            finalize(0, OWN3, s, dkv[gslot, 0], None)
+            pl.when(member(s, MERGE))(lambda: give(gslot, 2, 1, 1, s).start())
+
+            def last_two():
+                part_wait(1, s)
+                start(load(part.at[1, s], 2))
+                finish(load(part.at[1, s], 2))
+                finalize(2, LAST2, s, dkv[gslot, 1] + sums[2], 2)
+            choose(member(s, LAST2), last_two, lambda: give(gslot, 1, 2, 1, s).start())
         put(s, slot)
         for at, i in EARLY_X.items():
             pl.when((c == 1) & (s == at))(lambda: pass_x(i))
@@ -482,69 +530,83 @@
     for s in range(NS - NG, NS):
         grads_out(s, False)
 
-    def finals(i, lag):
-        def end(k):
-            return jnp.clip(k + 1 - lag + jnp.maximum(k - (NS - 1 - lag), 0), 0, NS)
-
-        def deco(body):
-            def one(s, x):
-                body(s)
-                return x
-            lax.fori_loop(end(i - 1), end(i), one, 0)
-        return deco
-
     def home(i, x):
+        def behind(lag, body):
+            s = i - lag
+            pl.when((s >= 0) & (s < NS))(lambda: body(s))
+
         @pl.when(c == 0)
         def _():
-            @pl.when(around(i))
+            @pl.when(member(i, ROUND))
             def _():
                 part_wait(2, i)
                 relay(i).start()
-            @finals(i, LAG[0])
-            def _(s):
-                part_wait(1, s)
-                part_wait(0, s)
-                total(s, (hold.at[1, s], part.at[1, s], part.at[0, s]))
+            pl.when(member(i, ON1))(lambda: pass_on(i, PASS_0, 1, 1, 1, 2))
+            pl.when(member(i, ON2))(lambda: pass_on(i, PASS_0, 1, 0, 2, 2))
+            behind(LAG[0], lambda s: pl.when(member(s, HERE0))(lambda: total(0, HERE0, s, 1, (1, 0), None)))
 
         @pl.when(c == 1)
         def _():
-            pl.when((i >= len(EARLY_X)) & (i < NS))(lambda: pass_x(i))
-            @finals(i, LAG[1])
-            def _(s):
-                part_wait(1, s)
-                total(s, (hold.at[1, s], part.at[1, s]))
+            later = tuple(s for s in PASS_X if s not in EARLY_X.values())
+            pl.when(member(i, later))(lambda: pass_x(i))
+
+            def body(s):
+                pl.when(member(s, ON1))(lambda: total(1, ON1, s, 0, (0, 2), 0))
+                pl.when(member(s, OWN1))(lambda: total(0, OWN1, s, 1, (1,), None))
+            behind(LAG[1], body)
 
         @pl.when(c == 2)
         def _():
-            pl.when(around(i) & (i > max(EARLY_Y.values())))(lambda: pass_y(i))
-            @finals(i, LAG[2])
-            def _(s):
-                part_wait(1, s)
-                total(s, (hold.at[1, s], part.at[1, s]))
+            later = tuple(s for s in ROUND if s not in EARLY_Y.values())
+            pl.when(member(i, later))(lambda: pass_y(i))
+
+            def body(s):
+                pl.when(member(s, ON2))(lambda: total(1, ON2, s, 2, (2,), 0))
+                pl.when(member(s, OWN2))(lambda: total(0, OWN2, s, 1, (1,), None))
+            behind(LAG[2], body)
         return x
 
     @pl.when(c < 3)
     def _():
-        lax.fori_loop(0, NS + 1, home, 0)
+        lax.fori_loop(0, NS + max(LAG), home, 0)
+
+    def down_wait(n):
+        for which, ref in ((0, dk), (1, dv)):
+            rows = ref.at[pl.ds(0, n)]
+            remote(rows, rows, hop_s, down_r.at[which], mate).wait_recv()
 
     @pl.when(c == 0)
     def _():
         for s in ROUND:
             relay(s).wait_send()
+        for sl in range(2):
+            passed(0, sl, 1, 2).wait_send()
         remote(kvr.at[1], kvr.at[1], hop_s, kv_r.at[0, 0], mate).wait_send()
+        final_drain(0, HERE0, None)
+        down_wait(len(PASS_0))
 
     @pl.when(c == 1)
     def _():
         for sl in range(2):
-            passed(0, sl, 0).wait_send()
+            passed(0, sl, 0, 0).wait_send()
         remote(kvr.at[0], kvr.at[0], hop_s, kv_r.at[0, 0], mate).wait_send()
+        final_drain(0, OWN1, None)
+        final_drain(1, ON1, 0)
+        down_wait(len(FAR1))
 
     @pl.when(c == 2)
     def _():
         for sl in range(2):
-            passed(0, sl, 2).wait_send()
-    final_wait(NS - 2, 0)
-    final_wait(NS - 1, 1)
+            passed(0, sl, 0, 2).wait_send()
+        final_drain(0, OWN2, None)
+        final_drain(1, ON2, 0)
+        down_wait(len(LAST2))
+
+    @pl.when(c == 3)
+    def _():
+        final_drain(0, OWN3, None)
+        final_drain(1, FAR1, 1)
+        final_drain(2, LAST2, 2)
     for which, ref in ((0, k), (1, v)):
         for way in range(2):
             @pl.when((c < 2) | ((c == 2) & (way == 0)))
@@ -585,17 +647,17 @@
             out_shape=[
                 shape((nb, rows, hd), bf), shape((nb, rows, hd), bf), shape((nb, piece, hd), bf), shape((nb, piece, hd), bf),
                 shape((NS, 2, rows, hd), bf), shape((4, NS, 2, 256, 256), bf),
-                shape((3, NS, 256, 512), f32), shape((2, NS, 256, 512), f32),
+                shape((3, NS, 256, 512), f32), shape((3, NS, 256, 512), f32),
             ],
             scratch_shapes=[
                 pltpu.VMEM((n_dev, nb, piece), jnp.int32), pltpu.VMEM((2, 4, 2, 256, 256), bf), pltpu.VMEM((2, 4, rows, hd), bf),
                 pltpu.VMEM((2, 4, rows, hd), bf), pltpu.VMEM((NG, 4, 256, 512), f32), pltpu.VMEM((6, 256, 512), f32),
-                pltpu.VMEM((2, 2, 256, 256), bf),
+                pltpu.VMEM((3, 2, 2, 256, 256), bf),
                 pltpu.VMEM((4, 2, rows, 256), f32), pltpu.VMEM((4, 2, rows, 256), f32), pltpu.VMEM((4, 2, rows, 256), bf),
                 pltpu.VMEM((4, 2, rows, 128), f32), pltpu.VMEM((4, 2, rows, 128), f32), pltpu.VMEM((2, rows, 128), f32),
                 pltpu.VMEM((2, rows, 128), jnp.int32), pltpu.VMEM((2, rows, hd), f32),
                 dma((n_dev,)), dma((n_dev,)), dma((2, 10)), dma((2, 4)), dma((NG, 4)), dma((2,)), dma((2,)), dma((NJ,)), dma((3, 2)), dma((4, NJ)),
-                dma, dma((3, NS)), dma((2, 4)), dma((2,)), dma((3, 4)), dma((2,)), dma((NS,)),
+                dma, dma((3, NS)), dma((3, 2, 4)), dma((2,)), dma((3, 4)), dma((2,)), dma((NS,)), dma((2,)),
             ],
             compiler_params=pltpu.CompilerParams(has_side_effects=True, vmem_limit_bytes=62 * 1024 * 1024),
             name="attend",

time: 365 us -> 337 us (0.923)
  Pallas kernels: 337 us -> 308 us
    pallas_call x1, Pallas kernels: 337 us -> 308 us  [per_device(): pl.pallas_call(functools.partial(fused_kernel, hd ** (-0.5)), in_specs=[V...]
where the time goes in v12:
time: 337 us; the launch traced here: 336 us
  Pallas kernels  308 us (91%)
  local copies, waits for them, and re-layouts  26.6 us (8%)
    pallas_call x1, Pallas kernels, per_device(): pl.pallas_call(functools.partial(fused_kernel, hd ** (-0.5)), in_specs=[V...  308 us
    unnamed x10, local copies, waits for them, and re-layouts  26.6 us

profile of v12, /device:TPU:0, one launch (start us, length us, event | category | flops | bytes accessed | tf_op | source)
XLA Modules:
  0.0 335.7 jit_solution(3834555577474112959)
XLA Ops:
  0.6 308.5 %attend.1 = (bf16[32,1024,256]{2,1,0:T(8,128)(2,1)}, bf16[32,1024,256]{2,1,0:T(8,128)(2,1)}, bf16[32,128,256]{2,1,0:T(8,128)(2,1)}, bf16[32,128,256]{2,1,0:T(8,1...) custom-call(s32[32,128]{1,0:T(8,128)} %doc.1, ...), custom_call_target="tpu_custom_call" | custom-call | tf_op jit(solution)/shard_map/attend/pallas_call | solution.py:643
  309.1 0.0 copy-start
  309.1 14.6 %copy.15 = bf16[32,128,8,256]{3,2,1,0:T(8,128)(2,1)} copy(bf16[32,128,8,256]{3,2,1,0:T(8,128)(2,1)} %bitcast.15) | data formatting | bytes 33554432
  323.7 2.3 copy-done
  326.0 0.0 copy-start.2
  326.0 0.0 copy-start.1
  326.0 7.1 %copy.16 = bf16[32,128,8,256]{3,2,1,0:T(8,128)(2,1)} copy(bf16[32,128,8,256]{3,2,1,0:T(8,128)(2,1)S(1)} %bitcast.14) | data formatting | bytes 33554432
  333.0 0.0 copy-done.2
  333.0 1.3 copy.17
  334.4 0.0 copy-done.1
  334.4 1.3 copy.18
Async XLA Ops:
  309.1 16.9 %copy-start = (bf16[32,1024,256]{2,1,0:T(8,128)(2,1)S(1)}, bf16[32,1024,256]{2,1,0:T(8,128)(2,1)}, u32[]{:S(2)}) copy-start(bf16[32,1024,256]{2,1,0:T(8,128)(2,1)} %get-tuple-element.9) | copy-start | bytes 50331652
  326.0 7.1 %copy-start.2 = (bf16[32,128,256]{2,1,0:T(8,128)(2,1)S(1)}, bf16[32,128,256]{2,1,0:T(8,128)(2,1)}, u32[]{:S(2)}) copy-start(bf16[32,128,256]{2,1,0:T(8,128)(2,1)} %get-tuple-element.10) | copy-start | bytes 6291460
  326.0 8.4 %copy-start.1 = (bf16[32,128,256]{2,1,0:T(8,128)(2,1)S(1)}, bf16[32,128,256]{2,1,0:T(8,128)(2,1)}, u32[]{:S(2)}) copy-start(bf16[32,128,256]{2,1,0:T(8,128)(2,1)} %get-tuple-element.11) | copy-start | bytes 6291460

commit v13 on v12

--- a/solution.py
+++ b/solution.py
@@ -623,6 +623,39 @@
     for which, ref in ((0, dk), (1, dv)):
         half = ref.at[pl.ds(other, NS)]
         remote(half, half, hop_s, dsend_r.at[which], mate).wait_recv()
+
+
+def place_kernel(slots, *refs):
+    srcs, dsts, (buf, rsem, wsem) = refs[:4], refs[4:8], refs[8:]
+    jobs = []
+    for src, dst in zip(srcs, dsts):
+        n = src.shape[0]
+        size = 512 * 1024 // (src.shape[1] * src.shape[2])
+        for i in range(0, n, size):
+            shape = (size,) + tuple(src.shape[1:])
+            jobs.append((src.at[pl.ds(i, size)], dst.at[pl.ds(i, size)], shape))
+
+    def view(slot, shape):
+        return buf.at[slot].reshape(shape)
+
+    def read(j):
+        return pltpu.make_async_copy(jobs[j][0], view(j % slots, jobs[j][2]), rsem.at[j % slots])
+
+    def write(j):
+        return pltpu.make_async_copy(view(j % slots, jobs[j][2]), jobs[j][1], wsem.at[j % slots])
+
+    ahead = slots // 2
+    for j in range(min(ahead, len(jobs))):
+        read(j).start()
+    for j in range(len(jobs)):
+        read(j).wait()
+        write(j).start()
+        if j + ahead < len(jobs):
+            if j + ahead >= slots:
+                write(j + ahead - slots).wait()
+            read(j + ahead).start()
+    for j in range(max(0, len(jobs) - slots), len(jobs)):
+        write(j).wait()
 
 
 ANY = pl.BlockSpec(memory_space=pl.ANY)
@@ -662,7 +695,15 @@
             compiler_params=pltpu.CompilerParams(has_side_effects=True, vmem_limit_bytes=62 * 1024 * 1024),
             name="attend",
         )(doc_id, query.reshape(nb, rows, hd), grad_out.reshape(nb, rows, hd), keys.reshape(nb, piece, hd), values.reshape(nb, piece, hd))
-        o, dq, dk, dv = outs[:4]
+        outs = [x.reshape(nb, -1, hd) for x in outs[:4]]
+        o, dq, dk, dv = pl.pallas_call(
+            functools.partial(place_kernel, 24),
+            in_specs=[ANY] * 4,
+            out_specs=[ANY] * 4,
+            out_shape=[shape(x.shape, bf) for x in outs],
+            scratch_shapes=[pltpu.VMEM((24, 2048, hd), bf), dma((24,)), dma((24,))],
+            name="place",
+        )(*outs)
         return o.reshape(query.shape), dq.reshape(query.shape), dk.reshape(keys.shape), dv.reshape(values.shape)
 
     return jax.shard_map(per_device, mesh=mesh, in_specs=(seq_spec, seq_spec, seq_spec, seq_spec, id_spec),

time: 337 us -> 336 us (level)
  local copies, waits for them, and re-layouts: 26.6 us -> 0 us
  Pallas kernels: 308 us -> 334 us
    unnamed x10 -> x0, local copies, waits for them, and re-layouts: 26.6 us -> none
    pallas_call x0 -> x1, Pallas kernels: none -> 25.7 us  [per_device(): pl.pallas_call(functools.partial(place_kernel, 24), in_specs=[ANY] * 4, o...]
where the time goes in v13:
time: 336 us; the launch traced here: 335 us
  Pallas kernels  334 us (99%)
    pallas_call x1, Pallas kernels, per_device(): pl.pallas_call(functools.partial(fused_kernel, hd ** (-0.5)), in_specs=[V...  308 us
    pallas_call x1, Pallas kernels, per_device(): pl.pallas_call(functools.partial(place_kernel, 24), in_specs=[ANY] * 4, o...  25.7 us

profile of v13, /device:TPU:0, one launch (start us, length us, event | category | flops | bytes accessed | tf_op | source)
XLA Modules:
  0.0 335.0 jit_solution(1181859833857036403)
XLA Ops:
  0.6 308.5 %attend.1 = (bf16[32,1024,256]{2,1,0:T(8,128)(2,1)}, bf16[32,1024,256]{2,1,0:T(8,128)(2,1)}, bf16[32,128,256]{2,1,0:T(8,128)(2,1)}, bf16[32,128,256]{2,1,0:T(8,1...) custom-call(s32[32,128]{1,0:T(8,128)} %doc.1, ...), custom_call_target="tpu_custom_call" | custom-call | tf_op jit(solution)/shard_map/attend/pallas_call | solution.py:676
  309.1 25.7 %place.1 = (bf16[32,1024,256]{2,1,0:T(8,128)(2,1)}, bf16[32,1024,256]{2,1,0:T(8,128)(2,1)}, bf16[32,128,256]{2,1,0:T(8,128)(2,1)}, bf16[32,128,256]{2,1,0:T(8,128)(2,1)}) custom-call(bf16[32,1024,256]{2,1,0:T(8,128)(2,1)} %get-tuple-element.12.refs_0_, bf16[32,1024,256]{2,1,0:T(8,128)(2,1)} %get-tuple-element.13.refs_1_, ...), custom_call_target="tpu_custom_call" | custom-call | tf_op jit(solution)/shard_map/place/pallas_call | solution.py:699

commit v14 on v13

--- a/solution.py
+++ b/solution.py
@@ -13,12 +13,12 @@
 NJ = NS
 AHEAD = 2
 NG = 4
-PLAN1 = 'RRMMRFRRFRFFRRMM'
-PLAN0 = 'ANNNAAANCCCNNCNN'
-LAST2 = (7, 8, 12)
-EARLY_X = {7: 1, 9: 2, 10: 3, 12: 7, 13: 8, 14: 9, 15: 10}
-EARLY_Y = {5: 0, 6: 1, 8: 4, 10: 6, 11: 7, 13: 9}
-LAG = (4, 7, 7)
+PLAN1 = 'RMRMRRFRRFRFFRMM'
+PLAN0 = 'NNNANCNNACCNCNNN'
+LAST2 = (5, 7, 12, 14)
+EARLY_X = {5: 0, 6: 1, 8: 2, 9: 4, 10: 5, 13: 6, 14: 7, 15: 9}
+EARLY_Y = {4: 0, 6: 2, 9: 4, 12: 5, 13: 7, 14: 8, 15: 10}
+LAG = (8, 6, 7)
 
 
 def where_plan(plan, kinds):
@@ -644,7 +644,7 @@
     def write(j):
         return pltpu.make_async_copy(view(j % slots, jobs[j][2]), jobs[j][1], wsem.at[j % slots])
 
-    ahead = slots // 2
+    ahead = slots
     for j in range(min(ahead, len(jobs))):
         read(j).start()
     for j in range(len(jobs)):
@@ -697,11 +697,12 @@
         )(doc_id, query.reshape(nb, rows, hd), grad_out.reshape(nb, rows, hd), keys.reshape(nb, piece, hd), values.reshape(nb, piece, hd))
         outs = [x.reshape(nb, -1, hd) for x in outs[:4]]
         o, dq, dk, dv = pl.pallas_call(
-            functools.partial(place_kernel, 24),
+            functools.partial(place_kernel, 36),
             in_specs=[ANY] * 4,
             out_specs=[ANY] * 4,
             out_shape=[shape(x.shape, bf) for x in outs],
-            scratch_shapes=[pltpu.VMEM((24, 2048, hd), bf), dma((24,)), dma((24,))],
+            scratch_shapes=[pltpu.VMEM((36, 2048, hd), bf), dma((36,)), dma((36,))],
+            compiler_params=pltpu.CompilerParams(vmem_limit_bytes=48 * 1024 * 1024),
             name="place",
         )(*outs)
         return o.reshape(query.shape), dq.reshape(query.shape), dk.reshape(keys.shape), dv.reshape(values.shape)

time: 336 us -> 336 us (level)
  Pallas kernels: 334 us -> 330 us
where the time goes in v14:
time: 336 us; the launch traced here: 334 us
  Pallas kernels  330 us (98%)
    pallas_call x1, Pallas kernels, per_device(): pl.pallas_call(functools.partial(fused_kernel, hd ** (-0.5)), in_specs=[V...  306 us
    pallas_call x1, Pallas kernels, per_device(): pl.pallas_call(functools.partial(place_kernel, 36), in_specs=[ANY] * 4, o...  24.5 us

profile of v14, /device:TPU:0, one launch (start us, length us, event | category | flops | bytes accessed | tf_op | source)
XLA Modules:
  0.0 334.5 jit_solution(15808361246357655828)
XLA Ops:
  0.6 306.0 %attend.1 = (bf16[32,1024,256]{2,1,0:T(8,128)(2,1)}, bf16[32,1024,256]{2,1,0:T(8,128)(2,1)}, bf16[32,128,256]{2,1,0:T(8,128)(2,1)}, bf16[32,128,256]{2,1,0:T(8,1...) custom-call(s32[32,128]{1,0:T(8,128)} %doc.1, ...), custom_call_target="tpu_custom_call" | custom-call | tf_op jit(solution)/shard_map/attend/pallas_call | solution.py:676
  306.6 0.0 copy-start
  306.7 1.6 copy-done
  308.2 0.0 copy-start.1
  308.2 1.6 copy-done.1
  309.8 24.5 %place.1 = (bf16[32,1024,256]{2,1,0:T(8,128)(2,1)}, bf16[32,1024,256]{2,1,0:T(8,128)(2,1)}, bf16[32,128,256]{2,1,0:T(8,128)(2,1)}, bf16[32,128,256]{2,1,0:T(8,128)(2,1)}) custom-call(bf16[32,1024,256]{2,1,0:T(8,128)(2,1)} %get-tuple-element.12.refs_0_, bf16[32,1024,256]{2,1,0:T(8,128)(2,1)} %get-tuple-element.13.refs_1_, bf16[32,128,256]{2,1,0:T(8,128)(2,1)S(1)} %copy-done, ...), custom_call_target="tpu_custom_call" | custom-call | tf_op jit(solution)/shard_map/place/pallas_call | solution.py:699
Async XLA Ops:
  306.6 1.6 copy-start
  308.2 1.6 copy-start.1

commit v15 on v14

--- a/solution.py
+++ b/solution.py
@@ -627,22 +627,14 @@
 
 def place_kernel(slots, *refs):
     srcs, dsts, (buf, rsem, wsem) = refs[:4], refs[4:8], refs[8:]
-    jobs = []
-    for src, dst in zip(srcs, dsts):
-        n = src.shape[0]
-        size = 512 * 1024 // (src.shape[1] * src.shape[2])
-        for i in range(0, n, size):
-            shape = (size,) + tuple(src.shape[1:])
-            jobs.append((src.at[pl.ds(i, size)], dst.at[pl.ds(i, size)], shape))
-
-    def view(slot, shape):
-        return buf.at[slot].reshape(shape)
+    size = buf.shape[1]
+    jobs = [(src.at[pl.ds(i, size)], dst.at[pl.ds(i, size)]) for src, dst in zip(srcs, dsts) for i in range(0, src.shape[0], size)]
 
     def read(j):
-        return pltpu.make_async_copy(jobs[j][0], view(j % slots, jobs[j][2]), rsem.at[j % slots])
+        return pltpu.make_async_copy(jobs[j][0], buf.at[j % slots], rsem.at[j % slots])
 
     def write(j):
-        return pltpu.make_async_copy(view(j % slots, jobs[j][2]), jobs[j][1], wsem.at[j % slots])
+        return pltpu.make_async_copy(buf.at[j % slots], jobs[j][1], wsem.at[j % slots])
 
     ahead = slots
     for j in range(min(ahead, len(jobs))):
@@ -695,14 +687,14 @@
             compiler_params=pltpu.CompilerParams(has_side_effects=True, vmem_limit_bytes=62 * 1024 * 1024),
             name="attend",
         )(doc_id, query.reshape(nb, rows, hd), grad_out.reshape(nb, rows, hd), keys.reshape(nb, piece, hd), values.reshape(nb, piece, hd))
-        outs = [x.reshape(nb, -1, hd) for x in outs[:4]]
+        outs = [x.reshape(-1, rows, hd) for x in outs[:4]]
         o, dq, dk, dv = pl.pallas_call(
             functools.partial(place_kernel, 36),
             in_specs=[ANY] * 4,
             out_specs=[ANY] * 4,
             out_shape=[shape(x.shape, bf) for x in outs],
-            scratch_shapes=[pltpu.VMEM((36, 2048, hd), bf), dma((36,)), dma((36,))],
-            compiler_params=pltpu.CompilerParams(vmem_limit_bytes=48 * 1024 * 1024),
+            scratch_shapes=[pltpu.VMEM((36, 2, rows, hd), bf), dma((36,)), dma((36,))],
+            compiler_params=pltpu.CompilerParams(vmem_limit_bytes=63 * 1024 * 1024),
             name="place",
         )(*outs)
         return o.reshape(query.shape), dq.reshape(query.shape), dk.reshape(keys.shape), dv.reshape(values.shape)

time: 336 us -> 334 us (level)
  no operation moved by 1% of the time
where the time goes in v15:
time: 334 us; the launch traced here: 333 us
  Pallas kernels  332 us (99%)
    pallas_call x1, Pallas kernels, per_device(): pl.pallas_call(functools.partial(fused_kernel, hd ** (-0.5)), in_specs=[V...  306 us
    pallas_call x1, Pallas kernels, per_device(): pl.pallas_call(functools.partial(place_kernel, 36), in_specs=[ANY] * 4, o...  25.9 us

profile of v15, /device:TPU:0, one launch (start us, length us, event | category | flops | bytes accessed | tf_op | source)
XLA Modules:
  0.0 332.7 jit_solution(15721028798661693009)
XLA Ops:
  0.6 306.0 %attend.1 = (bf16[32,1024,256]{2,1,0:T(8,128)(2,1)}, bf16[32,1024,256]{2,1,0:T(8,128)(2,1)}, bf16[32,128,256]{2,1,0:T(8,128)(2,1)}, bf16[32,128,256]{2,1,0:T(8,1...) custom-call(s32[32,128]{1,0:T(8,128)} %doc.1, ...), custom_call_target="tpu_custom_call" | custom-call | tf_op jit(solution)/shard_map/attend/pallas_call | solution.py:668
  306.6 25.9 %place.1 = (bf16[32,1024,256]{2,1,0:T(8,128)(2,1)}, bf16[32,1024,256]{2,1,0:T(8,128)(2,1)}, bf16[4,1024,256]{2,1,0:T(8,128)(2,1)}, bf16[4,1024,256]{2,1,0:T(8,128)(2,1)}) custom-call(bf16[32,1024,256]{2,1,0:T(8,128)(2,1)} %get-tuple-element.12.refs_0_, bf16[32,1024,256]{2,1,0:T(8,128)(2,1)} %get-tuple-element.13.refs_1_, bf16[4,1024,256]{2,1,0:T(8,128)(2,1)} %bitcast.18, ...), custom_call_target="tpu_custom_call" | custom-call | tf_op jit(solution)/shard_map/place/pallas_call | solution.py:691

commit v16 on v15

--- a/solution.py
+++ b/solution.py
@@ -13,12 +13,14 @@
 NJ = NS
 AHEAD = 2
 NG = 4
-PLAN1 = 'RMRMRRFRRFRFFRMM'
-PLAN0 = 'NNNANCNNACCNCNNN'
-LAST2 = (5, 7, 12, 14)
-EARLY_X = {5: 0, 6: 1, 8: 2, 9: 4, 10: 5, 13: 6, 14: 7, 15: 9}
-EARLY_Y = {4: 0, 6: 2, 9: 4, 12: 5, 13: 7, 14: 8, 15: 10}
-LAG = (8, 6, 7)
+PLAN1 = 'RRRMFMRRFRFRRMMM'
+PLAN0 = 'NNANANCCNCNNCNNA'
+LAST2 = (8, 9, 11)
+EARLY_X = {6: 0, 8: 1, 10: 3, 12: 5, 13: 6, 14: 7}
+EARLY_Y = {5: 0, 7: 1, 9: 2, 10: 6, 13: 7, 14: 9, 15: 11}
+LAG = (6, 8, 7)
+LATE_CHIP = 2
+VIA3 = (0, 1)
 
 
 def where_plan(plan, kinds):
@@ -94,9 +96,10 @@
             send_kv(1, 0, j)
             send_kv(2, 1, j)
 
-        @pl.when(c == 1)
-        def _():
-            send_kv(0, 1, j)
+        if not isinstance(j, int) or j not in VIA3:
+            @pl.when(c == 1)
+            def _():
+                send_kv(0, 1, j)
 
         @pl.when(c == 2)
         def _():
@@ -126,12 +129,28 @@
     for i in range(1, n_dev):
         doc_copy(i).wait()
 
+    def member(s, group):
+        out = jnp.bool_(False)
+        for one in group:
+            out = out | (s == one)
+        return out
+
+    def by_way_of_3(j):
+        @pl.when(c == 3)
+        def _():
+            kv_forward(1, 1, j).wait_recv()
+            kv_forward(1, 2, j).start()
+
     def arrive(j):
         remote(kvr.at[c, pl.ds(j, 1), :, pl.ds(0, 128)], kvr.at[c, pl.ds(j, 1), :, pl.ds(0, 128)],
                hop_s, kv_r.at[c, j], mate).wait_recv()
         remote(qgm.at[pl.ds(j, 1)], qgm.at[pl.ds(j, 1)], hop_s, q_r.at[j], mate).wait_recv()
         for a in range(3):
-            @pl.when(a < c)
+            need = a < c
+            if a == 1:
+                need = need & jnp.logical_not((c == 3) & member(j, VIA3))
+
+            @pl.when(need)
             def _():
                 kv_forward(a, a, j).wait_recv()
 
@@ -143,7 +162,7 @@
             def _():
                 send_kv(3, 0, j + 1)
 
-        @pl.when(c == 0)
+        @pl.when((c == 0) & jnp.logical_not(member(j, VIA3)))
         def _():
             kv_forward(1, 1, j).wait_recv()
             kv_forward(1, 2, j).start()
@@ -195,12 +214,6 @@
 
     def give(sl, d, chip, slot, s):
         return remote(dkv.at[sl, d], part.at[slot, s], gsem.at[sl, d], part_r.at[slot, s], dev(chip))
-
-    def member(s, group):
-        out = jnp.bool_(False)
-        for one in group:
-            out = out | (s == one)
-        return out
 
     def rank_in(s, group):
         count = jnp.int32(0)
@@ -465,16 +478,21 @@
     for d in range(1, 4):
         f_scr[d] = jnp.full((2, 1024, 128), NEG_BIG, jnp.float32)
         l_scr[d] = jnp.zeros((2, 1024, 128), jnp.float32)
+    by_way_of_3(VIA3[0])
     arrive(0)
+    for j in VIA3[1:]:
+        by_way_of_3(j)
     fetch(0, 0)
 
     def step(s, x):
         slot = lax.rem(s, 2)
 
-        @pl.when(s + 1 < NS)
-        def _():
+        late = (c >= LATE_CHIP) & (s == 0)
+
+        def ahead():
             arrive(s + 1)
             fetch(s + 1, 1 - slot)
+        pl.when((s + 1 < NS) & jnp.logical_not(late))(ahead)
 
         @pl.when(s >= 2)
         def _():
@@ -522,6 +540,7 @@
             pl.when((c == 1) & (s == at))(lambda: pass_x(i))
         for at, i in EARLY_Y.items():
             pl.when((c == 2) & (s == at))(lambda: pass_y(i))
+        pl.when(late)(ahead)
         return x
 
     lax.fori_loop(0, NS, step, 0)
@@ -581,7 +600,8 @@
             relay(s).wait_send()
         for sl in range(2):
             passed(0, sl, 1, 2).wait_send()
-        remote(kvr.at[1], kvr.at[1], hop_s, kv_r.at[0, 0], mate).wait_send()
+        sent = kvr.at[1, pl.ds(0, NS - len(VIA3))]
+        remote(sent, sent, hop_s, kv_r.at[0, 0], mate).wait_send()
         final_drain(0, HERE0, None)
         down_wait(len(PASS_0))
 
@@ -604,14 +624,17 @@
 
     @pl.when(c == 3)
     def _():
+        sent = kvr.at[1, pl.ds(0, len(VIA3))]
+        remote(sent, sent, hop_s, kv_r.at[0, 0], mate).wait_send()
         final_drain(0, OWN3, None)
         final_drain(1, FAR1, 1)
         final_drain(2, LAST2, 2)
     for which, ref in ((0, k), (1, v)):
-        for way in range(2):
-            @pl.when((c < 2) | ((c == 2) & (way == 0)))
-            def _():
-                remote(ref, ref, kv_s.at[way, which], kv_r.at[0, 0], mate).wait_send()
+        some = ref.at[pl.ds(0, 2 * (NS - len(VIA3)))]
+        for way, chips, sent in ((0, c < 3, ref), (1, c == 0, ref), (1, c == 1, some)):
+            @pl.when(chips)
+            def _():
+                remote(sent, sent, kv_s.at[way, which], kv_r.at[0, 0], mate).wait_send()
         half = ref.at[pl.ds(other, NS)]
         remote(half, half, kv_s.at[2, which], kv_r.at[0, 0], mate).wait_send()
     for which, ref in ((0, q), (1, g)):

time: 334 us -> 328 us (0.982)
  Pallas kernels: 332 us -> 326 us
    pallas_call x1, Pallas kernels: 306 us -> 300 us  [per_device(): pl.pallas_call(functools.partial(fused_kernel, hd ** (-0.5)), in_specs=[V...]
where the time goes in v16:
time: 328 us; the launch traced here: 327 us
  Pallas kernels  326 us (99%)
    pallas_call x1, Pallas kernels, per_device(): pl.pallas_call(functools.partial(fused_kernel, hd ** (-0.5)), in_specs=[V...  300 us
    pallas_call x1, Pallas kernels, per_device(): pl.pallas_call(functools.partial(place_kernel, 36), in_specs=[ANY] * 4, o...  25.9 us

profile of v16, /device:TPU:0, one launch (start us, length us, event | category | flops | bytes accessed | tf_op | source)
XLA Modules:
  0.0 327.0 jit_solution(2353460940187231423)
XLA Ops:
  0.6 300.4 %attend.1 = (bf16[32,1024,256]{2,1,0:T(8,128)(2,1)}, bf16[32,1024,256]{2,1,0:T(8,128)(2,1)}, bf16[32,128,256]{2,1,0:T(8,128)(2,1)}, bf16[32,128,256]{2,1,0:T(8,1...) custom-call(s32[32,128]{1,0:T(8,128)} %doc.1, ...), custom_call_target="tpu_custom_call" | custom-call | tf_op jit(solution)/shard_map/attend/pallas_call | solution.py:691
  301.0 25.9 %place.1 = (bf16[32,1024,256]{2,1,0:T(8,128)(2,1)}, bf16[32,1024,256]{2,1,0:T(8,128)(2,1)}, bf16[4,1024,256]{2,1,0:T(8,128)(2,1)}, bf16[4,1024,256]{2,1,0:T(8,128)(2,1)}) custom-call(bf16[32,1024,256]{2,1,0:T(8,128)(2,1)} %get-tuple-element.12.refs_0_, bf16[32,1024,256]{2,1,0:T(8,128)(2,1)} %get-tuple-element.13.refs_1_, bf16[4,1024,256]{2,1,0:T(8,128)(2,1)} %bitcast.18, ...), custom_call_target="tpu_custom_call" | custom-call | tf_op jit(solution)/shard_map/place/pallas_call | solution.py:714

commit v17 on v16

--- a/solution.py
+++ b/solution.py
@@ -13,12 +13,12 @@
 NJ = NS
 AHEAD = 2
 NG = 4
-PLAN1 = 'RRRMFMRRFRFRRMMM'
+PLAN1 = 'RMRMFRRRFRFRRMMM'
 PLAN0 = 'NNANANCCNCNNCNNA'
 LAST2 = (8, 9, 11)
-EARLY_X = {6: 0, 8: 1, 10: 3, 12: 5, 13: 6, 14: 7}
-EARLY_Y = {5: 0, 7: 1, 9: 2, 10: 6, 13: 7, 14: 9, 15: 11}
-LAG = (6, 8, 7)
+EARLY_X = {5: 0, 7: 1, 10: 3, 12: 5, 13: 6, 14: 7, 15: 8}
+EARLY_Y = {5: 0, 7: 2, 9: 5, 11: 6, 13: 7, 14: 9, 15: 11}
+LAG = (8, 8, 6)
 LATE_CHIP = 2
 VIA3 = (0, 1)
 

time: 328 us -> 328 us (level)
  no operation moved by 1% of the time
where the time goes in v17:
time: 328 us; the launch traced here: 327 us
  Pallas kernels  327 us (100%)
    pallas_call x1, Pallas kernels, per_device(): pl.pallas_call(functools.partial(fused_kernel, hd ** (-0.5)), in_specs=[V...  301 us
    pallas_call x1, Pallas kernels, per_device(): pl.pallas_call(functools.partial(place_kernel, 36), in_specs=[ANY] * 4, o...  25.9 us

profile of v17, /device:TPU:0, one launch (start us, length us, event | category | flops | bytes accessed | tf_op | source)
XLA Modules:
  0.0 327.4 jit_solution(6306899668013853189)
XLA Ops:
  0.6 300.7 %attend.1 = (bf16[32,1024,256]{2,1,0:T(8,128)(2,1)}, bf16[32,1024,256]{2,1,0:T(8,128)(2,1)}, bf16[32,128,256]{2,1,0:T(8,128)(2,1)}, bf16[32,128,256]{2,1,0:T(8,1...) custom-call(s32[32,128]{1,0:T(8,128)} %doc.1, ...), custom_call_target="tpu_custom_call" | custom-call | tf_op jit(solution)/shard_map/attend/pallas_call | solution.py:691
  301.3 25.9 %place.1 = (bf16[32,1024,256]{2,1,0:T(8,128)(2,1)}, bf16[32,1024,256]{2,1,0:T(8,128)(2,1)}, bf16[4,1024,256]{2,1,0:T(8,128)(2,1)}, bf16[4,1024,256]{2,1,0:T(8,128)(2,1)}) custom-call(bf16[32,1024,256]{2,1,0:T(8,128)(2,1)} %get-tuple-element.12.refs_0_, bf16[32,1024,256]{2,1,0:T(8,128)(2,1)} %get-tuple-element.13.refs_1_, bf16[4,1024,256]{2,1,0:T(8,128)(2,1)} %bitcast.18, ...), custom_call_target="tpu_custom_call" | custom-call | tf_op jit(solution)/shard_map/place/pallas_call | solution.py:714

commit v18 on v16

--- a/solution.py
+++ b/solution.py
@@ -659,7 +659,7 @@
     def write(j):
         return pltpu.make_async_copy(buf.at[j % slots], jobs[j][1], wsem.at[j % slots])
 
-    ahead = slots
+    ahead = 10
     for j in range(min(ahead, len(jobs))):
         read(j).start()
     for j in range(len(jobs)):
@@ -712,11 +712,11 @@
         )(doc_id, query.reshape(nb, rows, hd), grad_out.reshape(nb, rows, hd), keys.reshape(nb, piece, hd), values.reshape(nb, piece, hd))
         outs = [x.reshape(-1, rows, hd) for x in outs[:4]]
         o, dq, dk, dv = pl.pallas_call(
-            functools.partial(place_kernel, 36),
+            functools.partial(place_kernel, 14),
             in_specs=[ANY] * 4,
             out_specs=[ANY] * 4,
             out_shape=[shape(x.shape, bf) for x in outs],
-            scratch_shapes=[pltpu.VMEM((36, 2, rows, hd), bf), dma((36,)), dma((36,))],
+            scratch_shapes=[pltpu.VMEM((14, 4, rows, hd), bf), dma((14,)), dma((14,))],
             compiler_params=pltpu.CompilerParams(vmem_limit_bytes=63 * 1024 * 1024),
             name="place",
         )(*outs)

time: 328 us -> 327 us (level)
  no operation moved by 1% of the time
where the time goes in v18:
time: 327 us; the launch traced here: 326 us
  Pallas kernels  326 us (100%)
    pallas_call x1, Pallas kernels, per_device(): pl.pallas_call(functools.partial(fused_kernel, hd ** (-0.5)), in_specs=[V...  300 us
    pallas_call x1, Pallas kernels, per_device(): pl.pallas_call(functools.partial(place_kernel, 14), in_specs=[ANY] * 4, o...  25.4 us

profile of v18, /device:TPU:0, one launch (start us, length us, event | category | flops | bytes accessed | tf_op | source)
XLA Modules:
  0.0 326.4 jit_solution(18308588040187568540)
XLA Ops:
  0.6 300.4 %attend.1 = (bf16[32,1024,256]{2,1,0:T(8,128)(2,1)}, bf16[32,1024,256]{2,1,0:T(8,128)(2,1)}, bf16[32,128,256]{2,1,0:T(8,128)(2,1)}, bf16[32,128,256]{2,1,0:T(8,1...) custom-call(s32[32,128]{1,0:T(8,128)} %doc.1, ...), custom_call_target="tpu_custom_call" | custom-call | tf_op jit(solution)/shard_map/attend/pallas_call | solution.py:691
  301.0 25.4 %place.1 = (bf16[32,1024,256]{2,1,0:T(8,128)(2,1)}, bf16[32,1024,256]{2,1,0:T(8,128)(2,1)}, bf16[4,1024,256]{2,1,0:T(8,128)(2,1)}, bf16[4,1024,256]{2,1,0:T(8,128)(2,1)}) custom-call(bf16[32,1024,256]{2,1,0:T(8,128)(2,1)} %get-tuple-element.12.refs_0_, bf16[32,1024,256]{2,1,0:T(8,128)(2,1)} %get-tuple-element.13.refs_1_, bf16[4,1024,256]{2,1,0:T(8,128)(2,1)} %bitcast.18, ...), custom_call_target="tpu_custom_call" | custom-call | tf_op jit(solution)/shard_map/place/pallas_call | solution.py:714

commit v19 on v18

--- a/solution.py
+++ b/solution.py
@@ -249,7 +249,9 @@
         def _():
             choose(member(s, ROUND), lambda: local(1, 0), lambda: away(1, 3, 0))
             choose(member(s, LAST2), lambda: away(0, 3, 1), lambda: local(0, 1))
-            choose(member(s, ON2), lambda: local(2, 2), lambda: away(2, 0, 1))
+            pl.when(member(s, ON2))(lambda: local(2, 2))
+            if not begin:
+                pl.when(jnp.logical_not(member(s, ON2)))(lambda: away(2, 0, 1))
 
         if not begin:
             @pl.when(c == 3)
@@ -323,12 +325,12 @@
         def g_of(role):
             return qg[slot, 2 + role]
 
-        def far_loop(body):
+        def far_loop(body, down=False):
             for chip in range(1, 4):
                 @pl.when(c == chip)
                 def _():
-                    for d in range(1, chip + 1):
-                        body(d, 0)
+                    for d in (range(chip, 0, -1) if down else range(1, chip + 1)):
+                        body(d, d == chip)
 
         def scores(role, d, causal):
             sc = dot_nt(qg[slot, role], kvs[slot, d, 0]) * cs
@@ -411,16 +413,22 @@
             dkv[gslot, d, :, :256] = dot_tn(out[0], qg[slot, 0]) + dot_tn(out[1], qg[slot, 1])
             return [dot_nn(ds, kvs[slot, d, 0]) for ds in out]
 
+        def far_grads(d, farthest):
+            got = score_grads(d)
+            for role in range(2):
+                o_acc[role] = got[role] if farthest else o_acc[role] + got[role]
+            if farthest and d == 3:
+                give(gslot, 3, 1, 0, s).start()
+            if farthest and d == 2:
+                pl.when(jnp.logical_not(member(s, ON2)))(lambda: give(gslot, 2, 0, 1, s).start())
+        far_loop(far_grads, down=True)
+
+        @pl.when(c == 0)
+        def _():
+            o_acc[...] = jnp.zeros_like(o_acc)
         got = score_grads(0)
         for role in range(2):
-            o_acc[role] = got[role]
-
-        def far_grads(d, x):
-            got = score_grads(d)
-            for role in range(2):
-                o_acc[role] = o_acc[role] + got[role]
-            return x
-        far_loop(far_grads)
+            o_acc[role] = o_acc[role] + got[role]
         for role in range(2):
             outb[slot, 2 + role] = (o_acc[role] * scale).astype(jnp.bfloat16)
 
@@ -507,7 +515,6 @@
         @pl.when(c == 3)
         def _():
             gslot = lax.rem(s, NG)
-            give(gslot, 3, 1, 0, s).start()
             pl.when(member(s, ROUND))(lambda: give(gslot, 2, 2, 0, s).start())
 
             @pl.when(member(s, MERGE))

time: 327 us -> 327 us (level)
  no operation moved by 1% of the time
where the time goes in v19:
time: 327 us; the launch traced here: 326 us
  Pallas kernels  326 us (100%)
    pallas_call x1, Pallas kernels, per_device(): pl.pallas_call(functools.partial(fused_kernel, hd ** (-0.5)), in_specs=[V...  300 us
    pallas_call x1, Pallas kernels, per_device(): pl.pallas_call(functools.partial(place_kernel, 14), in_specs=[ANY] * 4, o...  25.4 us

profile of v19, /device:TPU:0, one launch (start us, length us, event | category | flops | bytes accessed | tf_op | source)
XLA Modules:
  0.0 326.2 jit_solution(18054221724578449970)
XLA Ops:
  0.6 300.1 %attend.1 = (bf16[32,1024,256]{2,1,0:T(8,128)(2,1)}, bf16[32,1024,256]{2,1,0:T(8,128)(2,1)}, bf16[32,128,256]{2,1,0:T(8,128)(2,1)}, bf16[32,128,256]{2,1,0:T(8,1...) custom-call(s32[32,128]{1,0:T(8,128)} %doc.1, ...), custom_call_target="tpu_custom_call" | custom-call | tf_op jit(solution)/shard_map/attend/pallas_call | solution.py:698
  300.7 25.4 %place.1 = (bf16[32,1024,256]{2,1,0:T(8,128)(2,1)}, bf16[32,1024,256]{2,1,0:T(8,128)(2,1)}, bf16[4,1024,256]{2,1,0:T(8,128)(2,1)}, bf16[4,1024,256]{2,1,0:T(8,128)(2,1)}) custom-call(bf16[32,1024,256]{2,1,0:T(8,128)(2,1)} %get-tuple-element.12.refs_0_, bf16[32,1024,256]{2,1,0:T(8,128)(2,1)} %get-tuple-element.13.refs_1_, bf16[4,1024,256]{2,1,0:T(8,128)(2,1)} %bitcast.18, ...), custom_call_target="tpu_custom_call" | custom-call | tf_op jit(solution)/shard_map/place/pallas_call | solution.py:721

commit v20 on v19

--- a/solution.py
+++ b/solution.py
@@ -13,12 +13,12 @@
 NJ = NS
 AHEAD = 2
 NG = 4
-PLAN1 = 'RRRMFMRRFRFRRMMM'
+PLAN1 = 'RMRMFRRRFRFRRMMM'
 PLAN0 = 'NNANANCCNCNNCNNA'
 LAST2 = (8, 9, 11)
-EARLY_X = {6: 0, 8: 1, 10: 3, 12: 5, 13: 6, 14: 7}
-EARLY_Y = {5: 0, 7: 1, 9: 2, 10: 6, 13: 7, 14: 9, 15: 11}
-LAG = (6, 8, 7)
+EARLY_X = {5: 0, 7: 1, 10: 3, 12: 5, 13: 6, 14: 7, 15: 8}
+EARLY_Y = {5: 0, 7: 2, 9: 5, 11: 6, 13: 7, 14: 9, 15: 11}
+LAG = (2, 8, 7)
 LATE_CHIP = 2
 VIA3 = (0, 1)
 

time: 327 us -> 328 us (level)
  no operation moved by 1% of the time
where the time goes in v20:
time: 328 us; the launch traced here: 327 us
  Pallas kernels  326 us (99%)
    pallas_call x1, Pallas kernels, per_device(): pl.pallas_call(functools.partial(fused_kernel, hd ** (-0.5)), in_specs=[V...  301 us
    pallas_call x1, Pallas kernels, per_device(): pl.pallas_call(functools.partial(place_kernel, 14), in_specs=[ANY] * 4, o...  25.4 us

profile of v20, /device:TPU:0, one launch (start us, length us, event | category | flops | bytes accessed | tf_op | source)
XLA Modules:
  0.0 326.6 jit_solution(9102129276947005512)
XLA Ops:
  0.6 300.5 %attend.1 = (bf16[32,1024,256]{2,1,0:T(8,128)(2,1)}, bf16[32,1024,256]{2,1,0:T(8,128)(2,1)}, bf16[32,128,256]{2,1,0:T(8,128)(2,1)}, bf16[32,128,256]{2,1,0:T(8,1...) custom-call(s32[32,128]{1,0:T(8,128)} %doc.1, ...), custom_call_target="tpu_custom_call" | custom-call | tf_op jit(solution)/shard_map/attend/pallas_call | solution.py:698
  301.2 25.4 %place.1 = (bf16[32,1024,256]{2,1,0:T(8,128)(2,1)}, bf16[32,1024,256]{2,1,0:T(8,128)(2,1)}, bf16[4,1024,256]{2,1,0:T(8,128)(2,1)}, bf16[4,1024,256]{2,1,0:T(8,128)(2,1)}) custom-call(bf16[32,1024,256]{2,1,0:T(8,128)(2,1)} %get-tuple-element.12.refs_0_, bf16[32,1024,256]{2,1,0:T(8,128)(2,1)} %get-tuple-element.13.refs_1_, bf16[4,1024,256]{2,1,0:T(8,128)(2,1)} %bitcast.18, ...), custom_call_target="tpu_custom_call" | custom-call | tf_op jit(solution)/shard_map/place/pallas_call | solution.py:721

commit v21 on v19

--- a/solution.py
+++ b/solution.py
@@ -472,9 +472,9 @@
 
     def total(kind, group, s, held, slots, chip):
         terms = [hold.at[held, s]] + [part.at[slot, s] for slot in slots]
-        for slot in slots:
-            part_wait(slot, s)
         for n, src in enumerate(terms):
+            if n:
+                part_wait(slots[n - 1], s)
             start(load(src, n))
         for n, src in enumerate(terms):
             finish(load(src, n))

time: 327 us -> 327 us (level)
  no operation moved by 1% of the time
where the time goes in v21:
time: 327 us; the launch traced here: 326 us
  Pallas kernels  326 us (100%)
    pallas_call x1, Pallas kernels, per_device(): pl.pallas_call(functools.partial(fused_kernel, hd ** (-0.5)), in_specs=[V...  300 us
    pallas_call x1, Pallas kernels, per_device(): pl.pallas_call(functools.partial(place_kernel, 14), in_specs=[ANY] * 4, o...  25.4 us

profile of v21, /device:TPU:0, one launch (start us, length us, event | category | flops | bytes accessed | tf_op | source)
XLA Modules:
  0.0 326.5 jit_solution(15341441112614494862)
XLA Ops:
  0.6 300.4 %attend.1 = (bf16[32,1024,256]{2,1,0:T(8,128)(2,1)}, bf16[32,1024,256]{2,1,0:T(8,128)(2,1)}, bf16[32,128,256]{2,1,0:T(8,128)(2,1)}, bf16[32,128,256]{2,1,0:T(8,1...) custom-call(s32[32,128]{1,0:T(8,128)} %doc.1, ...), custom_call_target="tpu_custom_call" | custom-call | tf_op jit(solution)/shard_map/attend/pallas_call | solution.py:698
  301.1 25.4 %place.1 = (bf16[32,1024,256]{2,1,0:T(8,128)(2,1)}, bf16[32,1024,256]{2,1,0:T(8,128)(2,1)}, bf16[4,1024,256]{2,1,0:T(8,128)(2,1)}, bf16[4,1024,256]{2,1,0:T(8,128)(2,1)}) custom-call(bf16[32,1024,256]{2,1,0:T(8,128)(2,1)} %get-tuple-element.12.refs_0_, bf16[32,1024,256]{2,1,0:T(8,128)(2,1)} %get-tuple-element.13.refs_1_, bf16[4,1024,256]{2,1,0:T(8,128)(2,1)} %bitcast.18, ...), custom_call_target="tpu_custom_call" | custom-call | tf_op jit(solution)/shard_map/place/pallas_call | solution.py:721
